TPU v7x, 32 devices: a whole 2x2x4 slice. The times are simulated.
32 devices in a mesh: dp: 8 (over z, core), tensor: 4 (over y, x).
Axes of the slice: x: 2, y: 2, z: 4, core: 2. Of those that a mesh axis runs over, the one named last changes fastest.
Arguments:
- block_input: bfloat16 [8192, 2048], P(('dp', 'tensor')), may hold values from -6 to 6
- attention_gain: float32 [2048], replicated, may hold values from 0.1 to 1.9
- query_weight: bfloat16 [2048, 2048], P('dp', 'tensor'), may hold values from -0.125 to 0.125
- key_matrix: bfloat16 [2048, 1024], P('dp', 'tensor'), may hold values from -0.125 to 0.125
- value_matrix: bfloat16 [2048, 1024], P('dp', 'tensor'), may hold values from -0.125 to 0.125
- query_gain: float32 [128], replicated, may hold values from 0.4 to 2
- key_gain: float32 [128], replicated, may hold values from 0.4 to 2
- output_weight: bfloat16 [2048, 2048], P('tensor', 'dp'), may hold values from -1 to 1
- feed_gain: float32 [2048], replicated, may hold values from 0.1 to 1.9
- gate_weight: bfloat16 [2048, 6144], P('dp', 'tensor'), may hold values from -0.125 to 0.125
- up_weight: bfloat16 [2048, 6144], P('dp', 'tensor'), may hold values from -0.125 to 0.125
- down_weight: bfloat16 [6144, 2048], P('tensor', 'dp'), may hold values from -0.078125 to 0.078125
- out_cotangent: bfloat16 [8192, 2048], P(('dp', 'tensor')), may hold values from -6 to 6
Outputs:
- block_output: bfloat16 [8192, 2048], P(('dp', 'tensor'))
- input_gradient: bfloat16 [8192, 2048], P(('dp', 'tensor'))
- attention_gain_gradient: float32 [2048], replicated
- query_gradient: float32 [2048, 2048], P('dp', 'tensor')
- key_gradient: float32 [2048, 1024], P('dp', 'tensor')
- value_gradient: float32 [2048, 1024], P('dp', 'tensor')
- query_gain_gradient: float32 [128], replicated
- key_gain_gradient: float32 [128], replicated
- output_gradient: float32 [2048, 2048], P('tensor', 'dp')
- feed_gain_gradient: float32 [2048], replicated
- gate_gradient: float32 [2048, 6144], P('dp', 'tensor')
- up_gradient: float32 [2048, 6144], P('dp', 'tensor')
- down_gradient: float32 [6144, 2048], P('tensor', 'dp')
All inputs are finite; a program needn't handle non-finite values.
Results may differ from a plain program's by a relative error of at most 0.019.
Values may be sent and summed in bfloat16 or wider, within the bound.
A program may use at most 256 MiB of HBM per device.

v0:
```python
import jax
import jax.numpy as jnp
from jax import lax
from jax.sharding import PartitionSpec as P

SEQUENCE_LENGTH = 1024


epsilon = 1e-06
rope_base = 1000000.0


def row_scale(values):
    return lax.rsqrt(jnp.mean(values * values, axis=-1, keepdims=True) + epsilon)


def rotate_half(values):
    half_size = values.shape[-1] // 2
    return jnp.concatenate([-values[..., half_size:], values[..., :half_size]], axis=-1)


def rope_tables(positions, head_size):
    half_size = head_size // 2
    frequency = rope_base ** (-(jnp.arange(half_size).astype(jnp.float32) * 2.0 / head_size))
    angles = positions[:, None] * frequency[None, :]
    angles = jnp.concatenate([angles, angles], axis=1)
    return (jnp.cos(angles)[:, None, :], jnp.sin(angles)[:, None, :])


def contract_rows(first_operand, second_operand):
    return lax.dot_general(
        first_operand, second_operand, (((0,), (0,)), ((), ())), preferred_element_type=jnp.float32
    )


def times_transposed(first_operand, second_operand):
    return lax.dot_general(
        first_operand, second_operand, (((1,), (1,)), ((), ())), preferred_element_type=jnp.float32
    )


def simple_product(first_operand, second_operand):
    return jnp.dot(first_operand, second_operand, preferred_element_type=jnp.float32)


def masked_scores(query_block, key_seq, first_row):
    scale_factor = query_block.shape[-1] ** (-0.5)
    scores = (
        jnp.einsum("qhgd,khd->hgqk", query_block, key_seq, preferred_element_type=jnp.float32)
        * scale_factor
    )
    visible = (first_row + jnp.arange(query_block.shape[0]))[:, None] >= jnp.arange(
        key_seq.shape[0]
    )[None, :]
    return jnp.where(visible, scores, -1e30)


def attend_forward(query_block, key_seq, value_seq, first_row):
    scores = masked_scores(query_block, key_seq, first_row)
    highest = jnp.max(scores, axis=-1, keepdims=True)
    log_total = highest[..., 0] + jnp.log(jnp.sum(jnp.exp(scores - highest), axis=-1))
    weights = jnp.exp(scores - log_total[..., None]).astype(jnp.bfloat16)
    mixed_block = jnp.einsum(
        "hgqk,khd->qhgd", weights, value_seq, preferred_element_type=jnp.float32
    ).astype(jnp.bfloat16)
    return (mixed_block, log_total)


def attend_backward(
    query_block, key_seq, value_seq, mixed_block, slope_block, total_block, first_row
):
    scale_factor = query_block.shape[-1] ** (-0.5)
    scores = masked_scores(query_block, key_seq, first_row)
    weights = jnp.exp(scores - total_block[..., None])
    value_part = jnp.einsum(
        "hgqk,qhgd->khd",
        weights.astype(jnp.bfloat16),
        slope_block,
        preferred_element_type=jnp.float32,
    )
    weight_slope = jnp.einsum(
        "qhgd,khd->hgqk", slope_block, value_seq, preferred_element_type=jnp.float32
    )
    centre = jnp.transpose(
        jnp.sum(slope_block.astype(jnp.float32) * mixed_block.astype(jnp.float32), axis=-1),
        (1, 2, 0),
    )
    score_slope = (weights * (weight_slope - centre[..., None])).astype(jnp.bfloat16)
    query_part = (
        jnp.einsum("hgqk,khd->qhgd", score_slope, key_seq, preferred_element_type=jnp.float32)
        * scale_factor
    )
    key_part = (
        jnp.einsum("hgqk,qhgd->khd", score_slope, query_block, preferred_element_type=jnp.float32)
        * scale_factor
    )
    return (query_part, key_part, value_part)


def head_norm_back(turn_slope, cosine, sine, unit_values, scale_values, gain_values):
    norm_slope = turn_slope * cosine - rotate_half(turn_slope) * sine
    gain_term = jnp.sum(norm_slope * unit_values, axis=(0, 1))
    unit_slope = norm_slope * gain_values
    raw_slope = (
        scale_values
        * (unit_slope - unit_values * jnp.mean(unit_slope * unit_values, axis=-1, keepdims=True))
    ).astype(jnp.bfloat16)
    return (raw_slope.reshape(raw_slope.shape[0], -1), gain_term)


def per_device(
    block_input,
    attention_gain,
    query_weight,
    key_matrix,
    value_matrix,
    query_gain,
    key_gain,
    output_weight,
    feed_gain,
    gate_weight,
    up_weight,
    down_weight,
    out_cotangent,
):
    local_rows = block_input.shape[0]
    grouped_rows = local_rows * lax.axis_size("tensor")
    head_size = query_gain.shape[0]
    query_heads = query_weight.shape[1] // head_size
    value_heads = key_matrix.shape[1] // head_size
    grouping_width = query_heads // value_heads
    sequences = grouped_rows // SEQUENCE_LENGTH
    block_rows = min(512, SEQUENCE_LENGTH)
    block_count = SEQUENCE_LENGTH // block_rows
    cosine, sine = rope_tables(
        (jnp.arange(grouped_rows) % SEQUENCE_LENGTH).astype(jnp.float32), head_size
    )
    gathered = (
        lax.all_gather(query_weight, "dp", axis=0, tiled=True),
        lax.all_gather(key_matrix, "dp", axis=0, tiled=True),
        lax.all_gather(value_matrix, "dp", axis=0, tiled=True),
        lax.all_gather(output_weight, "dp", axis=1, tiled=True),
        lax.all_gather(gate_weight, "dp", axis=0, tiled=True),
        lax.all_gather(up_weight, "dp", axis=0, tiled=True),
        lax.all_gather(down_weight, "dp", axis=1, tiled=True),
    )
    query_full, key_full, value_full, output_full, gate_full, up_full, down_full = gathered
    input_float = block_input.astype(jnp.float32)
    first_scale = row_scale(input_float)
    first_unit = input_float * first_scale
    mixer_local = (first_unit * attention_gain).astype(jnp.bfloat16)
    attention_output_rows = lax.all_gather(mixer_local, "tensor", axis=0, tiled=True)
    query_raw = simple_product(attention_output_rows, query_full).reshape(
        grouped_rows, query_heads, head_size
    )
    unnormed_key = simple_product(attention_output_rows, key_full).reshape(
        grouped_rows, value_heads, head_size
    )
    value_token_rows = simple_product(attention_output_rows, value_full).astype(jnp.bfloat16)
    query_scale = row_scale(query_raw)
    query_unit = query_raw * query_scale
    query_normed = query_unit * query_gain
    rotated_query = (query_normed * cosine + rotate_half(query_normed) * sine).astype(jnp.bfloat16)
    key_norm_scale = row_scale(unnormed_key)
    normalized_key = unnormed_key * key_norm_scale
    key_normed = normalized_key * key_gain
    rotated_key = (key_normed * cosine + rotate_half(key_normed) * sine).astype(jnp.bfloat16)
    query_sequences = rotated_query.reshape(
        sequences, SEQUENCE_LENGTH, value_heads, grouping_width, head_size
    )
    key_sequences = rotated_key.reshape(sequences, SEQUENCE_LENGTH, value_heads, head_size)
    value_sequences = value_token_rows.reshape(sequences, SEQUENCE_LENGTH, value_heads, head_size)

    def forward_sequence(operands):
        query_seq, key_seq, value_seq = operands
        mixed_parts = []
        total_parts = []
        for block_index in range(block_count):
            first_row = block_index * block_rows
            mixed_block, log_total = attend_forward(
                query_seq[first_row : first_row + block_rows], key_seq, value_seq, first_row
            )
            mixed_parts.append(mixed_block)
            total_parts.append(log_total)
        return (jnp.concatenate(mixed_parts, axis=0), jnp.concatenate(total_parts, axis=-1))

    mixed_seqs, totals = lax.map(
        forward_sequence, (query_sequences, key_sequences, value_sequences)
    )
    mixed_rows = mixed_seqs.reshape(grouped_rows, query_heads * head_size)
    attention_sum = lax.psum_scatter(
        simple_product(
            lax.slice_in_dim(mixed_rows, 0, local_rows * lax.axis_size("tensor"), axis=0),
            output_full,
        ),
        "tensor",
        scatter_dimension=0,
        tiled=True,
    )
    hidden_state = input_float + attention_sum
    second_scale = row_scale(hidden_state)
    second_unit = hidden_state * second_scale
    feed_local = (second_unit * feed_gain).astype(jnp.bfloat16)
    feed_rows = lax.all_gather(feed_local, "tensor", axis=0, tiled=True)
    gate_values = simple_product(feed_rows, gate_full)
    up_values = simple_product(feed_rows, up_full)
    gate_sigmoid = jax.nn.sigmoid(gate_values)
    hidden_rows = (gate_values * gate_sigmoid * up_values).astype(jnp.bfloat16)
    feed_sum = lax.psum_scatter(
        simple_product(
            lax.slice_in_dim(hidden_rows, 0, local_rows * lax.axis_size("tensor"), axis=0),
            down_full,
        ).astype(jnp.bfloat16),
        "tensor",
        scatter_dimension=0,
        tiled=True,
    ).astype(jnp.float32)
    block_output = (hidden_state + feed_sum).astype(jnp.bfloat16)
    regathered = (
        lax.all_gather(query_weight, "dp", axis=0, tiled=True),
        lax.all_gather(key_matrix, "dp", axis=0, tiled=True),
        lax.all_gather(value_matrix, "dp", axis=0, tiled=True),
        lax.all_gather(output_weight, "dp", axis=1, tiled=True),
        lax.all_gather(gate_weight, "dp", axis=0, tiled=True),
        lax.all_gather(up_weight, "dp", axis=0, tiled=True),
        lax.all_gather(down_weight, "dp", axis=1, tiled=True),
    )
    query_back, key_back, value_back, output_back, gate_back, up_back, down_back = regathered
    cotangent_rows = lax.all_gather(out_cotangent, "tensor", axis=0, tiled=True)
    hidden_slope = times_transposed(cotangent_rows, down_back)
    down_grad = contract_rows(hidden_rows, cotangent_rows)
    gate_slope = (
        hidden_slope * up_values * gate_sigmoid * (1.0 + gate_values * (1.0 - gate_sigmoid))
    ).astype(jnp.bfloat16)
    up_slope = (hidden_slope * gate_values * gate_sigmoid).astype(jnp.bfloat16)
    gate_grad = contract_rows(feed_rows, gate_slope)
    up_grad = contract_rows(feed_rows, up_slope)
    gate_part = lax.slice_in_dim(gate_slope, 0, local_rows * lax.axis_size("tensor"), axis=0)
    up_part = lax.slice_in_dim(up_slope, 0, local_rows * lax.axis_size("tensor"), axis=0)
    feed_back = lax.psum_scatter(
        times_transposed(gate_part, gate_back) + times_transposed(up_part, up_back),
        "tensor",
        scatter_dimension=0,
        tiled=True,
    )
    feed_gain_term = jnp.sum(feed_back * second_unit, axis=0)
    feed_unit_slope = feed_back * feed_gain
    state_slope = out_cotangent.astype(jnp.float32) + second_scale * (
        feed_unit_slope
        - second_unit * jnp.mean(feed_unit_slope * second_unit, axis=-1, keepdims=True)
    )
    state_rounded = state_slope.astype(jnp.bfloat16)
    state_rows = lax.all_gather(state_rounded, "tensor", axis=0, tiled=True)
    mixed_gradient = times_transposed(state_rows, output_back).astype(jnp.bfloat16)
    output_grad = contract_rows(mixed_rows, state_rows)
    gradient_sequences = mixed_gradient.reshape(
        sequences, SEQUENCE_LENGTH, value_heads, grouping_width, head_size
    )

    def backward_sequence(operands):
        query_seq, key_seq, value_seq, mixed_seq, slope_seq, total_seq = operands
        key_total = jnp.zeros(key_seq.shape, jnp.float32)
        value_total = jnp.zeros(value_seq.shape, jnp.float32)
        query_parts = []
        for block_index in range(block_count):
            first_row = block_index * block_rows
            last_row = first_row + block_rows
            query_part, key_part, value_part = attend_backward(
                query_seq[first_row:last_row],
                key_seq,
                value_seq,
                mixed_seq[first_row:last_row],
                slope_seq[first_row:last_row],
                total_seq[..., first_row:last_row],
                first_row,
            )
            query_parts.append(query_part)
            key_total = key_total + key_part
            value_total = value_total + value_part
        return (jnp.concatenate(query_parts, axis=0), key_total, value_total.astype(jnp.bfloat16))

    query_slope, key_rows_gradient, value_rows_gradient = lax.map(
        backward_sequence,
        (query_sequences, key_sequences, value_sequences, mixed_seqs, gradient_sequences, totals),
    )
    query_raw_slope, query_gain_term = head_norm_back(
        query_slope.reshape(grouped_rows, query_heads, head_size),
        cosine,
        sine,
        query_unit,
        query_scale,
        query_gain,
    )
    unnormed_key_gradient, key_gain_term = head_norm_back(
        key_rows_gradient.reshape(grouped_rows, value_heads, head_size),
        cosine,
        sine,
        normalized_key,
        key_norm_scale,
        key_gain,
    )
    value_gradient_rows = value_rows_gradient.reshape(grouped_rows, value_heads * head_size)
    query_grad = contract_rows(attention_output_rows, query_raw_slope)
    key_grad = contract_rows(attention_output_rows, unnormed_key_gradient)
    value_grad = contract_rows(attention_output_rows, value_gradient_rows)
    query_part = lax.slice_in_dim(query_raw_slope, 0, local_rows * lax.axis_size("tensor"), axis=0)
    key_part = lax.slice_in_dim(
        unnormed_key_gradient, 0, local_rows * lax.axis_size("tensor"), axis=0
    )
    value_part = lax.slice_in_dim(
        value_gradient_rows, 0, local_rows * lax.axis_size("tensor"), axis=0
    )
    mixer_back = lax.psum_scatter(
        (
            times_transposed(query_part, query_back)
            + times_transposed(key_part, key_back)
            + times_transposed(value_part, value_back)
        ).astype(jnp.bfloat16),
        "tensor",
        scatter_dimension=0,
        tiled=True,
    ).astype(jnp.float32)
    attention_gain_term = jnp.sum(mixer_back * first_unit, axis=0)
    mixer_unit_slope = mixer_back * attention_gain
    input_gradient = (
        state_slope
        + first_scale
        * (
            mixer_unit_slope
            - first_unit * jnp.mean(mixer_unit_slope * first_unit, axis=-1, keepdims=True)
        )
    ).astype(jnp.bfloat16)
    weight_totals = (
        lax.psum_scatter(
            query_grad.astype(jnp.bfloat16), "dp", scatter_dimension=0, tiled=True
        ).astype(jnp.float32),
        lax.psum_scatter(
            key_grad.astype(jnp.bfloat16), "dp", scatter_dimension=0, tiled=True
        ).astype(jnp.float32),
        lax.psum_scatter(
            value_grad.astype(jnp.bfloat16), "dp", scatter_dimension=0, tiled=True
        ).astype(jnp.float32),
        lax.psum_scatter(
            output_grad.astype(jnp.bfloat16), "dp", scatter_dimension=1, tiled=True
        ).astype(jnp.float32),
        lax.psum_scatter(
            gate_grad.astype(jnp.bfloat16), "dp", scatter_dimension=0, tiled=True
        ).astype(jnp.float32),
        lax.psum_scatter(
            up_grad.astype(jnp.bfloat16), "dp", scatter_dimension=0, tiled=True
        ).astype(jnp.float32),
        lax.psum_scatter(
            down_grad.astype(jnp.bfloat16), "dp", scatter_dimension=1, tiled=True
        ).astype(jnp.float32),
    )
    gain_totals = lax.psum(
        (attention_gain_term, feed_gain_term, query_gain_term, key_gain_term), ("dp", "tensor")
    )
    return (
        block_output,
        input_gradient,
        gain_totals[0],
        weight_totals[0],
        weight_totals[1],
        weight_totals[2],
        gain_totals[2],
        gain_totals[3],
        weight_totals[3],
        gain_totals[1],
        weight_totals[4],
        weight_totals[5],
        weight_totals[6],
    )


def solution(mesh):
    in_specs = (
        P(("dp", "tensor"), None),
        P(),
        P("dp", "tensor"),
        P("dp", "tensor"),
        P("dp", "tensor"),
        P(),
        P(),
        P("tensor", "dp"),
        P(),
        P("dp", "tensor"),
        P("dp", "tensor"),
        P("tensor", "dp"),
        P(("dp", "tensor"), None),
    )
    out_specs = (
        P(("dp", "tensor"), None),
        P(("dp", "tensor"), None),
        P(),
        P("dp", "tensor"),
        P("dp", "tensor"),
        P("dp", "tensor"),
        P(),
        P(),
        P("tensor", "dp"),
        P(),
        P("dp", "tensor"),
        P("dp", "tensor"),
        P("tensor", "dp"),
    )
    return jax.shard_map(
        per_device, mesh=mesh, in_specs=in_specs, out_specs=out_specs, check_vma=False
    )
```

profile of v0, /device:TPU:0, one launch (start us, length us, event | category | flops | bytes accessed | tf_op | source)
XLA Modules:
  0.0 1225.7 jit_solution(7663798207786850853)
XLA Ops:
  17.2 17.3 %all-gather.16.cloned.1.call-done = bf16[2048,256]{1,0:T(8,128)(2,1)} async-done(((bf16[256,256]{1,0:T(8,128)(2,1)}), bf16[2048,256]{1,0:T(8,128)(2,1)}) %all-gather.16.cloned.1.call-update) | async-done | bytes 1048592 | tf_op jit(solution)/shard_map/all_gather | solution.py:140
  34.6 54.6 %all-gather.12.cloned.1.call-done = bf16[1024,2048]{1,0:T(8,128)(2,1)} async-done(((bf16[256,2048]{1,0:T(8,128)(2,1)}), bf16[1024,2048]{1,0:T(8,128)(2,1)}) %all-gather.12.cloned.1.call-update) | async-done | bytes 4194320 | tf_op jit(solution)/shard_map/all_gather | solution.py:152
  89.2 3.8 multiply_reduce_fusion.9
  94.4 25.6 %all-gather.18.cloned.1.call-done = bf16[2048,512]{1,0:T(8,128)(2,1)} async-done(((bf16[256,512]{1,0:T(8,128)(2,1)}), bf16[2048,512]{1,0:T(8,128)(2,1)}) %all-gather.18.cloned.1.call-update) | async-done | bytes 2097168 | tf_op jit(solution)/shard_map/all_gather | solution.py:139
  120.0 5.3 multiply_reduce_fusion.4
  138.6 4.6 all-gather.14.cloned.1.call-done
  143.1 3.9 convolution_convert_fusion.11
  147.1 6.0 fusion.35
  155.8 19.0 %all-gather.20.cloned.1.call-done = bf16[512,2048]{1,0:T(8,128)(2,1)} async-done(((bf16[512,256]{1,0:T(8,128)(2,1)}), bf16[512,2048]{1,0:T(8,128)(2,1)}) %all-gather.20.cloned.1.call-update) | async-done | bytes 2097168 | tf_op jit(solution)/shard_map/all_gather | solution.py:142
  174.8 7.3 fusion.54
  182.9 84.7 %reduce-scatter.12.cloned.1.call-done = f32[256,2048]{1,0:T(8,128)} async-done(((f32[1024,2048]{1,0:T(8,128)}), f32[256,2048]{1,0:T(8,128)}) %reduce-scatter.12.cloned.1.call-update) | async-done | bytes 2097168 | tf_op jit(solution)/shard_map/reduce_scatter | solution.py:191
  272.9 61.1 %all-gather.24.cloned.1.call-done = bf16[2048,1536]{1,0:T(8,128)(2,1)} async-done(((bf16[256,1536]{1,0:T(8,128)(2,1)}), bf16[2048,1536]{1,0:T(8,128)(2,1)}) %all-gather.24.cloned.1.call-update) | async-done | bytes 6291472 | tf_op jit(solution)/shard_map/all_gather | solution.py:143
  334.0 53.7 %all-gather.22.cloned.1.call-done = bf16[1024,2048]{1,0:T(8,128)(2,1)} async-done(((bf16[256,2048]{1,0:T(8,128)(2,1)}), bf16[1024,2048]{1,0:T(8,128)(2,1)}) %all-gather.22.cloned.1.call-update) | async-done | bytes 4194320 | tf_op jit(solution)/shard_map/all_gather | solution.py:204
  387.6 12.1 fusion.55
  399.7 54.3 %all-gather.26.cloned.1.call-done = bf16[2048,1536]{1,0:T(8,128)(2,1)} async-done(((bf16[256,1536]{1,0:T(8,128)(2,1)}), bf16[2048,1536]{1,0:T(8,128)(2,1)}) %all-gather.26.cloned.1.call-update) | async-done | bytes 6291472 | tf_op jit(solution)/shard_map/all_gather | solution.py:144
  454.0 11.7 fusion.56
  465.8 41.2 %all-gather.30.cloned.1.call-done = bf16[1024,2048]{1,0:T(8,128)(2,1)} async-done(((bf16[256,2048]{1,0:T(8,128)(2,1)}), bf16[1024,2048]{1,0:T(8,128)(2,1)}) %all-gather.30.cloned.1.call-update) | async-done | bytes 4194320 | tf_op jit(solution)/shard_map/all_gather | solution.py:229
  507.0 66.8 %all-gather.28.cloned.1.call-done = bf16[1536,2048]{1,0:T(8,128)(2,1)} async-done(((bf16[1536,256]{1,0:T(8,128)(2,1)}), bf16[1536,2048]{1,0:T(8,128)(2,1)}) %all-gather.28.cloned.1.call-update) | async-done | bytes 6291472 | tf_op jit(solution)/shard_map/all_gather | solution.py:145
  573.7 15.9 %multiply_convert_fusion = (bf16[1024,1536]{1,0:T(8,128)(2,1)S(1)}, bf16[1024,1536]{1,0:T(8,128)(2,1)S(1)}, bf16[1024,1536]{1,0:T(8,128)(2,1)}) fusion(f32[1024,1536]{1,0:T(8,128)} %fusion.55, f32[1024,1536]{1,0:T(8,128)} %fusion.56, bf16[1024,2048]{1,0:T(8,128)(2,1)} %all-gather.30.cloned.1.call-done, bf16[1536,2048]{1,0:T(8,128)(2,1)} %all-gather.28.cloned.1.call-done), kind=kOutput, calls=%fused_computation.18 | convolution fusion | flops 6467616768 | bytes 32505856 | tf_op jit(solution)/shard_map/dot_general | solution.py:37
  589.6 11.1 fusion.57
  600.8 9.1 convolution_add_fusion
  610.0 84.6 %reduce-scatter.16.cloned.1.call-done = f32[256,2048]{1,0:T(8,128)} async-done(((f32[1024,2048]{1,0:T(8,128)}), f32[256,2048]{1,0:T(8,128)}) %reduce-scatter.16.cloned.1.call-update) | async-done | bytes 2097168 | tf_op jit(solution)/shard_map/reduce_scatter | solution.py:240
  698.6 11.4 convolution_convert_fusion.2
  710.1 11.5 convolution_convert_fusion.1
  721.7 11.3 convolution_convert_fusion
  733.3 18.0 %all-gather.32.cloned.1.call-done = bf16[1024,2048]{1,0:T(8,128)(2,1)} async-done(((bf16[256,2048]{1,0:T(8,128)(2,1)}), bf16[1024,2048]{1,0:T(8,128)(2,1)}) %all-gather.32.cloned.1.call-update) | async-done | bytes 4194320 | tf_op jit(solution)/shard_map/all_gather | solution.py:253
  751.3 5.4 convolution_convert_fusion.8
  758.3 6.5 convolution_bitcast_fusion
  770.7 8.7 fusion.1
  779.4 7.0 fusion.3
  786.5 3.9 convolution_bitcast_fusion.2
  790.4 2.7 fusion.31
  798.2 6.3 convolution_convert_fusion.4
  804.8 3.3 convolution_multiply_fusion.1
  817.4 3.6 fusion.27
  821.9 3.7 convolution_convert_fusion.5
  830.9 3.4 add_convert_fusion
  834.6 11.1 convolution_convert_fusion.3
  848.4 45.2 %reduce-scatter.30.cloned.1.call-done = bf16[256,1536]{1,0:T(8,128)(2,1)} async-done(((bf16[2048,1536]{1,0:T(8,128)(2,1)}), bf16[256,1536]{1,0:T(8,128)(2,1)}) %reduce-scatter.30.cloned.1.call-update) | async-done | bytes 786448 | tf_op jit(solution)/shard_map/reduce_scatter | solution.py:349
  896.1 67.9 %reduce-scatter.32.cloned.1.call-done = bf16[1536,256]{1,0:T(8,128)(2,1)} async-done(((bf16[1536,2048]{1,0:T(8,128)(2,1)}), bf16[1536,256]{1,0:T(8,128)(2,1)}) %reduce-scatter.32.cloned.1.call-update) | async-done | bytes 786448 | tf_op jit(solution)/shard_map/reduce_scatter | solution.py:352
  966.4 30.8 %reduce-scatter.24.cloned.1.call-done = bf16[256,256]{1,0:T(8,128)(2,1)} async-done(((bf16[2048,256]{1,0:T(8,128)(2,1)}), bf16[256,256]{1,0:T(8,128)(2,1)}) %reduce-scatter.24.cloned.1.call-update) | async-done | bytes 131088 | tf_op jit(solution)/shard_map/reduce_scatter | solution.py:340
  998.8 31.4 %reduce-scatter.22.cloned.1.call-done = bf16[256,256]{1,0:T(8,128)(2,1)} async-done(((bf16[2048,256]{1,0:T(8,128)(2,1)}), bf16[256,256]{1,0:T(8,128)(2,1)}) %reduce-scatter.22.cloned.1.call-update) | async-done | bytes 131088 | tf_op jit(solution)/shard_map/reduce_scatter | solution.py:337
  1031.8 34.9 %reduce-scatter.26.cloned.1.call-done = bf16[512,256]{1,0:T(8,128)(2,1)} async-done(((bf16[512,2048]{1,0:T(8,128)(2,1)}), bf16[512,256]{1,0:T(8,128)(2,1)}) %reduce-scatter.26.cloned.1.call-update) | async-done | bytes 262160 | tf_op jit(solution)/shard_map/reduce_scatter | solution.py:343
  1068.5 35.1 %reduce-scatter.20.cloned.1.call-done = bf16[256,512]{1,0:T(8,128)(2,1)} async-done(((bf16[2048,512]{1,0:T(8,128)(2,1)}), bf16[256,512]{1,0:T(8,128)(2,1)}) %reduce-scatter.20.cloned.1.call-update) | async-done | bytes 262160 | tf_op jit(solution)/shard_map/reduce_scatter | solution.py:334
  1105.4 52.4 %reduce-scatter.18.cloned.1.call-done = bf16[256,2048]{1,0:T(8,128)(2,1)} async-done(((bf16[1024,2048]{1,0:T(8,128)(2,1)}), bf16[256,2048]{1,0:T(8,128)(2,1)}) %reduce-scatter.18.cloned.1.call-update) | async-done | bytes 1048592 | tf_op jit(solution)/shard_map/reduce_scatter | solution.py:313
  1159.8 40.1 %all-reduce = (f32[2048]{0:T(1024)}, f32[128]{0:T(128)}, f32[128]{0:T(128)}, f32[2048]{0:T(1024)}) all-reduce(f32[2048]{0:T(1024)S(1)} %get-tuple-element.53, f32[128]{0:T(128)S(1)} %reduce_sum.170, f32[128]{0:T(128)S(1)} %get-tuple-element.65, f32[2048]{0:T(1024)S(1)} %get-tuple-element.51), channel_id=1, replica_groups=mesh['dp'=8,'tensor'=4] {'dp','tensor'}, use_global_device_ids=true, to_apply=%region_19.20 | all-reduce | flops 4352 | bytes 34816 | tf_op jit(solution)/shard_map/psum | solution.py:356
  1200.0 13.7 %reduce-scatter.14.cloned.1.call-done = bf16[256,2048]{1,0:T(8,128)(2,1)} async-done(((bf16[1024,2048]{1,0:T(8,128)(2,1)}), bf16[256,2048]{1,0:T(8,128)(2,1)}) %reduce-scatter.14.cloned.1.call-update) | async-done | bytes 1048592 | tf_op jit(solution)/shard_map/reduce_scatter | solution.py:209
  1213.6 5.0 fusion.15
  (256 shorter events, 82.0 us)
Async XLA Ops:
  7.2 27.4 %all-gather.16.cloned.1.call-start = ((), (), s32[]{:S(2)}) async-start(), calls=%async_computation.13 | async-start | bytes 1179648 | tf_op jit(solution)/shard_map/all_gather | solution.py:140
  7.9 81.3 %all-gather.12.cloned.1.call-start = ((), (), s32[]{:S(2)}) async-start(), calls=%async_computation.11 | async-start | bytes 5242880 | tf_op jit(solution)/shard_map/all_gather | solution.py:152
  12.0 108.0 %all-gather.18.cloned.1.call-start = ((), (), s32[]{:S(2)}) async-start(), calls=%async_computation.14 | async-start | bytes 2359296 | tf_op jit(solution)/shard_map/all_gather | solution.py:139
  12.8 130.4 %all-gather.14.cloned.1.call-start = ((), (), s32[]{:S(2)}) async-start(), calls=%async_computation.12 | async-start | bytes 1179648 | tf_op jit(solution)/shard_map/all_gather | solution.py:141
  13.3 161.5 %all-gather.20.cloned.1.call-start = ((), (), s32[]{:S(2)}) async-start(), calls=%async_computation.15 | async-start | bytes 2359296 | tf_op jit(solution)/shard_map/all_gather | solution.py:142
  13.9 253.7 %reduce-scatter.12.cloned.1.call-start = ((), (), s32[]{:S(2)}) async-start(), calls=%async_computation.16 | async-start | bytes 10485760 | tf_op jit(solution)/shard_map/reduce_scatter | solution.py:191
  14.2 138.9 %copy-start.25 = (pred[512,1024]{0,1:T(8,128)(4,1)}, pred[512,1024]{0,1:T(8,128)(4,1)S(1)}, u32[]{:S(2)}) copy-start(pred[512,1024]{0,1:T(8,128)(4,1)S(1)} %iota_compare_fusion.1) | copy-start | bytes 1572868
  16.8 110.8 %copy-start.14 = (f32[1024,128]{0,1:T(8,128)}, f32[1024,128]{0,1:T(8,128)S(1)}, u32[]{:S(2)}) copy-start(f32[1024,128]{0,1:T(8,128)S(1)} %get-tuple-element.98) | copy-start | bytes 1572868
  17.2 129.9 %copy-start.27 = (pred[512,1024]{0,1:T(8,128)(4,1)}, pred[512,1024]{0,1:T(8,128)(4,1)S(1)}, u32[]{:S(2)}) copy-start(pred[512,1024]{0,1:T(8,128)(4,1)S(1)} %iota_compare_fusion) | copy-start | bytes 1572868
  17.2 75.8 %copy-start.58 = (f32[128]{0:T(128)S(1)}, f32[128]{0:T(128)}, u32[]{:S(2)}) copy-start(f32[128]{0:T(128)} %param.19) | copy-start | bytes 1540
  93.0 34.6 %copy-start.7 = (f32[1024,256]{0,1:T(8,128)}, f32[1024,256]{0,1:T(8,128)S(1)}, u32[]{:S(2)}) copy-start(f32[1024,256]{0,1:T(8,128)S(1)} %get-tuple-element.100) | copy-start | bytes 3145732
  93.0 34.6 %copy-start.50 = (f32[1024,2]{0,1:T(2,128)}, f32[1024,2]{0,1:T(2,128)S(1)}, u32[]{:S(2)}) copy-start(f32[1024,2]{0,1:T(2,128)S(1)} %add_rsqrt_fusion.1) | copy-start | bytes 24580
  94.4 30.9 %copy-start.56 = (f32[128]{0:T(128)S(1)}, f32[128]{0:T(128)}, u32[]{:S(2)}) copy-start(f32[128]{0:T(128)} %param.18) | copy-start | bytes 1540
  143.1 10.0 slice-start
  155.6 26.5 %copy-start.36 = (bf16[512,2,2,128]{0,3,2,1:T(8,128)(2,1)}, bf16[512,2,2,128]{0,3,2,1:T(8,128)(2,1)S(1)}, u32[]{:S(2)}) copy-start(bf16[512,2,2,128]{0,3,2,1:T(8,128)(2,1)S(1)} %fusion.34) | copy-start | bytes 1572868
  155.8 26.3 %copy-start.42 = (bf16[1024,2,2,128]{0,3,2,1:T(8,128)(2,1)}, bf16[1024,2,2,128]{0,3,2,1:T(8,128)(2,1)S(1)}, u32[]{:S(2)}) copy-start(bf16[1024,2,2,128]{0,3,2,1:T(8,128)(2,1)S(1)} %pad_maximum_fusion.1) | copy-start | bytes 3145732
  182.1 85.5 %copy-start.5 = (bf16[256,2048]{1,0:T(8,128)(2,1)S(1)}, bf16[256,2048]{1,0:T(8,128)(2,1)}, u32[]{:S(2)}) copy-start(bf16[256,2048]{1,0:T(8,128)(2,1)} %param.13) | copy-start | bytes 3145732
  182.1 87.4 %copy-start.52 = (f32[2048]{0:T(1024)S(1)}, f32[2048]{0:T(1024)}, u32[]{:S(2)}) copy-start(f32[2048]{0:T(1024)} %param.21) | copy-start | bytes 24580
  182.1 151.8 %all-gather.24.cloned.1.call-start = ((), (), s32[]{:S(2)}) async-start(), calls=%async_computation.18 | async-start | bytes 7077888 | tf_op jit(solution)/shard_map/all_gather | solution.py:143
  182.9 204.8 %all-gather.22.cloned.1.call-start = ((), (), s32[]{:S(2)}) async-start(), calls=%async_computation.17 | async-start | bytes 5242880 | tf_op jit(solution)/shard_map/all_gather | solution.py:204
  270.8 183.2 %all-gather.26.cloned.1.call-start = ((), (), s32[]{:S(2)}) async-start(), calls=%async_computation.19 | async-start | bytes 7077888 | tf_op jit(solution)/shard_map/all_gather | solution.py:144
  271.5 235.4 %all-gather.30.cloned.1.call-start = ((), (), s32[]{:S(2)}) async-start(), calls=%async_computation.22 | async-start | bytes 5242880 | tf_op jit(solution)/shard_map/all_gather | solution.py:229
  272.1 301.6 %all-gather.28.cloned.1.call-start = ((), (), s32[]{:S(2)}) async-start(), calls=%async_computation.20 | async-start | bytes 7077888 | tf_op jit(solution)/shard_map/all_gather | solution.py:145
  272.8 421.7 %reduce-scatter.16.cloned.1.call-start = ((), (), s32[]{:S(2)}) async-start(), calls=%async_computation.23 | async-start | bytes 10485760 | tf_op jit(solution)/shard_map/reduce_scatter | solution.py:240
  589.6 11.1 copy-start.67
  589.6 11.2 copy-start.68
  589.6 11.2 copy-start.60
  609.9 87.0 %copy-start.22 = (bf16[256,2048]{1,0:T(8,128)(2,1)S(1)}, bf16[256,2048]{1,0:T(8,128)(2,1)}, u32[]{:S(2)}) copy-start(bf16[256,2048]{1,0:T(8,128)(2,1)} %param.25) | copy-start | bytes 3145732
  609.9 141.4 %all-gather.32.cloned.1.call-start = ((), (), s32[]{:S(2)}) async-start(), calls=%async_computation.24 | async-start | bytes 5242880 | tf_op jit(solution)/shard_map/all_gather | solution.py:253
  698.6 147.2 %reduce-scatter.28.cloned.1.call-start = ((), (), s32[]{:S(2)}) async-start(), calls=%async_computation.30 | async-start | bytes 7077888 | tf_op jit(solution)/shard_map/reduce_scatter | solution.py:346
  710.1 183.5 %reduce-scatter.30.cloned.1.call-start = ((), (), s32[]{:S(2)}) async-start(), calls=%async_computation.31 | async-start | bytes 7077888 | tf_op jit(solution)/shard_map/reduce_scatter | solution.py:349
  721.6 242.3 %reduce-scatter.32.cloned.1.call-start = ((), (), s32[]{:S(2)}) async-start(), calls=%async_computation.32 | async-start | bytes 7077888 | tf_op jit(solution)/shard_map/reduce_scatter | solution.py:352
  733.0 23.7 %copy-start.35 = (bf16[512,2,2,128]{0,3,2,1:T(8,128)(2,1)S(1)}, bf16[512,2,2,128]{0,3,2,1:T(8,128)(2,1)}, u32[]{:S(2)}) copy-start(bf16[512,2,2,128]{0,3,2,1:T(8,128)(2,1)} %copy-done.34) | copy-start | bytes 1572868
  733.0 264.2 %reduce-scatter.24.cloned.1.call-start = ((), (), s32[]{:S(2)}) async-start(), calls=%async_computation.28 | async-start | bytes 1179648 | tf_op jit(solution)/shard_map/reduce_scatter | solution.py:340
  751.3 7.0 copy-start.28
  751.3 13.6 %slice-start.2 = ((s8[8388608]{0:T(1024)(128)(4,1)}), s8[4194304]{0:T(1024)(128)(4,1)S(1)}, s32[]{:S(2)}) async-start(s8[8388608]{0:T(1024)(128)(4,1)} %bitcast.226), calls=%async_computation.35 | async-start | bytes 8388608
  756.7 8.2 slice-start.3
  770.7 8.7 copy-start.46
  770.7 8.7 copy-start.66
  779.4 7.1 copy-start.31
  786.4 243.8 %reduce-scatter.22.cloned.1.call-start = ((), (), s32[]{:S(2)}) async-start(), calls=%async_computation.27 | async-start | bytes 1179648 | tf_op jit(solution)/shard_map/reduce_scatter | solution.py:337
  798.2 268.5 %reduce-scatter.26.cloned.1.call-start = ((), (), s32[]{:S(2)}) async-start(), calls=%async_computation.29 | async-start | bytes 2359296 | tf_op jit(solution)/shard_map/reduce_scatter | solution.py:343
  804.5 299.0 %reduce-scatter.20.cloned.1.call-start = ((), (), s32[]{:S(2)}) async-start(), calls=%async_computation.26 | async-start | bytes 2359296 | tf_op jit(solution)/shard_map/reduce_scatter | solution.py:334
  825.7 332.1 %reduce-scatter.18.cloned.1.call-start = ((), (), s32[]{:S(2)}) async-start(), calls=%async_computation.25 | async-start | bytes 5242880 | tf_op jit(solution)/shard_map/reduce_scatter | solution.py:313
  834.3 379.3 %reduce-scatter.14.cloned.1.call-start = ((), (), s32[]{:S(2)}) async-start(), calls=%async_computation.21 | async-start | bytes 5242880 | tf_op jit(solution)/shard_map/reduce_scatter | solution.py:209
  845.7 312.0 %copy-start.6 = (bf16[256,2048]{1,0:T(8,128)(2,1)S(1)}, bf16[256,2048]{1,0:T(8,128)(2,1)}, u32[]{:S(2)}) copy-start(bf16[256,2048]{1,0:T(8,128)(2,1)} %param.13) | copy-start | bytes 3145732
  845.8 312.0 %copy-start.53 = (f32[2048]{0:T(1024)S(1)}, f32[2048]{0:T(1024)}, u32[]{:S(2)}) copy-start(f32[2048]{0:T(1024)} %param.14) | copy-start | bytes 24580
  845.8 312.0 %copy-start.55 = (f32[256]{0:T(256)S(1)}, f32[256]{0:T(256)}, u32[]{:S(2)}) copy-start(f32[256]{0:T(256)} %copy-done.54) | copy-start | bytes 3076
  (47 other events, 153.9 us)
Sparse Core Ops, SparseCore 0:
  9.6 24.9 all-gather.15
  37.0 52.1 all-gather.11
  90.8 29.1 all-gather.17
  121.5 21.6 all-gather.13
  144.6 30.1 all-gather.19
  182.2 85.2 reduce-scatter.11
  269.2 64.7 all-gather.23
  336.4 51.2 all-gather.21
  389.3 64.6 all-gather.25
  455.7 51.2 all-gather.29
  508.5 65.1 all-gather.27
  610.0 84.4 reduce-scatter.15
  698.7 52.5 all-gather.31
  753.4 69.7 reduce-scatter.27
  825.4 68.1 reduce-scatter.29
  895.8 68.1 reduce-scatter.31
  966.1 31.0 reduce-scatter.23
  999.3 30.8 reduce-scatter.21
  1032.5 34.1 reduce-scatter.25
  1068.8 34.6 reduce-scatter.19
  1106.5 51.1 reduce-scatter.17
  1160.7 52.8 reduce-scatter.13
where the time goes:
time: 1240 us; the launch traced here: 1230 us
  waiting for transfers between devices  902 us (73%)
  matrix products  201 us (16%)
  other arithmetic  53.6 us (4%)
  blocking collectives  40.1 us (3%)
  between operations  15.8 us (1%)
    reduce_scatter x1, waiting for transfers between devices, per_device(): lax.psum_scatter(simple_product(lax.slice_in_dim(mixed_rows, 0, local_row...  84.7 us
    reduce_scatter x1, waiting for transfers between devices, per_device(): lax.psum_scatter(times_transposed(gate_part, gate_back) + times_transpose...  84.6 us
    reduce_scatter x1, waiting for transfers between devices, per_device(): lax.psum_scatter(down_grad.astype(jnp.bfloat16), 'dp', scatter_dimension=...  67.9 us
    all_gather x1, waiting for transfers between devices, per_device(): lax.all_gather(down_weight, 'dp', axis=1, tiled=True)  66.8 us
    all_gather x1, waiting for transfers between devices, per_device(): lax.all_gather(gate_weight, 'dp', axis=0, tiled=True)  61.1 us
    dot_general x7, matrix products, simple_product(): jnp.dot(first_operand, second_operand, preferred_element_type=jnp.float32)  55.2 us
    all_gather x1, waiting for transfers between devices, per_device(): lax.all_gather(mixer_local, 'tensor', axis=0, tiled=True)  54.6 us
    all_gather x1, waiting for transfers between devices, per_device(): lax.all_gather(up_weight, 'dp', axis=0, tiled=True)  54.3 us
  transfers between devices with their start and end apart: 22, of which 21 were waited for; matrix products, arithmetic and copies ran while one was open for 17% of the time, Pallas kernels for 0%

commit v1 on v0

--- a/solution.py
+++ b/solution.py
@@ -1,13 +1,19 @@
+import functools
+
 import jax
 import jax.numpy as jnp
 from jax import lax
+from jax.experimental import pallas as pl
+from jax.experimental.pallas import tpu as pltpu
 from jax.sharding import PartitionSpec as P
 
 SEQUENCE_LENGTH = 1024
-
 
 epsilon = 1e-06
 rope_base = 1000000.0
+
+MESH = pl.DeviceIdType.MESH
+VMEM_LIMIT = 62 * 1024 * 1024
 
 
 def row_scale(values):
@@ -41,6 +47,291 @@
 
 def simple_product(first_operand, second_operand):
     return jnp.dot(first_operand, second_operand, preferred_element_type=jnp.float32)
+
+
+def remote(source, target, send_sem, recv_sem, peer):
+    return pltpu.make_async_remote_copy(
+        src_ref=source,
+        dst_ref=target,
+        send_sem=send_sem,
+        recv_sem=recv_sem,
+        device_id={"tensor": peer},
+        device_id_type=MESH,
+    )
+
+
+def greet(peers):
+    barrier = pltpu.get_barrier_semaphore()
+    for peer in peers:
+        pl.semaphore_signal(barrier, inc=1, device_id={"tensor": peer}, device_id_type=MESH)
+    pl.semaphore_wait(barrier, len(peers))
+
+
+def square_peers(me):
+    column = lax.rem(me, 2)
+    row = me // 2
+    return row * 2 + (1 - column), (1 - row) * 2 + column, (1 - row) * 2 + (1 - column)
+
+
+def gather_kernel_square(count, *refs):
+    own_refs, out_refs, held_refs = refs[:count], refs[count : 2 * count], refs[2 * count : 3 * count]
+    send_sem, recv_sem, local_sem = refs[3 * count :]
+    me = lax.axis_index("tensor")
+    beside, below, across = square_peers(me)
+    greet((beside, below))
+    rows = own_refs[0].shape[0]
+    half = rows // 2
+    first, second = pl.ds(0, half), pl.ds(half, half)
+    copies = []
+    stores = []
+
+    def store(k, source, slot, part, sem):
+        start = slot * rows + (half if part == 1 else 0)
+        size = rows if part is None else half
+        copy = pltpu.make_async_copy(
+            source, out_refs[k].at[pl.ds(pl.multiple_of(start, half), size)], local_sem.at[k, sem]
+        )
+        copy.start()
+        stores.append(copy)
+
+    for k in range(count):
+        own, held = own_refs[k], held_refs[k]
+
+        def send(index, source, slot, part, peer):
+            copy = remote(
+                source, held.at[slot, part], send_sem.at[k, index], recv_sem.at[k, index], peer
+            )
+            copy.start()
+            copies.append(copy)
+            return copy
+
+        x_first = send(0, own.at[first], me, first, beside)
+        y_second = send(1, own.at[second], me, second, below)
+        x_second = send(2, own.at[second], me, second, beside)
+        y_first = send(3, own.at[first], me, first, below)
+        store(k, own, me, None, 0)
+        x_first.wait_recv()
+        y_pass = send(4, held.at[beside, first], beside, first, below)
+        y_second.wait_recv()
+        x_pass = send(5, held.at[below, second], below, second, beside)
+        store(k, held.at[beside, first], beside, 0, 1)
+        store(k, held.at[below, second], below, 1, 2)
+    for k in range(count):
+        held = held_refs[k]
+        x_second, y_first, y_pass, x_pass = copies[6 * k + 2 : 6 * k + 6]
+        x_second.wait_recv()
+        store(k, held.at[beside, second], beside, 1, 3)
+        y_first.wait_recv()
+        store(k, held.at[below, first], below, 0, 4)
+        y_pass.wait_recv()
+        store(k, held.at[across, first], across, 0, 5)
+        x_pass.wait_recv()
+        store(k, held.at[across, second], across, 1, 6)
+    for copy in copies:
+        copy.wait_send()
+    for copy in stores:
+        copy.wait()
+
+
+def gather_kernel_direct(size, count, *refs):
+    own_refs, out_refs, held_refs = refs[:count], refs[count : 2 * count], refs[2 * count : 3 * count]
+    send_sem, recv_sem, local_sem = refs[3 * count :]
+    me = lax.axis_index("tensor")
+    peers = [lax.rem(me + step, size) for step in range(1, size)]
+    greet(peers)
+    rows = own_refs[0].shape[0]
+    copies = []
+    stores = []
+    for k in range(count):
+        for step, peer in enumerate(peers):
+            copy = remote(
+                own_refs[k], held_refs[k].at[me], send_sem.at[k, step], recv_sem.at[k, step], peer
+            )
+            copy.start()
+            copies.append(copy)
+    for k in range(count):
+        for step in range(size):
+            source = own_refs[k]
+            slot = lax.rem(me + size - step, size)
+            if step > 0:
+                copies[k * (size - 1) + step - 1].wait_recv()
+                source = held_refs[k].at[slot]
+            copy = pltpu.make_async_copy(
+                source,
+                out_refs[k].at[pl.ds(pl.multiple_of(slot * rows, rows), rows)],
+                local_sem.at[k, step],
+            )
+            copy.start()
+            stores.append(copy)
+    for copy in copies:
+        copy.wait_send()
+    for copy in stores:
+        copy.wait()
+
+
+def gather_rows(arrays, size, collective_id):
+    count = len(arrays)
+    rows, columns = arrays[0].shape
+    square = size == 4
+    body = (
+        functools.partial(gather_kernel_square, count)
+        if square
+        else functools.partial(gather_kernel_direct, size, count)
+    )
+    sends = 6 if square else size - 1
+    locals_ = 7 if square else size
+    return pl.pallas_call(
+        body,
+        out_shape=[jax.ShapeDtypeStruct((size * rows, columns), a.dtype) for a in arrays],
+        in_specs=[pl.BlockSpec(memory_space=pltpu.VMEM)] * count,
+        out_specs=[pl.BlockSpec(memory_space=pl.ANY)] * count,
+        scratch_shapes=[pltpu.VMEM((size, rows, columns), a.dtype) for a in arrays]
+        + [
+            pltpu.SemaphoreType.DMA((count, sends)),
+            pltpu.SemaphoreType.DMA((count, sends)),
+            pltpu.SemaphoreType.DMA((count, locals_)),
+        ],
+        compiler_params=pltpu.CompilerParams(
+            collective_id=collective_id, has_side_effects=True, vmem_limit_bytes=VMEM_LIMIT
+        ),
+        cost_estimate=pl.CostEstimate(
+            flops=0, bytes_accessed=count * 30 * size * rows * columns, transcendentals=0
+        ),
+        name="gather_rows",
+    )(*arrays)
+
+
+def block_product(left_ref, start, rows, weight_ref, write):
+    total = weight_ref.shape[0]
+    tile = min(512, total)
+    left = left_ref[pl.ds(pl.multiple_of(start, rows), rows), :]
+
+    def step(index, carry):
+        columns = pl.ds(pl.multiple_of(index * tile, tile), tile)
+        write(columns, times_transposed(left, weight_ref[columns, :]))
+        return carry
+
+    lax.fori_loop(0, total // tile, step, 0)
+
+
+def scatter_kernel_square(
+    left_ref, weight_ref, out_ref, outgoing, passing, arriving, send_sem, recv_sem
+):
+    me = lax.axis_index("tensor")
+    beside, below, across = square_peers(me)
+    rows = out_ref.shape[0]
+    half = rows // 2
+    first, second = pl.ds(0, half), pl.ds(half, half)
+    greet((beside, below))
+
+    def fill(slot, owner):
+        def write(columns, values):
+            outgoing[slot, :, columns] = values.astype(outgoing.dtype)
+
+        block_product(left_ref, owner * rows, rows, weight_ref, write)
+
+    def send(index, source, target, peer):
+        copy = remote(source, target, send_sem.at[index], recv_sem.at[index], peer)
+        copy.start()
+        return copy
+
+    fill(0, across)
+    x_pass = send(0, outgoing.at[0, first], passing.at[0], beside)
+    y_pass = send(1, outgoing.at[0, second], passing.at[1], below)
+    fill(1, beside)
+    x_first = send(2, outgoing.at[1, first], arriving.at[0, first], beside)
+    fill(2, below)
+    y_second = send(3, outgoing.at[2, second], arriving.at[1, second], below)
+
+    def write_own(columns, values):
+        out_ref[:, columns] = values
+
+    block_product(left_ref, me * rows, rows, weight_ref, write_own)
+    y_pass.wait_recv()
+    outgoing[1, second, :] = (
+        outgoing[1, second, :].astype(jnp.float32) + passing[1].astype(jnp.float32)
+    ).astype(outgoing.dtype)
+    x_second = send(4, outgoing.at[1, second], arriving.at[0, second], beside)
+    x_pass.wait_recv()
+    outgoing[2, first, :] = (
+        outgoing[2, first, :].astype(jnp.float32) + passing[0].astype(jnp.float32)
+    ).astype(outgoing.dtype)
+    y_first = send(5, outgoing.at[2, first], arriving.at[1, first], below)
+    x_first.wait_recv()
+    y_second.wait_recv()
+    out_ref[first, :] += arriving[0, first, :].astype(jnp.float32)
+    out_ref[second, :] += arriving[1, second, :].astype(jnp.float32)
+    x_second.wait_recv()
+    y_first.wait_recv()
+    out_ref[second, :] += arriving[0, second, :].astype(jnp.float32)
+    out_ref[first, :] += arriving[1, first, :].astype(jnp.float32)
+    for copy in (x_pass, y_pass, x_first, y_second, x_second, y_first):
+        copy.wait_send()
+
+
+def scatter_kernel_direct(size, left_ref, weight_ref, out_ref, outgoing, arriving, send_sem, recv_sem):
+    me = lax.axis_index("tensor")
+    rows = out_ref.shape[0]
+    peers = [lax.rem(me + step, size) for step in range(1, size)]
+    greet(peers)
+    copies = []
+    for step, peer in enumerate(peers):
+
+        def write(columns, values, step=step):
+            outgoing[step, :, columns] = values.astype(outgoing.dtype)
+
+        block_product(left_ref, peer * rows, rows, weight_ref, write)
+        copy = remote(
+            outgoing.at[step], arriving.at[step], send_sem.at[step], recv_sem.at[step], peer
+        )
+        copy.start()
+        copies.append(copy)
+
+    def write_own(columns, values):
+        out_ref[:, columns] = values
+
+    block_product(left_ref, me * rows, rows, weight_ref, write_own)
+    for step, copy in enumerate(copies):
+        copy.wait_recv()
+        out_ref[...] += arriving[step].astype(jnp.float32)
+    for copy in copies:
+        copy.wait_send()
+
+
+def product_scatter(left, weight, size, collective_id):
+    total_rows, depth = left.shape
+    columns = weight.shape[0]
+    rows = total_rows // size
+    square = size == 4
+    if square:
+        body = scatter_kernel_square
+        buffers = [
+            pltpu.VMEM((3, rows, columns), jnp.bfloat16),
+            pltpu.VMEM((2, rows // 2, columns), jnp.bfloat16),
+            pltpu.VMEM((2, rows, columns), jnp.bfloat16),
+        ]
+        sends = 6
+    else:
+        body = functools.partial(scatter_kernel_direct, size)
+        buffers = [pltpu.VMEM((size - 1, rows, columns), jnp.bfloat16)] * 2
+        sends = size - 1
+    return pl.pallas_call(
+        body,
+        out_shape=jax.ShapeDtypeStruct((rows, columns), jnp.float32),
+        in_specs=[pl.BlockSpec(memory_space=pltpu.VMEM)] * 2,
+        out_specs=pl.BlockSpec(memory_space=pltpu.VMEM),
+        scratch_shapes=buffers
+        + [pltpu.SemaphoreType.DMA((sends,)), pltpu.SemaphoreType.DMA((sends,))],
+        compiler_params=pltpu.CompilerParams(
+            collective_id=collective_id, has_side_effects=True, vmem_limit_bytes=VMEM_LIMIT
+        ),
+        cost_estimate=pl.CostEstimate(
+            flops=2 * total_rows * depth * columns,
+            bytes_accessed=30 * total_rows * columns,
+            transcendentals=0,
+        ),
+        name="product_scatter",
+    )(left, weight)
 
 
 def masked_scores(query_block, key_seq, first_row):
@@ -123,40 +414,49 @@
     down_weight,
     out_cotangent,
 ):
+    size = lax.axis_size("tensor")
     local_rows = block_input.shape[0]
-    grouped_rows = local_rows * lax.axis_size("tensor")
+    grouped_rows = local_rows * size
     head_size = query_gain.shape[0]
-    query_heads = query_weight.shape[1] // head_size
-    value_heads = key_matrix.shape[1] // head_size
+    query_columns = query_weight.shape[1]
+    key_columns = key_matrix.shape[1]
+    query_heads = query_columns // head_size
+    value_heads = key_columns // head_size
+    hidden_columns = gate_weight.shape[1]
     grouping_width = query_heads // value_heads
     sequences = grouped_rows // SEQUENCE_LENGTH
     block_rows = min(512, SEQUENCE_LENGTH)
     block_count = SEQUENCE_LENGTH // block_rows
-    cosine, sine = rope_tables(
-        (jnp.arange(grouped_rows) % SEQUENCE_LENGTH).astype(jnp.float32), head_size
-    )
-    gathered = (
-        lax.all_gather(query_weight, "dp", axis=0, tiled=True),
-        lax.all_gather(key_matrix, "dp", axis=0, tiled=True),
-        lax.all_gather(value_matrix, "dp", axis=0, tiled=True),
-        lax.all_gather(output_weight, "dp", axis=1, tiled=True),
-        lax.all_gather(gate_weight, "dp", axis=0, tiled=True),
-        lax.all_gather(up_weight, "dp", axis=0, tiled=True),
-        lax.all_gather(down_weight, "dp", axis=1, tiled=True),
-    )
-    query_full, key_full, value_full, output_full, gate_full, up_full, down_full = gathered
+    qkv_columns = query_columns + 2 * key_columns
+
+    mixing_full = lax.all_gather(
+        jnp.concatenate([query_weight, key_matrix, value_matrix, output_weight.T], axis=1),
+        "dp",
+        axis=0,
+        tiled=True,
+    )
+    feeding_full = lax.all_gather(
+        jnp.concatenate([gate_weight, up_weight], axis=1), "dp", axis=0, tiled=True
+    )
+    down_full = lax.all_gather(down_weight.T, "dp", axis=0, tiled=True)
+
     input_float = block_input.astype(jnp.float32)
     first_scale = row_scale(input_float)
     first_unit = input_float * first_scale
     mixer_local = (first_unit * attention_gain).astype(jnp.bfloat16)
-    attention_output_rows = lax.all_gather(mixer_local, "tensor", axis=0, tiled=True)
-    query_raw = simple_product(attention_output_rows, query_full).reshape(
-        grouped_rows, query_heads, head_size
-    )
-    unnormed_key = simple_product(attention_output_rows, key_full).reshape(
+    mixer_rows, cotangent_rows = gather_rows((mixer_local, out_cotangent), size, 0)
+
+    cosine, sine = rope_tables(
+        (jnp.arange(grouped_rows) % SEQUENCE_LENGTH).astype(jnp.float32), head_size
+    )
+    qkv_full = mixing_full[:, :qkv_columns]
+    output_full = mixing_full[:, qkv_columns:]
+    qkv_raw = simple_product(mixer_rows, qkv_full)
+    query_raw = qkv_raw[:, :query_columns].reshape(grouped_rows, query_heads, head_size)
+    unnormed_key = qkv_raw[:, query_columns : query_columns + key_columns].reshape(
         grouped_rows, value_heads, head_size
     )
-    value_token_rows = simple_product(attention_output_rows, value_full).astype(jnp.bfloat16)
+    value_token_rows = qkv_raw[:, query_columns + key_columns :].astype(jnp.bfloat16)
     query_scale = row_scale(query_raw)
     query_unit = query_raw * query_scale
     query_normed = query_unit * query_gain
@@ -188,71 +488,37 @@
         forward_sequence, (query_sequences, key_sequences, value_sequences)
     )
     mixed_rows = mixed_seqs.reshape(grouped_rows, query_heads * head_size)
-    attention_sum = lax.psum_scatter(
-        simple_product(
-            lax.slice_in_dim(mixed_rows, 0, local_rows * lax.axis_size("tensor"), axis=0),
-            output_full,
-        ),
-        "tensor",
-        scatter_dimension=0,
-        tiled=True,
-    )
-    hidden_state = input_float + attention_sum
+    hidden_state = input_float + product_scatter(mixed_rows, output_full, size, 1)
     second_scale = row_scale(hidden_state)
     second_unit = hidden_state * second_scale
     feed_local = (second_unit * feed_gain).astype(jnp.bfloat16)
-    feed_rows = lax.all_gather(feed_local, "tensor", axis=0, tiled=True)
-    gate_values = simple_product(feed_rows, gate_full)
-    up_values = simple_product(feed_rows, up_full)
+    (feed_rows,) = gather_rows((feed_local,), size, 2)
+    both_values = simple_product(feed_rows, feeding_full)
+    gate_values = both_values[:, :hidden_columns]
+    up_values = both_values[:, hidden_columns:]
     gate_sigmoid = jax.nn.sigmoid(gate_values)
     hidden_rows = (gate_values * gate_sigmoid * up_values).astype(jnp.bfloat16)
-    feed_sum = lax.psum_scatter(
-        simple_product(
-            lax.slice_in_dim(hidden_rows, 0, local_rows * lax.axis_size("tensor"), axis=0),
-            down_full,
-        ).astype(jnp.bfloat16),
-        "tensor",
-        scatter_dimension=0,
-        tiled=True,
-    ).astype(jnp.float32)
-    block_output = (hidden_state + feed_sum).astype(jnp.bfloat16)
-    regathered = (
-        lax.all_gather(query_weight, "dp", axis=0, tiled=True),
-        lax.all_gather(key_matrix, "dp", axis=0, tiled=True),
-        lax.all_gather(value_matrix, "dp", axis=0, tiled=True),
-        lax.all_gather(output_weight, "dp", axis=1, tiled=True),
-        lax.all_gather(gate_weight, "dp", axis=0, tiled=True),
-        lax.all_gather(up_weight, "dp", axis=0, tiled=True),
-        lax.all_gather(down_weight, "dp", axis=1, tiled=True),
-    )
-    query_back, key_back, value_back, output_back, gate_back, up_back, down_back = regathered
-    cotangent_rows = lax.all_gather(out_cotangent, "tensor", axis=0, tiled=True)
-    hidden_slope = times_transposed(cotangent_rows, down_back)
-    down_grad = contract_rows(hidden_rows, cotangent_rows)
+    down_grad = contract_rows(cotangent_rows, hidden_rows).astype(jnp.bfloat16)
+    down_total = lax.psum_scatter(down_grad, "dp", scatter_dimension=0, tiled=True)
+
+    hidden_slope = simple_product(cotangent_rows, down_full)
     gate_slope = (
         hidden_slope * up_values * gate_sigmoid * (1.0 + gate_values * (1.0 - gate_sigmoid))
     ).astype(jnp.bfloat16)
     up_slope = (hidden_slope * gate_values * gate_sigmoid).astype(jnp.bfloat16)
-    gate_grad = contract_rows(feed_rows, gate_slope)
-    up_grad = contract_rows(feed_rows, up_slope)
-    gate_part = lax.slice_in_dim(gate_slope, 0, local_rows * lax.axis_size("tensor"), axis=0)
-    up_part = lax.slice_in_dim(up_slope, 0, local_rows * lax.axis_size("tensor"), axis=0)
-    feed_back = lax.psum_scatter(
-        times_transposed(gate_part, gate_back) + times_transposed(up_part, up_back),
-        "tensor",
-        scatter_dimension=0,
-        tiled=True,
-    )
+    feed_slope = jnp.concatenate([gate_slope, up_slope], axis=1)
+    feed_grad = contract_rows(feed_rows, feed_slope).astype(jnp.bfloat16)
+    feed_total = lax.psum_scatter(feed_grad, "dp", scatter_dimension=0, tiled=True)
+    feed_back = product_scatter(feed_slope, feeding_full, size, 3)
     feed_gain_term = jnp.sum(feed_back * second_unit, axis=0)
     feed_unit_slope = feed_back * feed_gain
     state_slope = out_cotangent.astype(jnp.float32) + second_scale * (
         feed_unit_slope
         - second_unit * jnp.mean(feed_unit_slope * second_unit, axis=-1, keepdims=True)
     )
-    state_rounded = state_slope.astype(jnp.bfloat16)
-    state_rows = lax.all_gather(state_rounded, "tensor", axis=0, tiled=True)
-    mixed_gradient = times_transposed(state_rows, output_back).astype(jnp.bfloat16)
-    output_grad = contract_rows(mixed_rows, state_rows)
+    (state_rows,) = gather_rows((state_slope.astype(jnp.bfloat16),), size, 4)
+    mixed_gradient = simple_product(state_rows, output_full).astype(jnp.bfloat16)
+    output_grad = contract_rows(state_rows, mixed_rows).astype(jnp.bfloat16)
     gradient_sequences = mixed_gradient.reshape(
         sequences, SEQUENCE_LENGTH, value_heads, grouping_width, head_size
     )
@@ -300,26 +566,14 @@
         key_gain,
     )
     value_gradient_rows = value_rows_gradient.reshape(grouped_rows, value_heads * head_size)
-    query_grad = contract_rows(attention_output_rows, query_raw_slope)
-    key_grad = contract_rows(attention_output_rows, unnormed_key_gradient)
-    value_grad = contract_rows(attention_output_rows, value_gradient_rows)
-    query_part = lax.slice_in_dim(query_raw_slope, 0, local_rows * lax.axis_size("tensor"), axis=0)
-    key_part = lax.slice_in_dim(
-        unnormed_key_gradient, 0, local_rows * lax.axis_size("tensor"), axis=0
-    )
-    value_part = lax.slice_in_dim(
-        value_gradient_rows, 0, local_rows * lax.axis_size("tensor"), axis=0
-    )
-    mixer_back = lax.psum_scatter(
-        (
-            times_transposed(query_part, query_back)
-            + times_transposed(key_part, key_back)
-            + times_transposed(value_part, value_back)
-        ).astype(jnp.bfloat16),
-        "tensor",
-        scatter_dimension=0,
-        tiled=True,
+    qkv_slope = jnp.concatenate(
+        [query_raw_slope, unnormed_key_gradient, value_gradient_rows], axis=1
+    )
+    qkv_grad = contract_rows(mixer_rows, qkv_slope).astype(jnp.bfloat16)
+    mixing_total = lax.psum_scatter(
+        jnp.concatenate([qkv_grad, output_grad], axis=1), "dp", scatter_dimension=0, tiled=True
     ).astype(jnp.float32)
+    mixer_back = product_scatter(qkv_slope, qkv_full, size, 5)
     attention_gain_term = jnp.sum(mixer_back * first_unit, axis=0)
     mixer_unit_slope = mixer_back * attention_gain
     input_gradient = (
@@ -330,46 +584,26 @@
             - first_unit * jnp.mean(mixer_unit_slope * first_unit, axis=-1, keepdims=True)
         )
     ).astype(jnp.bfloat16)
-    weight_totals = (
-        lax.psum_scatter(
-            query_grad.astype(jnp.bfloat16), "dp", scatter_dimension=0, tiled=True
-        ).astype(jnp.float32),
-        lax.psum_scatter(
-            key_grad.astype(jnp.bfloat16), "dp", scatter_dimension=0, tiled=True
-        ).astype(jnp.float32),
-        lax.psum_scatter(
-            value_grad.astype(jnp.bfloat16), "dp", scatter_dimension=0, tiled=True
-        ).astype(jnp.float32),
-        lax.psum_scatter(
-            output_grad.astype(jnp.bfloat16), "dp", scatter_dimension=1, tiled=True
-        ).astype(jnp.float32),
-        lax.psum_scatter(
-            gate_grad.astype(jnp.bfloat16), "dp", scatter_dimension=0, tiled=True
-        ).astype(jnp.float32),
-        lax.psum_scatter(
-            up_grad.astype(jnp.bfloat16), "dp", scatter_dimension=0, tiled=True
-        ).astype(jnp.float32),
-        lax.psum_scatter(
-            down_grad.astype(jnp.bfloat16), "dp", scatter_dimension=1, tiled=True
-        ).astype(jnp.float32),
-    )
+    feed_sum = product_scatter(hidden_rows, down_full, size, 6)
+    block_output = (hidden_state + feed_sum).astype(jnp.bfloat16)
     gain_totals = lax.psum(
         (attention_gain_term, feed_gain_term, query_gain_term, key_gain_term), ("dp", "tensor")
     )
+    feed_total = feed_total.astype(jnp.float32)
     return (
         block_output,
         input_gradient,
         gain_totals[0],
-        weight_totals[0],
-        weight_totals[1],
-        weight_totals[2],
+        mixing_total[:, :query_columns],
+        mixing_total[:, query_columns : query_columns + key_columns],
+        mixing_total[:, query_columns + key_columns : qkv_columns],
         gain_totals[2],
         gain_totals[3],
-        weight_totals[3],
+        mixing_total[:, qkv_columns:].T,
         gain_totals[1],
-        weight_totals[4],
-        weight_totals[5],
-        weight_totals[6],
+        feed_total[:, :hidden_columns],
+        feed_total[:, hidden_columns:],
+        down_total.astype(jnp.float32).T,
     )
 
 

time: 1240 us -> 762 us (0.61)
  waiting for transfers between devices: 902 us -> 88.4 us
  Pallas kernels: 0 us -> 326 us
  matrix products: 201 us -> 126 us
  local copies, waits for them, and re-layouts: 11.2 us -> 77.4 us
  other arithmetic: 53.6 us -> 77.1 us
    all_gather x11 -> x3, waiting for transfers between devices: 416 us -> 0.6 us  [the longest x1 0.57 us: per_device(): down_full = lax.all_gather(down_weight.T, 'dp', axis=0, tiled=True)]
    reduce_scatter x11 -> x3, waiting for transfers between devices: 481 us -> 87.7 us  [the longest x1 87.7 us: per_device(): lax.psum_scatter(feed_grad, 'dp', scatter_dimension=0, tiled=True)]
    pallas_call x0 -> x7, Pallas kernels: none -> 326 us  [the longest x4 176 us: product_scatter(): pl.pallas_call(body, out_shape=jax.ShapeDtypeStruct((rows, columns), jnp....]
    dot_general x7 -> x0, matrix products: 49.9 us -> none  [times_transposed(): lax.dot_general(first_operand, second_operand, (((1,), (1,)), ((), ())),...]
    unnamed x146 -> x144, local copies, waits for them, and re-layouts: 11 us -> 26.8 us
    mul x0 -> x8, local copies, waits for them, and re-layouts: none -> 15.8 us  [the longest x3 6.68 us: per_device(): query_unit = query_raw * query_scale]
    slice x0 -> x10, local copies, waits for them, and re-layouts: none -> 15.6 us  [the longest x1 4.72 us: per_device(): qkv_full = mixing_full[:, :qkv_columns]]
    convert_element_type x8 -> x2, other arithmetic: 15.8 us -> 1.76 us  [the longest x1 1.65 us: per_device(): state_rows, = gather_rows((state_slope.astype(jnp.bfloat16),), size, 4)]
  transfers between devices with their start and end apart: 22 -> 6, of which waited for: 21 -> 2; matrix products, arithmetic and copies ran while one was open for 17% -> 19% of each run, Pallas kernels for 0% -> 32%
where the time goes in v1:
time: 762 us; the launch traced here: 751 us
  Pallas kernels  326 us (43%)
  matrix products  126 us (17%)
  waiting for transfers between devices  88.4 us (12%)
  local copies, waits for them, and re-layouts  77.4 us (10%)
  other arithmetic  77.1 us (10%)
  blocking collectives  39.7 us (5%)
  between operations  15.6 us (2%)
    pallas_call x4, Pallas kernels, product_scatter(): pl.pallas_call(body, out_shape=jax.ShapeDtypeStruct((rows, columns), jnp....  176 us
    pallas_call x3, Pallas kernels, gather_rows(): pl.pallas_call(body, out_shape=[jax.ShapeDtypeStruct((size * rows, column...  150 us
    reduce_scatter x1, waiting for transfers between devices, per_device(): lax.psum_scatter(feed_grad, 'dp', scatter_dimension=0, tiled=True)  87.7 us
    dot_general x4, matrix products, simple_product(): jnp.dot(first_operand, second_operand, preferred_element_type=jnp.float32)  48.4 us
    dot_general x4, matrix products, contract_rows(): lax.dot_general(first_operand, second_operand, (((0,), (0,)), ((), ())),...  42.3 us
    psum x1, blocking collectives, per_device(): lax.psum((attention_gain_term, feed_gain_term, query_gain_term, key_gain_...  39.7 us
    unnamed x144, local copies, waits for them, and re-layouts  26.8 us
  transfers between devices with their start and end apart: 6, of which 2 were waited for; matrix products, arithmetic and copies ran while one was open for 19% of the time, Pallas kernels for 32%

profile of v1, /device:TPU:0, one launch (start us, length us, event | category | flops | bytes accessed | tf_op | source)
XLA Modules:
  0.0 751.2 jit_solution(2309460908566778303)
XLA Ops:
  10.5 2.6 pad_maximum_fusion.4
  22.6 2.9 copy.282
  27.4 75.2 %gather_rows.3 = (bf16[1024,2048]{1,0:T(8,128)(2,1)}, bf16[1024,2048]{1,0:T(8,128)(2,1)}) custom-call(bf16[256,2048]{1,0:T(8,128)(2,1)} %fusion.12.refs_0_, bf16[256,2048]{1,0:T(8,128)(2,1)} %refs_1_.1), custom_call_target="tpu_custom_call" | custom-call | bytes 125829120 | tf_op jit(solution)/shard_map/gather_rows/pallas_call | solution.py:183
  102.6 7.8 %fusion.51 = f32[1024,1024]{0,1:T(8,128)S(1)} fusion(bf16[1024,2048]{1,0:T(8,128)(2,1)} %get-tuple-element.53, bf16[2048,1536]{1,0:T(8,128)(2,1)} %all-gather.4.cloned.1.call-done), kind=kOutput, calls=%fused_computation.133 | convolution fusion | flops 4294967296 | bytes 12582912 | tf_op jit(solution)/shard_map/dot_general | solution.py:49
  118.4 2.4 multiply_multiply_fusion
  120.8 3.2 slice_negate_fusion
  126.1 4.6 fusion.25
  138.9 2.2 fusion.6
  143.0 2.4 fusion.35
  145.5 2.4 fusion.34
  151.0 3.0 slice.144.weight_ref
  154.0 40.5 %product_scatter.4 = f32[256,2048]{1,0:T(8,128)} custom-call(bf16[1024,512]{1,0:T(8,128)(2,1)} %copy.267.left_ref, bf16[2048,512]{1,0:T(8,128)(2,1)} %slice.144.weight_ref), custom_call_target="tpu_custom_call" | custom-call | flops 2147483648 | bytes 62914560 | tf_op jit(solution)/shard_map/product_scatter/pallas_call | solution.py:318
  199.0 37.1 %gather_rows.4 = bf16[1024,2048]{1,0:T(8,128)(2,1)} custom-call(bf16[256,2048]{1,0:T(8,128)(2,1)} %multiply_convert_fusion.3.refs_0_), custom_call_target="tpu_custom_call" | custom-call | bytes 62914560 | tf_op jit(solution)/shard_map/gather_rows/pallas_call | solution.py:183
  237.7 2.9 copy.284
  240.6 19.6 %fusion.60 = f32[1024,3072]{1,0:T(8,128)} fusion(bf16[1024,2048]{1,0:T(8,128)(2,1)} %gather_rows.4, bf16[2048,3072]{1,0:T(8,128)(2,1)} %all-gather.6.cloned.1.call-done.weight_ref), kind=kOutput, calls=%fused_computation.141 | convolution fusion | flops 12884901888 | bytes 29360128 | tf_op jit(solution)/shard_map/dot_general | solution.py:49
  260.8 15.8 %multiply_convert_fusion.1 = (bf16[1024,1536]{1,0:T(8,128)(2,1)S(1)}, bf16[1024,1536]{1,0:T(8,128)(2,1)S(1)}, bf16[1024,1536]{1,0:T(8,128)(2,1)}) fusion(f32[1024,3072]{1,0:T(8,128)} %fusion.60, bf16[1024,2048]{1,0:T(8,128)(2,1)} %get-tuple-element.64, bf16[2048,1536]{1,0:T(8,128)(2,1)} %all-gather.8.cloned.1.call-done.weight_ref), kind=kOutput, calls=%fused_computation.19 | convolution fusion | flops 6467616768 | bytes 32505856 | tf_op jit(solution)/shard_map/dot_general | solution.py:49
  279.2 3.6 pad_maximum_fusion.left_ref
  282.8 49.7 %product_scatter.6 = f32[256,2048]{1,0:T(8,128)} custom-call(bf16[1024,3072]{1,0:T(8,128)(2,1)} %pad_maximum_fusion.left_ref, bf16[2048,3072]{1,0:T(8,128)(2,1)} %all-gather.6.cloned.1.call-done.weight_ref), custom_call_target="tpu_custom_call" | custom-call | flops 12884901888 | bytes 62914560 | tf_op jit(solution)/shard_map/product_scatter/pallas_call | solution.py:318
  332.5 3.0 multiply_reduce_fusion
  337.6 38.0 %gather_rows.5 = bf16[1024,2048]{1,0:T(8,128)(2,1)} custom-call(bf16[256,2048]{1,0:T(8,128)(2,1)} %fusion.53.refs_0_), custom_call_target="tpu_custom_call" | custom-call | bytes 62914560 | tf_op jit(solution)/shard_map/gather_rows/pallas_call | solution.py:183
  375.7 5.3 convolution_convert_fusion.4
  381.5 6.2 convolution_bitcast_fusion
  387.8 3.6 fusion.1
  391.4 2.5 convolution_bitcast_fusion.2
  395.1 3.7 convolution_convert_fusion.3
  398.9 3.4 fusion.33
  404.3 6.5 fusion.3
  421.6 3.4 neg.28
  425.1 2.8 copy.220
  427.8 2.7 copy.287
  430.6 5.2 multiply_reduce_fusion.1
  435.8 3.0 copy.283
  440.2 2.5 copy.280
  443.0 4.9 maximum_multiply_fusion.1
  451.3 2.2 mul.426
  453.6 7.7 %fusion.28 = (f32[512]{0:T(512)S(1)}, bf16[1024,512]{1,0:T(8,128)(2,1)S(1)}) fusion(f32[1024,512]{1,0:T(8,128)} %copy.283, f32[1024,512]{1,0:T(8,128)} %copy.282, f32[512,512]{1,0:T(8,128)} %copy.281, f32[512,512]{1,0:T(8,128)} %copy.280, f32[1024,512]{1,0:T(8,128)S(1)} %copy-done.10, f32[1024,512]{1,0:T(8,128)} %copy.284, ...), kind=kLoop, calls=%fused_computation.60 | loop fusion | flops 7339520 | bytes 22024192 | tf_op jit(solution)/shard_map/reduce_sum | solution.py:393
  461.3 7.0 convolution_convert_fusion.2
  468.4 3.4 pad_maximum_fusion.1
  471.9 11.6 %convolution_convert_fusion.1 = bf16[2048,1536]{1,0:T(8,128)(2,1)} fusion(bf16[1024,2048]{1,0:T(8,128)(2,1)} %get-tuple-element.64, bf16[1024,1536]{1,0:T(8,128)(2,1)} %get-tuple-element.149.left_ref), kind=kOutput, calls=%fused_computation.13 | convolution fusion | flops 6445596672 | bytes 13631488 | tf_op jit(solution)/shard_map/dot_general | solution.py:37
  483.5 20.0 %convolution_convert_fusion = bf16[2048,3072]{1,0:T(8,128)(2,1)} fusion(bf16[1024,2048]{1,0:T(8,128)(2,1)} %gather_rows.4, bf16[1024,1536]{1,0:T(8,128)(2,1)} %copy-done.41, bf16[1024,1536]{1,0:T(8,128)(2,1)} %copy-done.40), kind=kOutput, calls=%fused_computation | convolution fusion | flops 12903776256 | bytes 23068672 | tf_op jit(solution)/shard_map/dot_general | solution.py:37
  503.5 4.7 slice.134.weight_ref
  510.0 41.4 %product_scatter.7 = f32[256,2048]{1,0:T(8,128)} custom-call(bf16[1024,1024]{1,0:T(8,128)(2,1)} %pad_maximum_fusion.3.left_ref, bf16[2048,1024]{1,0:T(8,128)(2,1)} %slice.134.weight_ref), custom_call_target="tpu_custom_call" | custom-call | flops 4294967296 | bytes 62914560 | tf_op jit(solution)/shard_map/product_scatter/pallas_call | solution.py:318
  551.4 2.3 fusion.18
  553.7 39.7 %all-reduce = (f32[2048]{0:T(1024)}, f32[128]{0:T(128)}, f32[128]{0:T(128)}, f32[2048]{0:T(1024)}) all-reduce(f32[2048]{0:T(1024)S(1)} %get-tuple-element.132, f32[128]{0:T(128)S(1)} %reduce_sum.170, f32[128]{0:T(128)S(1)} %get-tuple-element.134, f32[2048]{0:T(1024)S(1)} %get-tuple-element.130), channel_id=1, replica_groups=mesh['dp'=8,'tensor'=4] {'dp','tensor'}, use_global_device_ids=true, to_apply=%region_15.16 | all-reduce | flops 4352 | bytes 34816 | tf_op jit(solution)/shard_map/psum | solution.py:589
  593.3 44.6 %product_scatter.5 = f32[256,2048]{1,0:T(8,128)} custom-call(bf16[1024,1536]{1,0:T(8,128)(2,1)} %get-tuple-element.149.left_ref, bf16[2048,1536]{1,0:T(8,128)(2,1)} %all-gather.8.cloned.1.call-done.weight_ref), custom_call_target="tpu_custom_call" | custom-call | flops 6442450944 | bytes 62914560 | tf_op jit(solution)/shard_map/product_scatter/pallas_call | solution.py:318
  637.9 6.3 fusion.17
  652.8 87.7 %reduce-scatter.6.cloned.1.call-done = bf16[256,3072]{1,0:T(8,128)(2,1)} async-done(((bf16[2048,3072]{1,0:T(8,128)(2,1)}), bf16[256,3072]{1,0:T(8,128)(2,1)}) %reduce-scatter.6.cloned.1.call-update) | async-done | bytes 1572880 | tf_op jit(solution)/shard_map/reduce_scatter | solution.py:511
  740.5 3.4 fusion.56
  (234 shorter events, 78.7 us)
Async XLA Ops:
  7.2 3.3 copy-start.50
  7.2 95.5 %all-gather.4.cloned.1.call-start = ((), (), s32[]{:S(2)}) async-start(), calls=%async_computation.3 | async-start | bytes 7077888 | tf_op jit(solution)/shard_map/all_gather | solution.py:432
  10.4 5.0 copy-start.8
  10.5 230.2 %all-gather.6.cloned.1.call-start = ((), (), s32[]{:S(2)}) async-start(), calls=%async_computation.4 | async-start | bytes 14155776 | tf_op jit(solution)/shard_map/all_gather | solution.py:438
  13.1 247.6 %all-gather.8.cloned.1.call-start = ((), (), s32[]{:S(2)}) async-start(), calls=%async_computation.5 | async-start | bytes 7077888 | tf_op jit(solution)/shard_map/all_gather | solution.py:441
  14.4 629.9 %reduce-scatter.4.cloned.1.call-start = ((), (), s32[]{:S(2)}) async-start(), calls=%async_computation.6 | async-start | bytes 7077888 | tf_op jit(solution)/shard_map/reduce_scatter | solution.py:573
  15.7 10.5 %copy-start.57 = (f32[256]{0:T(256)}, f32[256]{0:T(256)S(1)}, u32[]{:S(2)}) copy-start(f32[256]{0:T(256)S(1)} %add_rsqrt_fusion.3) | copy-start | bytes 3076
  18.8 6.7 copy-start.12
  18.8 6.7 copy-start.19
  21.0 4.5 copy-start.59
  21.0 5.1 copy-start.55
  120.8 3.2 copy-start.5
  131.2 2.8 copy-start.33
  133.1 5.7 copy-start.31
  134.0 4.8 copy-start.23
  136.7 6.3 copy-start.3
  141.1 4.3 copy-start.2
  194.5 3.3 copy-start.54
  282.8 52.7 %copy-start.25 = (bf16[256,2048]{1,0:T(8,128)(2,1)S(1)}, bf16[256,2048]{1,0:T(8,128)(2,1)}, u32[]{:S(2)}) copy-start(bf16[256,2048]{1,0:T(8,128)(2,1)} %refs_1_.1) | copy-start | bytes 3145732
  332.4 3.0 copy-start.1
  332.5 3.5 copy-start.11
  375.6 5.5 copy-start.44
  375.6 5.5 copy-start.46
  375.7 5.8 copy-start.29
  381.0 6.7 slice-start.2
  381.1 17.7 %copy-start.53 = (bf16[512,512]{0,1:T(8,128)(2,1)}, bf16[512,512]{0,1:T(8,128)(2,1)S(1)}, u32[]{:S(2)}) copy-start(bf16[512,512]{0,1:T(8,128)(2,1)S(1)} %get-tuple-element.162) | copy-start | bytes 1572868
  381.5 6.3 slice-start.3
  381.5 6.3 copy-start.52
  387.8 3.6 copy-start.34
  391.4 3.3 copy-start.36
  393.9 4.9 slice-start
  395.1 22.0 %copy-start.15 = (f32[2,128,2,512]{3,1,2,0:T(8,128)}, f32[2,128,2,512]{3,1,2,0:T(8,128)S(1)}, u32[]{:S(2)}) copy-start(f32[2,128,2,512]{3,1,2,0:T(8,128)S(1)} %convolution_multiply_fusion) | copy-start | bytes 3145732
  395.1 3.7 slice-start.1
  395.1 3.7 copy-start.27
  425.1 5.5 copy-start.14
  425.1 5.5 copy-start.22
  425.1 5.5 copy-start.60
  435.8 3.0 copy-start.16
  447.8 3.1 copy-start.30
  453.6 7.7 %copy-start.47 = (bf16[1024,256]{1,0:T(8,128)(2,1)S(1)}, bf16[1024,256]{1,0:T(8,128)(2,1)}, u32[]{:S(2)}) copy-start(bf16[1024,256]{1,0:T(8,128)(2,1)} %copy.279) | copy-start | bytes 1572868
  461.3 7.0 copy-start.42
  471.8 177.1 %reduce-scatter.8.cloned.1.call-start = ((), (), s32[]{:S(2)}) async-start(), calls=%async_computation.8 | async-start | bytes 7077888 | tf_op jit(solution)/shard_map/reduce_scatter | solution.py:502
  483.5 257.0 %reduce-scatter.6.cloned.1.call-start = ((), (), s32[]{:S(2)}) async-start(), calls=%async_computation.7 | async-start | bytes 14155776 | tf_op jit(solution)/shard_map/reduce_scatter | solution.py:511
  503.5 4.8 copy-start.48
  510.0 41.4 %copy-start.9 = (bf16[256,2048]{1,0:T(8,128)(2,1)S(1)}, bf16[256,2048]{1,0:T(8,128)(2,1)}, u32[]{:S(2)}) copy-start(bf16[256,2048]{1,0:T(8,128)(2,1)} %param.13) | copy-start | bytes 3145732
  510.0 41.4 %copy-start.56 = (f32[2048]{0:T(1024)S(1)}, f32[2048]{0:T(1024)}, u32[]{:S(2)}) copy-start(f32[2048]{0:T(1024)} %param.14) | copy-start | bytes 24580
  510.0 41.4 %copy-start.58 = (f32[256]{0:T(256)S(1)}, f32[256]{0:T(256)}, u32[]{:S(2)}) copy-start(f32[256]{0:T(256)} %copy-done.57) | copy-start | bytes 3076
  648.1 3.8 copy-start.35
  (26 other events, 51.7 us)
Sparse Core Ops, SparseCore 0:
  10.6 67.4 all-gather.3
  80.3 115.3 all-gather.5
  197.8 62.8 all-gather.7
  471.9 67.2 reduce-scatter.3
  541.4 69.2 reduce-scatter.7
  612.8 127.6 reduce-scatter.5

commit v2 on v1

v2 whole, which is shorter than its diff:
```python
import functools

import jax
import jax.numpy as jnp
import numpy as np
from jax import lax
from jax.experimental import pallas as pl
from jax.experimental.pallas import tpu as pltpu
from jax.sharding import PartitionSpec as P


SEQUENCE_LENGTH = 1024

epsilon = 1e-06
rope_base = 1000000.0

MESH = pl.DeviceIdType.MESH
VMEM_LIMIT = 62 * 1024 * 1024


def row_scale(values):
    return lax.rsqrt(jnp.mean(values * values, axis=-1, keepdims=True) + epsilon)


def contract_rows(first_operand, second_operand):
    return lax.dot_general(
        first_operand, second_operand, (((0,), (0,)), ((), ())), preferred_element_type=jnp.float32
    )


def times_transposed(first_operand, second_operand):
    return lax.dot_general(
        first_operand, second_operand, (((1,), (1,)), ((), ())), preferred_element_type=jnp.float32
    )


def simple_product(first_operand, second_operand):
    return jnp.dot(first_operand, second_operand, preferred_element_type=jnp.float32)


def remote(source, target, send_sem, recv_sem, peer, axis="tensor"):
    return pltpu.make_async_remote_copy(
        src_ref=source,
        dst_ref=target,
        send_sem=send_sem,
        recv_sem=recv_sem,
        device_id={axis: peer},
        device_id_type=MESH,
    )


def greet(peers):
    barrier = pltpu.get_barrier_semaphore()
    for axis, peer in peers:
        pl.semaphore_signal(barrier, inc=1, device_id={axis: peer}, device_id_type=MESH)
    pl.semaphore_wait(barrier, len(peers))


def square_peers(me):
    column = lax.rem(me, 2)
    row = me // 2
    return row * 2 + (1 - column), (1 - row) * 2 + column, (1 - row) * 2 + (1 - column)


def gather_kernel_square(count, *refs):
    own_refs, out_refs, held_refs = refs[:count], refs[count : 2 * count], refs[2 * count : 3 * count]
    send_sem, recv_sem, local_sem = refs[3 * count :]
    me = lax.axis_index("tensor")
    beside, below, across = square_peers(me)
    greet((("tensor", beside), ("tensor", below)))
    rows = own_refs[0].shape[0]
    half = rows // 2
    first, second = pl.ds(0, half), pl.ds(half, half)
    copies = []
    stores = []

    def store(k, source, slot, part, sem):
        start = slot * rows + (half if part == 1 else 0)
        size = rows if part is None else half
        copy = pltpu.make_async_copy(
            source, out_refs[k].at[pl.ds(pl.multiple_of(start, half), size)], local_sem.at[k, sem]
        )
        copy.start()
        stores.append(copy)

    for k in range(count):
        own, held = own_refs[k], held_refs[k]

        def send(index, source, slot, part, peer):
            copy = remote(
                source, held.at[slot, part], send_sem.at[k, index], recv_sem.at[k, index], peer
            )
            copy.start()
            copies.append(copy)
            return copy

        x_first = send(0, own.at[first], me, first, beside)
        y_second = send(1, own.at[second], me, second, below)
        x_second = send(2, own.at[second], me, second, beside)
        y_first = send(3, own.at[first], me, first, below)
        store(k, own, me, None, 0)
        x_first.wait_recv()
        y_pass = send(4, held.at[beside, first], beside, first, below)
        y_second.wait_recv()
        x_pass = send(5, held.at[below, second], below, second, beside)
        store(k, held.at[beside, first], beside, 0, 1)
        store(k, held.at[below, second], below, 1, 2)
    for k in range(count):
        held = held_refs[k]
        x_second, y_first, y_pass, x_pass = copies[6 * k + 2 : 6 * k + 6]
        x_second.wait_recv()
        store(k, held.at[beside, second], beside, 1, 3)
        y_first.wait_recv()
        store(k, held.at[below, first], below, 0, 4)
        y_pass.wait_recv()
        store(k, held.at[across, first], across, 0, 5)
        x_pass.wait_recv()
        store(k, held.at[across, second], across, 1, 6)
    for copy in copies:
        copy.wait_send()
    for copy in stores:
        copy.wait()


def gather_kernel_direct(size, count, *refs):
    own_refs, out_refs, held_refs = refs[:count], refs[count : 2 * count], refs[2 * count : 3 * count]
    send_sem, recv_sem, local_sem = refs[3 * count :]
    me = lax.axis_index("tensor")
    peers = [lax.rem(me + step, size) for step in range(1, size)]
    greet([("tensor", peer) for peer in peers])
    rows = own_refs[0].shape[0]
    copies = []
    stores = []
    for k in range(count):
        for step, peer in enumerate(peers):
            copy = remote(
                own_refs[k], held_refs[k].at[me], send_sem.at[k, step], recv_sem.at[k, step], peer
            )
            copy.start()
            copies.append(copy)
    for k in range(count):
        for step in range(size):
            source = own_refs[k]
            slot = lax.rem(me + size - step, size)
            if step > 0:
                copies[k * (size - 1) + step - 1].wait_recv()
                source = held_refs[k].at[slot]
            copy = pltpu.make_async_copy(
                source,
                out_refs[k].at[pl.ds(pl.multiple_of(slot * rows, rows), rows)],
                local_sem.at[k, step],
            )
            copy.start()
            stores.append(copy)
    for copy in copies:
        copy.wait_send()
    for copy in stores:
        copy.wait()


def gather_rows(arrays, size, collective_id):
    count = len(arrays)
    rows, columns = arrays[0].shape
    square = size == 4
    body = (
        functools.partial(gather_kernel_square, count)
        if square
        else functools.partial(gather_kernel_direct, size, count)
    )
    sends = 6 if square else size - 1
    locals_ = 7 if square else size
    return pl.pallas_call(
        body,
        out_shape=[jax.ShapeDtypeStruct((size * rows, columns), a.dtype) for a in arrays],
        in_specs=[pl.BlockSpec(memory_space=pltpu.VMEM)] * count,
        out_specs=[pl.BlockSpec(memory_space=pl.ANY)] * count,
        scratch_shapes=[pltpu.VMEM((size, rows, columns), a.dtype) for a in arrays]
        + [
            pltpu.SemaphoreType.DMA((count, sends)),
            pltpu.SemaphoreType.DMA((count, sends)),
            pltpu.SemaphoreType.DMA((count, locals_)),
        ],
        compiler_params=pltpu.CompilerParams(
            collective_id=collective_id, has_side_effects=True, vmem_limit_bytes=VMEM_LIMIT
        ),
        cost_estimate=pl.CostEstimate(
            flops=0, bytes_accessed=count * 30 * size * rows * columns, transcendentals=0
        ),
        name="gather_rows",
    )(*arrays)


def block_product(left_ref, start, rows, weight_ref, write):
    total = weight_ref.shape[0]
    tile = min(512, total)
    left = left_ref[pl.ds(pl.multiple_of(start, rows), rows), :]

    def step(index, carry):
        columns = pl.ds(pl.multiple_of(index * tile, tile), tile)
        write(columns, times_transposed(left, weight_ref[columns, :]))
        return carry

    lax.fori_loop(0, total // tile, step, 0)


def other_members(axis, count):
    me = lax.axis_index(axis)
    return [lax.rem(me + step, count) for step in range(1, count)]


def send_terms(axis, peers, source, landing, send_sem, recv_sem):
    me = lax.axis_index(axis)
    landing[me] = source[...]
    copies = []
    for step, peer in enumerate(peers):
        copy = remote(source, landing.at[me], send_sem.at[step], recv_sem.at[step], peer, axis)
        copy.start()
        copies.append(copy)
    return copies


def add_terms(landing, copies):
    for copy in copies:
        copy.wait_recv()
    total = landing[0]
    for index in range(1, landing.shape[0]):
        total = total + landing[index]
    return total


def scatter_kernel(sizes, with_terms, *refs):
    if with_terms:
        left_ref, weight_ref, terms_ref, out_ref, terms_out_ref = refs[:5]
        inner, outer, partial_ref = refs[-7:-4]
        inner_send, inner_recv, outer_send, outer_recv = refs[-4:]
        buffers = refs[5:-7]
    else:
        left_ref, weight_ref, out_ref = refs[:3]
        buffers = refs[3:]
    data_size, size = sizes
    if size == 4:
        beside, below, across = square_peers(lax.axis_index("tensor"))
        near = [("tensor", beside), ("tensor", below)]
    else:
        near = [("tensor", peer) for peer in other_members("tensor", size)]
    if with_terms:
        if size == 4:
            near.append(("tensor", across))
        near += [("dp", peer) for peer in other_members("dp", data_size)]
    greet(near)
    if with_terms:
        inner_copies = send_terms(
            "tensor", other_members("tensor", size), terms_ref, inner, inner_send, inner_recv
        )
    if size == 4:
        scatter_square(left_ref, weight_ref, out_ref, *buffers)
    else:
        scatter_direct(size, left_ref, weight_ref, out_ref, *buffers)
    if with_terms:
        partial_ref[...] = add_terms(inner, inner_copies)
        outer_copies = send_terms(
            "dp", other_members("dp", data_size), partial_ref, outer, outer_send, outer_recv
        )
        terms_out_ref[...] = add_terms(outer, outer_copies)
        for copy in inner_copies + outer_copies:
            copy.wait_send()


def scatter_square(left_ref, weight_ref, out_ref, outgoing, passing, arriving, send_sem, recv_sem):
    me = lax.axis_index("tensor")
    beside, below, across = square_peers(me)
    rows = out_ref.shape[0]
    half = rows // 2
    first, second = pl.ds(0, half), pl.ds(half, half)

    def fill(slot, owner):
        def write(columns, values):
            outgoing[slot, :, columns] = values.astype(outgoing.dtype)

        block_product(left_ref, owner * rows, rows, weight_ref, write)

    def send(index, source, target, peer):
        copy = remote(source, target, send_sem.at[index], recv_sem.at[index], peer)
        copy.start()
        return copy

    fill(0, across)
    x_pass = send(0, outgoing.at[0, first], passing.at[0], beside)
    y_pass = send(1, outgoing.at[0, second], passing.at[1], below)
    fill(1, beside)
    x_first = send(2, outgoing.at[1, first], arriving.at[0, first], beside)
    fill(2, below)
    y_second = send(3, outgoing.at[2, second], arriving.at[1, second], below)

    def write_own(columns, values):
        out_ref[:, columns] = values

    block_product(left_ref, me * rows, rows, weight_ref, write_own)
    y_pass.wait_recv()
    outgoing[1, second, :] = (
        outgoing[1, second, :].astype(jnp.float32) + passing[1].astype(jnp.float32)
    ).astype(outgoing.dtype)
    x_second = send(4, outgoing.at[1, second], arriving.at[0, second], beside)
    x_pass.wait_recv()
    outgoing[2, first, :] = (
        outgoing[2, first, :].astype(jnp.float32) + passing[0].astype(jnp.float32)
    ).astype(outgoing.dtype)
    y_first = send(5, outgoing.at[2, first], arriving.at[1, first], below)
    x_first.wait_recv()
    y_second.wait_recv()
    out_ref[first, :] += arriving[0, first, :].astype(jnp.float32)
    out_ref[second, :] += arriving[1, second, :].astype(jnp.float32)
    x_second.wait_recv()
    y_first.wait_recv()
    out_ref[second, :] += arriving[0, second, :].astype(jnp.float32)
    out_ref[first, :] += arriving[1, first, :].astype(jnp.float32)
    for copy in (x_pass, y_pass, x_first, y_second, x_second, y_first):
        copy.wait_send()


def scatter_direct(size, left_ref, weight_ref, out_ref, outgoing, arriving, send_sem, recv_sem):
    me = lax.axis_index("tensor")
    rows = out_ref.shape[0]
    copies = []
    for step, peer in enumerate(other_members("tensor", size)):

        def write(columns, values, step=step):
            outgoing[step, :, columns] = values.astype(outgoing.dtype)

        block_product(left_ref, peer * rows, rows, weight_ref, write)
        copy = remote(
            outgoing.at[step], arriving.at[step], send_sem.at[step], recv_sem.at[step], peer
        )
        copy.start()
        copies.append(copy)

    def write_own(columns, values):
        out_ref[:, columns] = values

    block_product(left_ref, me * rows, rows, weight_ref, write_own)
    for step, copy in enumerate(copies):
        copy.wait_recv()
        out_ref[...] += arriving[step].astype(jnp.float32)
    for copy in copies:
        copy.wait_send()


def product_scatter(left, weight, first_column, sizes, collective_id, terms=None):
    total_rows, depth = left.shape
    columns = weight.shape[0]
    data_size, size = sizes
    rows = total_rows // size
    if size == 4:
        buffers = [
            pltpu.VMEM((3, rows, columns), jnp.bfloat16),
            pltpu.VMEM((2, rows // 2, columns), jnp.bfloat16),
            pltpu.VMEM((2, rows, columns), jnp.bfloat16),
        ]
        sends = 6
    else:
        buffers = [pltpu.VMEM((size - 1, rows, columns), jnp.bfloat16)] * 2
        sends = size - 1
    buffers += [pltpu.SemaphoreType.DMA((sends,)), pltpu.SemaphoreType.DMA((sends,))]
    block = first_column // depth
    whole = pl.BlockSpec(memory_space=pltpu.VMEM)
    in_specs = [
        pl.BlockSpec((total_rows, depth), lambda i: (0, 0), pipeline_mode=pl.Buffered(1)),
        pl.BlockSpec((columns, depth), lambda i: (0, block), pipeline_mode=pl.Buffered(1)),
    ]
    out_specs = [pl.BlockSpec((rows, columns), lambda i: (0, 0))]
    out_shape = [jax.ShapeDtypeStruct((rows, columns), jnp.float32)]
    operands = [left, weight]
    if terms is not None:
        operands.append(terms)
        in_specs.append(pl.BlockSpec(terms.shape, lambda i: (0, 0)))
        out_specs.append(pl.BlockSpec(terms.shape, lambda i: (0, 0)))
        out_shape.append(jax.ShapeDtypeStruct(terms.shape, terms.dtype))
        buffers += [
            pltpu.VMEM((size, *terms.shape), terms.dtype),
            pltpu.VMEM((data_size, *terms.shape), terms.dtype),
            pltpu.VMEM(terms.shape, terms.dtype),
        ]
        for count in (size, size, data_size, data_size):
            buffers.append(pltpu.SemaphoreType.DMA((count - 1,)))
    out = pl.pallas_call(
        functools.partial(scatter_kernel, sizes, terms is not None),
        grid=(1,),
        out_shape=out_shape,
        in_specs=in_specs,
        out_specs=out_specs,
        scratch_shapes=buffers,
        compiler_params=pltpu.CompilerParams(
            collective_id=collective_id, has_side_effects=True, vmem_limit_bytes=VMEM_LIMIT
        ),
        cost_estimate=pl.CostEstimate(
            flops=2 * total_rows * depth * columns,
            bytes_accessed=30 * total_rows * columns,
            transcendentals=0,
        ),
        name="product_scatter",
    )(*operands)
    return out[0] if terms is None else out


LOG2E = 1.4426950408889634


def turn_tables(head_size):
    half_size = head_size // 2
    frequency = np.float32(rope_base) ** (
        -(np.arange(half_size, dtype=np.float32) * np.float32(2.0) / np.float32(head_size))
    )
    angles = np.arange(SEQUENCE_LENGTH, dtype=np.float32)[:, None] * frequency[None, :]
    cosine, sine = np.cos(angles), np.sin(angles)
    return (
        np.concatenate([cosine, cosine], axis=1).astype(np.float32),
        np.concatenate([-sine, sine], axis=1).astype(np.float32),
    )


def turn(values, cosine, sine):
    return values * cosine + pltpu.roll(values, values.shape[-1] // 2, 1) * sine


def turn_back(values, cosine, sine):
    return values * cosine - pltpu.roll(values, values.shape[-1] // 2, 1) * sine


def contract_first(first_operand, second_operand):
    return lax.dot_general(
        first_operand, second_operand, (((0,), (0,)), ((), ())), preferred_element_type=jnp.float32
    )


def visible_scores(key_rows, query_rows, first_row, multiplier):
    scores = times_transposed(key_rows, query_rows) * multiplier
    _, queries = scores.shape
    key_at = lax.broadcasted_iota(jnp.int32, (queries, queries), 0)
    query_at = lax.broadcasted_iota(jnp.int32, (queries, queries), 1)
    corner = jnp.where(query_at >= key_at, scores[first_row:], -1e30)
    if first_row == 0:
        return corner
    return jnp.concatenate([scores[:first_row], corner], axis=0)


def attention_forward_kernel(
    grouping, head_size, block, rows_ref, weight_ref, cosine_ref, sine_ref, query_gain_ref, key_gain_ref,
    raw_ref, mixed_ref, total_ref, query_ref, key_ref, value_ref,
):
    sequence = rows_ref.shape[0]
    multiplier = head_size ** (-0.5) * LOG2E
    cosine, sine = cosine_ref[...], sine_ref[...]
    raw_ref[...] = simple_product(rows_ref[...], weight_ref[...])
    for part in range(grouping + 1):
        raw = raw_ref[:, part * head_size : (part + 1) * head_size]
        gain = key_gain_ref[...] if part == grouping else query_gain_ref[...]
        turned = turn(raw * row_scale(raw) * gain, cosine, sine).astype(jnp.bfloat16)
        if part == grouping:
            key_ref[...] = turned
        else:
            query_ref[part] = turned
    value_ref[...] = raw_ref[:, (grouping + 1) * head_size :].astype(jnp.bfloat16)
    for part in range(grouping):
        totals = []
        for first_row in range(0, sequence, block):
            last_row = first_row + block
            scores = visible_scores(
                key_ref[:last_row, :], query_ref[part, first_row:last_row, :], first_row, multiplier
            )
            highest = jnp.max(scores, axis=0, keepdims=True)
            weights = jnp.exp2(scores - highest)
            total = jnp.sum(weights, axis=0, keepdims=True)
            weights = (weights * (1.0 / total)).astype(jnp.bfloat16)
            mixed_ref[first_row:last_row, part * head_size : (part + 1) * head_size] = contract_first(
                weights, value_ref[:last_row, :]
            ).astype(mixed_ref.dtype)
            totals.append(highest + jnp.log2(total))
        total_ref[0, part : part + 1, :] = jnp.concatenate(totals, axis=1)


def attention_forward(rows, weight, cosine, sine, query_gain, key_gain, heads, grouping):
    total_rows, depth = rows.shape
    head_size = query_gain.shape[0]
    sequences = total_rows // SEQUENCE_LENGTH
    width = (grouping + 2) * head_size
    block = min(256, SEQUENCE_LENGTH)
    table = pl.BlockSpec((SEQUENCE_LENGTH, head_size), lambda s, h: (0, 0))
    gain = pl.BlockSpec((1, head_size), lambda s, h: (0, 0))
    elements = heads * grouping * total_rows * SEQUENCE_LENGTH // 2
    return pl.pallas_call(
        functools.partial(attention_forward_kernel, grouping, head_size, block),
        grid=(sequences, heads),
        out_shape=[
            jax.ShapeDtypeStruct((total_rows, heads * width), jnp.float32),
            jax.ShapeDtypeStruct((total_rows, heads * grouping * head_size), jnp.bfloat16),
            jax.ShapeDtypeStruct((heads, grouping, total_rows), jnp.float32),
        ],
        in_specs=[
            pl.BlockSpec((SEQUENCE_LENGTH, depth), lambda s, h: (s, 0)),
            pl.BlockSpec((depth, width), lambda s, h: (0, h)),
            table,
            table,
            gain,
            gain,
        ],
        out_specs=[
            pl.BlockSpec((SEQUENCE_LENGTH, width), lambda s, h: (s, h)),
            pl.BlockSpec((SEQUENCE_LENGTH, grouping * head_size), lambda s, h: (s, h)),
            pl.BlockSpec((1, grouping, SEQUENCE_LENGTH), lambda s, h: (h, 0, s)),
        ],
        scratch_shapes=[
            pltpu.VMEM((grouping, SEQUENCE_LENGTH, head_size), jnp.bfloat16),
            pltpu.VMEM((SEQUENCE_LENGTH, head_size), jnp.bfloat16),
            pltpu.VMEM((SEQUENCE_LENGTH, head_size), jnp.bfloat16),
        ],
        compiler_params=pltpu.CompilerParams(vmem_limit_bytes=VMEM_LIMIT),
        cost_estimate=pl.CostEstimate(
            flops=2 * total_rows * depth * heads * width + 4 * elements * head_size,
            bytes_accessed=2 * (total_rows * depth + depth * heads * width),
            transcendentals=elements,
        ),
        name="attention_forward",
    )(rows, weight, cosine, sine, query_gain.reshape(1, -1), key_gain.reshape(1, -1))


def norm_back(turned_slope, raw, gain, cosine, sine):
    norm_slope = turn_back(turned_slope, cosine, sine)
    scale = row_scale(raw)
    unit = raw * scale
    term = norm_slope * unit
    unit_slope = norm_slope * gain
    slope = scale * (unit_slope - unit * jnp.mean(unit_slope * unit, axis=-1, keepdims=True))
    return slope.astype(jnp.bfloat16), jnp.sum(term, axis=0, keepdims=True)


def attention_backward_kernel(
    grouping, head_size, block, state_ref, weight_ref, raw_ref, mixed_ref, total_ref, cosine_ref, sine_ref,
    query_gain_ref, key_gain_ref, slope_ref, gain_ref, query_ref, key_ref, value_ref, out_slope_ref,
    turned_ref, key_sum_ref, value_sum_ref,
):
    sequence = state_ref.shape[0]
    scale_factor = head_size ** (-0.5)
    multiplier = scale_factor * LOG2E
    cosine, sine = cosine_ref[...], sine_ref[...]

    @pl.when((pl.program_id(0) == 0) & (pl.program_id(1) == 0))
    def _():
        gain_ref[...] = jnp.zeros_like(gain_ref)

    out_slope_ref[...] = simple_product(state_ref[...], weight_ref[...]).astype(jnp.bfloat16)
    for part in range(grouping + 1):
        raw = raw_ref[:, part * head_size : (part + 1) * head_size]
        gain = key_gain_ref[...] if part == grouping else query_gain_ref[...]
        turned = turn(raw * row_scale(raw) * gain, cosine, sine).astype(jnp.bfloat16)
        if part == grouping:
            key_ref[...] = turned
        else:
            query_ref[part] = turned
    value_ref[...] = raw_ref[:, (grouping + 1) * head_size :].astype(jnp.bfloat16)
    key_sum_ref[...] = jnp.zeros_like(key_sum_ref)
    value_sum_ref[...] = jnp.zeros_like(value_sum_ref)
    ones = jnp.ones((8, head_size), jnp.float32)
    for part in range(grouping):
        lanes = slice(part * head_size, (part + 1) * head_size)
        for first_row in range(0, sequence, block):
            last_row = first_row + block
            query_rows = query_ref[part, first_row:last_row, :]
            slope_rows = out_slope_ref[first_row:last_row, lanes]
            scores = visible_scores(key_ref[:last_row, :], query_rows, first_row, multiplier)
            weights = jnp.exp2(scores - total_ref[0, part : part + 1, first_row:last_row])
            value_sum_ref[:last_row, :] += simple_product(weights.astype(jnp.bfloat16), slope_rows)
            product = slope_rows.astype(jnp.float32) * mixed_ref[first_row:last_row, lanes].astype(jnp.float32)
            centre = lax.dot_general(
                ones,
                product,
                (((1,), (1,)), ((), ())),
                preferred_element_type=jnp.float32,
                precision=lax.Precision.HIGHEST,
            )[:1]
            weight_slope = times_transposed(value_ref[:last_row, :], slope_rows)
            score_slope = (weights * (weight_slope - centre)).astype(jnp.bfloat16)
            key_sum_ref[:last_row, :] += simple_product(score_slope, query_rows)
            turned_ref[first_row:last_row, :] = (
                contract_first(score_slope, key_ref[:last_row, :]) * scale_factor
            )
        slope, term = norm_back(
            turned_ref[...], raw_ref[:, lanes], query_gain_ref[...], cosine, sine
        )
        slope_ref[:, lanes] = slope
        gain_ref[0:1, :] += term
    lanes = slice(grouping * head_size, (grouping + 1) * head_size)
    slope, term = norm_back(
        key_sum_ref[...] * scale_factor, raw_ref[:, lanes], key_gain_ref[...], cosine, sine
    )
    slope_ref[:, lanes] = slope
    gain_ref[1:2, :] += term
    slope_ref[:, (grouping + 1) * head_size :] = value_sum_ref[...].astype(jnp.bfloat16)


def attention_backward(
    state_rows, weight, weight_start, raw, mixed, totals, cosine, sine, query_gain, key_gain, heads, grouping
):
    total_rows, depth = state_rows.shape
    head_size = query_gain.shape[0]
    sequences = total_rows // SEQUENCE_LENGTH
    width = (grouping + 2) * head_size
    out_width = grouping * head_size
    block = min(256, SEQUENCE_LENGTH)
    first_block = weight_start // out_width
    table = pl.BlockSpec((SEQUENCE_LENGTH, head_size), lambda s, h: (0, 0))
    gain = pl.BlockSpec((1, head_size), lambda s, h: (0, 0))
    elements = heads * grouping * total_rows * SEQUENCE_LENGTH // 2
    return pl.pallas_call(
        functools.partial(attention_backward_kernel, grouping, head_size, block),
        grid=(sequences, heads),
        out_shape=[
            jax.ShapeDtypeStruct((total_rows, heads * width), jnp.bfloat16),
            jax.ShapeDtypeStruct((8, head_size), jnp.float32),
        ],
        in_specs=[
            pl.BlockSpec((SEQUENCE_LENGTH, depth), lambda s, h: (s, 0)),
            pl.BlockSpec((depth, out_width), lambda s, h: (0, first_block + h)),
            pl.BlockSpec((SEQUENCE_LENGTH, width), lambda s, h: (s, h)),
            pl.BlockSpec((SEQUENCE_LENGTH, out_width), lambda s, h: (s, h)),
            pl.BlockSpec((1, grouping, SEQUENCE_LENGTH), lambda s, h: (h, 0, s)),
            table,
            table,
            gain,
            gain,
        ],
        out_specs=[
            pl.BlockSpec((SEQUENCE_LENGTH, width), lambda s, h: (s, h)),
            pl.BlockSpec((8, head_size), lambda s, h: (0, 0)),
        ],
        scratch_shapes=[
            pltpu.VMEM((grouping, SEQUENCE_LENGTH, head_size), jnp.bfloat16),
            pltpu.VMEM((SEQUENCE_LENGTH, head_size), jnp.bfloat16),
            pltpu.VMEM((SEQUENCE_LENGTH, head_size), jnp.bfloat16),
            pltpu.VMEM((SEQUENCE_LENGTH, out_width), jnp.bfloat16),
            pltpu.VMEM((SEQUENCE_LENGTH, head_size), jnp.float32),
            pltpu.VMEM((SEQUENCE_LENGTH, head_size), jnp.float32),
            pltpu.VMEM((SEQUENCE_LENGTH, head_size), jnp.float32),
        ],
        compiler_params=pltpu.CompilerParams(vmem_limit_bytes=VMEM_LIMIT),
        cost_estimate=pl.CostEstimate(
            flops=2 * total_rows * depth * heads * out_width + 10 * elements * head_size,
            bytes_accessed=2 * (total_rows * depth + depth * heads * out_width),
            transcendentals=elements,
        ),
        name="attention_backward",
    )(
        state_rows, weight, raw, mixed, totals, cosine, sine,
        query_gain.reshape(1, -1), key_gain.reshape(1, -1),
    )


def per_device(
    block_input,
    attention_gain,
    query_weight,
    key_matrix,
    value_matrix,
    query_gain,
    key_gain,
    output_weight,
    feed_gain,
    gate_weight,
    up_weight,
    down_weight,
    out_cotangent,
):
    size = lax.axis_size("tensor")
    sizes = (lax.axis_size("dp"), size)
    model_width = block_input.shape[1]
    head_size = query_gain.shape[0]
    query_columns = query_weight.shape[1]
    key_columns = key_matrix.shape[1]
    heads = key_columns // head_size
    grouping = query_columns // key_columns
    hidden_columns = gate_weight.shape[1]
    qkv_columns = query_columns + 2 * key_columns
    query_width = grouping * head_size
    width = query_width + 2 * head_size
    cosine, sine = turn_tables(head_size)

    mixing_parts = []
    for head in range(heads):
        mixing_parts += [
            query_weight[:, head * query_width : (head + 1) * query_width],
            key_matrix[:, head * head_size : (head + 1) * head_size],
            value_matrix[:, head * head_size : (head + 1) * head_size],
        ]
    mixing_full = lax.all_gather(
        jnp.concatenate([*mixing_parts, output_weight.T], axis=1), "dp", axis=0, tiled=True
    )
    feeding_full = lax.all_gather(
        jnp.concatenate([gate_weight, up_weight], axis=1), "dp", axis=0, tiled=True
    )
    down_full = lax.all_gather(down_weight.T, "dp", axis=0, tiled=True)

    input_float = block_input.astype(jnp.float32)
    first_scale = row_scale(input_float)
    first_unit = input_float * first_scale
    mixer_local = (first_unit * attention_gain).astype(jnp.bfloat16)
    mixer_rows, cotangent_rows = gather_rows((mixer_local, out_cotangent), size, 0)

    raw, mixed_rows, totals = attention_forward(
        mixer_rows, mixing_full, cosine, sine, query_gain, key_gain, heads, grouping
    )
    hidden_state = input_float + product_scatter(mixed_rows, mixing_full, qkv_columns, sizes, 1)
    second_scale = row_scale(hidden_state)
    second_unit = hidden_state * second_scale
    feed_local = (second_unit * feed_gain).astype(jnp.bfloat16)
    (feed_rows,) = gather_rows((feed_local,), size, 2)
    both_values = simple_product(feed_rows, feeding_full).astype(jnp.bfloat16)
    gate_values = both_values[:, :hidden_columns].astype(jnp.float32)
    up_values = both_values[:, hidden_columns:].astype(jnp.float32)
    gate_sigmoid = jax.nn.sigmoid(gate_values)
    hidden_rows = (gate_values * gate_sigmoid * up_values).astype(jnp.bfloat16)
    down_grad = contract_rows(cotangent_rows, hidden_rows).astype(jnp.bfloat16)
    down_grad, down_full = lax.optimization_barrier((down_grad, down_full))
    down_total = lax.psum_scatter(down_grad, "dp", scatter_dimension=0, tiled=True)

    hidden_slope = simple_product(cotangent_rows, down_full)
    gate_slope = (
        hidden_slope * up_values * gate_sigmoid * (1.0 + gate_values * (1.0 - gate_sigmoid))
    ).astype(jnp.bfloat16)
    up_slope = (hidden_slope * gate_values * gate_sigmoid).astype(jnp.bfloat16)
    feed_slope = jnp.concatenate([gate_slope, up_slope], axis=1)
    feed_grad = contract_rows(feed_rows, feed_slope).astype(jnp.bfloat16)
    feed_grad, feed_slope = lax.optimization_barrier((feed_grad, feed_slope))
    feed_total = lax.psum_scatter(feed_grad, "dp", scatter_dimension=0, tiled=True)
    feed_back = product_scatter(feed_slope, feeding_full, 0, sizes, 3)
    feed_gain_term = jnp.sum(feed_back * second_unit, axis=0)
    feed_unit_slope = feed_back * feed_gain
    state_slope = out_cotangent.astype(jnp.float32) + second_scale * (
        feed_unit_slope
        - second_unit * jnp.mean(feed_unit_slope * second_unit, axis=-1, keepdims=True)
    )
    (state_rows,) = gather_rows((state_slope.astype(jnp.bfloat16),), size, 4)
    qkv_slope, head_terms = attention_backward(
        state_rows, mixing_full, qkv_columns, raw, mixed_rows, totals, cosine, sine,
        query_gain, key_gain, heads, grouping,
    )
    mixing_grad = jnp.concatenate(
        [contract_rows(mixer_rows, qkv_slope), contract_rows(state_rows, mixed_rows)], axis=1
    ).astype(jnp.bfloat16)
    mixing_grad, qkv_slope = lax.optimization_barrier((mixing_grad, qkv_slope))
    mixing_total = lax.psum_scatter(
        mixing_grad, "dp", scatter_dimension=0, tiled=True
    ).astype(jnp.float32)
    mixer_back = product_scatter(qkv_slope, mixing_full, 0, sizes, 5)
    attention_gain_term = jnp.sum(mixer_back * first_unit, axis=0)
    mixer_unit_slope = mixer_back * attention_gain
    input_gradient = (
        state_slope
        + first_scale
        * (
            mixer_unit_slope
            - first_unit * jnp.mean(mixer_unit_slope * first_unit, axis=-1, keepdims=True)
        )
    ).astype(jnp.bfloat16)
    gain_rows = model_width // head_size
    terms = jnp.concatenate(
        [
            attention_gain_term.reshape(gain_rows, head_size),
            feed_gain_term.reshape(gain_rows, head_size),
            head_terms,
        ],
        axis=0,
    )
    feed_sum, terms = product_scatter(hidden_rows, down_full, 0, sizes, 6, terms)
    block_output = (hidden_state + feed_sum).astype(jnp.bfloat16)
    feed_total = feed_total.astype(jnp.float32)

    def column_parts(start, part_width):
        return jnp.concatenate(
            [
                mixing_total[:, head * width + start : head * width + start + part_width]
                for head in range(heads)
            ],
            axis=1,
        )

    return (
        block_output,
        input_gradient,
        terms[:gain_rows].reshape(-1),
        column_parts(0, query_width),
        column_parts(query_width, head_size),
        column_parts(query_width + head_size, head_size),
        terms[2 * gain_rows],
        terms[2 * gain_rows + 1],
        mixing_total[:, qkv_columns:].T,
        terms[gain_rows : 2 * gain_rows].reshape(-1),
        feed_total[:, :hidden_columns],
        feed_total[:, hidden_columns:],
        down_total.astype(jnp.float32).T,
    )


def solution(mesh):
    in_specs = (
        P(("dp", "tensor"), None),
        P(),
        P("dp", "tensor"),
        P("dp", "tensor"),
        P("dp", "tensor"),
        P(),
        P(),
        P("tensor", "dp"),
        P(),
        P("dp", "tensor"),
        P("dp", "tensor"),
        P("tensor", "dp"),
        P(("dp", "tensor"), None),
    )
    out_specs = (
        P(("dp", "tensor"), None),
        P(("dp", "tensor"), None),
        P(),
        P("dp", "tensor"),
        P("dp", "tensor"),
        P("dp", "tensor"),
        P(),
        P(),
        P("tensor", "dp"),
        P(),
        P("dp", "tensor"),
        P("dp", "tensor"),
        P("tensor", "dp"),
    )

    return jax.shard_map(
        per_device, mesh=mesh, in_specs=in_specs, out_specs=out_specs, check_vma=False
    )
```

time: 762 us -> 658 us (0.86)
  matrix products: 126 us -> 68.1 us
  local copies, waits for them, and re-layouts: 77.4 us -> 25.8 us
  Pallas kernels: 326 us -> 376 us
  other arithmetic: 77.1 us -> 34.8 us
  blocking collectives: 39.7 us -> 0 us
  waiting for transfers between devices: 88.4 us -> 128 us
    pallas_call x4 -> x6, Pallas kernels: 176 us -> 226 us  [the longest x4 182 us: product_scatter(): pl.pallas_call(functools.partial(scatter_kernel, sizes, terms is not None...]
    psum x1 -> x0, blocking collectives: 39.7 us -> none  [per_device(): lax.psum((attention_gain_term, feed_gain_term, query_gain_term, key_gain_...]
    dot_general x12 -> x0, matrix products: 35.6 us -> none  [the longest x2 10.1 us: attend_backward(): jnp.einsum('qhgd,khd->hgqk', slope_block, value_seq, preferred_element_ty...]
    all_gather x1, waiting for transfers between devices: 0.57 us -> 33.8 us  [per_device(): down_full = lax.all_gather(down_weight.T, 'dp', axis=0, tiled=True)]
    reduce_sum x8 -> x1, other arithmetic: 20.1 us -> 2.3 us  [per_device(): jnp.mean(mixer_unit_slope * first_unit, axis=-1, keepdims=True)]
    dot_general x4 -> x2, matrix products: 48.4 us -> 31.3 us  [simple_product(): jnp.dot(first_operand, second_operand, preferred_element_type=jnp.float32)]
    mul x9 -> x0, local copies, waits for them, and re-layouts: 16.4 us -> none  [the longest x3 6.68 us: per_device(): query_unit = query_raw * query_scale]
    slice x13 -> x2, local copies, waits for them, and re-layouts: 12.8 us -> 1.09 us  [column_parts(): mixing_total[:, head * width + start:head * width + start + part_width]]
  transfers between devices with their start and end apart: 6 -> 6, of which waited for: 2 -> 3; matrix products, arithmetic and copies ran while one was open for 19% -> 17% of each run, Pallas kernels for 32% -> 58%
where the time goes in v2:
time: 658 us; the launch traced here: 648 us
  Pallas kernels  376 us (57%)
  waiting for transfers between devices  128 us (19%)
  matrix products  68.1 us (10%)
  other arithmetic  34.8 us (5%)
  local copies, waits for them, and re-layouts  25.8 us (4%)
  between operations  14.9 us (2%)
    pallas_call x4, Pallas kernels, product_scatter(): pl.pallas_call(functools.partial(scatter_kernel, sizes, terms is not None...  182 us
    pallas_call x3, Pallas kernels, gather_rows(): pl.pallas_call(body, out_shape=[jax.ShapeDtypeStruct((size * rows, column...  151 us
    reduce_scatter x1, waiting for transfers between devices, per_device(): lax.psum_scatter(feed_grad, 'dp', scatter_dimension=0, tiled=True)  88.1 us
    dot_general x4, matrix products, contract_rows(): lax.dot_general(first_operand, second_operand, (((0,), (0,)), ((), ())),...  36.7 us
    all_gather x1, waiting for transfers between devices, per_device(): down_full = lax.all_gather(down_weight.T, 'dp', axis=0, tiled=True)  33.8 us
    dot_general x2, matrix products, simple_product(): jnp.dot(first_operand, second_operand, preferred_element_type=jnp.float32)  31.3 us
    pallas_call x1, Pallas kernels, attention_backward(): pl.pallas_call(functools.partial(attention_backward_kernel, grouping, hea...  26.8 us
    unnamed x44, local copies, waits for them, and re-layouts  17.8 us
  transfers between devices with their start and end apart: 6, of which 3 were waited for; matrix products, arithmetic and copies ran while one was open for 17% of the time, Pallas kernels for 58%

profile of v2, /device:TPU:0, one launch (start us, length us, event | category | flops | bytes accessed | tf_op | source)
XLA Modules:
  0.0 647.7 jit_solution(1415478237203882910)
XLA Ops:
  7.2 1.1 copy.28
  8.3 0.9 slice_dynamic-update-slice_fusion.1
  9.2 0.9 slice_dynamic-update-slice_fusion.5
  10.1 0.9 slice_dynamic-update-slice_fusion.4
  11.0 0.9 slice_dynamic-update-slice_fusion
  11.9 0.9 slice_dynamic-update-slice_fusion.3
  12.8 0.9 slice_dynamic-update-slice_fusion.2
  13.7 0.9 copy-done.8
  14.7 2.7 pad_maximum_fusion.2
  17.5 1.2 copy.29
  19.1 1.3 fusion.14.refs_0_
  20.4 75.2 %gather_rows.3 = (bf16[1024,2048]{1,0:T(8,128)(2,1)}, bf16[1024,2048]{1,0:T(8,128)(2,1)}) custom-call(bf16[256,2048]{1,0:T(8,128)(2,1)} %fusion.14.refs_0_, bf16[256,2048]{1,0:T(8,128)(2,1)} %refs_1_.1), custom_call_target="tpu_custom_call" | custom-call | bytes 125829120 | tf_op jit(solution)/shard_map/gather_rows/pallas_call | solution.py:172
  95.6 16.5 %attention_forward.1 = (f32[1024,1024]{1,0:T(8,128)}, bf16[1024,512]{1,0:T(8,128)(2,1)}, f32[2,2,1024]{2,1,0:T(2,128)}) custom-call(bf16[1024,2048]{1,0:T(8,128)(2,1)} %get-tuple-element.28.rows_ref, bf16[2048,1536]{1,0:T(8,128)(2,1)} %all-gather.4.cloned.1.call-done.weight_ref.refs_1_, f32[1024,128]{1,0:T(8,128)} %constant.16.clone.cosine_ref, ...), custom_call_target="tpu_custom_call" | custom-call | flops 5368709120 | bytes 8388608 | tf_op jit(solution)/shard_map/attention_forward/pallas_call | solution.py:490
  112.1 40.7 %product_scatter.4 = f32[256,2048]{1,0:T(8,128)} custom-call(bf16[1024,512]{1,0:T(8,128)(2,1)} %get-tuple-element.29.refs_0_.mixed_ref, bf16[2048,1536]{1,0:T(8,128)(2,1)} %all-gather.4.cloned.1.call-done.weight_ref.refs_1_), custom_call_target="tpu_custom_call" | custom-call | flops 2147483648 | bytes 62914560 | tf_op jit(solution)/shard_map/product_scatter/pallas_call | solution.py:385
  152.8 2.0 multiply_reduce_fusion.2
  154.8 1.3 copy-done
  156.1 1.2 multiply_convert_fusion.refs_0_
  157.3 37.4 %gather_rows.4 = bf16[1024,2048]{1,0:T(8,128)(2,1)} custom-call(bf16[256,2048]{1,0:T(8,128)(2,1)} %multiply_convert_fusion.refs_0_), custom_call_target="tpu_custom_call" | custom-call | bytes 62914560 | tf_op jit(solution)/shard_map/gather_rows/pallas_call | solution.py:172
  194.7 5.1 all-gather.6.cloned.1.call-done.refs_1_
  199.8 17.0 %convolution_convert_fusion.2 = bf16[1024,3072]{1,0:T(8,128)(2,1)S(1)} fusion(bf16[1024,2048]{1,0:T(8,128)(2,1)} %gather_rows.4, bf16[2048,3072]{1,0:T(8,128)(2,1)} %all-gather.6.cloned.1.call-done.refs_1_), kind=kOutput, calls=%fused_computation.20 | convolution fusion | flops 12888047616 | bytes 23068672 | tf_op jit(solution)/shard_map/dot_general | solution.py:38
  216.8 2.1 fusion.refs_0_
  218.9 1.1 copy-done.4
  220.0 1.7 copy-done.7
  222.1 9.0 %convolution_convert_fusion.1 = bf16[2048,1536]{1,0:T(8,128)(2,1)} fusion(bf16[1024,2048]{1,0:T(8,128)(2,1)S(1)} %copy-done.14, bf16[1024,1536]{1,0:T(8,128)(2,1)S(1)} %fusion.refs_0_), kind=kOutput, calls=%fused_computation.7 | convolution fusion | flops 6445596672 | bytes 13631488 | tf_op jit(solution)/shard_map/dot_general | solution.py:26
  231.1 33.8 %all-gather.8.cloned.1.call-done.refs_1_ = bf16[2048,1536]{1,0:T(8,128)(2,1)} async-done(((bf16[256,1536]{1,0:T(8,128)(2,1)}), bf16[2048,1536]{1,0:T(8,128)(2,1)}) %all-gather.8.cloned.1.call-update) | async-done | bytes 6291472 | tf_op jit(solution)/shard_map/all_gather | solution.py:699
  265.0 14.4 %fusion.3 = (bf16[1024,1536]{1,0:T(8,128)(2,1)S(1)}, bf16[1024,1536]{1,0:T(8,128)(2,1)}) fusion(bf16[1024,3072]{1,0:T(8,128)(2,1)} %copy-done.4, bf16[1024,2048]{1,0:T(8,128)(2,1)} %get-tuple-element.30, bf16[2048,1536]{1,0:T(8,128)(2,1)} %all-gather.8.cloned.1.call-done.refs_1_), kind=kOutput, calls=%fused_computation.11 | convolution fusion | flops 6466043904 | bytes 23068672 | tf_op jit(solution)/shard_map/dot_general | solution.py:38
  279.4 5.3 pad_maximum_fusion.refs_0_
  284.7 17.7 %convolution_convert_fusion = bf16[2048,3072]{1,0:T(8,128)(2,1)} fusion(bf16[1024,2048]{1,0:T(8,128)(2,1)S(1)} %copy-done.6, bf16[1024,1536]{1,0:T(8,128)(2,1)} %get-tuple-element.63, bf16[1024,1536]{1,0:T(8,128)(2,1)S(1)} %get-tuple-element.62), kind=kOutput, calls=%fused_computation | convolution fusion | flops 12903776256 | bytes 23068672 | tf_op jit(solution)/shard_map/dot_general | solution.py:26
  302.4 49.8 %product_scatter.5 = f32[256,2048]{1,0:T(8,128)} custom-call(bf16[1024,3072]{1,0:T(8,128)(2,1)} %pad_maximum_fusion.refs_0_, bf16[2048,3072]{1,0:T(8,128)(2,1)} %all-gather.6.cloned.1.call-done.refs_1_), custom_call_target="tpu_custom_call" | custom-call | flops 12884901888 | bytes 62914560 | tf_op jit(solution)/shard_map/product_scatter/pallas_call | solution.py:385
  352.2 2.9 multiply_reduce_fusion
  355.7 2.9 fusion.22.refs_0_
  358.6 38.0 %gather_rows.5.state_ref = bf16[1024,2048]{1,0:T(8,128)(2,1)} custom-call(bf16[256,2048]{1,0:T(8,128)(2,1)} %fusion.22.refs_0_), custom_call_target="tpu_custom_call" | custom-call | bytes 62914560 | tf_op jit(solution)/shard_map/gather_rows/pallas_call | solution.py:172
  396.6 26.8 %attention_backward.1 = (bf16[1024,1024]{1,0:T(8,128)(2,1)}, f32[8,128]{1,0:T(8,128)}) custom-call(bf16[1024,2048]{1,0:T(8,128)(2,1)} %gather_rows.5.state_ref, bf16[2048,1536]{1,0:T(8,128)(2,1)} %all-gather.4.cloned.1.call-done.weight_ref.refs_1_, f32[1024,1024]{1,0:T(8,128)} %get-tuple-element.33.raw_ref, ...), custom_call_target="tpu_custom_call" | custom-call | flops 4831838208 | bytes 6291456 | tf_op jit(solution)/shard_map/attention_backward/pallas_call | solution.py:613
  423.4 5.0 convolution_convert_fusion.4
  428.5 5.0 convolution_convert_fusion.3
  433.5 3.4 pad_maximum_fusion.1
  437.5 41.2 %product_scatter.6 = f32[256,2048]{1,0:T(8,128)} custom-call(bf16[1024,1024]{1,0:T(8,128)(2,1)} %get-tuple-element.36.refs_0_, bf16[2048,1536]{1,0:T(8,128)(2,1)} %all-gather.4.cloned.1.call-done.weight_ref.refs_1_), custom_call_target="tpu_custom_call" | custom-call | flops 4294967296 | bytes 62914560 | tf_op jit(solution)/shard_map/product_scatter/pallas_call | solution.py:385
  478.8 2.3 fusion.16
  481.7 50.6 %product_scatter.7 = (f32[256,2048]{1,0:T(8,128)}, f32[40,128]{1,0:T(8,128)}) custom-call(bf16[1024,1536]{1,0:T(8,128)(2,1)} %copy-done.7, bf16[2048,1536]{1,0:T(8,128)(2,1)} %all-gather.8.cloned.1.call-done.refs_1_, f32[40,128]{1,0:T(8,128)} %pad_maximum_fusion.6.refs_2_), custom_call_target="tpu_custom_call" | custom-call | flops 6442450944 | bytes 62914560 | tf_op jit(solution)/shard_map/product_scatter/pallas_call | solution.py:385
  532.3 1.3 slice_bitcast_fusion.3
  533.5 1.3 slice_bitcast_fusion.1
  534.8 6.3 fusion.20
  541.2 1.3 convert_bitcast_fusion
  542.5 1.6 copy.33
  544.1 1.1 fusion.24
  547.0 1.0 copy.30
  548.9 88.1 %reduce-scatter.6.cloned.1.call-done = bf16[256,3072]{1,0:T(8,128)(2,1)} async-done(((bf16[2048,3072]{1,0:T(8,128)(2,1)}), bf16[256,3072]{1,0:T(8,128)(2,1)}) %reduce-scatter.6.cloned.1.call-update) | async-done | bytes 1572880 | tf_op jit(solution)/shard_map/reduce_scatter | solution.py:732
  637.0 3.4 fusion.23
  (57 shorter events, 5.5 us)
Async XLA Ops:
  7.2 88.4 %all-gather.4.cloned.1.call-start = ((), (), s32[]{:S(2)}) async-start(), calls=%async_computation.3 | async-start | bytes 7077888 | tf_op jit(solution)/shard_map/all_gather | solution.py:693
  11.9 5.6 copy-start.9
  13.7 0.9 copy-start.8
  14.6 4.1 copy-start.2
  14.6 185.2 %all-gather.6.cloned.1.call-start = ((), (), s32[]{:S(2)}) async-start(), calls=%async_computation.4 | async-start | bytes 14155776 | tf_op jit(solution)/shard_map/all_gather | solution.py:696
  17.4 1.6 copy-start.11
  17.5 247.5 %all-gather.8.cloned.1.call-start = ((), (), s32[]{:S(2)}) async-start(), calls=%async_computation.5 | async-start | bytes 7077888 | tf_op jit(solution)/shard_map/all_gather | solution.py:699
  18.7 522.5 %reduce-scatter.8.cloned.1.call-start = ((), (), s32[]{:S(2)}) async-start(), calls=%async_computation.8 | async-start | bytes 7077888 | tf_op jit(solution)/shard_map/reduce_scatter | solution.py:722
  152.8 3.3 copy-start.10
  154.8 1.3 copy-start
  216.8 3.2 copy-start.4
  216.8 5.3 copy-start.14
  220.0 1.7 copy-start.7
  265.0 279.1 %reduce-scatter.4.cloned.1.call-start = ((), (), s32[]{:S(2)}) async-start(), calls=%async_computation.6 | async-start | bytes 7077888 | tf_op jit(solution)/shard_map/reduce_scatter | solution.py:749
  279.4 5.3 copy-start.6
  352.2 3.0 copy-start.1
  352.2 3.5 copy-start.3
  423.4 5.0 copy-start.13
  423.4 5.0 copy-start.15
  437.0 200.0 %reduce-scatter.6.cloned.1.call-start = ((), (), s32[]{:S(2)}) async-start(), calls=%async_computation.7 | async-start | bytes 14155776 | tf_op jit(solution)/shard_map/reduce_scatter | solution.py:732
  478.8 2.3 copy-start.12
  544.1 2.8 copy-start.5
Sparse Core Ops, SparseCore 0:
  14.8 67.4 all-gather.3
  84.4 115.3 all-gather.5
  202.0 62.8 all-gather.7
  267.1 68.3 reduce-scatter.7
  437.1 67.4 reduce-scatter.3
  506.7 130.2 reduce-scatter.5

commit v3 on v2

--- a/solution.py
+++ b/solution.py
@@ -14,18 +14,13 @@
 epsilon = 1e-06
 rope_base = 1000000.0
 
+
 MESH = pl.DeviceIdType.MESH
 VMEM_LIMIT = 62 * 1024 * 1024
 
 
 def row_scale(values):
     return lax.rsqrt(jnp.mean(values * values, axis=-1, keepdims=True) + epsilon)
-
-
-def contract_rows(first_operand, second_operand):
-    return lax.dot_general(
-        first_operand, second_operand, (((0,), (0,)), ((), ())), preferred_element_type=jnp.float32
-    )
 
 
 def times_transposed(first_operand, second_operand):
@@ -190,14 +185,18 @@
     )(*arrays)
 
 
-def block_product(left_ref, start, rows, weight_ref, write):
-    total = weight_ref.shape[0]
+def block_product(pairs, start, rows, write):
+    total = pairs[0][1].shape[0]
     tile = min(512, total)
-    left = left_ref[pl.ds(pl.multiple_of(start, rows), rows), :]
+    start = pl.multiple_of(start, rows)
 
     def step(index, carry):
         columns = pl.ds(pl.multiple_of(index * tile, tile), tile)
-        write(columns, times_transposed(left, weight_ref[columns, :]))
+        values = None
+        for left_ref, weight_ref in pairs:
+            part = times_transposed(left_ref[pl.ds(start, rows), :], weight_ref[columns, :])
+            values = part if values is None else values + part
+        write(columns, values)
         return carry
 
     lax.fori_loop(0, total // tile, step, 0)
@@ -228,15 +227,16 @@
     return total
 
 
-def scatter_kernel(sizes, with_terms, *refs):
+def scatter_kernel(sizes, pair_count, with_terms, *refs):
+    pairs = [refs[2 * p : 2 * p + 2] for p in range(pair_count)]
+    refs = refs[2 * pair_count :]
     if with_terms:
-        left_ref, weight_ref, terms_ref, out_ref, terms_out_ref = refs[:5]
+        terms_ref, out_ref, terms_out_ref = refs[:3]
         inner, outer, partial_ref = refs[-7:-4]
         inner_send, inner_recv, outer_send, outer_recv = refs[-4:]
-        buffers = refs[5:-7]
+        buffers = refs[3:-7]
     else:
-        left_ref, weight_ref, out_ref = refs[:3]
-        buffers = refs[3:]
+        out_ref, buffers = refs[0], refs[1:]
     data_size, size = sizes
     if size == 4:
         beside, below, across = square_peers(lax.axis_index("tensor"))
@@ -253,9 +253,9 @@
             "tensor", other_members("tensor", size), terms_ref, inner, inner_send, inner_recv
         )
     if size == 4:
-        scatter_square(left_ref, weight_ref, out_ref, *buffers)
+        scatter_square(pairs, out_ref, *buffers)
     else:
-        scatter_direct(size, left_ref, weight_ref, out_ref, *buffers)
+        scatter_direct(size, pairs, out_ref, *buffers)
     if with_terms:
         partial_ref[...] = add_terms(inner, inner_copies)
         outer_copies = send_terms(
@@ -266,59 +266,63 @@
             copy.wait_send()
 
 
-def scatter_square(left_ref, weight_ref, out_ref, outgoing, passing, arriving, send_sem, recv_sem):
+def scatter_square(pairs, out_ref, outgoing, passing, arriving, send_sem, recv_sem):
     me = lax.axis_index("tensor")
     beside, below, across = square_peers(me)
     rows = out_ref.shape[0]
     half = rows // 2
     first, second = pl.ds(0, half), pl.ds(half, half)
 
-    def fill(slot, owner):
+    def prepare(index, source, target, peer):
+        return remote(source, target, send_sem.at[index], recv_sem.at[index], peer)
+
+    x_pass = prepare(0, outgoing.at[0, first], passing.at[0], beside)
+    y_pass = prepare(1, outgoing.at[0, second], passing.at[1], below)
+    x_first = prepare(2, outgoing.at[1, first], arriving.at[0, first], beside)
+    y_second = prepare(3, outgoing.at[2, second], arriving.at[1, second], below)
+    x_second = prepare(4, outgoing.at[1, second], arriving.at[0, second], beside)
+    y_first = prepare(5, outgoing.at[2, first], arriving.at[1, first], below)
+
+    def fill(slot, carry):
+        owner = jnp.where(
+            slot == 0, across, jnp.where(slot == 1, beside, jnp.where(slot == 2, below, me))
+        )
+
         def write(columns, values):
             outgoing[slot, :, columns] = values.astype(outgoing.dtype)
 
-        block_product(left_ref, owner * rows, rows, weight_ref, write)
-
-    def send(index, source, target, peer):
-        copy = remote(source, target, send_sem.at[index], recv_sem.at[index], peer)
-        copy.start()
-        return copy
-
-    fill(0, across)
-    x_pass = send(0, outgoing.at[0, first], passing.at[0], beside)
-    y_pass = send(1, outgoing.at[0, second], passing.at[1], below)
-    fill(1, beside)
-    x_first = send(2, outgoing.at[1, first], arriving.at[0, first], beside)
-    fill(2, below)
-    y_second = send(3, outgoing.at[2, second], arriving.at[1, second], below)
-
-    def write_own(columns, values):
-        out_ref[:, columns] = values
-
-    block_product(left_ref, me * rows, rows, weight_ref, write_own)
+        block_product(pairs, owner * rows, rows, write)
+        pl.when(slot == 0)(x_pass.start)
+        pl.when(slot == 0)(y_pass.start)
+        pl.when(slot == 1)(x_first.start)
+        pl.when(slot == 2)(y_second.start)
+        return carry
+
+    lax.fori_loop(0, 4, fill, 0)
     y_pass.wait_recv()
     outgoing[1, second, :] = (
         outgoing[1, second, :].astype(jnp.float32) + passing[1].astype(jnp.float32)
     ).astype(outgoing.dtype)
-    x_second = send(4, outgoing.at[1, second], arriving.at[0, second], beside)
+    x_second.start()
     x_pass.wait_recv()
     outgoing[2, first, :] = (
         outgoing[2, first, :].astype(jnp.float32) + passing[0].astype(jnp.float32)
     ).astype(outgoing.dtype)
-    y_first = send(5, outgoing.at[2, first], arriving.at[1, first], below)
+    y_first.start()
     x_first.wait_recv()
     y_second.wait_recv()
-    out_ref[first, :] += arriving[0, first, :].astype(jnp.float32)
-    out_ref[second, :] += arriving[1, second, :].astype(jnp.float32)
     x_second.wait_recv()
     y_first.wait_recv()
-    out_ref[second, :] += arriving[0, second, :].astype(jnp.float32)
-    out_ref[first, :] += arriving[1, first, :].astype(jnp.float32)
+    out_ref[...] = (
+        outgoing[3].astype(jnp.float32)
+        + arriving[0].astype(jnp.float32)
+        + arriving[1].astype(jnp.float32)
+    )
     for copy in (x_pass, y_pass, x_first, y_second, x_second, y_first):
         copy.wait_send()
 
 
-def scatter_direct(size, left_ref, weight_ref, out_ref, outgoing, arriving, send_sem, recv_sem):
+def scatter_direct(size, pairs, out_ref, outgoing, arriving, send_sem, recv_sem):
     me = lax.axis_index("tensor")
     rows = out_ref.shape[0]
     copies = []
@@ -327,7 +331,7 @@
         def write(columns, values, step=step):
             outgoing[step, :, columns] = values.astype(outgoing.dtype)
 
-        block_product(left_ref, peer * rows, rows, weight_ref, write)
+        block_product(pairs, peer * rows, rows, write)
         copy = remote(
             outgoing.at[step], arriving.at[step], send_sem.at[step], recv_sem.at[step], peer
         )
@@ -337,7 +341,7 @@
     def write_own(columns, values):
         out_ref[:, columns] = values
 
-    block_product(left_ref, me * rows, rows, weight_ref, write_own)
+    block_product(pairs, me * rows, rows, write_own)
     for step, copy in enumerate(copies):
         copy.wait_recv()
         out_ref[...] += arriving[step].astype(jnp.float32)
@@ -345,14 +349,15 @@
         copy.wait_send()
 
 
-def product_scatter(left, weight, first_column, sizes, collective_id, terms=None):
-    total_rows, depth = left.shape
-    columns = weight.shape[0]
+def product_scatter(triples, sizes, collective_id, terms=None):
+    total_rows = triples[0][0].shape[0]
+    columns = triples[0][1].shape[0]
+    depth = sum(left.shape[1] for left, _, _ in triples)
     data_size, size = sizes
     rows = total_rows // size
     if size == 4:
         buffers = [
-            pltpu.VMEM((3, rows, columns), jnp.bfloat16),
+            pltpu.VMEM((4, rows, columns), jnp.bfloat16),
             pltpu.VMEM((2, rows // 2, columns), jnp.bfloat16),
             pltpu.VMEM((2, rows, columns), jnp.bfloat16),
         ]
@@ -361,15 +366,21 @@
         buffers = [pltpu.VMEM((size - 1, rows, columns), jnp.bfloat16)] * 2
         sends = size - 1
     buffers += [pltpu.SemaphoreType.DMA((sends,)), pltpu.SemaphoreType.DMA((sends,))]
-    block = first_column // depth
-    whole = pl.BlockSpec(memory_space=pltpu.VMEM)
-    in_specs = [
-        pl.BlockSpec((total_rows, depth), lambda i: (0, 0), pipeline_mode=pl.Buffered(1)),
-        pl.BlockSpec((columns, depth), lambda i: (0, block), pipeline_mode=pl.Buffered(1)),
-    ]
+    in_specs = []
+    operands = []
+    for left, weight, first_column in triples:
+        part = left.shape[1]
+        in_specs += [
+            pl.BlockSpec((total_rows, part), lambda i: (0, 0), pipeline_mode=pl.Buffered(1)),
+            pl.BlockSpec(
+                (columns, part),
+                lambda i, block=first_column // part: (0, block),
+                pipeline_mode=pl.Buffered(1),
+            ),
+        ]
+        operands += [left, weight]
     out_specs = [pl.BlockSpec((rows, columns), lambda i: (0, 0))]
     out_shape = [jax.ShapeDtypeStruct((rows, columns), jnp.float32)]
-    operands = [left, weight]
     if terms is not None:
         operands.append(terms)
         in_specs.append(pl.BlockSpec(terms.shape, lambda i: (0, 0)))
@@ -383,7 +394,7 @@
         for count in (size, size, data_size, data_size):
             buffers.append(pltpu.SemaphoreType.DMA((count - 1,)))
     out = pl.pallas_call(
-        functools.partial(scatter_kernel, sizes, terms is not None),
+        functools.partial(scatter_kernel, sizes, len(triples), terms is not None),
         grid=(1,),
         out_shape=out_shape,
         in_specs=in_specs,
@@ -410,12 +421,26 @@
     frequency = np.float32(rope_base) ** (
         -(np.arange(half_size, dtype=np.float32) * np.float32(2.0) / np.float32(head_size))
     )
-    angles = np.arange(SEQUENCE_LENGTH, dtype=np.float32)[:, None] * frequency[None, :]
-    cosine, sine = np.cos(angles), np.sin(angles)
-    return (
-        np.concatenate([cosine, cosine], axis=1).astype(np.float32),
-        np.concatenate([-sine, sine], axis=1).astype(np.float32),
-    )
+    frequency = frequency.astype(np.float64)
+    sign = np.concatenate([-np.ones(half_size), np.ones(half_size)])[None, :]
+    positions = np.concatenate([np.arange(0, SEQUENCE_LENGTH, 128), np.arange(128)])
+    angles = positions[:, None] * np.concatenate([frequency, frequency])[None, :]
+    return np.cos(angles).astype(np.float32), (sign * np.sin(angles)).astype(np.float32)
+
+
+def fill_tables(few_cosines_ref, few_sines_ref, cosine_ref, sine_ref):
+    coarse = few_cosines_ref.shape[0] - 128
+    near_cosine, near_sine = few_cosines_ref[coarse:, :], few_sines_ref[coarse:, :]
+
+    def step(index, carry):
+        far_cosine = few_cosines_ref[pl.ds(index, 1), :]
+        far_sine = few_sines_ref[pl.ds(index, 1), :]
+        rows = pl.ds(pl.multiple_of(index * 128, 128), 128)
+        cosine_ref[rows, :] = far_cosine * near_cosine - far_sine * near_sine
+        sine_ref[rows, :] = far_sine * near_cosine + far_cosine * near_sine
+        return carry
+
+    lax.fori_loop(0, coarse, step, 0)
 
 
 def turn(values, cosine, sine):
@@ -443,25 +468,40 @@
     return jnp.concatenate([scores[:first_row], corner], axis=0)
 
 
+def turn_heads(
+    grouping, head_size, raw_ref, query_gain_ref, key_gain_ref, cosine_ref, sine_ref, query_ref, key_ref, value_ref
+):
+    def turned(start, gain):
+        raw = raw_ref[:, pl.ds(start, head_size)]
+        return turn(raw * row_scale(raw) * gain, cosine_ref[...], sine_ref[...]).astype(jnp.bfloat16)
+
+    def step(part, carry):
+        query_ref[part] = turned(pl.multiple_of(part * head_size, head_size), query_gain_ref[...])
+        return carry
+
+    lax.fori_loop(0, grouping, step, 0)
+    key_ref[...] = turned(grouping * head_size, key_gain_ref[...])
+    value_ref[...] = raw_ref[:, (grouping + 1) * head_size :].astype(jnp.bfloat16)
+
+
 def attention_forward_kernel(
-    grouping, head_size, block, rows_ref, weight_ref, cosine_ref, sine_ref, query_gain_ref, key_gain_ref,
-    raw_ref, mixed_ref, total_ref, query_ref, key_ref, value_ref,
+    grouping, head_size, block, rows_ref, weight_ref, few_cosines_ref, few_sines_ref, query_gain_ref, key_gain_ref,
+    raw_ref, mixed_ref, total_ref, query_ref, key_ref, value_ref, cosine_ref, sine_ref,
 ):
     sequence = rows_ref.shape[0]
     multiplier = head_size ** (-0.5) * LOG2E
-    cosine, sine = cosine_ref[...], sine_ref[...]
+
+    @pl.when((pl.program_id(0) == 0) & (pl.program_id(1) == 0))
+    def _():
+        fill_tables(few_cosines_ref, few_sines_ref, cosine_ref, sine_ref)
+
     raw_ref[...] = simple_product(rows_ref[...], weight_ref[...])
-    for part in range(grouping + 1):
-        raw = raw_ref[:, part * head_size : (part + 1) * head_size]
-        gain = key_gain_ref[...] if part == grouping else query_gain_ref[...]
-        turned = turn(raw * row_scale(raw) * gain, cosine, sine).astype(jnp.bfloat16)
-        if part == grouping:
-            key_ref[...] = turned
-        else:
-            query_ref[part] = turned
-    value_ref[...] = raw_ref[:, (grouping + 1) * head_size :].astype(jnp.bfloat16)
-    for part in range(grouping):
-        totals = []
+    turn_heads(
+        grouping, head_size, raw_ref, query_gain_ref, key_gain_ref, cosine_ref, sine_ref, query_ref, key_ref, value_ref
+    )
+
+    def head_step(part, carry):
+        lanes = pl.ds(pl.multiple_of(part * head_size, head_size), head_size)
         for first_row in range(0, sequence, block):
             last_row = first_row + block
             scores = visible_scores(
@@ -471,20 +511,22 @@
             weights = jnp.exp2(scores - highest)
             total = jnp.sum(weights, axis=0, keepdims=True)
             weights = (weights * (1.0 / total)).astype(jnp.bfloat16)
-            mixed_ref[first_row:last_row, part * head_size : (part + 1) * head_size] = contract_first(
+            mixed_ref[first_row:last_row, lanes] = contract_first(
                 weights, value_ref[:last_row, :]
             ).astype(mixed_ref.dtype)
-            totals.append(highest + jnp.log2(total))
-        total_ref[0, part : part + 1, :] = jnp.concatenate(totals, axis=1)
-
-
-def attention_forward(rows, weight, cosine, sine, query_gain, key_gain, heads, grouping):
+            total_ref[0, pl.ds(part, 1), first_row:last_row] = highest + jnp.log2(total)
+        return carry
+
+    lax.fori_loop(0, grouping, head_step, 0)
+
+
+def attention_forward(rows, weight, tables, query_gain, key_gain, heads, grouping):
     total_rows, depth = rows.shape
     head_size = query_gain.shape[0]
     sequences = total_rows // SEQUENCE_LENGTH
     width = (grouping + 2) * head_size
     block = min(256, SEQUENCE_LENGTH)
-    table = pl.BlockSpec((SEQUENCE_LENGTH, head_size), lambda s, h: (0, 0))
+    table = pl.BlockSpec(tables[0].shape, lambda s, h: (0, 0))
     gain = pl.BlockSpec((1, head_size), lambda s, h: (0, 0))
     elements = heads * grouping * total_rows * SEQUENCE_LENGTH // 2
     return pl.pallas_call(
@@ -512,6 +554,8 @@
             pltpu.VMEM((grouping, SEQUENCE_LENGTH, head_size), jnp.bfloat16),
             pltpu.VMEM((SEQUENCE_LENGTH, head_size), jnp.bfloat16),
             pltpu.VMEM((SEQUENCE_LENGTH, head_size), jnp.bfloat16),
+            pltpu.VMEM((SEQUENCE_LENGTH, head_size), jnp.float32),
+            pltpu.VMEM((SEQUENCE_LENGTH, head_size), jnp.float32),
         ],
         compiler_params=pltpu.CompilerParams(vmem_limit_bytes=VMEM_LIMIT),
         cost_estimate=pl.CostEstimate(
@@ -520,7 +564,7 @@
             transcendentals=elements,
         ),
         name="attention_forward",
-    )(rows, weight, cosine, sine, query_gain.reshape(1, -1), key_gain.reshape(1, -1))
+    )(rows, weight, *tables, query_gain.reshape(1, -1), key_gain.reshape(1, -1))
 
 
 def norm_back(turned_slope, raw, gain, cosine, sine):
@@ -534,40 +578,35 @@
 
 
 def attention_backward_kernel(
-    grouping, head_size, block, state_ref, weight_ref, raw_ref, mixed_ref, total_ref, cosine_ref, sine_ref,
+    grouping, head_size, block, state_ref, weight_ref, raw_ref, mixed_ref, total_ref, few_cosines_ref, few_sines_ref,
     query_gain_ref, key_gain_ref, slope_ref, gain_ref, query_ref, key_ref, value_ref, out_slope_ref,
-    turned_ref, key_sum_ref, value_sum_ref,
+    turned_ref, key_sum_ref, value_sum_ref, cosine_ref, sine_ref,
 ):
     sequence = state_ref.shape[0]
     scale_factor = head_size ** (-0.5)
     multiplier = scale_factor * LOG2E
-    cosine, sine = cosine_ref[...], sine_ref[...]
 
     @pl.when((pl.program_id(0) == 0) & (pl.program_id(1) == 0))
     def _():
         gain_ref[...] = jnp.zeros_like(gain_ref)
+        fill_tables(few_cosines_ref, few_sines_ref, cosine_ref, sine_ref)
 
     out_slope_ref[...] = simple_product(state_ref[...], weight_ref[...]).astype(jnp.bfloat16)
-    for part in range(grouping + 1):
-        raw = raw_ref[:, part * head_size : (part + 1) * head_size]
-        gain = key_gain_ref[...] if part == grouping else query_gain_ref[...]
-        turned = turn(raw * row_scale(raw) * gain, cosine, sine).astype(jnp.bfloat16)
-        if part == grouping:
-            key_ref[...] = turned
-        else:
-            query_ref[part] = turned
-    value_ref[...] = raw_ref[:, (grouping + 1) * head_size :].astype(jnp.bfloat16)
+    turn_heads(
+        grouping, head_size, raw_ref, query_gain_ref, key_gain_ref, cosine_ref, sine_ref, query_ref, key_ref, value_ref
+    )
     key_sum_ref[...] = jnp.zeros_like(key_sum_ref)
     value_sum_ref[...] = jnp.zeros_like(value_sum_ref)
     ones = jnp.ones((8, head_size), jnp.float32)
-    for part in range(grouping):
-        lanes = slice(part * head_size, (part + 1) * head_size)
+
+    def head_step(part, carry):
+        lanes = pl.ds(pl.multiple_of(part * head_size, head_size), head_size)
         for first_row in range(0, sequence, block):
             last_row = first_row + block
             query_rows = query_ref[part, first_row:last_row, :]
             slope_rows = out_slope_ref[first_row:last_row, lanes]
             scores = visible_scores(key_ref[:last_row, :], query_rows, first_row, multiplier)
-            weights = jnp.exp2(scores - total_ref[0, part : part + 1, first_row:last_row])
+            weights = jnp.exp2(scores - total_ref[0, pl.ds(part, 1), first_row:last_row])
             value_sum_ref[:last_row, :] += simple_product(weights.astype(jnp.bfloat16), slope_rows)
             product = slope_rows.astype(jnp.float32) * mixed_ref[first_row:last_row, lanes].astype(jnp.float32)
             centre = lax.dot_general(
@@ -584,13 +623,16 @@
                 contract_first(score_slope, key_ref[:last_row, :]) * scale_factor
             )
         slope, term = norm_back(
-            turned_ref[...], raw_ref[:, lanes], query_gain_ref[...], cosine, sine
+            turned_ref[...], raw_ref[:, lanes], query_gain_ref[...], cosine_ref[...], sine_ref[...]
         )
         slope_ref[:, lanes] = slope
         gain_ref[0:1, :] += term
+        return carry
+
+    lax.fori_loop(0, grouping, head_step, 0)
     lanes = slice(grouping * head_size, (grouping + 1) * head_size)
     slope, term = norm_back(
-        key_sum_ref[...] * scale_factor, raw_ref[:, lanes], key_gain_ref[...], cosine, sine
+        key_sum_ref[...] * scale_factor, raw_ref[:, lanes], key_gain_ref[...], cosine_ref[...], sine_ref[...]
     )
     slope_ref[:, lanes] = slope
     gain_ref[1:2, :] += term
@@ -598,7 +640,7 @@
 
 
 def attention_backward(
-    state_rows, weight, weight_start, raw, mixed, totals, cosine, sine, query_gain, key_gain, heads, grouping
+    state_rows, weight, weight_start, raw, mixed, totals, tables, query_gain, key_gain, heads, grouping
 ):
     total_rows, depth = state_rows.shape
     head_size = query_gain.shape[0]
@@ -607,9 +649,10 @@
     out_width = grouping * head_size
     block = min(256, SEQUENCE_LENGTH)
     first_block = weight_start // out_width
-    table = pl.BlockSpec((SEQUENCE_LENGTH, head_size), lambda s, h: (0, 0))
+    table = pl.BlockSpec(tables[0].shape, lambda s, h: (0, 0))
     gain = pl.BlockSpec((1, head_size), lambda s, h: (0, 0))
     elements = heads * grouping * total_rows * SEQUENCE_LENGTH // 2
+    whole_rows = pltpu.VMEM((SEQUENCE_LENGTH, head_size), jnp.float32)
     return pl.pallas_call(
         functools.partial(attention_backward_kernel, grouping, head_size, block),
         grid=(sequences, heads),
@@ -637,9 +680,11 @@
             pltpu.VMEM((SEQUENCE_LENGTH, head_size), jnp.bfloat16),
             pltpu.VMEM((SEQUENCE_LENGTH, head_size), jnp.bfloat16),
             pltpu.VMEM((SEQUENCE_LENGTH, out_width), jnp.bfloat16),
-            pltpu.VMEM((SEQUENCE_LENGTH, head_size), jnp.float32),
-            pltpu.VMEM((SEQUENCE_LENGTH, head_size), jnp.float32),
-            pltpu.VMEM((SEQUENCE_LENGTH, head_size), jnp.float32),
+            whole_rows,
+            whole_rows,
+            whole_rows,
+            whole_rows,
+            whole_rows,
         ],
         compiler_params=pltpu.CompilerParams(vmem_limit_bytes=VMEM_LIMIT),
         cost_estimate=pl.CostEstimate(
@@ -649,9 +694,234 @@
         ),
         name="attention_backward",
     )(
-        state_rows, weight, raw, mixed, totals, cosine, sine,
+        state_rows, weight, raw, mixed, totals, *tables,
         query_gain.reshape(1, -1), key_gain.reshape(1, -1),
     )
+
+
+def feed_half_kernel(half, tile, rows_ref, cotangent_ref, weight_ref, hidden_ref, slope_ref):
+    rows, cotangent = rows_ref[...], cotangent_ref[...]
+
+    def step(index, carry):
+        start = pl.multiple_of(index * tile, tile)
+        gate = simple_product(rows, weight_ref[:, pl.ds(start, tile)])
+        up = simple_product(rows, weight_ref[:, pl.ds(half + start, tile)])
+        back = simple_product(cotangent, weight_ref[:, pl.ds(2 * half + start, tile)])
+        sigmoid = 1.0 / (1.0 + jnp.exp(-gate))
+        gated = gate * sigmoid
+        hidden_ref[:, pl.ds(start, tile)] = (gated * up).astype(jnp.bfloat16)
+        slope_ref[:, pl.ds(start, tile)] = (
+            back * up * sigmoid * (1.0 + gate * (1.0 - sigmoid))
+        ).astype(jnp.bfloat16)
+        slope_ref[:, pl.ds(half + start, tile)] = (back * gated).astype(jnp.bfloat16)
+        return carry
+
+    lax.fori_loop(0, half // tile, step, 0)
+
+
+def feed_half(rows, cotangent, weight):
+    total_rows, depth = rows.shape
+    half = weight.shape[1] // 3
+    block = min(512, total_rows)
+    tile = 256 if half % 256 == 0 else 128
+    row_block = pl.BlockSpec((block, depth), lambda i: (i, 0))
+    return pl.pallas_call(
+        functools.partial(feed_half_kernel, half, tile),
+        grid=(total_rows // block,),
+        out_shape=[
+            jax.ShapeDtypeStruct((total_rows, half), jnp.bfloat16),
+            jax.ShapeDtypeStruct((total_rows, 2 * half), jnp.bfloat16),
+        ],
+        in_specs=[
+            row_block,
+            row_block,
+            pl.BlockSpec(weight.shape, lambda i: (0, 0), pipeline_mode=pl.Buffered(1)),
+        ],
+        out_specs=[
+            pl.BlockSpec((block, half), lambda i: (i, 0)),
+            pl.BlockSpec((block, 2 * half), lambda i: (i, 0)),
+        ],
+        compiler_params=pltpu.CompilerParams(vmem_limit_bytes=VMEM_LIMIT),
+        cost_estimate=pl.CostEstimate(
+            flops=6 * total_rows * depth * half,
+            bytes_accessed=2 * (2 * total_rows * depth + 3 * depth * half),
+            transcendentals=total_rows * half,
+        ),
+        name="feed_half",
+    )(rows, cotangent, weight)
+
+
+def grad_kernel(pair_count, with_other, order_ref, *refs):
+    pairs = [refs[2 * p : 2 * p + 2] for p in range(pair_count)]
+    refs = refs[2 * pair_count :]
+    step = pl.program_id(0)
+    if with_other:
+        other_ref, refs = refs[0], refs[1:]
+        out_refs, held_ref, copy_sem = refs[:-3], refs[-3], refs[-2]
+    else:
+        out_ref = refs[0]
+    turned_ref = refs[-1]
+    start = 0
+    for left_ref, right_ref in pairs:
+        turned_ref[...] = left_ref[...].T
+        width = right_ref.shape[1]
+        tile = next(t for t in (768, 512, 384, 256, 128) if width % t == 0)
+        for column in range(0, width, tile):
+            values = simple_product(turned_ref[...], right_ref[:, column : column + tile])
+            columns = slice(start + column, start + column + tile)
+            if with_other:
+                values = values + other_ref[0, :, columns].astype(jnp.float32)
+                held_ref[step, :, columns] = values.astype(jnp.bfloat16)
+            else:
+                out_ref[0, :, columns] = values.astype(jnp.bfloat16)
+        start += width
+    if with_other:
+        copies = [
+            pltpu.make_async_copy(held_ref.at[index], out_ref, copy_sem.at[index])
+            for index, out_ref in enumerate(out_refs)
+        ]
+        for index, copy in enumerate(copies):
+            pl.when(step == index)(copy.start)
+
+        @pl.when(step == len(copies) - 1)
+        def _():
+            for copy in copies:
+                copy.wait()
+
+
+def grad_blocks(order, pairs, other=None):
+    count = order.shape[0]
+    total_rows, depth = pairs[0][0].shape
+    block = depth // lax.axis_size("dp")
+    width = sum(right.shape[1] for _, right in pairs)
+    in_specs = []
+    operands = []
+    for left, right in pairs:
+        in_specs += [
+            pl.BlockSpec((total_rows, block), lambda k, at: (0, at[k])),
+            pl.BlockSpec(right.shape, lambda k, at: (0, 0), pipeline_mode=pl.Buffered(1)),
+        ]
+        operands += [left, right]
+    scratch = [pltpu.VMEM((block, total_rows), jnp.bfloat16)]
+    if other is not None:
+        in_specs.append(pl.BlockSpec((1, block, width), lambda k, at: (k, 0, 0)))
+        operands.append(other)
+        out_shape = [jax.ShapeDtypeStruct((block, width), jnp.bfloat16)] * count
+        out_specs = [pl.BlockSpec(memory_space=pl.ANY)] * count
+        scratch = [
+            pltpu.VMEM((count, block, width), jnp.bfloat16),
+            pltpu.SemaphoreType.DMA((count,)),
+        ] + scratch
+    else:
+        out_shape = [jax.ShapeDtypeStruct((count, block, width), jnp.bfloat16)]
+        out_specs = [pl.BlockSpec((1, block, width), lambda k, at: (k, 0, 0))]
+    out = pl.pallas_call(
+        functools.partial(grad_kernel, len(pairs), other is not None),
+        grid_spec=pltpu.PrefetchScalarGridSpec(
+            num_scalar_prefetch=1,
+            grid=(count,),
+            in_specs=in_specs,
+            out_specs=out_specs,
+            scratch_shapes=scratch,
+        ),
+        out_shape=out_shape,
+        compiler_params=pltpu.CompilerParams(vmem_limit_bytes=VMEM_LIMIT),
+        cost_estimate=pl.CostEstimate(
+            flops=2 * total_rows * count * block * width,
+            bytes_accessed=2 * (total_rows * count * block * len(pairs) + width * (total_rows + count * block)),
+            transcendentals=0,
+        ),
+        name="grad_blocks",
+    )(order, *operands)
+    return out if other is not None else out[0]
+
+
+def reduce_over_chips(pairs, sizes):
+    data_size = sizes[0]
+    chips = data_size // 2
+    me = lax.axis_index("dp")
+    chip, core = me // 2, lax.rem(me, 2)
+    ahead = lax.rem(chip + jnp.arange(chips, dtype=jnp.int32), chips) * 2
+    other = lax.ppermute(
+        grad_blocks(ahead + (1 - core), pairs),
+        "dp",
+        [(device, device ^ 1) for device in range(data_size)],
+    )
+    blocks = grad_blocks(ahead + core, pairs, other)
+    arrivals = []
+    for step in range(1, chips):
+        arrivals.append(
+            lax.ppermute(
+                blocks[step],
+                "dp",
+                [(device, (device + 2 * step) % data_size) for device in range(data_size)],
+            )
+        )
+    return blocks, arrivals
+
+
+def pack_mixing_kernel(heads, query_ref, key_ref, value_ref, output_ref, out_ref):
+    query_width = query_ref.shape[1] // heads
+    head_size = key_ref.shape[1] // heads
+    start = 0
+    for head in range(heads):
+        for ref, part in ((query_ref, query_width), (key_ref, head_size), (value_ref, head_size)):
+            out_ref[:, start : start + part] = ref[:, head * part : (head + 1) * part]
+            start += part
+    out_ref[:, start:] = output_ref[...].T
+
+
+def pack_feed_kernel(gate_ref, up_ref, down_ref, first_ref, second_ref):
+    half = gate_ref.shape[1] // 2
+    for index, out_ref in enumerate((first_ref, second_ref)):
+        part = slice(index * half, (index + 1) * half)
+        out_ref[:, :half] = gate_ref[:, part]
+        out_ref[:, half : 2 * half] = up_ref[:, part]
+        out_ref[:, 2 * half :] = down_ref[part, :].T
+
+
+def finish_mixing_kernel(heads, total_ref, query_ref, key_ref, value_ref, output_ref):
+    query_width = query_ref.shape[1] // heads
+    head_size = key_ref.shape[1] // heads
+    start = 0
+    for head in range(heads):
+        for ref, part in ((query_ref, query_width), (key_ref, head_size), (value_ref, head_size)):
+            ref[:, head * part : (head + 1) * part] = total_ref[:, start : start + part].astype(
+                jnp.float32
+            )
+            start += part
+    output_ref[...] = total_ref[:, start:].astype(jnp.float32).T
+
+
+def finish_feed_kernel(*refs):
+    first_refs, second_ref = refs[:-4], refs[-4]
+    gate_ref, up_ref, down_ref = refs[-3:]
+    half = gate_ref.shape[1] // 2
+
+    def first_part(columns):
+        return sum(ref[:, columns].astype(jnp.float32) for ref in first_refs)
+
+    def second_part(columns):
+        return second_ref[:, columns].astype(jnp.float32)
+
+    for index, part_of in enumerate((first_part, second_part)):
+        part = slice(index * half, (index + 1) * half)
+        gate_ref[:, part] = part_of(slice(0, half))
+        up_ref[:, part] = part_of(slice(half, 2 * half))
+        down_ref[part, :] = part_of(slice(2 * half, 3 * half)).T
+
+
+def whole_call(body, shapes, *operands):
+    return pl.pallas_call(
+        body,
+        out_shape=shapes,
+        in_specs=[pl.BlockSpec(memory_space=pltpu.VMEM)] * len(operands),
+        out_specs=[pl.BlockSpec(memory_space=pltpu.VMEM)] * len(shapes),
+        compiler_params=pltpu.CompilerParams(vmem_limit_bytes=VMEM_LIMIT),
+        cost_estimate=pl.CostEstimate(
+            flops=0, bytes_accessed=4 * sum(operand.size for operand in operands), transcendentals=0
+        ),
+    )(*operands)
 
 
 def per_device(
@@ -679,24 +949,22 @@
     grouping = query_columns // key_columns
     hidden_columns = gate_weight.shape[1]
     qkv_columns = query_columns + 2 * key_columns
-    query_width = grouping * head_size
-    width = query_width + 2 * head_size
-    cosine, sine = turn_tables(head_size)
-
-    mixing_parts = []
-    for head in range(heads):
-        mixing_parts += [
-            query_weight[:, head * query_width : (head + 1) * query_width],
-            key_matrix[:, head * head_size : (head + 1) * head_size],
-            value_matrix[:, head * head_size : (head + 1) * head_size],
-        ]
-    mixing_full = lax.all_gather(
-        jnp.concatenate([*mixing_parts, output_weight.T], axis=1), "dp", axis=0, tiled=True
-    )
-    feeding_full = lax.all_gather(
-        jnp.concatenate([gate_weight, up_weight], axis=1), "dp", axis=0, tiled=True
-    )
-    down_full = lax.all_gather(down_weight.T, "dp", axis=0, tiled=True)
+    half = hidden_columns // 2
+    tables = turn_tables(head_size)
+
+    block_width = query_weight.shape[0]
+    (mixing_local,) = whole_call(
+        functools.partial(pack_mixing_kernel, heads),
+        [jax.ShapeDtypeStruct((block_width, qkv_columns + query_columns), jnp.bfloat16)],
+        query_weight, key_matrix, value_matrix, output_weight,
+    )
+    mixing_full = lax.all_gather(mixing_local, "dp", axis=0, tiled=True)
+    feed_locals = whole_call(
+        pack_feed_kernel,
+        [jax.ShapeDtypeStruct((block_width, 3 * half), jnp.bfloat16)] * 2,
+        gate_weight, up_weight, down_weight,
+    )
+    feed_full = [lax.all_gather(part, "dp", axis=0, tiled=True) for part in feed_locals]
 
     input_float = block_input.astype(jnp.float32)
     first_scale = row_scale(input_float)
@@ -705,32 +973,31 @@
     mixer_rows, cotangent_rows = gather_rows((mixer_local, out_cotangent), size, 0)
 
     raw, mixed_rows, totals = attention_forward(
-        mixer_rows, mixing_full, cosine, sine, query_gain, key_gain, heads, grouping
-    )
-    hidden_state = input_float + product_scatter(mixed_rows, mixing_full, qkv_columns, sizes, 1)
+        mixer_rows, mixing_full, tables, query_gain, key_gain, heads, grouping
+    )
+    hidden_state = input_float + product_scatter(
+        [(mixed_rows, mixing_full, qkv_columns)], sizes, 1
+    )
     second_scale = row_scale(hidden_state)
     second_unit = hidden_state * second_scale
     feed_local = (second_unit * feed_gain).astype(jnp.bfloat16)
     (feed_rows,) = gather_rows((feed_local,), size, 2)
-    both_values = simple_product(feed_rows, feeding_full).astype(jnp.bfloat16)
-    gate_values = both_values[:, :hidden_columns].astype(jnp.float32)
-    up_values = both_values[:, hidden_columns:].astype(jnp.float32)
-    gate_sigmoid = jax.nn.sigmoid(gate_values)
-    hidden_rows = (gate_values * gate_sigmoid * up_values).astype(jnp.bfloat16)
-    down_grad = contract_rows(cotangent_rows, hidden_rows).astype(jnp.bfloat16)
-    down_grad, down_full = lax.optimization_barrier((down_grad, down_full))
-    down_total = lax.psum_scatter(down_grad, "dp", scatter_dimension=0, tiled=True)
-
-    hidden_slope = simple_product(cotangent_rows, down_full)
-    gate_slope = (
-        hidden_slope * up_values * gate_sigmoid * (1.0 + gate_values * (1.0 - gate_sigmoid))
-    ).astype(jnp.bfloat16)
-    up_slope = (hidden_slope * gate_values * gate_sigmoid).astype(jnp.bfloat16)
-    feed_slope = jnp.concatenate([gate_slope, up_slope], axis=1)
-    feed_grad = contract_rows(feed_rows, feed_slope).astype(jnp.bfloat16)
-    feed_grad, feed_slope = lax.optimization_barrier((feed_grad, feed_slope))
-    feed_total = lax.psum_scatter(feed_grad, "dp", scatter_dimension=0, tiled=True)
-    feed_back = product_scatter(feed_slope, feeding_full, 0, sizes, 3)
+
+    hidden_first, slope_first = feed_half(feed_rows, cotangent_rows, feed_full[0])
+    blocks, arrivals = reduce_over_chips(
+        [(feed_rows, slope_first), (cotangent_rows, hidden_first)], sizes
+    )
+    blocks, later_full = lax.optimization_barrier((blocks, feed_full[1]))
+    hidden_second, slope_second = feed_half(feed_rows, cotangent_rows, later_full)
+    plain_order = jnp.arange(sizes[0], dtype=jnp.int32)
+    second_grad = grad_blocks(
+        plain_order, [(feed_rows, slope_second), (cotangent_rows, hidden_second)]
+    ).reshape(model_width, -1)
+    second_grad, slope_second = lax.optimization_barrier((second_grad, slope_second))
+    second_total = lax.psum_scatter(second_grad, "dp", scatter_dimension=0, tiled=True)
+    feed_back = product_scatter(
+        [(slope_first, feed_full[0], 0), (slope_second, later_full, 0)], sizes, 3
+    )
     feed_gain_term = jnp.sum(feed_back * second_unit, axis=0)
     feed_unit_slope = feed_back * feed_gain
     state_slope = out_cotangent.astype(jnp.float32) + second_scale * (
@@ -739,17 +1006,15 @@
     )
     (state_rows,) = gather_rows((state_slope.astype(jnp.bfloat16),), size, 4)
     qkv_slope, head_terms = attention_backward(
-        state_rows, mixing_full, qkv_columns, raw, mixed_rows, totals, cosine, sine,
+        state_rows, mixing_full, qkv_columns, raw, mixed_rows, totals, tables,
         query_gain, key_gain, heads, grouping,
     )
-    mixing_grad = jnp.concatenate(
-        [contract_rows(mixer_rows, qkv_slope), contract_rows(state_rows, mixed_rows)], axis=1
-    ).astype(jnp.bfloat16)
+    mixing_grad = grad_blocks(
+        plain_order, [(mixer_rows, qkv_slope), (state_rows, mixed_rows)]
+    ).reshape(model_width, -1)
     mixing_grad, qkv_slope = lax.optimization_barrier((mixing_grad, qkv_slope))
-    mixing_total = lax.psum_scatter(
-        mixing_grad, "dp", scatter_dimension=0, tiled=True
-    ).astype(jnp.float32)
-    mixer_back = product_scatter(qkv_slope, mixing_full, 0, sizes, 5)
+    mixing_total = lax.psum_scatter(mixing_grad, "dp", scatter_dimension=0, tiled=True)
+    mixer_back = product_scatter([(qkv_slope, mixing_full, 0)], sizes, 5)
     attention_gain_term = jnp.sum(mixer_back * first_unit, axis=0)
     mixer_unit_slope = mixer_back * attention_gain
     input_gradient = (
@@ -769,33 +1034,46 @@
         ],
         axis=0,
     )
-    feed_sum, terms = product_scatter(hidden_rows, down_full, 0, sizes, 6, terms)
+    feed_sum, terms = product_scatter(
+        [(hidden_first, feed_full[0], 2 * half), (hidden_second, later_full, 2 * half)],
+        sizes,
+        6,
+        terms,
+    )
     block_output = (hidden_state + feed_sum).astype(jnp.bfloat16)
-    feed_total = feed_total.astype(jnp.float32)
-
-    def column_parts(start, part_width):
-        return jnp.concatenate(
-            [
-                mixing_total[:, head * width + start : head * width + start + part_width]
-                for head in range(heads)
-            ],
-            axis=1,
-        )
-
+    query_gradient, key_gradient, value_gradient, output_gradient = whole_call(
+        functools.partial(finish_mixing_kernel, heads),
+        [
+            jax.ShapeDtypeStruct((block_width, query_columns), jnp.float32),
+            jax.ShapeDtypeStruct((block_width, key_columns), jnp.float32),
+            jax.ShapeDtypeStruct((block_width, key_columns), jnp.float32),
+            jax.ShapeDtypeStruct((query_columns, block_width), jnp.float32),
+        ],
+        mixing_total,
+    )
+    gate_gradient, up_gradient, down_gradient = whole_call(
+        finish_feed_kernel,
+        [
+            jax.ShapeDtypeStruct((block_width, hidden_columns), jnp.float32),
+            jax.ShapeDtypeStruct((block_width, hidden_columns), jnp.float32),
+            jax.ShapeDtypeStruct((hidden_columns, block_width), jnp.float32),
+        ],
+        blocks[0], *arrivals, second_total,
+    )
     return (
         block_output,
         input_gradient,
         terms[:gain_rows].reshape(-1),
-        column_parts(0, query_width),
-        column_parts(query_width, head_size),
-        column_parts(query_width + head_size, head_size),
+        query_gradient,
+        key_gradient,
+        value_gradient,
         terms[2 * gain_rows],
         terms[2 * gain_rows + 1],
-        mixing_total[:, qkv_columns:].T,
+        output_gradient,
         terms[gain_rows : 2 * gain_rows].reshape(-1),
-        feed_total[:, :hidden_columns],
-        feed_total[:, hidden_columns:],
-        down_total.astype(jnp.float32).T,
+        gate_gradient,
+        up_gradient,
+        down_gradient,
     )
 
 

time: 658 us -> 707 us (1.074); the launches traced: 648 us -> 706 us
  Pallas kernels: 376 us -> 538 us
  matrix products: 68.1 us -> 0 us
  local copies, waits for them, and re-layouts: 25.8 us -> 5.44 us
  other arithmetic: 34.8 us -> 20.7 us
    pallas_call x4 -> x14, Pallas kernels: 182 us -> 346 us  [the longest x4 244 us: product_scatter(): pl.pallas_call(functools.partial(scatter_kernel, sizes, len(triples), ter...]
    dot_general x6 -> x0, matrix products: 68.1 us -> none  [the longest x4 36.7 us: contract_rows(): lax.dot_general(first_operand, second_operand, (((0,), (0,)), ((), ())),...]
    all_gather x3, waiting for transfers between devices: 38.9 us -> 20 us  [the longest x2 20 us: per_device(): lax.all_gather(part, 'dp', axis=0, tiled=True)]
    unnamed x44 -> x14, local copies, waits for them, and re-layouts: 17.8 us -> 1.84 us
    concatenate x5 -> x0, other arithmetic: 11.5 us -> none  [the longest x1 5.32 us: per_device(): feed_slope = jnp.concatenate([gate_slope, up_slope], axis=1)]
    ppermute x0 -> x4, waiting for transfers between devices: none -> 8.18 us  [the longest x1 8.17 us: reduce_over_chips(): lax.ppermute(grad_blocks(ahead + (1 - core), pairs), 'dp', [(device, devi...]
    reduce_scatter x2 -> x1, waiting for transfers between devices: 88.1 us -> 94.3 us  [per_device(): lax.psum_scatter(second_grad, 'dp', scatter_dimension=0, tiled=True)]
  transfers between devices with their start and end apart: 6 -> 9, of which waited for: 3 -> 3; matrix products, arithmetic and copies ran while one was open for 17% -> 2% of each run, Pallas kernels for 58% -> 53%
where the time goes in v3:
time: 707 us; the launch traced here: 706 us
  Pallas kernels  538 us (76%)
  waiting for transfers between devices  124 us (18%)
  other arithmetic  20.7 us (3%)
  between operations  14 us (2%)
    pallas_call x4, Pallas kernels, product_scatter(): pl.pallas_call(functools.partial(scatter_kernel, sizes, len(triples), ter...  244 us
    pallas_call x3, Pallas kernels, gather_rows(): pl.pallas_call(body, out_shape=[jax.ShapeDtypeStruct((size * rows, column...  150 us
    reduce_scatter x1, waiting for transfers between devices, per_device(): lax.psum_scatter(second_grad, 'dp', scatter_dimension=0, tiled=True)  94.3 us
    pallas_call x4, Pallas kernels, grad_blocks(): pl.pallas_call(functools.partial(grad_kernel, len(pairs), other is not No...  52.6 us
    pallas_call x2, Pallas kernels, feed_half(): pl.pallas_call(functools.partial(feed_half_kernel, half, tile), grid=(tot...  36.8 us
    pallas_call x1, Pallas kernels, attention_backward(): pl.pallas_call(functools.partial(attention_backward_kernel, grouping, hea...  23.2 us
    all_gather x2, waiting for transfers between devices, per_device(): lax.all_gather(part, 'dp', axis=0, tiled=True)  20 us
    pallas_call x1, Pallas kernels, attention_forward(): pl.pallas_call(functools.partial(attention_forward_kernel, grouping, head...  18.4 us
  transfers between devices with their start and end apart: 9, of which 3 were waited for; matrix products, arithmetic and copies ran while one was open for 2% of the time, Pallas kernels for 53%

profile of v3, /device:TPU:0, one launch (start us, length us, event | category | flops | bytes accessed | tf_op | source)
XLA Modules:
  0.0 706.2 jit_solution(3654806976978471497)
XLA Ops:
  7.2 0.0 all-gather.4.cloned.1.call-start
  7.2 2.2 shard_map.246
  9.4 0.0 all-gather.6.cloned.1.call-start
  9.5 3.3 shard_map.247
  12.8 0.0 all-gather.8.cloned.1.call-start
  12.9 0.7 all-gather.8.cloned.1.call-update
  13.6 0.3 fusion.11
  13.9 1.3 fusion.4.refs_0_
  15.2 75.2 %gather_rows.3 = (bf16[1024,2048]{1,0:T(8,128)(2,1)}, bf16[1024,2048]{1,0:T(8,128)(2,1)}) custom-call(bf16[256,2048]{1,0:T(8,128)(2,1)} %fusion.4.refs_0_, bf16[256,2048]{1,0:T(8,128)(2,1)} %refs_1_.1), custom_call_target="tpu_custom_call" | custom-call | bytes 125829120 | tf_op jit(solution)/shard_map/gather_rows/pallas_call | solution.py:167
  90.4 0.5 broadcast_add_fusion.order_ref
  90.9 18.4 %attention_forward.1 = (f32[1024,1024]{1,0:T(8,128)}, bf16[1024,512]{1,0:T(8,128)(2,1)}, f32[2,2,1024]{2,1,0:T(2,128)}) custom-call(bf16[1024,2048]{1,0:T(8,128)(2,1)} %get-tuple-element.45.rows_ref.refs_0_, bf16[2048,1536]{1,0:T(8,128)(2,1)} %all-gather.4.cloned.1.call-done.weight_ref.refs_1_, f32[136,128]{1,0:T(8,128)} %constant.41.clone.few_cosines_ref, ...), custom_call_target="tpu_custom_call" | custom-call | flops 5368709120 | bytes 8388608 | tf_op jit(solution)/shard_map/attention_forward/pallas_call | solution.py:532
  109.4 40.4 %product_scatter.4 = f32[256,2048]{1,0:T(8,128)} custom-call(bf16[1024,512]{1,0:T(8,128)(2,1)} %get-tuple-element.46.refs_0_.mixed_ref.refs_3_, bf16[2048,1536]{1,0:T(8,128)(2,1)} %all-gather.4.cloned.1.call-done.weight_ref.refs_1_), custom_call_target="tpu_custom_call" | custom-call | flops 2147483648 | bytes 62914560 | tf_op jit(solution)/shard_map/product_scatter/pallas_call | solution.py:396
  149.8 2.0 multiply_reduce_fusion.2
  151.8 1.3 copy-done
  153.1 1.2 multiply_convert_fusion.refs_0_
  154.3 37.1 %gather_rows.4.rows_ref.refs_0_ = bf16[1024,2048]{1,0:T(8,128)(2,1)} custom-call(bf16[256,2048]{1,0:T(8,128)(2,1)} %multiply_convert_fusion.refs_0_), custom_call_target="tpu_custom_call" | custom-call | bytes 62914560 | tf_op jit(solution)/shard_map/gather_rows/pallas_call | solution.py:167
  191.4 18.4 %feed_half.2 = (bf16[1024,768]{1,0:T(8,128)(2,1)}, bf16[1024,1536]{1,0:T(8,128)(2,1)}) custom-call(bf16[1024,2048]{1,0:T(8,128)(2,1)} %gather_rows.4.rows_ref.refs_0_, bf16[1024,2048]{1,0:T(8,128)(2,1)} %get-tuple-element.47.cotangent_ref.refs_2_, bf16[2048,2304]{1,0:T(8,128)(2,1)} %all-gather.6.cloned.1.call-done.weight_ref.refs_1_), custom_call_target="tpu_custom_call" | custom-call | flops 9663676416 | bytes 17825792 | tf_op jit(solution)/shard_map/feed_half/pallas_call | solution.py:728
  209.8 10.6 %grad_blocks.4 = bf16[4,256,2304]{2,1,0:T(8,128)(2,1)} custom-call(s32[4]{0:T(128)} %broadcast_add_fusion.order_ref, bf16[1024,2048]{1,0:T(8,128)(2,1)} %gather_rows.4.rows_ref.refs_0_, bf16[1024,1536]{1,0:T(8,128)(2,1)} %get-tuple-element.50.refs_1_.refs_0_, bf16[1024,2048]{1,0:T(8,128)(2,1)} %get-tuple-element.47.cotangent_ref.refs_2_, ...), custom_call_target="tpu_custom_call" | custom-call | flops 4831838208 | bytes 13631488 | tf_op jit(solution)/shard_map/grad_blocks/pallas_call | solution.py:818
  220.5 0.5 broadcast_add_fusion.1.order_ref
  221.0 8.2 %collective-permute-done.refs_4_ = bf16[4,256,2304]{2,1,0:T(8,128)(2,1)} collective-permute-done((bf16[4,256,2304]{2,1,0:T(8,128)(2,1)}, bf16[4,256,2304]{2,1,0:T(8,128)(2,1)}, u32[]{:S(2)}, u32[]{:S(2)}) %collective-permute-start) | collective-permute-done | bytes 4718624 | tf_op jit(solution)/shard_map/ppermute | solution.py:845
  229.2 11.5 %grad_blocks.5 = (bf16[256,2304]{1,0:T(8,128)(2,1)}, bf16[256,2304]{1,0:T(8,128)(2,1)}, bf16[256,2304]{1,0:T(8,128)(2,1)}, bf16[256,2304]{1,0:T(8,128)(2,1)}) custom-call(s32[4]{0:T(128)} %broadcast_add_fusion.1.order_ref, bf16[1024,2048]{1,0:T(8,128)(2,1)} %gather_rows.4.rows_ref.refs_0_, bf16[1024,1536]{1,0:T(8,128)(2,1)} %get-tuple-element.50.refs_1_.refs_0_, ...), custom_call_target="tpu_custom_call" | custom-call | flops 4831838208 | bytes 13631488 | tf_op jit(solution)/shard_map/grad_blocks/pallas_call | solution.py:818
  240.7 19.9 %all-gather.8.cloned.1.call-done.weight_ref.refs_3_ = bf16[2048,2304]{1,0:T(8,128)(2,1)} async-done(((bf16[256,2304]{1,0:T(8,128)(2,1)}), bf16[2048,2304]{1,0:T(8,128)(2,1)}) %all-gather.8.cloned.1.call-update) | async-done | bytes 9437200 | tf_op jit(solution)/shard_map/all_gather | solution.py:967
  260.6 18.3 %feed_half.3 = (bf16[1024,768]{1,0:T(8,128)(2,1)}, bf16[1024,1536]{1,0:T(8,128)(2,1)}) custom-call(bf16[1024,2048]{1,0:T(8,128)(2,1)} %gather_rows.4.rows_ref.refs_0_, bf16[1024,2048]{1,0:T(8,128)(2,1)} %get-tuple-element.47.cotangent_ref.refs_2_, bf16[2048,2304]{1,0:T(8,128)(2,1)} %all-gather.8.cloned.1.call-done.weight_ref.refs_3_), custom_call_target="tpu_custom_call" | custom-call | flops 9663676416 | bytes 17825792 | tf_op jit(solution)/shard_map/feed_half/pallas_call | solution.py:728
  279.0 0.5 iota.10.order_ref
  279.5 16.9 %grad_blocks.6 = bf16[8,256,2304]{2,1,0:T(8,128)(2,1)} custom-call(s32[8]{0:T(128)} %iota.10.order_ref, bf16[1024,2048]{1,0:T(8,128)(2,1)} %gather_rows.4.rows_ref.refs_0_, bf16[1024,1536]{1,0:T(8,128)(2,1)} %get-tuple-element.59.refs_1_.refs_2_, bf16[1024,2048]{1,0:T(8,128)(2,1)} %get-tuple-element.47.cotangent_ref.refs_2_, ...), custom_call_target="tpu_custom_call" | custom-call | flops 9663676416 | bytes 22544384 | tf_op jit(solution)/shard_map/grad_blocks/pallas_call | solution.py:818
  296.3 49.6 %product_scatter.5 = f32[256,2048]{1,0:T(8,128)} custom-call(bf16[1024,1536]{1,0:T(8,128)(2,1)} %get-tuple-element.50.refs_1_.refs_0_, bf16[2048,2304]{1,0:T(8,128)(2,1)} %all-gather.6.cloned.1.call-done.weight_ref.refs_1_, bf16[1024,1536]{1,0:T(8,128)(2,1)} %get-tuple-element.59.refs_1_.refs_2_, ...), custom_call_target="tpu_custom_call" | custom-call | flops 12884901888 | bytes 62914560 | tf_op jit(solution)/shard_map/product_scatter/pallas_call | solution.py:396
  346.0 2.9 multiply_reduce_fusion
  349.0 0.5 copy-done.3
  349.5 2.9 fusion.14.refs_0_
  352.4 38.1 %gather_rows.5.state_ref.refs_2_ = bf16[1024,2048]{1,0:T(8,128)(2,1)} custom-call(bf16[256,2048]{1,0:T(8,128)(2,1)} %fusion.14.refs_0_), custom_call_target="tpu_custom_call" | custom-call | bytes 62914560 | tf_op jit(solution)/shard_map/gather_rows/pallas_call | solution.py:167
  390.4 23.2 %attention_backward.1 = (bf16[1024,1024]{1,0:T(8,128)(2,1)}, f32[8,128]{1,0:T(8,128)}) custom-call(bf16[1024,2048]{1,0:T(8,128)(2,1)} %gather_rows.5.state_ref.refs_2_, bf16[2048,1536]{1,0:T(8,128)(2,1)} %all-gather.4.cloned.1.call-done.weight_ref.refs_1_, f32[1024,1024]{1,0:T(8,128)} %get-tuple-element.60.raw_ref, ...), custom_call_target="tpu_custom_call" | custom-call | flops 4831838208 | bytes 6291456 | tf_op jit(solution)/shard_map/attention_backward/pallas_call | solution.py:656
  413.6 0.5 iota.9.order_ref
  414.1 13.6 %grad_blocks.7 = bf16[8,256,1536]{2,1,0:T(8,128)(2,1)} custom-call(s32[8]{0:T(128)} %iota.9.order_ref, bf16[1024,2048]{1,0:T(8,128)(2,1)} %get-tuple-element.45.rows_ref.refs_0_, bf16[1024,1024]{1,0:T(8,128)(2,1)} %get-tuple-element.63.refs_1_.refs_0_, bf16[1024,2048]{1,0:T(8,128)(2,1)} %gather_rows.5.state_ref.refs_2_, ...), custom_call_target="tpu_custom_call" | custom-call | flops 6442450944 | bytes 17825792 | tf_op jit(solution)/shard_map/grad_blocks/pallas_call | solution.py:818
  427.8 0.0 reduce-scatter.5.cloned.1.call-start
  427.8 0.5 reduce-scatter.5.cloned.1.call-update
  428.3 0.1 collective-permute-start.1
  428.4 1.3 collective-permute-start.2
  429.7 2.5 collective-permute-start.3
  432.2 41.4 %product_scatter.6 = f32[256,2048]{1,0:T(8,128)} custom-call(bf16[1024,1024]{1,0:T(8,128)(2,1)} %get-tuple-element.63.refs_1_.refs_0_, bf16[2048,1536]{1,0:T(8,128)(2,1)} %all-gather.4.cloned.1.call-done.weight_ref.refs_1_), custom_call_target="tpu_custom_call" | custom-call | flops 4294967296 | bytes 62914560 | tf_op jit(solution)/shard_map/product_scatter/pallas_call | solution.py:396
  473.6 2.2 fusion.6
  475.9 0.6 pad_maximum_fusion.refs_4_
  476.5 112.1 %product_scatter.7 = (f32[256,2048]{1,0:T(8,128)}, f32[40,128]{1,0:T(8,128)}) custom-call(bf16[1024,768]{1,0:T(8,128)(2,1)} %get-tuple-element.49.refs_3_.refs_0_, bf16[2048,2304]{1,0:T(8,128)(2,1)} %all-gather.6.cloned.1.call-done.weight_ref.refs_1_, bf16[1024,768]{1,0:T(8,128)(2,1)} %get-tuple-element.57.refs_3_.refs_2_, ...), custom_call_target="tpu_custom_call" | custom-call | flops 6442450944 | bytes 62914560 | tf_op jit(solution)/shard_map/product_scatter/pallas_call | solution.py:396
  588.6 1.3 slice_bitcast_fusion.2
  589.9 1.3 slice_bitcast_fusion
  591.2 6.2 fusion.10
  597.4 2.3 shard_map.248
  599.8 94.3 %reduce-scatter.5.cloned.1.call-done.refs_4_ = bf16[256,2304]{1,0:T(8,128)(2,1)} async-done(((bf16[2048,2304]{1,0:T(8,128)(2,1)}), bf16[256,2304]{1,0:T(8,128)(2,1)}) %reduce-scatter.5.cloned.1.call-update) | async-done | bytes 1179664 | tf_op jit(solution)/shard_map/reduce_scatter | solution.py:997
  694.1 5.6 shard_map.249
  (27 shorter events, 0.2 us)
Async XLA Ops:
  7.2 83.7 %all-gather.4.cloned.1.call-start = ((), (), s32[]{:S(2)}) async-start(), calls=%async_computation.2 | async-start | bytes 7077888 | tf_op jit(solution)/shard_map/all_gather | solution.py:961
  9.4 4.2 copy-start.2
  9.4 182.0 %all-gather.6.cloned.1.call-start = ((), (), s32[]{:S(2)}) async-start(), calls=%async_computation.3 | async-start | bytes 10616832 | tf_op jit(solution)/shard_map/all_gather | solution.py:967
  12.8 1.1 copy-start.5
  12.8 247.8 %all-gather.8.cloned.1.call-start = ((), (), s32[]{:S(2)}) async-start(), calls=%async_computation.4 | async-start | bytes 10616832 | tf_op jit(solution)/shard_map/all_gather | solution.py:967
  13.6 583.8 %reduce-scatter.3.cloned.1.call-start = ((), (), s32[]{:S(2)}) async-start(), calls=%async_computation.5 | async-start | bytes 7077888 | tf_op jit(solution)/shard_map/reduce_scatter | solution.py:1016
  149.8 3.3 copy-start.4
  151.8 1.3 copy-start
  220.5 8.7 %collective-permute-start = (bf16[4,256,2304]{2,1,0:T(8,128)(2,1)}, bf16[4,256,2304]{2,1,0:T(8,128)(2,1)}, u32[]{:S(2)}, u32[]{:S(2)}) collective-permute-start(bf16[4,256,2304]{2,1,0:T(8,128)(2,1)} %grad_blocks.4), channel_id=1, source_target_pairs={{0,4},{4,0},{8,12},{12,8},{16,20},{20,16},{24,28},{28,24},{1,5},{5... | collective-permute-start | bytes 14155784 | tf_op jit(solution)/shard_map/ppermute | solution.py:845
  346.0 3.0 copy-start.1
  346.0 3.5 copy-start.3
  427.8 266.3 %reduce-scatter.5.cloned.1.call-start = ((), (), s32[]{:S(2)}) async-start(), calls=%async_computation.6 | async-start | bytes 10616832 | tf_op jit(solution)/shard_map/reduce_scatter | solution.py:997
  428.3 171.4 %collective-permute-start.1 = (bf16[256,2304]{1,0:T(8,128)(2,1)}, bf16[256,2304]{1,0:T(8,128)(2,1)}, u32[]{:S(2)}, u32[]{:S(2)}) collective-permute-start(bf16[256,2304]{1,0:T(8,128)(2,1)} %get-tuple-element.52), channel_id=1, source_target_pairs={{0,8},{4,12},{8,16},{12,20},{16,24},{20,28},{24,0},{28,4},{1,9},{5... | collective-permute-start | bytes 3538952 | tf_op jit(solution)/shard_map/ppermute | solution.py:854
  428.4 171.3 %collective-permute-start.2 = (bf16[256,2304]{1,0:T(8,128)(2,1)}, bf16[256,2304]{1,0:T(8,128)(2,1)}, u32[]{:S(2)}, u32[]{:S(2)}) collective-permute-start(bf16[256,2304]{1,0:T(8,128)(2,1)} %get-tuple-element.53), channel_id=1, source_target_pairs={{0,16},{4,20},{8,24},{12,28},{16,0},{20,4},{24,8},{28,12},{1,17},{... | collective-permute-start | bytes 3538952 | tf_op jit(solution)/shard_map/ppermute | solution.py:854
  429.7 170.1 %collective-permute-start.3 = (bf16[256,2304]{1,0:T(8,128)(2,1)}, bf16[256,2304]{1,0:T(8,128)(2,1)}, u32[]{:S(2)}, u32[]{:S(2)}) collective-permute-start(bf16[256,2304]{1,0:T(8,128)(2,1)} %get-tuple-element.54), channel_id=1, source_target_pairs={{0,24},{4,28},{8,0},{12,4},{16,8},{20,12},{24,16},{28,20},{1,25},{... | collective-permute-start | bytes 3538952 | tf_op jit(solution)/shard_map/ppermute | solution.py:854
  473.6 2.3 copy-start.6
Sparse Core Ops, SparseCore 0:
  10.2 67.4 all-gather.3
  79.9 89.3 all-gather.5
  171.5 89.1 all-gather.7
  427.9 151.3 reduce-scatter.2
  581.4 112.5 reduce-scatter.4

commit v4 on v3

--- a/solution.py
+++ b/solution.py
@@ -57,124 +57,121 @@
     return row * 2 + (1 - column), (1 - row) * 2 + column, (1 - row) * 2 + (1 - column)
 
 
-def gather_kernel_square(count, *refs):
-    own_refs, out_refs, held_refs = refs[:count], refs[count : 2 * count], refs[2 * count : 3 * count]
-    send_sem, recv_sem, local_sem = refs[3 * count :]
-    me = lax.axis_index("tensor")
-    beside, below, across = square_peers(me)
-    greet((("tensor", beside), ("tensor", below)))
-    rows = own_refs[0].shape[0]
-    half = rows // 2
-    first, second = pl.ds(0, half), pl.ds(half, half)
-    copies = []
-    stores = []
-
-    def store(k, source, slot, part, sem):
-        start = slot * rows + (half if part == 1 else 0)
-        size = rows if part is None else half
-        copy = pltpu.make_async_copy(
-            source, out_refs[k].at[pl.ds(pl.multiple_of(start, half), size)], local_sem.at[k, sem]
-        )
+def neighbours(size):
+    if size == 4:
+        beside, below, _ = square_peers(lax.axis_index("tensor"))
+        return [("tensor", beside), ("tensor", below)]
+    return [("tensor", peer) for peer in other_members("tensor", size)]
+
+
+def other_members(axis, count):
+    me = lax.axis_index(axis)
+    return [lax.rem(me + step, count) for step in range(1, count)]
+
+
+class Gather:
+    def __init__(self, size, own_ref, out_ref, held_ref, send_sem, recv_sem, local_sem):
+        self.size, self.own, self.out, self.held = size, own_ref, out_ref, held_ref
+        self.send_sem, self.recv_sem, self.local_sem = send_sem, recv_sem, local_sem
+        self.me = lax.axis_index("tensor")
+        self.rows = own_ref.shape[0]
+        self.copies, self.stores = [], []
+
+    @staticmethod
+    def scratch(size, rows, columns):
+        sends, local = (6, 7) if size == 4 else (size - 1, size)
+        return [
+            pltpu.VMEM((size, rows, columns), jnp.bfloat16),
+            pltpu.SemaphoreType.DMA((sends,)),
+            pltpu.SemaphoreType.DMA((sends,)),
+            pltpu.SemaphoreType.DMA((local,)),
+        ]
+
+    def send(self, source, target, peer):
+        index = len(self.copies)
+        copy = remote(source, target, self.send_sem.at[index], self.recv_sem.at[index], peer)
         copy.start()
-        stores.append(copy)
-
-    for k in range(count):
-        own, held = own_refs[k], held_refs[k]
-
-        def send(index, source, slot, part, peer):
-            copy = remote(
-                source, held.at[slot, part], send_sem.at[k, index], recv_sem.at[k, index], peer
-            )
-            copy.start()
-            copies.append(copy)
-            return copy
-
-        x_first = send(0, own.at[first], me, first, beside)
-        y_second = send(1, own.at[second], me, second, below)
-        x_second = send(2, own.at[second], me, second, beside)
-        y_first = send(3, own.at[first], me, first, below)
-        store(k, own, me, None, 0)
+        self.copies.append(copy)
+        return copy
+
+    def store(self, source, start, count):
+        target = self.out.at[pl.ds(pl.multiple_of(start, count), count)]
+        copy = pltpu.make_async_copy(source, target, self.local_sem.at[len(self.stores)])
+        copy.start()
+        self.stores.append(copy)
+
+    def start(self):
+        own, held, rows = self.own, self.held, self.rows
+        if self.size != 4:
+            for peer in other_members("tensor", self.size):
+                self.send(own, held.at[self.me], peer)
+            self.store(own, self.me * rows, rows)
+            return
+        beside, below, _ = square_peers(self.me)
+        half = rows // 2
+        first, second = pl.ds(0, half), pl.ds(half, half)
+        x_first = self.send(own.at[first], held.at[self.me, first], beside)
+        y_second = self.send(own.at[second], held.at[self.me, second], below)
+        self.send(own.at[second], held.at[self.me, second], beside)
+        self.send(own.at[first], held.at[self.me, first], below)
+        self.store(own, self.me * rows, rows)
         x_first.wait_recv()
-        y_pass = send(4, held.at[beside, first], beside, first, below)
+        self.send(held.at[beside, first], held.at[beside, first], below)
         y_second.wait_recv()
-        x_pass = send(5, held.at[below, second], below, second, beside)
-        store(k, held.at[beside, first], beside, 0, 1)
-        store(k, held.at[below, second], below, 1, 2)
-    for k in range(count):
-        held = held_refs[k]
-        x_second, y_first, y_pass, x_pass = copies[6 * k + 2 : 6 * k + 6]
-        x_second.wait_recv()
-        store(k, held.at[beside, second], beside, 1, 3)
-        y_first.wait_recv()
-        store(k, held.at[below, first], below, 0, 4)
-        y_pass.wait_recv()
-        store(k, held.at[across, first], across, 0, 5)
-        x_pass.wait_recv()
-        store(k, held.at[across, second], across, 1, 6)
-    for copy in copies:
-        copy.wait_send()
-    for copy in stores:
-        copy.wait()
-
-
-def gather_kernel_direct(size, count, *refs):
-    own_refs, out_refs, held_refs = refs[:count], refs[count : 2 * count], refs[2 * count : 3 * count]
-    send_sem, recv_sem, local_sem = refs[3 * count :]
-    me = lax.axis_index("tensor")
-    peers = [lax.rem(me + step, size) for step in range(1, size)]
-    greet([("tensor", peer) for peer in peers])
-    rows = own_refs[0].shape[0]
-    copies = []
-    stores = []
-    for k in range(count):
-        for step, peer in enumerate(peers):
-            copy = remote(
-                own_refs[k], held_refs[k].at[me], send_sem.at[k, step], recv_sem.at[k, step], peer
-            )
-            copy.start()
-            copies.append(copy)
-    for k in range(count):
-        for step in range(size):
-            source = own_refs[k]
-            slot = lax.rem(me + size - step, size)
-            if step > 0:
-                copies[k * (size - 1) + step - 1].wait_recv()
-                source = held_refs[k].at[slot]
-            copy = pltpu.make_async_copy(
-                source,
-                out_refs[k].at[pl.ds(pl.multiple_of(slot * rows, rows), rows)],
-                local_sem.at[k, step],
-            )
-            copy.start()
-            stores.append(copy)
-    for copy in copies:
-        copy.wait_send()
-    for copy in stores:
-        copy.wait()
+        self.send(held.at[below, second], held.at[below, second], beside)
+        self.store(held.at[beside, first], beside * rows, half)
+        self.store(held.at[below, second], below * rows + half, half)
+
+    def finish(self):
+        held, rows = self.held, self.rows
+        if self.size != 4:
+            for step, copy in enumerate(self.copies):
+                copy.wait_recv()
+                slot = lax.rem(self.me + self.size - step - 1, self.size)
+                self.store(held.at[slot], slot * rows, rows)
+        else:
+            beside, below, across = square_peers(self.me)
+            half = rows // 2
+            first, second = pl.ds(0, half), pl.ds(half, half)
+            x_second, y_first, y_pass, x_pass = self.copies[2:]
+            x_second.wait_recv()
+            self.store(held.at[beside, second], beside * rows + half, half)
+            y_first.wait_recv()
+            self.store(held.at[below, first], below * rows, half)
+            y_pass.wait_recv()
+            self.store(held.at[across, first], across * rows, half)
+            x_pass.wait_recv()
+            self.store(held.at[across, second], across * rows + half, half)
+        for copy in self.copies:
+            copy.wait_send()
+        for copy in self.stores:
+            copy.wait()
+
+
+def gather_kernel(size, count, *refs):
+    own_refs, out_refs, rest = refs[:count], refs[count : 2 * count], refs[2 * count :]
+    greet(neighbours(size))
+    gathers = [
+        Gather(size, own_refs[k], out_refs[k], *rest[4 * k : 4 * k + 4]) for k in range(count)
+    ]
+    for gather in gathers:
+        gather.start()
+    for gather in gathers:
+        gather.finish()
 
 
 def gather_rows(arrays, size, collective_id):
     count = len(arrays)
     rows, columns = arrays[0].shape
-    square = size == 4
-    body = (
-        functools.partial(gather_kernel_square, count)
-        if square
-        else functools.partial(gather_kernel_direct, size, count)
-    )
-    sends = 6 if square else size - 1
-    locals_ = 7 if square else size
+    scratch = []
+    for _ in arrays:
+        scratch += Gather.scratch(size, rows, columns)
     return pl.pallas_call(
-        body,
+        functools.partial(gather_kernel, size, count),
         out_shape=[jax.ShapeDtypeStruct((size * rows, columns), a.dtype) for a in arrays],
         in_specs=[pl.BlockSpec(memory_space=pltpu.VMEM)] * count,
         out_specs=[pl.BlockSpec(memory_space=pl.ANY)] * count,
-        scratch_shapes=[pltpu.VMEM((size, rows, columns), a.dtype) for a in arrays]
-        + [
-            pltpu.SemaphoreType.DMA((count, sends)),
-            pltpu.SemaphoreType.DMA((count, sends)),
-            pltpu.SemaphoreType.DMA((count, locals_)),
-        ],
+        scratch_shapes=scratch,
         compiler_params=pltpu.CompilerParams(
             collective_id=collective_id, has_side_effects=True, vmem_limit_bytes=VMEM_LIMIT
         ),
@@ -202,9 +199,115 @@
     lax.fori_loop(0, total // tile, step, 0)
 
 
-def other_members(axis, count):
-    me = lax.axis_index(axis)
-    return [lax.rem(me + step, count) for step in range(1, count)]
+class Scatter:
+    def __init__(self, size, outgoing, *rest):
+        self.size, self.outgoing = size, outgoing
+        if size == 4:
+            self.passing, rest = rest[0], rest[1:]
+        self.arriving, self.send_sem, self.recv_sem = rest
+        self.rows = outgoing.shape[1]
+        self.me = lax.axis_index("tensor")
+
+    @staticmethod
+    def scratch(size, rows, columns):
+        if size == 4:
+            sends = 6
+            buffers = [
+                pltpu.VMEM((4, rows, columns), jnp.bfloat16),
+                pltpu.VMEM((2, rows // 2, columns), jnp.bfloat16),
+                pltpu.VMEM((2, rows, columns), jnp.bfloat16),
+            ]
+        else:
+            sends = size - 1
+            buffers = [
+                pltpu.VMEM((size, rows, columns), jnp.bfloat16),
+                pltpu.VMEM((size - 1, rows, columns), jnp.bfloat16),
+            ]
+        return buffers + [pltpu.SemaphoreType.DMA((sends,)), pltpu.SemaphoreType.DMA((sends,))]
+
+    def prepare(self, index, source, target, peer):
+        return remote(source, target, self.send_sem.at[index], self.recv_sem.at[index], peer)
+
+    def fill(self, pairs):
+        size, me, outgoing, arriving, rows = self.size, self.me, self.outgoing, self.arriving, self.rows
+        if size == 4:
+            beside, below, across = square_peers(me)
+            half = rows // 2
+            first, second = pl.ds(0, half), pl.ds(half, half)
+            self.copies = [
+                self.prepare(0, outgoing.at[0, first], self.passing.at[0], beside),
+                self.prepare(1, outgoing.at[0, second], self.passing.at[1], below),
+                self.prepare(2, outgoing.at[1, first], arriving.at[0, first], beside),
+                self.prepare(3, outgoing.at[2, second], arriving.at[1, second], below),
+                self.prepare(4, outgoing.at[1, second], arriving.at[0, second], beside),
+                self.prepare(5, outgoing.at[2, first], arriving.at[1, first], below),
+            ]
+            starts = ((0, 0), (0, 1), (1, 2), (2, 3))
+        else:
+            self.copies = [
+                self.prepare(step, outgoing.at[step], arriving.at[step], peer)
+                for step, peer in enumerate(other_members("tensor", size))
+            ]
+            starts = tuple((step, step) for step in range(size - 1))
+
+        def step(slot, carry):
+            if size == 4:
+                owner = jnp.where(
+                    slot == 0, across, jnp.where(slot == 1, beside, jnp.where(slot == 2, below, me))
+                )
+            else:
+                owner = lax.rem(me + slot + 1, size)
+
+            def write(columns, values):
+                outgoing[slot, :, columns] = values.astype(outgoing.dtype)
+
+            block_product(pairs, owner * rows, rows, write)
+            for at, index in starts:
+                pl.when(slot == at)(self.copies[index].start)
+            return carry
+
+        lax.fori_loop(0, size, step, 0)
+
+    def relay(self):
+        if self.size != 4:
+            return
+        half = self.rows // 2
+        x_pass, y_pass, _, _, x_second, y_first = self.copies
+        for arrival, source, slot, start, onward in (
+            (y_pass, 1, 1, half, x_second),
+            (x_pass, 0, 2, 0, y_first),
+        ):
+            arrival.wait_recv()
+            piece = pl.ds(start, half)
+            self.outgoing[slot, piece, :] = (
+                self.outgoing[slot, piece, :].astype(jnp.float32)
+                + self.passing[source].astype(jnp.float32)
+            ).astype(self.outgoing.dtype)
+            onward.start()
+
+    def collect(self):
+        for copy in self.copies[2:] if self.size == 4 else self.copies:
+            copy.wait_recv()
+
+    def total(self, piece):
+        total = self.outgoing[self.size - 1, piece, :].astype(jnp.float32)
+        for index in range(self.arriving.shape[0]):
+            total = total + self.arriving[index, piece, :].astype(jnp.float32)
+        return total
+
+    def drain(self):
+        for copy in self.copies:
+            copy.wait_send()
+
+
+def over_pieces(rows, body):
+    count = min(32, rows)
+
+    def step(index, carry):
+        body(pl.ds(pl.multiple_of(index * count, count), count))
+        return carry
+
+    lax.fori_loop(0, rows // count, step, 0)
 
 
 def send_terms(axis, peers, source, landing, send_sem, recv_sem):
@@ -227,190 +330,166 @@
     return total
 
 
-def scatter_kernel(sizes, pair_count, with_terms, *refs):
-    pairs = [refs[2 * p : 2 * p + 2] for p in range(pair_count)]
-    refs = refs[2 * pair_count :]
-    if with_terms:
-        terms_ref, out_ref, terms_out_ref = refs[:3]
-        inner, outer, partial_ref = refs[-7:-4]
-        inner_send, inner_recv, outer_send, outer_recv = refs[-4:]
-        buffers = refs[3:-7]
-    else:
-        out_ref, buffers = refs[0], refs[1:]
+def split_pairs(refs, count):
+    return [refs[2 * p : 2 * p + 2] for p in range(count)], refs[2 * count :]
+
+
+def store_row(target_ref, row_ref):
+    width = target_ref.shape[1]
+    for index in range(row_ref.shape[1] // width):
+        target_ref[index : index + 1, :] = row_ref[:, index * width : (index + 1) * width]
+
+
+def between_forward_kernel(size, pair_count, *refs):
+    pairs, refs = split_pairs(refs, pair_count)
+    input_ref, gain_ref, gathered_ref, state_ref, own_ref = refs[:5]
+    buffers = 5 if size == 4 else 4
+    scatter = Scatter(size, *refs[5 : 5 + buffers])
+    gather = Gather(size, own_ref, gathered_ref, *refs[5 + buffers :])
+    greet(neighbours(size))
+    scatter.fill(pairs)
+    scatter.relay()
+    scatter.collect()
+
+    def norm(piece):
+        state = input_ref[piece, :].astype(jnp.float32) + scatter.total(piece)
+        state_ref[piece, :] = state
+        own_ref[piece, :] = (state * row_scale(state) * gain_ref[...]).astype(own_ref.dtype)
+
+    over_pieces(own_ref.shape[0], norm)
+    gather.start()
+    gather.finish()
+    scatter.drain()
+
+
+def between_backward_kernel(size, pair_count, *refs):
+    pairs, refs = split_pairs(refs, pair_count)
+    state_ref, cotangent_ref, gain_ref, gathered_ref, slope_ref, term_ref, own_ref, sum_ref = refs[:8]
+    buffers = 5 if size == 4 else 4
+    scatter = Scatter(size, *refs[8 : 8 + buffers])
+    gather = Gather(size, own_ref, gathered_ref, *refs[8 + buffers :])
+    greet(neighbours(size))
+    scatter.fill(pairs)
+    scatter.relay()
+    sum_ref[...] = jnp.zeros_like(sum_ref)
+    scatter.collect()
+
+    def norm(piece):
+        back = scatter.total(piece)
+        state = state_ref[piece, :]
+        scale = row_scale(state)
+        unit = state * scale
+        sum_ref[...] += jnp.sum(back * unit, axis=0, keepdims=True)
+        unit_slope = back * gain_ref[...]
+        slope = cotangent_ref[piece, :].astype(jnp.float32) + scale * (
+            unit_slope - unit * jnp.mean(unit_slope * unit, axis=-1, keepdims=True)
+        )
+        slope_ref[piece, :] = slope
+        own_ref[piece, :] = slope.astype(own_ref.dtype)
+
+    over_pieces(own_ref.shape[0], norm)
+    gather.start()
+    store_row(term_ref, sum_ref)
+    gather.finish()
+    scatter.drain()
+
+
+def last_kernel(sizes, pair_counts, *refs):
     data_size, size = sizes
-    if size == 4:
-        beside, below, across = square_peers(lax.axis_index("tensor"))
-        near = [("tensor", beside), ("tensor", below)]
-    else:
-        near = [("tensor", peer) for peer in other_members("tensor", size)]
-    if with_terms:
-        if size == 4:
-            near.append(("tensor", across))
-        near += [("dp", peer) for peer in other_members("dp", data_size)]
-    greet(near)
-    if with_terms:
-        inner_copies = send_terms(
-            "tensor", other_members("tensor", size), terms_ref, inner, inner_send, inner_recv
-        )
-    if size == 4:
-        scatter_square(pairs, out_ref, *buffers)
-    else:
-        scatter_direct(size, pairs, out_ref, *buffers)
-    if with_terms:
-        partial_ref[...] = add_terms(inner, inner_copies)
-        outer_copies = send_terms(
-            "dp", other_members("dp", data_size), partial_ref, outer, outer_send, outer_recv
-        )
-        terms_out_ref[...] = add_terms(outer, outer_copies)
-        for copy in inner_copies + outer_copies:
-            copy.wait_send()
-
-
-def scatter_square(pairs, out_ref, outgoing, passing, arriving, send_sem, recv_sem):
-    me = lax.axis_index("tensor")
-    beside, below, across = square_peers(me)
-    rows = out_ref.shape[0]
-    half = rows // 2
-    first, second = pl.ds(0, half), pl.ds(half, half)
-
-    def prepare(index, source, target, peer):
-        return remote(source, target, send_sem.at[index], recv_sem.at[index], peer)
-
-    x_pass = prepare(0, outgoing.at[0, first], passing.at[0], beside)
-    y_pass = prepare(1, outgoing.at[0, second], passing.at[1], below)
-    x_first = prepare(2, outgoing.at[1, first], arriving.at[0, first], beside)
-    y_second = prepare(3, outgoing.at[2, second], arriving.at[1, second], below)
-    x_second = prepare(4, outgoing.at[1, second], arriving.at[0, second], beside)
-    y_first = prepare(5, outgoing.at[2, first], arriving.at[1, first], below)
-
-    def fill(slot, carry):
-        owner = jnp.where(
-            slot == 0, across, jnp.where(slot == 1, beside, jnp.where(slot == 2, below, me))
-        )
-
-        def write(columns, values):
-            outgoing[slot, :, columns] = values.astype(outgoing.dtype)
-
-        block_product(pairs, owner * rows, rows, write)
-        pl.when(slot == 0)(x_pass.start)
-        pl.when(slot == 0)(y_pass.start)
-        pl.when(slot == 1)(x_first.start)
-        pl.when(slot == 2)(y_second.start)
-        return carry
-
-    lax.fori_loop(0, 4, fill, 0)
-    y_pass.wait_recv()
-    outgoing[1, second, :] = (
-        outgoing[1, second, :].astype(jnp.float32) + passing[1].astype(jnp.float32)
-    ).astype(outgoing.dtype)
-    x_second.start()
-    x_pass.wait_recv()
-    outgoing[2, first, :] = (
-        outgoing[2, first, :].astype(jnp.float32) + passing[0].astype(jnp.float32)
-    ).astype(outgoing.dtype)
-    y_first.start()
-    x_first.wait_recv()
-    y_second.wait_recv()
-    x_second.wait_recv()
-    y_first.wait_recv()
-    out_ref[...] = (
-        outgoing[3].astype(jnp.float32)
-        + arriving[0].astype(jnp.float32)
-        + arriving[1].astype(jnp.float32)
-    )
-    for copy in (x_pass, y_pass, x_first, y_second, x_second, y_first):
+    mixing_pairs, refs = split_pairs(refs, pair_counts[0])
+    feed_pairs, refs = split_pairs(refs, pair_counts[1])
+    input_ref, gain_ref, slope_ref, state_ref, terms_ref = refs[:5]
+    output_ref, gradient_ref, terms_out_ref, sum_ref, partial_ref, inner, outer = refs[5:12]
+    inner_send, inner_recv, outer_send, outer_recv = refs[12:16]
+    buffers = 5 if size == 4 else 4
+    mixing = Scatter(size, *refs[16 : 16 + buffers])
+    feed = Scatter(size, *refs[16 + buffers :])
+    greet(
+        [("tensor", peer) for peer in other_members("tensor", size)]
+        + [("dp", peer) for peer in other_members("dp", data_size)]
+    )
+    mixing.fill(mixing_pairs)
+    feed.fill(feed_pairs)
+    mixing.relay()
+    sum_ref[...] = jnp.zeros_like(sum_ref)
+    feed.relay()
+    mixing.collect()
+
+    def norm(piece):
+        back = mixing.total(piece)
+        values = input_ref[piece, :].astype(jnp.float32)
+        scale = row_scale(values)
+        unit = values * scale
+        sum_ref[...] += jnp.sum(back * unit, axis=0, keepdims=True)
+        unit_slope = back * gain_ref[...]
+        gradient_ref[piece, :] = (
+            slope_ref[piece, :]
+            + scale * (unit_slope - unit * jnp.mean(unit_slope * unit, axis=-1, keepdims=True))
+        ).astype(gradient_ref.dtype)
+
+    over_pieces(output_ref.shape[0], norm)
+    kept = partial_ref.shape[0] - terms_ref.shape[0]
+    partial_ref[kept:, :] = terms_ref[...]
+    store_row(partial_ref, sum_ref)
+    inner_copies = send_terms(
+        "tensor", other_members("tensor", size), partial_ref, inner, inner_send, inner_recv
+    )
+    terms_out_ref[...] = add_terms(inner, inner_copies)
+    outer_copies = send_terms(
+        "dp", other_members("dp", data_size), terms_out_ref, outer, outer_send, outer_recv
+    )
+    feed.collect()
+
+    def finish(piece):
+        output_ref[piece, :] = (state_ref[piece, :] + feed.total(piece)).astype(output_ref.dtype)
+
+    over_pieces(output_ref.shape[0], finish)
+    total = add_terms(outer, outer_copies)
+    for copy in outer_copies:
         copy.wait_send()
-
-
-def scatter_direct(size, pairs, out_ref, outgoing, arriving, send_sem, recv_sem):
-    me = lax.axis_index("tensor")
-    rows = out_ref.shape[0]
-    copies = []
-    for step, peer in enumerate(other_members("tensor", size)):
-
-        def write(columns, values, step=step):
-            outgoing[step, :, columns] = values.astype(outgoing.dtype)
-
-        block_product(pairs, peer * rows, rows, write)
-        copy = remote(
-            outgoing.at[step], arriving.at[step], send_sem.at[step], recv_sem.at[step], peer
-        )
-        copy.start()
-        copies.append(copy)
-
-    def write_own(columns, values):
-        out_ref[:, columns] = values
-
-    block_product(pairs, me * rows, rows, write_own)
-    for step, copy in enumerate(copies):
-        copy.wait_recv()
-        out_ref[...] += arriving[step].astype(jnp.float32)
-    for copy in copies:
+    terms_out_ref[...] = total
+    for copy in inner_copies:
         copy.wait_send()
-
-
-def product_scatter(triples, sizes, collective_id, terms=None):
-    total_rows = triples[0][0].shape[0]
-    columns = triples[0][1].shape[0]
-    depth = sum(left.shape[1] for left, _, _ in triples)
-    data_size, size = sizes
-    rows = total_rows // size
-    if size == 4:
-        buffers = [
-            pltpu.VMEM((4, rows, columns), jnp.bfloat16),
-            pltpu.VMEM((2, rows // 2, columns), jnp.bfloat16),
-            pltpu.VMEM((2, rows, columns), jnp.bfloat16),
-        ]
-        sends = 6
-    else:
-        buffers = [pltpu.VMEM((size - 1, rows, columns), jnp.bfloat16)] * 2
-        sends = size - 1
-    buffers += [pltpu.SemaphoreType.DMA((sends,)), pltpu.SemaphoreType.DMA((sends,))]
+    mixing.drain()
+    feed.drain()
+
+
+def scatter_call(body, triple_lists, others, outs, gathered, scratch, collective_id):
     in_specs = []
     operands = []
-    for left, weight, first_column in triples:
+    flops = 0
+    for left, weight, first_column in (triple for triples in triple_lists for triple in triples):
         part = left.shape[1]
+        flops += 2 * left.size * weight.shape[0]
         in_specs += [
-            pl.BlockSpec((total_rows, part), lambda i: (0, 0), pipeline_mode=pl.Buffered(1)),
+            pl.BlockSpec(left.shape, lambda i: (0, 0), pipeline_mode=pl.Buffered(1)),
             pl.BlockSpec(
-                (columns, part),
+                (weight.shape[0], part),
                 lambda i, block=first_column // part: (0, block),
                 pipeline_mode=pl.Buffered(1),
             ),
         ]
         operands += [left, weight]
-    out_specs = [pl.BlockSpec((rows, columns), lambda i: (0, 0))]
-    out_shape = [jax.ShapeDtypeStruct((rows, columns), jnp.float32)]
-    if terms is not None:
-        operands.append(terms)
-        in_specs.append(pl.BlockSpec(terms.shape, lambda i: (0, 0)))
-        out_specs.append(pl.BlockSpec(terms.shape, lambda i: (0, 0)))
-        out_shape.append(jax.ShapeDtypeStruct(terms.shape, terms.dtype))
-        buffers += [
-            pltpu.VMEM((size, *terms.shape), terms.dtype),
-            pltpu.VMEM((data_size, *terms.shape), terms.dtype),
-            pltpu.VMEM(terms.shape, terms.dtype),
-        ]
-        for count in (size, size, data_size, data_size):
-            buffers.append(pltpu.SemaphoreType.DMA((count - 1,)))
-    out = pl.pallas_call(
-        functools.partial(scatter_kernel, sizes, len(triples), terms is not None),
+    for other in others:
+        in_specs.append(pl.BlockSpec(other.shape, lambda i: (0, 0), pipeline_mode=pl.Buffered(1)))
+        operands.append(other)
+    out_specs = [pl.BlockSpec(out.shape, lambda i: (0, 0)) for out in outs]
+    if gathered:
+        out_specs[0] = pl.BlockSpec(memory_space=pl.ANY)
+    return pl.pallas_call(
+        body,
         grid=(1,),
-        out_shape=out_shape,
+        out_shape=outs,
         in_specs=in_specs,
         out_specs=out_specs,
-        scratch_shapes=buffers,
+        scratch_shapes=scratch,
         compiler_params=pltpu.CompilerParams(
             collective_id=collective_id, has_side_effects=True, vmem_limit_bytes=VMEM_LIMIT
         ),
         cost_estimate=pl.CostEstimate(
-            flops=2 * total_rows * depth * columns,
-            bytes_accessed=30 * total_rows * columns,
-            transcendentals=0,
+            flops=flops, bytes_accessed=150_000_000, transcendentals=0
         ),
-        name="product_scatter",
     )(*operands)
-    return out[0] if terms is None else out
 
 
 LOG2E = 1.4426950408889634
@@ -836,6 +915,10 @@
     return out if other is not None else out[0]
 
 
+def add_rounded(first, second):
+    return (first.astype(jnp.float32) + second.astype(jnp.float32)).astype(jnp.bfloat16)
+
+
 def reduce_over_chips(pairs, sizes):
     data_size = sizes[0]
     chips = data_size // 2
@@ -848,16 +931,20 @@
         [(device, device ^ 1) for device in range(data_size)],
     )
     blocks = grad_blocks(ahead + core, pairs, other)
-    arrivals = []
+    up = down = None
     for step in range(1, chips):
-        arrivals.append(
-            lax.ppermute(
-                blocks[step],
-                "dp",
-                [(device, (device + 2 * step) % data_size) for device in range(data_size)],
-            )
+        rising, falling = blocks[chips - step], blocks[step]
+        if up is not None:
+            rising, falling = add_rounded(rising, up), add_rounded(falling, down)
+        up = lax.ppermute(
+            rising, "dp", [(device, device + 2) for device in range(2 * step)]
         )
-    return blocks, arrivals
+        down = lax.ppermute(
+            falling,
+            "dp",
+            [(device, device - 2) for device in range(data_size - 2 * step, data_size)],
+        )
+    return blocks, (up, down)
 
 
 def pack_mixing_kernel(heads, query_ref, key_ref, value_ref, output_ref, out_ref):
@@ -975,13 +1062,25 @@
     raw, mixed_rows, totals = attention_forward(
         mixer_rows, mixing_full, tables, query_gain, key_gain, heads, grouping
     )
-    hidden_state = input_float + product_scatter(
-        [(mixed_rows, mixing_full, qkv_columns)], sizes, 1
-    )
-    second_scale = row_scale(hidden_state)
-    second_unit = hidden_state * second_scale
-    feed_local = (second_unit * feed_gain).astype(jnp.bfloat16)
-    (feed_rows,) = gather_rows((feed_local,), size, 2)
+    local_shape = block_input.shape
+    local_rows = local_shape[0]
+    gain_rows = model_width // head_size
+    gathered_shape = jax.ShapeDtypeStruct((size * local_rows, model_width), jnp.bfloat16)
+    local_float = jax.ShapeDtypeStruct(local_shape, jnp.float32)
+    local_half = jax.ShapeDtypeStruct(local_shape, jnp.bfloat16)
+    row_sum = pltpu.VMEM((1, model_width), jnp.float32)
+    own_rows = pltpu.VMEM(local_shape, jnp.bfloat16)
+    scatter_scratch = Scatter.scratch(size, *local_shape)
+    gather_scratch = Gather.scratch(size, *local_shape)
+    feed_rows, hidden_state = scatter_call(
+        functools.partial(between_forward_kernel, size, 1),
+        [[(mixed_rows, mixing_full, qkv_columns)]],
+        [block_input, feed_gain.reshape(1, -1)],
+        [gathered_shape, local_float],
+        True,
+        [own_rows, *scatter_scratch, *gather_scratch],
+        1,
+    )
 
     hidden_first, slope_first = feed_half(feed_rows, cotangent_rows, feed_full[0])
     blocks, arrivals = reduce_over_chips(
@@ -995,16 +1094,15 @@
     ).reshape(model_width, -1)
     second_grad, slope_second = lax.optimization_barrier((second_grad, slope_second))
     second_total = lax.psum_scatter(second_grad, "dp", scatter_dimension=0, tiled=True)
-    feed_back = product_scatter(
-        [(slope_first, feed_full[0], 0), (slope_second, later_full, 0)], sizes, 3
-    )
-    feed_gain_term = jnp.sum(feed_back * second_unit, axis=0)
-    feed_unit_slope = feed_back * feed_gain
-    state_slope = out_cotangent.astype(jnp.float32) + second_scale * (
-        feed_unit_slope
-        - second_unit * jnp.mean(feed_unit_slope * second_unit, axis=-1, keepdims=True)
-    )
-    (state_rows,) = gather_rows((state_slope.astype(jnp.bfloat16),), size, 4)
+    state_rows, state_slope, feed_term = scatter_call(
+        functools.partial(between_backward_kernel, size, 2),
+        [[(slope_first, feed_full[0], 0), (slope_second, later_full, 0)]],
+        [hidden_state, out_cotangent, feed_gain.reshape(1, -1)],
+        [gathered_shape, local_float, jax.ShapeDtypeStruct((gain_rows, head_size), jnp.float32)],
+        True,
+        [own_rows, row_sum, *scatter_scratch, *gather_scratch],
+        2,
+    )
     qkv_slope, head_terms = attention_backward(
         state_rows, mixing_full, qkv_columns, raw, mixed_rows, totals, tables,
         query_gain, key_gain, heads, grouping,
@@ -1014,33 +1112,33 @@
     ).reshape(model_width, -1)
     mixing_grad, qkv_slope = lax.optimization_barrier((mixing_grad, qkv_slope))
     mixing_total = lax.psum_scatter(mixing_grad, "dp", scatter_dimension=0, tiled=True)
-    mixer_back = product_scatter([(qkv_slope, mixing_full, 0)], sizes, 5)
-    attention_gain_term = jnp.sum(mixer_back * first_unit, axis=0)
-    mixer_unit_slope = mixer_back * attention_gain
-    input_gradient = (
-        state_slope
-        + first_scale
-        * (
-            mixer_unit_slope
-            - first_unit * jnp.mean(mixer_unit_slope * first_unit, axis=-1, keepdims=True)
-        )
-    ).astype(jnp.bfloat16)
-    gain_rows = model_width // head_size
-    terms = jnp.concatenate(
+    terms_shape = (2 * gain_rows + head_terms.shape[0], head_size)
+    block_output, input_gradient, terms = scatter_call(
+        functools.partial(last_kernel, sizes, (1, 2)),
         [
-            attention_gain_term.reshape(gain_rows, head_size),
-            feed_gain_term.reshape(gain_rows, head_size),
-            head_terms,
-        ],
-        axis=0,
-    )
-    feed_sum, terms = product_scatter(
-        [(hidden_first, feed_full[0], 2 * half), (hidden_second, later_full, 2 * half)],
-        sizes,
-        6,
-        terms,
-    )
-    block_output = (hidden_state + feed_sum).astype(jnp.bfloat16)
+            [(qkv_slope, mixing_full, 0)],
+            [(hidden_first, feed_full[0], 2 * half), (hidden_second, later_full, 2 * half)],
+        ],
+        [
+            block_input,
+            attention_gain.reshape(1, -1),
+            state_slope,
+            hidden_state,
+            jnp.concatenate([feed_term, head_terms], axis=0),
+        ],
+        [local_half, local_half, jax.ShapeDtypeStruct(terms_shape, jnp.float32)],
+        False,
+        [
+            row_sum,
+            pltpu.VMEM(terms_shape, jnp.float32),
+            pltpu.VMEM((size, *terms_shape), jnp.float32),
+            pltpu.VMEM((sizes[0], *terms_shape), jnp.float32),
+            *[pltpu.SemaphoreType.DMA((count - 1,)) for count in (size, size, *sizes[:1] * 2)],
+            *scatter_scratch,
+            *scatter_scratch,
+        ],
+        3,
+    )
     query_gradient, key_gradient, value_gradient, output_gradient = whole_call(
         functools.partial(finish_mixing_kernel, heads),
         [

time: 707 us -> 670 us (0.948)
  Pallas kernels: 538 us -> 476 us
  waiting for transfers between devices: 124 us -> 152 us
  other arithmetic: 20.7 us -> 5.26 us
  starting transfers between devices: 4.07 us -> 14.9 us
    ppermute x3 -> x6, waiting for transfers between devices: 0.01 us -> 96.4 us  [the longest x3 96.4 us: reduce_over_chips(): lax.ppermute(rising, 'dp', [(device, device + 2) for device in range(2 *...]
    reduce_scatter x1, waiting for transfers between devices: 94.3 us -> 20 us  [per_device(): lax.psum_scatter(second_grad, 'dp', scatter_dimension=0, tiled=True)]
    pallas_call x7 -> x4, Pallas kernels: 394 us -> 333 us  [the longest x3 257 us: scatter_call(): pl.pallas_call(body, grid=(1,), out_shape=outs, in_specs=in_specs, out_sp...]
    ppermute x3 -> x6, starting transfers between devices: 3.87 us -> 14.7 us  [the longest x3 11.9 us: reduce_over_chips(): lax.ppermute(rising, 'dp', [(device, device + 2) for device in range(2 *...]
    convert_element_type x3, other arithmetic: 10.3 us -> 2.04 us  [add_rounded(): (first.astype(jnp.float32) + second.astype(jnp.float32)).astype(jnp.bfloa...]
  transfers between devices with their start and end apart: 9 -> 12, of which waited for: 3 -> 5; matrix products, arithmetic and copies ran while one was open for 2% -> 1% of each run, Pallas kernels for 53% -> 46%
where the time goes in v4:
time: 670 us; the launch traced here: 669 us
  Pallas kernels  476 us (71%)
  waiting for transfers between devices  152 us (23%)
  starting transfers between devices  14.9 us (2%)
  between operations  14 us (2%)
  local copies, waits for them, and re-layouts  6.87 us (1%)
    pallas_call x3, Pallas kernels, scatter_call(): pl.pallas_call(body, grid=(1,), out_shape=outs, in_specs=in_specs, out_sp...  257 us
    ppermute x3, waiting for transfers between devices, reduce_over_chips(): lax.ppermute(rising, 'dp', [(device, device + 2) for device in range(2 *...  96.4 us
    pallas_call x1, Pallas kernels, gather_rows(): pl.pallas_call(functools.partial(gather_kernel, size, count), out_shape=[...  75.1 us
    pallas_call x4, Pallas kernels, grad_blocks(): pl.pallas_call(functools.partial(grad_kernel, len(pairs), other is not No...  52.3 us
    pallas_call x2, Pallas kernels, feed_half(): pl.pallas_call(functools.partial(feed_half_kernel, half, tile), grid=(tot...  36.7 us
    all_gather x2, waiting for transfers between devices, per_device(): lax.all_gather(part, 'dp', axis=0, tiled=True)  25.7 us
    pallas_call x1, Pallas kernels, attention_backward(): pl.pallas_call(functools.partial(attention_backward_kernel, grouping, hea...  23.2 us
    reduce_scatter x1, waiting for transfers between devices, per_device(): lax.psum_scatter(second_grad, 'dp', scatter_dimension=0, tiled=True)  20 us
  transfers between devices with their start and end apart: 12, of which 5 were waited for; matrix products, arithmetic and copies ran while one was open for 1% of the time, Pallas kernels for 46%

profile of v4, /device:TPU:0, one launch (start us, length us, event | category | flops | bytes accessed | tf_op | source)
XLA Modules:
  0.0 668.8 jit_solution(1281751924076198214)
XLA Ops:
  7.2 2.2 shard_map.246
  9.4 0.0 all-gather.6.cloned.1.call-start
  9.5 3.3 shard_map.248
  12.8 0.0 all-gather.8.cloned.1.call-start
  12.9 0.7 all-gather.8.cloned.1.call-update
  13.6 0.3 fusion.2
  13.9 1.3 fusion.4.refs_0_
  15.2 75.1 %gather_rows.1 = (bf16[1024,2048]{1,0:T(8,128)(2,1)}, bf16[1024,2048]{1,0:T(8,128)(2,1)}) custom-call(bf16[256,2048]{1,0:T(8,128)(2,1)} %fusion.4.refs_0_, bf16[256,2048]{1,0:T(8,128)(2,1)} %refs_5_.1), custom_call_target="tpu_custom_call" | custom-call | bytes 125829120 | tf_op jit(solution)/shard_map/gather_rows/pallas_call | solution.py:169
  90.4 0.5 broadcast_add_fusion.order_ref
  90.9 18.5 %attention_forward.1 = (f32[1024,1024]{1,0:T(8,128)}, bf16[1024,512]{1,0:T(8,128)(2,1)}, f32[2,2,1024]{2,1,0:T(2,128)}) custom-call(bf16[1024,2048]{1,0:T(8,128)(2,1)} %get-tuple-element.51.rows_ref.refs_0_, bf16[2048,1536]{1,0:T(8,128)(2,1)} %all-gather.4.cloned.1.call-done.weight_ref.refs_1_, f32[136,128]{1,0:T(8,128)} %constant.38.clone.few_cosines_ref, ...), custom_call_target="tpu_custom_call" | custom-call | flops 5368709120 | bytes 8388608 | tf_op jit(solution)/shard_map/attention_forward/pallas_call | solution.py:611
  109.4 76.4 %shard_map.247 = (bf16[1024,2048]{1,0:T(8,128)(2,1)}, f32[256,2048]{1,0:T(8,128)}) custom-call(bf16[1024,512]{1,0:T(8,128)(2,1)} %get-tuple-element.52.refs_0_.mixed_ref.refs_3_, bf16[2048,1536]{1,0:T(8,128)(2,1)} %all-gather.4.cloned.1.call-done.weight_ref.refs_1_, bf16[256,2048]{1,0:T(8,128)(2,1)} %refs_6_.1, f32[1,2048]{1,0:T(1,128)} %bitcast.16), custom_call_target="tpu_custom_call" | custom-call | flops 2147483648 | bytes 150000000 | tf_op jit(solution)/shard_map/pallas_call | solution.py:479
  185.8 18.4 %feed_half.2 = (bf16[1024,768]{1,0:T(8,128)(2,1)}, bf16[1024,1536]{1,0:T(8,128)(2,1)}) custom-call(bf16[1024,2048]{1,0:T(8,128)(2,1)} %get-tuple-element.53.rows_ref.refs_0_, bf16[1024,2048]{1,0:T(8,128)(2,1)} %get-tuple-element.54.cotangent_ref.refs_2_, bf16[2048,2304]{1,0:T(8,128)(2,1)} %all-gather.6.cloned.1.call-done.weight_ref.refs_1_.refs_3_), custom_call_target="tpu_custom_call" | custom-call | flops 9663676416 | bytes 17825792 | tf_op jit(solution)/shard_map/feed_half/pallas_call | solution.py:807
  204.2 10.5 %grad_blocks.4 = bf16[4,256,2304]{2,1,0:T(8,128)(2,1)} custom-call(s32[4]{0:T(128)} %broadcast_add_fusion.order_ref, bf16[1024,2048]{1,0:T(8,128)(2,1)} %get-tuple-element.53.rows_ref.refs_0_, bf16[1024,1536]{1,0:T(8,128)(2,1)} %get-tuple-element.56.refs_1_.refs_0_, bf16[1024,2048]{1,0:T(8,128)(2,1)} %get-tuple-element.54.cotangent_ref.refs_2_, ...), custom_call_target="tpu_custom_call" | custom-call | flops 4831838208 | bytes 13631488 | tf_op jit(solution)/shard_map/grad_blocks/pallas_call | solution.py:897
  214.7 0.5 broadcast_add_fusion.1.order_ref
  215.2 8.2 %collective-permute-done.refs_4_ = bf16[4,256,2304]{2,1,0:T(8,128)(2,1)} collective-permute-done((bf16[4,256,2304]{2,1,0:T(8,128)(2,1)}, bf16[4,256,2304]{2,1,0:T(8,128)(2,1)}, u32[]{:S(2)}, u32[]{:S(2)}) %collective-permute-start) | collective-permute-done | bytes 4718624 | tf_op jit(solution)/shard_map/ppermute | solution.py:928
  223.5 11.5 %grad_blocks.5 = (bf16[256,2304]{1,0:T(8,128)(2,1)}, bf16[256,2304]{1,0:T(8,128)(2,1)}, bf16[256,2304]{1,0:T(8,128)(2,1)}, bf16[256,2304]{1,0:T(8,128)(2,1)}) custom-call(s32[4]{0:T(128)} %broadcast_add_fusion.1.order_ref, bf16[1024,2048]{1,0:T(8,128)(2,1)} %get-tuple-element.53.rows_ref.refs_0_, bf16[1024,1536]{1,0:T(8,128)(2,1)} %get-tuple-element.56.refs_1_.refs_0_, ...), custom_call_target="tpu_custom_call" | custom-call | flops 4831838208 | bytes 13631488 | tf_op jit(solution)/shard_map/grad_blocks/pallas_call | solution.py:897
  235.0 25.6 %all-gather.8.cloned.1.call-done.weight_ref.refs_3_.refs_5_ = bf16[2048,2304]{1,0:T(8,128)(2,1)} async-done(((bf16[256,2304]{1,0:T(8,128)(2,1)}), bf16[2048,2304]{1,0:T(8,128)(2,1)}) %all-gather.8.cloned.1.call-update) | async-done | bytes 9437200 | tf_op jit(solution)/shard_map/all_gather | solution.py:1054
  260.6 18.3 %feed_half.3 = (bf16[1024,768]{1,0:T(8,128)(2,1)}, bf16[1024,1536]{1,0:T(8,128)(2,1)}) custom-call(bf16[1024,2048]{1,0:T(8,128)(2,1)} %get-tuple-element.53.rows_ref.refs_0_, bf16[1024,2048]{1,0:T(8,128)(2,1)} %get-tuple-element.54.cotangent_ref.refs_2_, bf16[2048,2304]{1,0:T(8,128)(2,1)} %all-gather.8.cloned.1.call-done.weight_ref.refs_3_.refs_5_), custom_call_target="tpu_custom_call" | custom-call | flops 9663676416 | bytes 17825792 | tf_op jit(solution)/shard_map/feed_half/pallas_call | solution.py:807
  278.9 0.5 iota.9.order_ref
  279.5 16.7 %grad_blocks.6 = bf16[8,256,2304]{2,1,0:T(8,128)(2,1)} custom-call(s32[8]{0:T(128)} %iota.9.order_ref, bf16[1024,2048]{1,0:T(8,128)(2,1)} %get-tuple-element.53.rows_ref.refs_0_, bf16[1024,1536]{1,0:T(8,128)(2,1)} %get-tuple-element.66.refs_1_.refs_2_, bf16[1024,2048]{1,0:T(8,128)(2,1)} %get-tuple-element.54.cotangent_ref.refs_2_, ...), custom_call_target="tpu_custom_call" | custom-call | flops 9663676416 | bytes 22544384 | tf_op jit(solution)/shard_map/grad_blocks/pallas_call | solution.py:897
  296.1 88.0 %shard_map.249 = (bf16[1024,2048]{1,0:T(8,128)(2,1)}, f32[256,2048]{1,0:T(8,128)}, f32[16,128]{1,0:T(8,128)}) custom-call(bf16[1024,1536]{1,0:T(8,128)(2,1)} %get-tuple-element.56.refs_1_.refs_0_, bf16[2048,2304]{1,0:T(8,128)(2,1)} %all-gather.6.cloned.1.call-done.weight_ref.refs_1_.refs_3_, bf16[1024,1536]{1,0:T(8,128)(2,1)} %get-tuple-element.66.refs_1_.refs_2_, ...), custom_call_target="tpu_custom_call" | custom-call | flops 12884901888 | bytes 150000000 | tf_op jit(solution)/shard_map/pallas_call | solution.py:479
  384.1 23.2 %attention_backward.1 = (bf16[1024,1024]{1,0:T(8,128)(2,1)}, f32[8,128]{1,0:T(8,128)}) custom-call(bf16[1024,2048]{1,0:T(8,128)(2,1)} %get-tuple-element.68.state_ref.refs_2_, bf16[2048,1536]{1,0:T(8,128)(2,1)} %all-gather.4.cloned.1.call-done.weight_ref.refs_1_, f32[1024,1024]{1,0:T(8,128)} %get-tuple-element.69.raw_ref, ...), custom_call_target="tpu_custom_call" | custom-call | flops 4831838208 | bytes 6291456 | tf_op jit(solution)/shard_map/attention_backward/pallas_call | solution.py:735
  407.3 0.5 iota.8.order_ref
  407.8 13.6 %grad_blocks.7 = bf16[8,256,1536]{2,1,0:T(8,128)(2,1)} custom-call(s32[8]{0:T(128)} %iota.8.order_ref, bf16[1024,2048]{1,0:T(8,128)(2,1)} %get-tuple-element.51.rows_ref.refs_0_, bf16[1024,1024]{1,0:T(8,128)(2,1)} %get-tuple-element.72.refs_1_.refs_0_, bf16[1024,2048]{1,0:T(8,128)(2,1)} %get-tuple-element.68.state_ref.refs_2_, ...), custom_call_target="tpu_custom_call" | custom-call | flops 6442450944 | bytes 17825792 | tf_op jit(solution)/shard_map/grad_blocks/pallas_call | solution.py:897
  421.5 0.0 reduce-scatter.5.cloned.1.call-start
  421.5 0.5 reduce-scatter.5.cloned.1.call-update
  422.0 0.6 copy-done.2
  422.7 1.5 collective-permute-start.1
  424.2 0.7 collective-permute-start.4
  424.9 48.9 %collective-permute-done.1 = bf16[256,2304]{1,0:T(8,128)(2,1)S(1)} collective-permute-done((bf16[256,2304]{1,0:T(8,128)(2,1)S(1)}, bf16[256,2304]{1,0:T(8,128)(2,1)S(1)}, u32[]{:S(2)}, u32[]{:S(2)}) %collective-permute-start.1) | collective-permute-done | bytes 1179680 | tf_op jit(solution)/shard_map/ppermute | solution.py:939
  473.9 0.5 fusion.1
  474.3 0.7 collective-permute-start.5
  475.1 5.0 collective-permute-start.2
  480.1 0.6 pad_maximum_fusion.refs_10_
  480.7 0.3 add_convert_fusion
  481.0 1.3 collective-permute-start.6
  482.3 47.5 %collective-permute-done.2 = bf16[256,2304]{1,0:T(8,128)(2,1)S(1)} collective-permute-done((bf16[256,2304]{1,0:T(8,128)(2,1)S(1)}, bf16[256,2304]{1,0:T(8,128)(2,1)S(1)}, u32[]{:S(2)}, u32[]{:S(2)}) %collective-permute-start.2) | collective-permute-done | bytes 1179680 | tf_op jit(solution)/shard_map/ppermute | solution.py:939
  529.8 1.3 add_convert_fusion.1
  531.1 5.4 collective-permute-start.3
  536.5 93.0 %shard_map.250 = (bf16[256,2048]{1,0:T(8,128)(2,1)}, bf16[256,2048]{1,0:T(8,128)(2,1)}, f32[40,128]{1,0:T(8,128)}) custom-call(bf16[1024,1024]{1,0:T(8,128)(2,1)} %get-tuple-element.72.refs_1_.refs_0_, bf16[2048,1536]{1,0:T(8,128)(2,1)} %all-gather.4.cloned.1.call-done.weight_ref.refs_1_, bf16[1024,768]{1,0:T(8,128)(2,1)} %get-tuple-element.57.refs_3_.refs_2_, ...), custom_call_target="tpu_custom_call" | custom-call | flops 10737418240 | bytes 150000000 | tf_op jit(solution)/shard_map/pallas_call | solution.py:479
  629.5 1.3 slice_bitcast_fusion.2
  630.8 1.3 slice_bitcast_fusion
  632.1 2.4 shard_map.251
  634.5 20.0 %reduce-scatter.5.cloned.1.call-done.refs_3_ = bf16[256,2304]{1,0:T(8,128)(2,1)} async-done(((bf16[2048,2304]{1,0:T(8,128)(2,1)}), bf16[256,2304]{1,0:T(8,128)(2,1)}) %reduce-scatter.5.cloned.1.call-update) | async-done | bytes 1179664 | tf_op jit(solution)/shard_map/reduce_scatter | solution.py:1096
  654.5 5.1 shard_map.252
  659.7 1.0 copy.30
  660.6 0.6 copy-done.4
  661.3 1.0 copy.31
  (30 shorter events, 0.2 us)
Async XLA Ops:
  7.2 83.7 %all-gather.4.cloned.1.call-start = ((), (), s32[]{:S(2)}) async-start(), calls=%async_computation.2 | async-start | bytes 7077888 | tf_op jit(solution)/shard_map/all_gather | solution.py:1048
  9.4 4.2 copy-start
  9.4 176.4 %all-gather.6.cloned.1.call-start = ((), (), s32[]{:S(2)}) async-start(), calls=%async_computation.3 | async-start | bytes 10616832 | tf_op jit(solution)/shard_map/all_gather | solution.py:1054
  12.8 1.1 copy-start.6
  12.8 247.8 %all-gather.8.cloned.1.call-start = ((), (), s32[]{:S(2)}) async-start(), calls=%async_computation.4 | async-start | bytes 10616832 | tf_op jit(solution)/shard_map/all_gather | solution.py:1054
  13.6 618.5 %reduce-scatter.3.cloned.1.call-start = ((), (), s32[]{:S(2)}) async-start(), calls=%async_computation.5 | async-start | bytes 7077888 | tf_op jit(solution)/shard_map/reduce_scatter | solution.py:1114
  214.7 8.8 %collective-permute-start = (bf16[4,256,2304]{2,1,0:T(8,128)(2,1)}, bf16[4,256,2304]{2,1,0:T(8,128)(2,1)}, u32[]{:S(2)}, u32[]{:S(2)}) collective-permute-start(bf16[4,256,2304]{2,1,0:T(8,128)(2,1)} %grad_blocks.4), channel_id=1, source_target_pairs={{0,4},{4,0},{8,12},{12,8},{16,20},{20,16},{24,28},{28,24},{1,5},{5... | collective-permute-start | bytes 14155784 | tf_op jit(solution)/shard_map/ppermute | solution.py:928
  421.4 1.3 copy-start.2
  421.4 2.8 copy-start.1
  421.4 52.4 %copy-start.3 = (bf16[256,2304]{1,0:T(8,128)(2,1)S(1)}, bf16[256,2304]{1,0:T(8,128)(2,1)}, u32[]{:S(2)}) copy-start(bf16[256,2304]{1,0:T(8,128)(2,1)} %get-tuple-element.60) | copy-start | bytes 3538948
  421.5 233.1 %reduce-scatter.5.cloned.1.call-start = ((), (), s32[]{:S(2)}) async-start(), calls=%async_computation.6 | async-start | bytes 10616832 | tf_op jit(solution)/shard_map/reduce_scatter | solution.py:1096
  422.7 57.4 %copy-start.7 = (f32[16,128]{1,0:T(8,128)S(1)}, f32[16,128]{1,0:T(8,128)}, u32[]{:S(2)}) copy-start(f32[16,128]{1,0:T(8,128)} %get-tuple-element.74) | copy-start | bytes 24580
  422.7 57.4 %copy-start.8 = (f32[8,128]{1,0:T(8,128)S(1)}, f32[8,128]{1,0:T(8,128)}, u32[]{:S(2)}) copy-start(f32[8,128]{1,0:T(8,128)} %get-tuple-element.75) | copy-start | bytes 12292
  422.7 51.1 %collective-permute-start.1 = (bf16[256,2304]{1,0:T(8,128)(2,1)S(1)}, bf16[256,2304]{1,0:T(8,128)(2,1)S(1)}, u32[]{:S(2)}, u32[]{:S(2)}) collective-permute-start(bf16[256,2304]{1,0:T(8,128)(2,1)S(1)} %copy-done.2), channel_id=1, source_target_pairs={{0,8},{4,12},{1,9},{5,13},{2,10},{6,14},{3,11},{7,15}} | collective-permute-start | bytes 3538952 | tf_op jit(solution)/shard_map/ppermute | solution.py:939
  424.2 49.6 %collective-permute-start.4 = (bf16[256,2304]{1,0:T(8,128)(2,1)S(1)}, bf16[256,2304]{1,0:T(8,128)(2,1)S(1)}, u32[]{:S(2)}, u32[]{:S(2)}) collective-permute-start(bf16[256,2304]{1,0:T(8,128)(2,1)S(1)} %copy-done.1), channel_id=1, source_target_pairs={{24,16},{28,20},{25,17},{29,21},{26,18},{30,22},{27,19},{31,23}} | collective-permute-start | bytes 3538952 | tf_op jit(solution)/shard_map/ppermute | solution.py:942
  474.3 6.4 collective-permute-start.5
  475.1 54.7 %collective-permute-start.2 = (bf16[256,2304]{1,0:T(8,128)(2,1)S(1)}, bf16[256,2304]{1,0:T(8,128)(2,1)S(1)}, u32[]{:S(2)}, u32[]{:S(2)}) collective-permute-start(bf16[256,2304]{1,0:T(8,128)(2,1)S(1)} %get-tuple-element.90), channel_id=1, source_target_pairs={{0,8},{4,12},{8,16},{12,20},{1,9},{5,13},{9,17},{13,21},{2,10},{6,... | collective-permute-start | bytes 3538952 | tf_op jit(solution)/shard_map/ppermute | solution.py:939
  481.0 153.5 %collective-permute-start.6 = (bf16[256,2304]{1,0:T(8,128)(2,1)S(1)}, bf16[256,2304]{1,0:T(8,128)(2,1)}, u32[]{:S(2)}, u32[]{:S(2)}) collective-permute-start(bf16[256,2304]{1,0:T(8,128)(2,1)S(1)} %add_convert_fusion), channel_id=1, source_target_pairs={{8,0},{12,4},{16,8},{20,12},{24,16},{28,20},{9,1},{13,5},{17,9},{2... | collective-permute-start | bytes 3538952 | tf_op jit(solution)/shard_map/ppermute | solution.py:942
  531.1 103.4 %collective-permute-start.3 = (bf16[256,2304]{1,0:T(8,128)(2,1)}, bf16[256,2304]{1,0:T(8,128)(2,1)}, u32[]{:S(2)}, u32[]{:S(2)}) collective-permute-start(bf16[256,2304]{1,0:T(8,128)(2,1)} %add_convert_fusion.1), channel_id=1, source_target_pairs={{0,8},{4,12},{8,16},{12,20},{16,24},{20,28},{1,9},{5,13},{9,17},{1... | collective-permute-start | bytes 3538952 | tf_op jit(solution)/shard_map/ppermute | solution.py:939
  634.5 25.2 %copy-start.5 = (bf16[256,2048]{1,0:T(8,128)(2,1)S(1)}, bf16[256,2048]{1,0:T(8,128)(2,1)}, u32[]{:S(2)}) copy-start(bf16[256,2048]{1,0:T(8,128)(2,1)} %get-tuple-element.108) | copy-start | bytes 3145732
  659.7 1.6 copy-start.4
Sparse Core Ops, SparseCore 0:
  10.2 67.4 all-gather.3
  79.9 89.3 all-gather.5
  171.5 89.1 all-gather.7
  421.5 119.2 reduce-scatter.2
  543.0 111.4 reduce-scatter.4

commit v5 on v4

--- a/solution.py
+++ b/solution.py
@@ -207,6 +207,7 @@
         self.arriving, self.send_sem, self.recv_sem = rest
         self.rows = outgoing.shape[1]
         self.me = lax.axis_index("tensor")
+        self.copies, self.starts = self.plan()
 
     @staticmethod
     def scratch(size, rows, columns):
@@ -228,30 +229,33 @@
     def prepare(self, index, source, target, peer):
         return remote(source, target, self.send_sem.at[index], self.recv_sem.at[index], peer)
 
+    def plan(self):
+        outgoing, arriving = self.outgoing, self.arriving
+        if self.size != 4:
+            copies = [
+                self.prepare(step, outgoing.at[step], arriving.at[step], peer)
+                for step, peer in enumerate(other_members("tensor", self.size))
+            ]
+            return copies, tuple((step, step) for step in range(self.size - 1))
+        beside, below, _ = square_peers(self.me)
+        half = self.rows // 2
+        first, second = pl.ds(0, half), pl.ds(half, half)
+        copies = [
+            self.prepare(0, outgoing.at[0, first], self.passing.at[0], beside),
+            self.prepare(1, outgoing.at[0, second], self.passing.at[1], below),
+            self.prepare(2, outgoing.at[1, first], arriving.at[0, first], beside),
+            self.prepare(3, outgoing.at[2, second], arriving.at[1, second], below),
+            self.prepare(4, outgoing.at[1, second], arriving.at[0, second], beside),
+            self.prepare(5, outgoing.at[2, first], arriving.at[1, first], below),
+        ]
+        return copies, ((0, 0), (0, 1), (1, 2), (2, 3))
+
     def fill(self, pairs):
-        size, me, outgoing, arriving, rows = self.size, self.me, self.outgoing, self.arriving, self.rows
-        if size == 4:
-            beside, below, across = square_peers(me)
-            half = rows // 2
-            first, second = pl.ds(0, half), pl.ds(half, half)
-            self.copies = [
-                self.prepare(0, outgoing.at[0, first], self.passing.at[0], beside),
-                self.prepare(1, outgoing.at[0, second], self.passing.at[1], below),
-                self.prepare(2, outgoing.at[1, first], arriving.at[0, first], beside),
-                self.prepare(3, outgoing.at[2, second], arriving.at[1, second], below),
-                self.prepare(4, outgoing.at[1, second], arriving.at[0, second], beside),
-                self.prepare(5, outgoing.at[2, first], arriving.at[1, first], below),
-            ]
-            starts = ((0, 0), (0, 1), (1, 2), (2, 3))
-        else:
-            self.copies = [
-                self.prepare(step, outgoing.at[step], arriving.at[step], peer)
-                for step, peer in enumerate(other_members("tensor", size))
-            ]
-            starts = tuple((step, step) for step in range(size - 1))
+        size, me, rows = self.size, self.me, self.rows
 
         def step(slot, carry):
             if size == 4:
+                beside, below, across = square_peers(me)
                 owner = jnp.where(
                     slot == 0, across, jnp.where(slot == 1, beside, jnp.where(slot == 2, below, me))
                 )
@@ -259,10 +263,10 @@
                 owner = lax.rem(me + slot + 1, size)
 
             def write(columns, values):
-                outgoing[slot, :, columns] = values.astype(outgoing.dtype)
+                self.outgoing[slot, :, columns] = values.astype(self.outgoing.dtype)
 
             block_product(pairs, owner * rows, rows, write)
-            for at, index in starts:
+            for at, index in self.starts:
                 pl.when(slot == at)(self.copies[index].start)
             return carry
 
@@ -300,6 +304,106 @@
             copy.wait_send()
 
 
+class Chain:
+    def __init__(
+        self, chips, steps, rising_refs, falling_refs, up_ref, down_ref,
+        rise, fall, up, down, load_sem, send_sem, recv_sem,
+    ):
+        self.chips, self.steps = chips, steps
+        self.rise, self.fall, self.up, self.down = rise, fall, up, down
+        device = lax.axis_index("dp")
+        self.chip = device // 2
+        count = len(steps)
+        self.loads = [
+            pltpu.make_async_copy(source, target, load_sem.at[index])
+            for index, (source, target) in enumerate(
+                [(up_ref, up.at[0]), (down_ref, down.at[0])]
+                + [(ref, rise.at[index]) for index, ref in enumerate(rising_refs)]
+                + [(ref, fall.at[index]) for index, ref in enumerate(falling_refs)]
+            )
+        ]
+        above = lax.rem(device + 2, 2 * chips)
+        under = lax.rem(device + 2 * chips - 2, 2 * chips)
+        self.neighbours = [("dp", above), ("dp", under)]
+        self.rises = [
+            remote(rise.at[i], up.at[i + 1], send_sem.at[i], recv_sem.at[i], above, "dp")
+            for i in range(count)
+        ]
+        self.falls = [
+            remote(
+                fall.at[i], down.at[i + 1], send_sem.at[count + i], recv_sem.at[count + i], under, "dp"
+            )
+            for i in range(count)
+        ]
+
+    @staticmethod
+    def scratch(count, rows, columns):
+        return [
+            pltpu.VMEM((count, rows, columns), jnp.bfloat16),
+            pltpu.VMEM((count, rows, columns), jnp.bfloat16),
+            pltpu.VMEM((count + 1, rows, columns), jnp.bfloat16),
+            pltpu.VMEM((count + 1, rows, columns), jnp.bfloat16),
+            pltpu.SemaphoreType.DMA((2 * count + 2,)),
+            pltpu.SemaphoreType.DMA((2 * count,)),
+            pltpu.SemaphoreType.DMA((2 * count,)),
+        ]
+
+    def load(self):
+        for copy in self.loads:
+            copy.start()
+
+    def step(self, index):
+        if index == 0:
+            for copy in self.loads:
+                copy.wait()
+        step = self.steps[index]
+        rows = self.rise.shape[1]
+        sends_up = self.chip < step
+        sends_down = self.chip >= self.chips - step
+
+        @pl.when(sends_up & (self.chip > 0))
+        def _():
+            def add(piece):
+                self.rise[index, piece, :] = add_rounded(
+                    self.rise[index, piece, :], self.up[index, piece, :]
+                )
+
+            over_pieces(rows, add)
+
+        pl.when(sends_up)(self.rises[index].start)
+
+        @pl.when(sends_down & (self.chip < self.chips - 1))
+        def _():
+            def add(piece):
+                self.fall[index, piece, :] = add_rounded(
+                    self.fall[index, piece, :], self.down[index, piece, :]
+                )
+
+            over_pieces(rows, add)
+
+        pl.when(sends_down)(self.falls[index].start)
+
+    def arrives(self, index):
+        step = self.steps[index]
+        from_under = (self.chip > 0) & (self.chip <= step)
+        from_above = (self.chip < self.chips - 1) & (self.chip >= self.chips - step - 1)
+        return from_under, from_above
+
+    def wait(self, index):
+        from_under, from_above = self.arrives(index)
+        pl.when(from_under)(self.rises[index].wait_recv)
+        pl.when(from_above)(self.falls[index].wait_recv)
+
+    def drain(self):
+        for index, step in enumerate(self.steps):
+            pl.when(self.chip < step)(self.rises[index].wait_send)
+            pl.when(self.chip >= self.chips - step)(self.falls[index].wait_send)
+
+
+def add_rounded(first, second):
+    return (first.astype(jnp.float32) + second.astype(jnp.float32)).astype(jnp.bfloat16)
+
+
 def over_pieces(rows, body):
     count = min(32, rows)
 
@@ -362,13 +466,22 @@
     scatter.drain()
 
 
-def between_backward_kernel(size, pair_count, *refs):
+def between_backward_kernel(size, chips, steps, pair_count, *refs):
     pairs, refs = split_pairs(refs, pair_count)
-    state_ref, cotangent_ref, gain_ref, gathered_ref, slope_ref, term_ref, own_ref, sum_ref = refs[:8]
+    state_ref, cotangent_ref, gain_ref = refs[:3]
+    chain_count = 2 * len(steps) + 2
+    chain_refs, refs = refs[3 : 3 + chain_count], refs[3 + chain_count :]
+    gathered_ref, slope_ref, term_ref, up_out_ref, down_out_ref, own_ref, sum_ref = refs[:7]
     buffers = 5 if size == 4 else 4
-    scatter = Scatter(size, *refs[8 : 8 + buffers])
-    gather = Gather(size, own_ref, gathered_ref, *refs[8 + buffers :])
-    greet(neighbours(size))
+    scatter = Scatter(size, *refs[7 : 7 + buffers])
+    gather = Gather(size, own_ref, gathered_ref, *refs[7 + buffers : 11 + buffers])
+    chain = Chain(
+        chips, steps, chain_refs[: len(steps)], chain_refs[len(steps) : -2], *chain_refs[-2:],
+        *refs[11 + buffers :],
+    )
+    chain.load()
+    greet(neighbours(size) + chain.neighbours)
+    chain.step(0)
     scatter.fill(pairs)
     scatter.relay()
     sum_ref[...] = jnp.zeros_like(sum_ref)
@@ -390,29 +503,44 @@
     over_pieces(own_ref.shape[0], norm)
     gather.start()
     store_row(term_ref, sum_ref)
+    chain.wait(0)
+    for index in range(1, len(steps)):
+        chain.step(index)
+        chain.wait(index)
+    last = len(steps)
+    from_under, from_above = chain.arrives(last - 1)
+    for arrived, landing, out_ref in (
+        (from_under, chain.up, up_out_ref),
+        (from_above, chain.down, down_out_ref),
+    ):
+
+        @pl.when(arrived)
+        def _(landing=landing, out_ref=out_ref):
+            out_ref[...] = landing[last]
+
+        @pl.when(jnp.logical_not(arrived))
+        def _(out_ref=out_ref):
+            out_ref[...] = jnp.zeros_like(out_ref)
+
     gather.finish()
     scatter.drain()
-
-
-def last_kernel(sizes, pair_counts, *refs):
+    chain.drain()
+
+
+def last_kernel(sizes, pair_count, *refs):
     data_size, size = sizes
-    mixing_pairs, refs = split_pairs(refs, pair_counts[0])
-    feed_pairs, refs = split_pairs(refs, pair_counts[1])
-    input_ref, gain_ref, slope_ref, state_ref, terms_ref = refs[:5]
-    output_ref, gradient_ref, terms_out_ref, sum_ref, partial_ref, inner, outer = refs[5:12]
-    inner_send, inner_recv, outer_send, outer_recv = refs[12:16]
-    buffers = 5 if size == 4 else 4
-    mixing = Scatter(size, *refs[16 : 16 + buffers])
-    feed = Scatter(size, *refs[16 + buffers :])
+    pairs, refs = split_pairs(refs, pair_count)
+    input_ref, gain_ref, slope_ref, terms_ref = refs[:4]
+    gradient_ref, terms_out_ref, sum_ref, partial_ref, inner, outer = refs[4:10]
+    inner_send, inner_recv, outer_send, outer_recv = refs[10:14]
+    mixing = Scatter(size, *refs[14:])
     greet(
         [("tensor", peer) for peer in other_members("tensor", size)]
         + [("dp", peer) for peer in other_members("dp", data_size)]
     )
-    mixing.fill(mixing_pairs)
-    feed.fill(feed_pairs)
+    mixing.fill(pairs)
     mixing.relay()
     sum_ref[...] = jnp.zeros_like(sum_ref)
-    feed.relay()
     mixing.collect()
 
     def norm(piece):
@@ -427,7 +555,7 @@
             + scale * (unit_slope - unit * jnp.mean(unit_slope * unit, axis=-1, keepdims=True))
         ).astype(gradient_ref.dtype)
 
-    over_pieces(output_ref.shape[0], norm)
+    over_pieces(gradient_ref.shape[0], norm)
     kept = partial_ref.shape[0] - terms_ref.shape[0]
     partial_ref[kept:, :] = terms_ref[...]
     store_row(partial_ref, sum_ref)
@@ -438,12 +566,6 @@
     outer_copies = send_terms(
         "dp", other_members("dp", data_size), terms_out_ref, outer, outer_send, outer_recv
     )
-    feed.collect()
-
-    def finish(piece):
-        output_ref[piece, :] = (state_ref[piece, :] + feed.total(piece)).astype(output_ref.dtype)
-
-    over_pieces(output_ref.shape[0], finish)
     total = add_terms(outer, outer_copies)
     for copy in outer_copies:
         copy.wait_send()
@@ -451,10 +573,9 @@
     for copy in inner_copies:
         copy.wait_send()
     mixing.drain()
-    feed.drain()
-
-
-def scatter_call(body, triple_lists, others, outs, gathered, scratch, collective_id):
+
+
+def scatter_call(body, triple_lists, others, outs, gathered, scratch, collective_id, far=()):
     in_specs = []
     operands = []
     flops = 0
@@ -473,6 +594,9 @@
     for other in others:
         in_specs.append(pl.BlockSpec(other.shape, lambda i: (0, 0), pipeline_mode=pl.Buffered(1)))
         operands.append(other)
+    for other in far:
+        in_specs.append(pl.BlockSpec(memory_space=pl.ANY))
+        operands.append(other)
     out_specs = [pl.BlockSpec(out.shape, lambda i: (0, 0)) for out in outs]
     if gathered:
         out_specs[0] = pl.BlockSpec(memory_space=pl.ANY)
@@ -656,7 +780,79 @@
     return slope.astype(jnp.bfloat16), jnp.sum(term, axis=0, keepdims=True)
 
 
-def attention_backward_kernel(
+def attention_backward_kernel(size, chips, grouping, head_size, block, pair_count, *refs):
+    pairs, refs = split_pairs(refs, pair_count)
+    (
+        state_ref, weight_ref, raw_ref, mixed_ref, total_ref, few_cosines_ref, few_sines_ref,
+        query_gain_ref, key_gain_ref, hidden_state_ref,
+    ) = refs[:10]
+    chain_refs, own_block_ref = refs[10:14], refs[14]
+    slope_ref, gain_ref, output_ref, chain_total_ref = refs[15:19]
+    (
+        query_ref, key_ref, value_ref, out_slope_ref, turned_ref, key_sum_ref, value_sum_ref, cosine_ref, sine_ref,
+    ) = refs[19:28]
+    buffers = 5 if size == 4 else 4
+    scatter = Scatter(size, *refs[28 : 28 + buffers])
+    own_block, own_sem = refs[28 + buffers : 30 + buffers]
+    chain = Chain(
+        chips, (chips - 1,), chain_refs[:1], chain_refs[1:2], *chain_refs[2:], *refs[30 + buffers :]
+    )
+    own_load = pltpu.make_async_copy(own_block_ref, own_block, own_sem.at[0])
+    step = pl.program_id(0) * pl.num_programs(1) + pl.program_id(1)
+    steps = pl.num_programs(0) * pl.num_programs(1)
+
+    @pl.when(step == 0)
+    def _():
+        chain.load()
+        own_load.start()
+        greet(neighbours(size) + chain.neighbours)
+        chain.step(0)
+        scatter.fill(pairs)
+
+    attend_backward_head(
+        grouping, head_size, block, state_ref, weight_ref, raw_ref, mixed_ref, total_ref, few_cosines_ref,
+        few_sines_ref, query_gain_ref, key_gain_ref, slope_ref, gain_ref, query_ref, key_ref, value_ref,
+        out_slope_ref, turned_ref, key_sum_ref, value_sum_ref, cosine_ref, sine_ref,
+    )
+
+    @pl.when(step == 0)
+    def _():
+        scatter.relay()
+
+    @pl.when(step == steps - 1)
+    def _():
+        scatter.collect()
+
+        def finish(piece):
+            output_ref[piece, :] = (hidden_state_ref[piece, :] + scatter.total(piece)).astype(
+                output_ref.dtype
+            )
+
+        over_pieces(output_ref.shape[0], finish)
+        own_load.wait()
+        chain.wait(0)
+        from_under, from_above = chain.arrives(0)
+
+        @pl.when(from_under)
+        def _():
+            def add(piece):
+                own_block[piece, :] = add_rounded(own_block[piece, :], chain.up[1, piece, :])
+
+            over_pieces(own_block.shape[0], add)
+
+        @pl.when(from_above)
+        def _():
+            def add(piece):
+                own_block[piece, :] = add_rounded(own_block[piece, :], chain.down[1, piece, :])
+
+            over_pieces(own_block.shape[0], add)
+
+        chain_total_ref[...] = own_block[...]
+        scatter.drain()
+        chain.drain()
+
+
+def attend_backward_head(
     grouping, head_size, block, state_ref, weight_ref, raw_ref, mixed_ref, total_ref, few_cosines_ref, few_sines_ref,
     query_gain_ref, key_gain_ref, slope_ref, gain_ref, query_ref, key_ref, value_ref, out_slope_ref,
     turned_ref, key_sum_ref, value_sum_ref, cosine_ref, sine_ref,
@@ -719,7 +915,8 @@
 
 
 def attention_backward(
-    state_rows, weight, weight_start, raw, mixed, totals, tables, query_gain, key_gain, heads, grouping
+    state_rows, weight, weight_start, raw, mixed, totals, tables, query_gain, key_gain, heads, grouping,
+    triples, hidden_state, chain_arrays, own_block, sizes, collective_id,
 ):
     total_rows, depth = state_rows.shape
     head_size = query_gain.shape[0]
@@ -728,31 +925,59 @@
     out_width = grouping * head_size
     block = min(256, SEQUENCE_LENGTH)
     first_block = weight_start // out_width
+    data_size, size = sizes
+    chips = data_size // 2
+    single = pl.Buffered(1)
     table = pl.BlockSpec(tables[0].shape, lambda s, h: (0, 0))
     gain = pl.BlockSpec((1, head_size), lambda s, h: (0, 0))
     elements = heads * grouping * total_rows * SEQUENCE_LENGTH // 2
     whole_rows = pltpu.VMEM((SEQUENCE_LENGTH, head_size), jnp.float32)
+    in_specs = []
+    operands = []
+    for left, other_weight, first_column in triples:
+        part = left.shape[1]
+        in_specs += [
+            pl.BlockSpec(left.shape, lambda s, h: (0, 0), pipeline_mode=single),
+            pl.BlockSpec(
+                (other_weight.shape[0], part),
+                lambda s, h, at=first_column // part: (0, at),
+                pipeline_mode=single,
+            ),
+        ]
+        operands += [left, other_weight]
+    in_specs += [
+        pl.BlockSpec((SEQUENCE_LENGTH, depth), lambda s, h: (s, 0), pipeline_mode=single),
+        pl.BlockSpec((depth, out_width), lambda s, h: (0, first_block + h)),
+        pl.BlockSpec((SEQUENCE_LENGTH, width), lambda s, h: (s, h)),
+        pl.BlockSpec((SEQUENCE_LENGTH, out_width), lambda s, h: (s, h)),
+        pl.BlockSpec((1, grouping, SEQUENCE_LENGTH), lambda s, h: (h, 0, s)),
+        table,
+        table,
+        gain,
+        gain,
+        pl.BlockSpec(hidden_state.shape, lambda s, h: (0, 0), pipeline_mode=single),
+    ] + [pl.BlockSpec(memory_space=pl.ANY)] * 5
+    operands += [
+        state_rows, weight, raw, mixed, totals, *tables, query_gain.reshape(1, -1), key_gain.reshape(1, -1),
+        hidden_state, *chain_arrays, own_block,
+    ]
     return pl.pallas_call(
-        functools.partial(attention_backward_kernel, grouping, head_size, block),
+        functools.partial(
+            attention_backward_kernel, size, chips, grouping, head_size, block, len(triples)
+        ),
         grid=(sequences, heads),
         out_shape=[
             jax.ShapeDtypeStruct((total_rows, heads * width), jnp.bfloat16),
             jax.ShapeDtypeStruct((8, head_size), jnp.float32),
-        ],
-        in_specs=[
-            pl.BlockSpec((SEQUENCE_LENGTH, depth), lambda s, h: (s, 0)),
-            pl.BlockSpec((depth, out_width), lambda s, h: (0, first_block + h)),
-            pl.BlockSpec((SEQUENCE_LENGTH, width), lambda s, h: (s, h)),
-            pl.BlockSpec((SEQUENCE_LENGTH, out_width), lambda s, h: (s, h)),
-            pl.BlockSpec((1, grouping, SEQUENCE_LENGTH), lambda s, h: (h, 0, s)),
-            table,
-            table,
-            gain,
-            gain,
-        ],
+            jax.ShapeDtypeStruct(hidden_state.shape, jnp.bfloat16),
+            jax.ShapeDtypeStruct(own_block.shape, jnp.bfloat16),
+        ],
+        in_specs=in_specs,
         out_specs=[
             pl.BlockSpec((SEQUENCE_LENGTH, width), lambda s, h: (s, h)),
             pl.BlockSpec((8, head_size), lambda s, h: (0, 0)),
+            pl.BlockSpec(hidden_state.shape, lambda s, h: (0, 0)),
+            pl.BlockSpec(own_block.shape, lambda s, h: (0, 0)),
         ],
         scratch_shapes=[
             pltpu.VMEM((grouping, SEQUENCE_LENGTH, head_size), jnp.bfloat16),
@@ -764,18 +989,21 @@
             whole_rows,
             whole_rows,
             whole_rows,
-        ],
-        compiler_params=pltpu.CompilerParams(vmem_limit_bytes=VMEM_LIMIT),
+            *Scatter.scratch(size, *hidden_state.shape),
+            pltpu.VMEM(own_block.shape, jnp.bfloat16),
+            pltpu.SemaphoreType.DMA((1,)),
+            *Chain.scratch(1, *own_block.shape),
+        ],
+        compiler_params=pltpu.CompilerParams(
+            collective_id=collective_id, has_side_effects=True, vmem_limit_bytes=VMEM_LIMIT
+        ),
         cost_estimate=pl.CostEstimate(
             flops=2 * total_rows * depth * heads * out_width + 10 * elements * head_size,
-            bytes_accessed=2 * (total_rows * depth + depth * heads * out_width),
+            bytes_accessed=100_000_000,
             transcendentals=elements,
         ),
         name="attention_backward",
-    )(
-        state_rows, weight, raw, mixed, totals, *tables,
-        query_gain.reshape(1, -1), key_gain.reshape(1, -1),
-    )
+    )(*operands)
 
 
 def feed_half_kernel(half, tile, rows_ref, cotangent_ref, weight_ref, hidden_ref, slope_ref):
@@ -915,10 +1143,6 @@
     return out if other is not None else out[0]
 
 
-def add_rounded(first, second):
-    return (first.astype(jnp.float32) + second.astype(jnp.float32)).astype(jnp.bfloat16)
-
-
 def reduce_over_chips(pairs, sizes):
     data_size = sizes[0]
     chips = data_size // 2
@@ -931,20 +1155,13 @@
         [(device, device ^ 1) for device in range(data_size)],
     )
     blocks = grad_blocks(ahead + core, pairs, other)
-    up = down = None
-    for step in range(1, chips):
-        rising, falling = blocks[chips - step], blocks[step]
-        if up is not None:
-            rising, falling = add_rounded(rising, up), add_rounded(falling, down)
-        up = lax.ppermute(
-            rising, "dp", [(device, device + 2) for device in range(2 * step)]
-        )
-        down = lax.ppermute(
-            falling,
-            "dp",
-            [(device, device - 2) for device in range(data_size - 2 * step, data_size)],
-        )
-    return blocks, (up, down)
+    up = lax.ppermute(blocks[chips - 1], "dp", [(device, device + 2) for device in range(2)])
+    down = lax.ppermute(
+        blocks[1],
+        "dp",
+        [(device, device - 2) for device in range(data_size - 2, data_size)],
+    )
+    return blocks, up, down
 
 
 def pack_mixing_kernel(heads, query_ref, key_ref, value_ref, output_ref, out_ref):
@@ -959,15 +1176,17 @@
 
 
 def pack_feed_kernel(gate_ref, up_ref, down_ref, first_ref, second_ref):
-    half = gate_ref.shape[1] // 2
-    for index, out_ref in enumerate((first_ref, second_ref)):
-        part = slice(index * half, (index + 1) * half)
-        out_ref[:, :half] = gate_ref[:, part]
-        out_ref[:, half : 2 * half] = up_ref[:, part]
-        out_ref[:, 2 * half :] = down_ref[part, :].T
-
-
-def finish_mixing_kernel(heads, total_ref, query_ref, key_ref, value_ref, output_ref):
+    start = 0
+    for out_ref in (first_ref, second_ref):
+        width = out_ref.shape[1] // 3
+        part = slice(start, start + width)
+        out_ref[:, :width] = gate_ref[:, part]
+        out_ref[:, width : 2 * width] = up_ref[:, part]
+        out_ref[:, 2 * width :] = down_ref[part, :].T
+        start += width
+
+
+def finish_mixing_kernel(heads, total_ref, output_total_ref, query_ref, key_ref, value_ref, output_ref):
     query_width = query_ref.shape[1] // heads
     head_size = key_ref.shape[1] // heads
     start = 0
@@ -977,25 +1196,18 @@
                 jnp.float32
             )
             start += part
-    output_ref[...] = total_ref[:, start:].astype(jnp.float32).T
-
-
-def finish_feed_kernel(*refs):
-    first_refs, second_ref = refs[:-4], refs[-4]
-    gate_ref, up_ref, down_ref = refs[-3:]
-    half = gate_ref.shape[1] // 2
-
-    def first_part(columns):
-        return sum(ref[:, columns].astype(jnp.float32) for ref in first_refs)
-
-    def second_part(columns):
-        return second_ref[:, columns].astype(jnp.float32)
-
-    for index, part_of in enumerate((first_part, second_part)):
-        part = slice(index * half, (index + 1) * half)
-        gate_ref[:, part] = part_of(slice(0, half))
-        up_ref[:, part] = part_of(slice(half, 2 * half))
-        down_ref[part, :] = part_of(slice(2 * half, 3 * half)).T
+    output_ref[...] = output_total_ref[...].astype(jnp.float32).T
+
+
+def finish_feed_kernel(first_ref, second_ref, gate_ref, up_ref, down_ref):
+    start = 0
+    for total_ref in (first_ref, second_ref):
+        width = total_ref.shape[1] // 3
+        part = slice(start, start + width)
+        gate_ref[:, part] = total_ref[:, :width].astype(jnp.float32)
+        up_ref[:, part] = total_ref[:, width : 2 * width].astype(jnp.float32)
+        down_ref[part, :] = total_ref[:, 2 * width :].astype(jnp.float32).T
+        start += width
 
 
 def whole_call(body, shapes, *operands):
@@ -1036,7 +1248,8 @@
     grouping = query_columns // key_columns
     hidden_columns = gate_weight.shape[1]
     qkv_columns = query_columns + 2 * key_columns
-    half = hidden_columns // 2
+    first_columns = hidden_columns * 2 // 3 // 256 * 256 or hidden_columns // 2
+    second_columns = hidden_columns - first_columns
     tables = turn_tables(head_size)
 
     block_width = query_weight.shape[0]
@@ -1048,7 +1261,10 @@
     mixing_full = lax.all_gather(mixing_local, "dp", axis=0, tiled=True)
     feed_locals = whole_call(
         pack_feed_kernel,
-        [jax.ShapeDtypeStruct((block_width, 3 * half), jnp.bfloat16)] * 2,
+        [
+            jax.ShapeDtypeStruct((block_width, 3 * columns), jnp.bfloat16)
+            for columns in (first_columns, second_columns)
+        ],
         gate_weight, up_weight, down_weight,
     )
     feed_full = [lax.all_gather(part, "dp", axis=0, tiled=True) for part in feed_locals]
@@ -1083,7 +1299,7 @@
     )
 
     hidden_first, slope_first = feed_half(feed_rows, cotangent_rows, feed_full[0])
-    blocks, arrivals = reduce_over_chips(
+    blocks, up, down = reduce_over_chips(
         [(feed_rows, slope_first), (cotangent_rows, hidden_first)], sizes
     )
     blocks, later_full = lax.optimization_barrier((blocks, feed_full[1]))
@@ -1094,39 +1310,59 @@
     ).reshape(model_width, -1)
     second_grad, slope_second = lax.optimization_barrier((second_grad, slope_second))
     second_total = lax.psum_scatter(second_grad, "dp", scatter_dimension=0, tiled=True)
-    state_rows, state_slope, feed_term = scatter_call(
-        functools.partial(between_backward_kernel, size, 2),
+    chips = sizes[0] // 2
+    middle_steps = tuple(range(2, chips - 1))
+    chain_block = jax.ShapeDtypeStruct(blocks[0].shape, jnp.bfloat16)
+    state_rows, state_slope, feed_term, up, down = scatter_call(
+        functools.partial(between_backward_kernel, size, chips, middle_steps, 2),
         [[(slope_first, feed_full[0], 0), (slope_second, later_full, 0)]],
         [hidden_state, out_cotangent, feed_gain.reshape(1, -1)],
-        [gathered_shape, local_float, jax.ShapeDtypeStruct((gain_rows, head_size), jnp.float32)],
+        [
+            gathered_shape,
+            local_float,
+            jax.ShapeDtypeStruct((gain_rows, head_size), jnp.float32),
+            chain_block,
+            chain_block,
+        ],
         True,
-        [own_rows, row_sum, *scatter_scratch, *gather_scratch],
+        [
+            own_rows,
+            row_sum,
+            *scatter_scratch,
+            *gather_scratch,
+            *Chain.scratch(len(middle_steps), *blocks[0].shape),
+        ],
         2,
-    )
-    qkv_slope, head_terms = attention_backward(
+        [blocks[chips - step] for step in middle_steps]
+        + [blocks[step] for step in middle_steps]
+        + [up, down],
+    )
+    output_grad = grad_blocks(plain_order, [(state_rows, mixed_rows)]).reshape(model_width, -1)
+    output_grad, state_rows = lax.optimization_barrier((output_grad, state_rows))
+    output_total = lax.psum_scatter(output_grad, "dp", scatter_dimension=0, tiled=True)
+    qkv_slope, head_terms, block_output, first_total = attention_backward(
         state_rows, mixing_full, qkv_columns, raw, mixed_rows, totals, tables,
         query_gain, key_gain, heads, grouping,
-    )
-    mixing_grad = grad_blocks(
-        plain_order, [(mixer_rows, qkv_slope), (state_rows, mixed_rows)]
-    ).reshape(model_width, -1)
+        [
+            (hidden_first, feed_full[0], 2 * first_columns),
+            (hidden_second, later_full, 2 * second_columns),
+        ],
+        hidden_state, [blocks[1], blocks[chips - 1], up, down], blocks[0], sizes, 4,
+    )
+    mixing_grad = grad_blocks(plain_order, [(mixer_rows, qkv_slope)]).reshape(model_width, -1)
     mixing_grad, qkv_slope = lax.optimization_barrier((mixing_grad, qkv_slope))
     mixing_total = lax.psum_scatter(mixing_grad, "dp", scatter_dimension=0, tiled=True)
     terms_shape = (2 * gain_rows + head_terms.shape[0], head_size)
-    block_output, input_gradient, terms = scatter_call(
-        functools.partial(last_kernel, sizes, (1, 2)),
-        [
-            [(qkv_slope, mixing_full, 0)],
-            [(hidden_first, feed_full[0], 2 * half), (hidden_second, later_full, 2 * half)],
-        ],
+    input_gradient, terms = scatter_call(
+        functools.partial(last_kernel, sizes, 1),
+        [[(qkv_slope, mixing_full, 0)]],
         [
             block_input,
             attention_gain.reshape(1, -1),
             state_slope,
-            hidden_state,
             jnp.concatenate([feed_term, head_terms], axis=0),
         ],
-        [local_half, local_half, jax.ShapeDtypeStruct(terms_shape, jnp.float32)],
+        [local_half, jax.ShapeDtypeStruct(terms_shape, jnp.float32)],
         False,
         [
             row_sum,
@@ -1135,7 +1371,6 @@
             pltpu.VMEM((sizes[0], *terms_shape), jnp.float32),
             *[pltpu.SemaphoreType.DMA((count - 1,)) for count in (size, size, *sizes[:1] * 2)],
             *scatter_scratch,
-            *scatter_scratch,
         ],
         3,
     )
@@ -1147,7 +1382,7 @@
             jax.ShapeDtypeStruct((block_width, key_columns), jnp.float32),
             jax.ShapeDtypeStruct((query_columns, block_width), jnp.float32),
         ],
-        mixing_total,
+        mixing_total, output_total,
     )
     gate_gradient, up_gradient, down_gradient = whole_call(
         finish_feed_kernel,
@@ -1156,7 +1391,7 @@
             jax.ShapeDtypeStruct((block_width, hidden_columns), jnp.float32),
             jax.ShapeDtypeStruct((hidden_columns, block_width), jnp.float32),
         ],
-        blocks[0], *arrivals, second_total,
+        first_total, second_total,
     )
     return (
         block_output,

time: 670 us -> 605 us (0.903)
  waiting for transfers between devices: 152 us -> 85 us
  Pallas kernels: 476 us -> 489 us
  starting transfers between devices: 14.9 us -> 3.83 us
    ppermute x6 -> x2, waiting for transfers between devices: 96.4 us -> 4.7 us  [the longest x1 4.7 us: reduce_over_chips(): lax.ppermute(blocks[chips - 1], 'dp', [(device, device + 2) for device in...]
    pallas_call x1, Pallas kernels: 23.2 us -> 64.7 us  [attention_backward(): pl.pallas_call(functools.partial(attention_backward_kernel, size, chips,...]
    reduce_scatter x1, waiting for transfers between devices: 20 us -> 59.8 us  [per_device(): lax.psum_scatter(second_grad, 'dp', scatter_dimension=0, tiled=True)]
    pallas_call x3, Pallas kernels: 257 us -> 222 us  [scatter_call(): pl.pallas_call(body, grid=(1,), out_shape=outs, in_specs=in_specs, out_sp...]
    all_gather x2, waiting for transfers between devices: 25.7 us -> 8.82 us  [per_device(): lax.all_gather(part, 'dp', axis=0, tiled=True)]
    ppermute x6 -> x2, starting transfers between devices: 14.7 us -> 3.25 us  [the longest x1 1.86 us: reduce_over_chips(): lax.ppermute(blocks[1], 'dp', [(device, device - 2) for device in range(d...]
    pallas_call x4 -> x5, Pallas kernels: 52.3 us -> 59.5 us  [grad_blocks(): pl.pallas_call(functools.partial(grad_kernel, len(pairs), other is not No...]
  transfers between devices with their start and end apart: 12 -> 9, of which waited for: 5 -> 5; matrix products, arithmetic and copies ran while one was open for 1% -> 1% of each run, Pallas kernels for 46% -> 63%
where the time goes in v5:
time: 605 us; the launch traced here: 603 us
  Pallas kernels  489 us (81%)
  waiting for transfers between devices  85 us (14%)
  between operations  14.3 us (2%)
  local copies, waits for them, and re-layouts  8.02 us (1%)
    pallas_call x3, Pallas kernels, scatter_call(): pl.pallas_call(body, grid=(1,), out_shape=outs, in_specs=in_specs, out_sp...  222 us
    pallas_call x1, Pallas kernels, gather_rows(): pl.pallas_call(functools.partial(gather_kernel, size, count), out_shape=[...  75.1 us
    pallas_call x1, Pallas kernels, attention_backward(): pl.pallas_call(functools.partial(attention_backward_kernel, size, chips,...  64.7 us
    reduce_scatter x1, waiting for transfers between devices, per_device(): lax.psum_scatter(second_grad, 'dp', scatter_dimension=0, tiled=True)  59.8 us
    pallas_call x5, Pallas kernels, grad_blocks(): pl.pallas_call(functools.partial(grad_kernel, len(pairs), other is not No...  59.5 us
    pallas_call x2, Pallas kernels, feed_half(): pl.pallas_call(functools.partial(feed_half_kernel, half, tile), grid=(tot...  36.9 us
    pallas_call x1, Pallas kernels, attention_forward(): pl.pallas_call(functools.partial(attention_forward_kernel, grouping, head...  18.5 us
  transfers between devices with their start and end apart: 9, of which 5 were waited for; matrix products, arithmetic and copies ran while one was open for 1% of the time, Pallas kernels for 63%

profile of v5, /device:TPU:0, one launch (start us, length us, event | category | flops | bytes accessed | tf_op | source)
XLA Modules:
  0.0 603.4 jit_solution(15755281449668402705)
XLA Ops:
  7.2 0.0 all-gather.4.cloned.1.call-start
  7.2 2.2 shard_map.246
  9.4 0.0 all-gather.6.cloned.1.call-start
  9.5 3.3 shard_map.248
  12.9 0.0 all-gather.8.cloned.1.call-start
  12.9 0.7 all-gather.8.cloned.1.call-update
  13.6 0.0 reduce-scatter.6.cloned.1.call-start
  13.7 0.3 fusion
  14.0 1.3 fusion.2.refs_0_
  15.2 75.1 %gather_rows.1 = (bf16[1024,2048]{1,0:T(8,128)(2,1)}, bf16[1024,2048]{1,0:T(8,128)(2,1)}) custom-call(bf16[256,2048]{1,0:T(8,128)(2,1)} %fusion.2.refs_0_, bf16[256,2048]{1,0:T(8,128)(2,1)} %refs_5_.1), custom_call_target="tpu_custom_call" | custom-call | bytes 125829120 | tf_op jit(solution)/shard_map/gather_rows/pallas_call | solution.py:169
  90.4 0.5 broadcast_add_fusion.order_ref
  90.9 18.5 %attention_forward.1 = (f32[1024,1024]{1,0:T(8,128)}, bf16[1024,512]{1,0:T(8,128)(2,1)}, f32[2,2,1024]{2,1,0:T(2,128)}) custom-call(bf16[1024,2048]{1,0:T(8,128)(2,1)} %get-tuple-element.59.rows_ref.refs_0_, bf16[2048,1536]{1,0:T(8,128)(2,1)} %all-gather.4.cloned.1.call-done.weight_ref.refs_1_.refs_5_, f32[136,128]{1,0:T(8,128)} %constant.38.clone.few_cosines_ref.refs_9_, ...), custom_call_target="tpu_custom_call" | custom-call | flops 5368709120 | bytes 8388608 | tf_op jit(solution)/shard_map/attention_forward/pallas_call | solution.py:735
  109.4 77.4 %shard_map.247 = (bf16[1024,2048]{1,0:T(8,128)(2,1)}, f32[256,2048]{1,0:T(8,128)}) custom-call(bf16[1024,512]{1,0:T(8,128)(2,1)} %get-tuple-element.60.refs_0_.refs_1_.refs_7_, bf16[2048,1536]{1,0:T(8,128)(2,1)} %all-gather.4.cloned.1.call-done.weight_ref.refs_1_.refs_5_, bf16[256,2048]{1,0:T(8,128)(2,1)} %refs_2_.3, f32[1,2048]{1,0:T(1,128)} %bitcast.18), custom_call_target="tpu_custom_call" | custom-call | flops 2147483648 | bytes 150000000 | tf_op jit(solution)/shard_map/pallas_call | solution.py:603
  186.8 8.5 %all-gather.6.cloned.1.call-done.weight_ref.refs_1_ = bf16[2048,3072]{1,0:T(8,128)(2,1)} async-done(((bf16[256,3072]{1,0:T(8,128)(2,1)}), bf16[2048,3072]{1,0:T(8,128)(2,1)}) %all-gather.6.cloned.1.call-update) | async-done | bytes 12582928 | tf_op jit(solution)/shard_map/all_gather | solution.py:1270
  195.3 23.5 %feed_half.2 = (bf16[1024,1024]{1,0:T(8,128)(2,1)}, bf16[1024,2048]{1,0:T(8,128)(2,1)}) custom-call(bf16[1024,2048]{1,0:T(8,128)(2,1)} %get-tuple-element.61.rows_ref.refs_0_, bf16[1024,2048]{1,0:T(8,128)(2,1)} %get-tuple-element.62.cotangent_ref.refs_2_, bf16[2048,3072]{1,0:T(8,128)(2,1)} %all-gather.6.cloned.1.call-done.weight_ref.refs_1_), custom_call_target="tpu_custom_call" | custom-call | flops 12884901888 | bytes 20971520 | tf_op jit(solution)/shard_map/feed_half/pallas_call | solution.py:1035
  218.7 12.5 %grad_blocks.5 = bf16[4,256,3072]{2,1,0:T(8,128)(2,1)} custom-call(s32[4]{0:T(128)} %broadcast_add_fusion.order_ref, bf16[1024,2048]{1,0:T(8,128)(2,1)} %get-tuple-element.61.rows_ref.refs_0_, bf16[1024,2048]{1,0:T(8,128)(2,1)} %get-tuple-element.65.refs_1_.refs_0_, bf16[1024,2048]{1,0:T(8,128)(2,1)} %get-tuple-element.62.cotangent_ref.refs_2_, ...), custom_call_target="tpu_custom_call" | custom-call | flops 6442450944 | bytes 16777216 | tf_op jit(solution)/shard_map/grad_blocks/pallas_call | solution.py:1125
  231.2 0.3 collective-permute-start
  231.6 0.5 broadcast_add_fusion.1.order_ref
  232.1 10.5 %collective-permute-done.refs_4_ = bf16[4,256,3072]{2,1,0:T(8,128)(2,1)} collective-permute-done((bf16[4,256,3072]{2,1,0:T(8,128)(2,1)}, bf16[4,256,3072]{2,1,0:T(8,128)(2,1)}, u32[]{:S(2)}, u32[]{:S(2)}) %collective-permute-start) | collective-permute-done | bytes 6291488 | tf_op jit(solution)/shard_map/ppermute | solution.py:1152
  242.6 13.7 %grad_blocks.6 = (bf16[256,3072]{1,0:T(8,128)(2,1)}, bf16[256,3072]{1,0:T(8,128)(2,1)}, bf16[256,3072]{1,0:T(8,128)(2,1)}, bf16[256,3072]{1,0:T(8,128)(2,1)}) custom-call(s32[4]{0:T(128)} %broadcast_add_fusion.1.order_ref, bf16[1024,2048]{1,0:T(8,128)(2,1)} %get-tuple-element.61.rows_ref.refs_0_, bf16[1024,2048]{1,0:T(8,128)(2,1)} %get-tuple-element.65.refs_1_.refs_0_, ...), custom_call_target="tpu_custom_call" | custom-call | flops 6442450944 | bytes 16777216 | tf_op jit(solution)/shard_map/grad_blocks/pallas_call | solution.py:1125
  256.2 1.4 collective-permute-start.1
  257.6 1.9 collective-permute-start.2
  259.5 0.3 all-gather.8.cloned.1.call-done.weight_ref.refs_3_
  259.8 13.4 %feed_half.3 = (bf16[1024,512]{1,0:T(8,128)(2,1)}, bf16[1024,1024]{1,0:T(8,128)(2,1)}) custom-call(bf16[1024,2048]{1,0:T(8,128)(2,1)} %get-tuple-element.61.rows_ref.refs_0_, bf16[1024,2048]{1,0:T(8,128)(2,1)} %get-tuple-element.62.cotangent_ref.refs_2_, bf16[2048,1536]{1,0:T(8,128)(2,1)} %all-gather.8.cloned.1.call-done.weight_ref.refs_3_), custom_call_target="tpu_custom_call" | custom-call | flops 6442450944 | bytes 14680064 | tf_op jit(solution)/shard_map/feed_half/pallas_call | solution.py:1035
  273.3 0.5 iota.12.order_ref
  273.8 13.7 %grad_blocks.7 = bf16[8,256,1536]{2,1,0:T(8,128)(2,1)} custom-call(s32[8]{0:T(128)} %iota.12.order_ref, bf16[1024,2048]{1,0:T(8,128)(2,1)} %get-tuple-element.61.rows_ref.refs_0_, bf16[1024,1024]{1,0:T(8,128)(2,1)} %get-tuple-element.74.refs_1_.refs_2_, bf16[1024,2048]{1,0:T(8,128)(2,1)} %get-tuple-element.62.cotangent_ref.refs_2_, ...), custom_call_target="tpu_custom_call" | custom-call | flops 6442450944 | bytes 17825792 | tf_op jit(solution)/shard_map/grad_blocks/pallas_call | solution.py:1125
  287.4 4.7 collective-permute-done.1.refs_9_
  292.1 1.2 copy-done.6
  293.3 90.8 %shard_map.249 = (bf16[1024,2048]{1,0:T(8,128)(2,1)}, f32[256,2048]{1,0:T(8,128)}, f32[16,128]{1,0:T(8,128)}, bf16[256,3072]{1,0:T(8,128)(2,1)}, bf16[256,3072]{1,0:T(8,128)(2,1)}) custom-call(bf16[1024,2048]{1,0:T(8,128)(2,1)} %get-tuple-element.65.refs_1_.refs_0_, bf16[2048,3072]{1,0:T(8,128)(2,1)} %all-gather.6.cloned.1.call-done.weight_ref.refs_1_, ...), custom_call_target="tpu_custom_call" | custom-call | flops 12884901888 | bytes 150000000 | tf_op jit(solution)/shard_map/pallas_call | solution.py:603
  384.1 0.5 iota.11.order_ref
  384.6 8.9 %grad_blocks.8 = bf16[8,256,512]{2,1,0:T(8,128)(2,1)} custom-call(s32[8]{0:T(128)} %iota.11.order_ref, bf16[1024,2048]{1,0:T(8,128)(2,1)} %get-tuple-element.78.refs_0_.refs_4_, bf16[1024,512]{1,0:T(8,128)(2,1)} %get-tuple-element.60.refs_0_.refs_1_.refs_7_), custom_call_target="tpu_custom_call" | custom-call | flops 2147483648 | bytes 7340032 | tf_op jit(solution)/shard_map/grad_blocks/pallas_call | solution.py:1125
  393.5 0.0 reduce-scatter.4.cloned.1.call-start
  393.6 64.7 %attention_backward.1 = (bf16[1024,1024]{1,0:T(8,128)(2,1)}, f32[8,128]{1,0:T(8,128)}, bf16[256,2048]{1,0:T(8,128)(2,1)}, bf16[256,3072]{1,0:T(8,128)(2,1)}) custom-call(bf16[1024,1024]{1,0:T(8,128)(2,1)} %get-tuple-element.64.refs_3_.refs_0_, bf16[2048,3072]{1,0:T(8,128)(2,1)} %all-gather.6.cloned.1.call-done.weight_ref.refs_1_, ...), custom_call_target="tpu_custom_call" | custom-call | flops 4831838208 | bytes 100000000 | tf_op jit(solution)/shard_map/attention_backward/pallas_call | solution.py:964
  458.3 0.5 iota.13.order_ref
  458.8 10.8 %grad_blocks.9 = bf16[8,256,1024]{2,1,0:T(8,128)(2,1)} custom-call(s32[8]{0:T(128)} %iota.13.order_ref, bf16[1024,2048]{1,0:T(8,128)(2,1)} %get-tuple-element.59.rows_ref.refs_0_, bf16[1024,1024]{1,0:T(8,128)(2,1)} %get-tuple-element.88.refs_1_.refs_0_), custom_call_target="tpu_custom_call" | custom-call | flops 4294967296 | bytes 10485760 | tf_op jit(solution)/shard_map/grad_blocks/pallas_call | solution.py:1125
  469.7 0.0 reduce-scatter.8.cloned.1.call-start
  469.8 0.5 reduce-scatter.8.cloned.1.call-update
  470.3 0.1 copy-done.4
  470.4 0.6 pad_maximum_fusion.refs_5_
  471.0 54.2 %shard_map.250 = (bf16[256,2048]{1,0:T(8,128)(2,1)}, f32[40,128]{1,0:T(8,128)}) custom-call(bf16[1024,1024]{1,0:T(8,128)(2,1)} %get-tuple-element.88.refs_1_.refs_0_, bf16[2048,1536]{1,0:T(8,128)(2,1)} %all-gather.4.cloned.1.call-done.weight_ref.refs_1_.refs_5_, bf16[256,2048]{1,0:T(8,128)(2,1)} %refs_2_.3, f32[1,2048]{1,0:T(1,128)} %bitcast.20, ...), custom_call_target="tpu_custom_call" | custom-call | flops 4294967296 | bytes 150000000 | tf_op jit(solution)/shard_map/pallas_call | solution.py:603
  525.2 1.3 slice_bitcast_fusion.2
  526.5 1.3 slice_bitcast_fusion
  527.8 2.3 shard_map.251
  530.1 59.8 %reduce-scatter.8.cloned.1.call-done.second_ref = bf16[256,1536]{1,0:T(8,128)(2,1)} async-done(((bf16[2048,1536]{1,0:T(8,128)(2,1)}), bf16[256,1536]{1,0:T(8,128)(2,1)}) %reduce-scatter.8.cloned.1.call-update) | async-done | bytes 786448 | tf_op jit(solution)/shard_map/reduce_scatter | solution.py:1312
  589.9 4.1 shard_map.252
  594.0 1.0 copy.30
  595.0 0.6 copy-done.2
  595.6 1.0 copy.31
  (20 shorter events, 0.1 us)
Async XLA Ops:
  7.2 83.7 %all-gather.4.cloned.1.call-start = ((), (), s32[]{:S(2)}) async-start(), calls=%async_computation.3 | async-start | bytes 7077888 | tf_op jit(solution)/shard_map/all_gather | solution.py:1261
  9.4 4.2 copy-start
  9.4 185.8 %all-gather.6.cloned.1.call-start = ((), (), s32[]{:S(2)}) async-start(), calls=%async_computation.4 | async-start | bytes 14155776 | tf_op jit(solution)/shard_map/all_gather | solution.py:1270
  12.8 1.1 copy-start.3
  12.9 247.0 %all-gather.8.cloned.1.call-start = ((), (), s32[]{:S(2)}) async-start(), calls=%async_computation.5 | async-start | bytes 7077888 | tf_op jit(solution)/shard_map/all_gather | solution.py:1270
  13.6 514.2 %reduce-scatter.6.cloned.1.call-start = ((), (), s32[]{:S(2)}) async-start(), calls=%async_computation.7 | async-start | bytes 2359296 | tf_op jit(solution)/shard_map/reduce_scatter | solution.py:1342
  231.2 11.3 %collective-permute-start = (bf16[4,256,3072]{2,1,0:T(8,128)(2,1)}, bf16[4,256,3072]{2,1,0:T(8,128)(2,1)}, u32[]{:S(2)}, u32[]{:S(2)}) collective-permute-start(bf16[4,256,3072]{2,1,0:T(8,128)(2,1)} %grad_blocks.5), channel_id=1, source_target_pairs={{0,4},{4,0},{8,12},{12,8},{16,20},{20,16},{24,28},{28,24},{1,5},{5... | collective-permute-start | bytes 18874376 | tf_op jit(solution)/shard_map/ppermute | solution.py:1152
  256.2 35.9 %collective-permute-start.1 = (bf16[256,3072]{1,0:T(8,128)(2,1)}, bf16[256,3072]{1,0:T(8,128)(2,1)S(1)}, u32[]{:S(2)}, u32[]{:S(2)}) collective-permute-start(bf16[256,3072]{1,0:T(8,128)(2,1)} %get-tuple-element.82.refs_15_), channel_id=1, source_target_pairs={{0,8},{4,12},{1,9},{5,13},{2,10},{6,14},{3,11},{7,15}} | collective-permute-start | bytes 4718600 | tf_op jit(solution)/shard_map/ppermute | solution.py:1158
  257.6 34.5 %collective-permute-start.2 = (bf16[256,3072]{1,0:T(8,128)(2,1)}, bf16[256,3072]{1,0:T(8,128)(2,1)}, u32[]{:S(2)}, u32[]{:S(2)}) collective-permute-start(bf16[256,3072]{1,0:T(8,128)(2,1)} %get-tuple-element.81.refs_14_), channel_id=1, source_target_pairs={{24,16},{28,20},{25,17},{29,21},{26,18},{30,22},{27,19},{31,23}} | collective-permute-start | bytes 4718600 | tf_op jit(solution)/shard_map/ppermute | solution.py:1159
  292.1 1.2 copy-start.6
  393.5 134.3 %reduce-scatter.4.cloned.1.call-start = ((), (), s32[]{:S(2)}) async-start(), calls=%async_computation.6 | async-start | bytes 4718592 | tf_op jit(solution)/shard_map/reduce_scatter | solution.py:1354
  469.7 0.7 copy-start.4
  469.7 0.7 copy-start.5
  469.7 120.2 %reduce-scatter.8.cloned.1.call-start = ((), (), s32[]{:S(2)}) async-start(), calls=%async_computation.8 | async-start | bytes 7077888 | tf_op jit(solution)/shard_map/reduce_scatter | solution.py:1312
  525.2 68.9 %copy-start.1 = (bf16[256,2048]{1,0:T(8,128)(2,1)S(1)}, bf16[256,2048]{1,0:T(8,128)(2,1)}, u32[]{:S(2)}) copy-start(bf16[256,2048]{1,0:T(8,128)(2,1)} %get-tuple-element.122) | copy-start | bytes 3145732
  594.0 1.6 copy-start.2
Sparse Core Ops, SparseCore 0:
  10.2 67.4 all-gather.3
  79.9 115.3 all-gather.5
  196.9 62.8 all-gather.7
  393.6 46.2 reduce-scatter.5
  469.8 49.6 reduce-scatter.3
  521.7 68.1 reduce-scatter.7

commit v6 on v5

--- a/solution.py
+++ b/solution.py
@@ -182,16 +182,54 @@
     )(*arrays)
 
 
-def block_product(pairs, start, rows, write):
-    total = pairs[0][1].shape[0]
-    tile = min(512, total)
+class Operand:
+    def __init__(self, size, first_column, left_far, weight_far, left, weight, left_sem, weight_sem):
+        self.left, self.weight = left, weight
+        self.rows = left.shape[0] // size
+        self.tile = min(512, weight.shape[0])
+        self.far = left_far, weight_far
+        self.first_column = first_column
+        self.left_sem, self.weight_sem = left_sem, weight_sem
+
+    @staticmethod
+    def scratch(size, left, weight):
+        width = left.shape[1]
+        return [
+            pltpu.VMEM(left.shape, left.dtype),
+            pltpu.VMEM((weight.shape[0], width), weight.dtype),
+            pltpu.SemaphoreType.DMA((size,)),
+            pltpu.SemaphoreType.DMA((max(1, weight.shape[0] // 512),)),
+        ]
+
+    def left_copy(self, slot, owner):
+        piece = pl.ds(pl.multiple_of(owner * self.rows, self.rows), self.rows)
+        return pltpu.make_async_copy(self.far[0].at[piece], self.left.at[piece], self.left_sem.at[slot])
+
+    def weight_copy(self, index):
+        piece = pl.ds(pl.multiple_of(index * self.tile, self.tile), self.tile)
+        columns = pl.ds(self.first_column, self.left.shape[1])
+        return pltpu.make_async_copy(
+            self.far[1].at[piece, columns], self.weight.at[piece], self.weight_sem.at[index]
+        )
+
+
+def block_product(operands, start, rows, fresh, write):
+    total = operands[0].weight.shape[0]
+    tile = operands[0].tile
     start = pl.multiple_of(start, rows)
 
     def step(index, carry):
+        @pl.when(fresh)
+        def _():
+            for operand in operands:
+                operand.weight_copy(index).wait()
+
         columns = pl.ds(pl.multiple_of(index * tile, tile), tile)
         values = None
-        for left_ref, weight_ref in pairs:
-            part = times_transposed(left_ref[pl.ds(start, rows), :], weight_ref[columns, :])
+        for operand in operands:
+            part = times_transposed(
+                operand.left[pl.ds(start, rows), :], operand.weight[columns, :]
+            )
             values = part if values is None else values + part
         write(columns, values)
         return carry
@@ -250,27 +288,44 @@
         ]
         return copies, ((0, 0), (0, 1), (1, 2), (2, 3))
 
-    def fill(self, pairs):
-        size, me, rows = self.size, self.me, self.rows
+    def owner(self, slot):
+        if self.size != 4:
+            return lax.rem(self.me + slot + 1, self.size)
+        beside, below, across = square_peers(self.me)
+        return jnp.where(
+            slot == 0, across, jnp.where(slot == 1, beside, jnp.where(slot == 2, below, self.me))
+        )
+
+    def load(self, operands):
+        tiles = operands[0].weight.shape[0] // operands[0].tile
+        for operand in operands:
+            operand.left_copy(0, self.owner(0)).start()
+        for index in range(tiles):
+            for operand in operands:
+                operand.weight_copy(index).start()
+        for slot in range(1, self.size):
+            for operand in operands:
+                operand.left_copy(slot, self.owner(slot)).start()
+
+    def fill(self, operands, look=None):
+        rows = self.rows
 
         def step(slot, carry):
-            if size == 4:
-                beside, below, across = square_peers(me)
-                owner = jnp.where(
-                    slot == 0, across, jnp.where(slot == 1, beside, jnp.where(slot == 2, below, me))
-                )
-            else:
-                owner = lax.rem(me + slot + 1, size)
+            owner = self.owner(slot)
+            for operand in operands:
+                operand.left_copy(slot, owner).wait()
 
             def write(columns, values):
                 self.outgoing[slot, :, columns] = values.astype(self.outgoing.dtype)
-
-            block_product(pairs, owner * rows, rows, write)
+                if look is not None:
+                    look(owner, columns, values)
+
+            block_product(operands, owner * rows, rows, slot == 0, write)
             for at, index in self.starts:
                 pl.when(slot == at)(self.copies[index].start)
             return carry
 
-        lax.fori_loop(0, size, step, 0)
+        lax.fori_loop(0, self.size, step, 0)
 
     def relay(self):
         if self.size != 4:
@@ -434,8 +489,14 @@
     return total
 
 
-def split_pairs(refs, count):
-    return [refs[2 * p : 2 * p + 2] for p in range(count)], refs[2 * count :]
+def split_operands(refs, size, first_columns):
+    count = len(first_columns)
+    far, refs, scratch = refs[: 2 * count], refs[2 * count : -4 * count], refs[-4 * count :]
+    operands = [
+        Operand(size, first, *far[2 * p : 2 * p + 2], *scratch[4 * p : 4 * p + 4])
+        for p, first in enumerate(first_columns)
+    ]
+    return operands, refs
 
 
 def store_row(target_ref, row_ref):
@@ -444,14 +505,15 @@
         target_ref[index : index + 1, :] = row_ref[:, index * width : (index + 1) * width]
 
 
-def between_forward_kernel(size, pair_count, *refs):
-    pairs, refs = split_pairs(refs, pair_count)
+def between_forward_kernel(size, first_columns, *refs):
+    operands, refs = split_operands(refs, size, first_columns)
     input_ref, gain_ref, gathered_ref, state_ref, own_ref = refs[:5]
     buffers = 5 if size == 4 else 4
     scatter = Scatter(size, *refs[5 : 5 + buffers])
     gather = Gather(size, own_ref, gathered_ref, *refs[5 + buffers :])
+    scatter.load(operands)
     greet(neighbours(size))
-    scatter.fill(pairs)
+    scatter.fill(operands)
     scatter.relay()
     scatter.collect()
 
@@ -466,23 +528,30 @@
     scatter.drain()
 
 
-def between_backward_kernel(size, chips, steps, pair_count, *refs):
-    pairs, refs = split_pairs(refs, pair_count)
+def between_backward_kernel(size, chips, steps, first_columns, *refs):
+    operands, refs = split_operands(refs, size, first_columns)
     state_ref, cotangent_ref, gain_ref = refs[:3]
     chain_count = 2 * len(steps) + 2
-    chain_refs, refs = refs[3 : 3 + chain_count], refs[3 + chain_count :]
-    gathered_ref, slope_ref, term_ref, up_out_ref, down_out_ref, own_ref, sum_ref = refs[:7]
+    chain_refs, last_refs, refs = refs[3 : 3 + chain_count], refs[3 + chain_count : 5 + chain_count], refs[5 + chain_count :]
+    gathered_ref, slope_ref, term_ref, rising_ref, falling_ref, own_ref, sum_ref, last_sem = refs[:8]
     buffers = 5 if size == 4 else 4
-    scatter = Scatter(size, *refs[7 : 7 + buffers])
-    gather = Gather(size, own_ref, gathered_ref, *refs[7 + buffers : 11 + buffers])
+    scatter = Scatter(size, *refs[8 : 8 + buffers])
+    gather = Gather(size, own_ref, gathered_ref, *refs[8 + buffers : 12 + buffers])
     chain = Chain(
         chips, steps, chain_refs[: len(steps)], chain_refs[len(steps) : -2], *chain_refs[-2:],
-        *refs[11 + buffers :],
-    )
+        *refs[12 + buffers :],
+    )
+    last_loads = [
+        pltpu.make_async_copy(source, target, last_sem.at[index])
+        for index, (source, target) in enumerate(zip(last_refs, (rising_ref, falling_ref)))
+    ]
     chain.load()
+    scatter.load(operands)
+    for load in last_loads:
+        load.start()
     greet(neighbours(size) + chain.neighbours)
     chain.step(0)
-    scatter.fill(pairs)
+    scatter.fill(operands)
     scatter.relay()
     sum_ref[...] = jnp.zeros_like(sum_ref)
     scatter.collect()
@@ -507,40 +576,61 @@
     for index in range(1, len(steps)):
         chain.step(index)
         chain.wait(index)
+    for load in last_loads:
+        load.wait()
     last = len(steps)
-    from_under, from_above = chain.arrives(last - 1)
-    for arrived, landing, out_ref in (
-        (from_under, chain.up, up_out_ref),
-        (from_above, chain.down, down_out_ref),
+    for needed, landing, out_ref in (
+        ((chain.chip > 0) & (chain.chip < chips - 1), chain.up, rising_ref),
+        ((chain.chip > 0) & (chain.chip < chips - 1), chain.down, falling_ref),
     ):
 
-        @pl.when(arrived)
+        @pl.when(needed)
         def _(landing=landing, out_ref=out_ref):
-            out_ref[...] = landing[last]
-
-        @pl.when(jnp.logical_not(arrived))
-        def _(out_ref=out_ref):
-            out_ref[...] = jnp.zeros_like(out_ref)
+            def add(piece):
+                out_ref[piece, :] = add_rounded(out_ref[piece, :], landing[last, piece, :])
+
+            over_pieces(out_ref.shape[0], add)
 
     gather.finish()
     scatter.drain()
     chain.drain()
 
 
-def last_kernel(sizes, pair_count, *refs):
+def last_kernel(sizes, first_columns, *refs):
     data_size, size = sizes
-    pairs, refs = split_pairs(refs, pair_count)
-    input_ref, gain_ref, slope_ref, terms_ref = refs[:4]
-    gradient_ref, terms_out_ref, sum_ref, partial_ref, inner, outer = refs[4:10]
-    inner_send, inner_recv, outer_send, outer_recv = refs[10:14]
-    mixing = Scatter(size, *refs[14:])
+    operands, refs = split_operands(refs, size, first_columns)
+    input_ref, gain_ref, slope_ref, terms_ref, rows_ref = refs[:5]
+    gradient_ref, terms_out_ref, sum_ref, partial_ref, group_ref, inner, outer = refs[5:12]
+    inner_send, inner_recv, outer_send, outer_recv = refs[12:16]
+    mixing = Scatter(size, *refs[16:])
+    rows = gradient_ref.shape[0]
+    mixing.load(operands)
     greet(
         [("tensor", peer) for peer in other_members("tensor", size)]
         + [("dp", peer) for peer in other_members("dp", data_size)]
     )
-    mixing.fill(pairs)
+    sum_ref[...] = jnp.zeros_like(sum_ref)
+
+    def look(owner, columns, values):
+        piece = pl.ds(pl.multiple_of(owner * rows, rows), rows)
+        sum_ref[:, columns] += jnp.sum(
+            values * rows_ref[piece, columns].astype(jnp.float32), axis=0, keepdims=True
+        )
+
+    mixing.fill(operands, look)
+    sum_ref[...] = sum_ref[...] / gain_ref[...]
+    kept = partial_ref.shape[0] - terms_ref.shape[0]
+    partial_ref[kept:, :] = terms_ref[...]
+    store_row(partial_ref, sum_ref)
+    inner_copies = send_terms(
+        "tensor", other_members("tensor", size), partial_ref, inner, inner_send, inner_recv
+    )
     mixing.relay()
-    sum_ref[...] = jnp.zeros_like(sum_ref)
+    group_ref[...] = add_terms(inner, inner_copies)
+    outer_copies = send_terms(
+        "dp", other_members("dp", data_size), group_ref, outer, outer_send, outer_recv
+    )
+    terms_out_ref[...] = add_terms(outer, outer_copies)
     mixing.collect()
 
     def norm(piece):
@@ -548,72 +638,45 @@
         values = input_ref[piece, :].astype(jnp.float32)
         scale = row_scale(values)
         unit = values * scale
-        sum_ref[...] += jnp.sum(back * unit, axis=0, keepdims=True)
         unit_slope = back * gain_ref[...]
         gradient_ref[piece, :] = (
             slope_ref[piece, :]
             + scale * (unit_slope - unit * jnp.mean(unit_slope * unit, axis=-1, keepdims=True))
         ).astype(gradient_ref.dtype)
 
-    over_pieces(gradient_ref.shape[0], norm)
-    kept = partial_ref.shape[0] - terms_ref.shape[0]
-    partial_ref[kept:, :] = terms_ref[...]
-    store_row(partial_ref, sum_ref)
-    inner_copies = send_terms(
-        "tensor", other_members("tensor", size), partial_ref, inner, inner_send, inner_recv
-    )
-    terms_out_ref[...] = add_terms(inner, inner_copies)
-    outer_copies = send_terms(
-        "dp", other_members("dp", data_size), terms_out_ref, outer, outer_send, outer_recv
-    )
-    total = add_terms(outer, outer_copies)
-    for copy in outer_copies:
-        copy.wait_send()
-    terms_out_ref[...] = total
-    for copy in inner_copies:
+    over_pieces(rows, norm)
+    for copy in inner_copies + outer_copies:
         copy.wait_send()
     mixing.drain()
 
 
-def scatter_call(body, triple_lists, others, outs, gathered, scratch, collective_id, far=()):
-    in_specs = []
-    operands = []
-    flops = 0
-    for left, weight, first_column in (triple for triples in triple_lists for triple in triples):
-        part = left.shape[1]
-        flops += 2 * left.size * weight.shape[0]
-        in_specs += [
-            pl.BlockSpec(left.shape, lambda i: (0, 0), pipeline_mode=pl.Buffered(1)),
-            pl.BlockSpec(
-                (weight.shape[0], part),
-                lambda i, block=first_column // part: (0, block),
-                pipeline_mode=pl.Buffered(1),
-            ),
-        ]
-        operands += [left, weight]
+def scatter_call(body, triples, size, others, far, outs, gathered, scratch, collective_id):
+    far_spec = pl.BlockSpec(memory_space=pl.ANY)
+    operands = [array for left, weight, _ in triples for array in (left, weight)]
+    in_specs = [far_spec] * len(operands)
     for other in others:
         in_specs.append(pl.BlockSpec(other.shape, lambda i: (0, 0), pipeline_mode=pl.Buffered(1)))
-        operands.append(other)
-    for other in far:
-        in_specs.append(pl.BlockSpec(memory_space=pl.ANY))
-        operands.append(other)
+    in_specs += [far_spec] * len(far)
     out_specs = [pl.BlockSpec(out.shape, lambda i: (0, 0)) for out in outs]
     if gathered:
-        out_specs[0] = pl.BlockSpec(memory_space=pl.ANY)
+        out_specs[0] = far_spec
     return pl.pallas_call(
-        body,
+        functools.partial(body, tuple(first for _, _, first in triples)),
         grid=(1,),
         out_shape=outs,
         in_specs=in_specs,
         out_specs=out_specs,
-        scratch_shapes=scratch,
+        scratch_shapes=list(scratch)
+        + [part for left, weight, _ in triples for part in Operand.scratch(size, left, weight)],
         compiler_params=pltpu.CompilerParams(
             collective_id=collective_id, has_side_effects=True, vmem_limit_bytes=VMEM_LIMIT
         ),
         cost_estimate=pl.CostEstimate(
-            flops=flops, bytes_accessed=150_000_000, transcendentals=0
+            flops=sum(2 * left.size * weight.shape[0] for left, weight, _ in triples),
+            bytes_accessed=150_000_000,
+            transcendentals=0,
         ),
-    )(*operands)
+    )(*operands, *others, *far)
 
 
 LOG2E = 1.4426950408889634
@@ -780,34 +843,22 @@
     return slope.astype(jnp.bfloat16), jnp.sum(term, axis=0, keepdims=True)
 
 
-def attention_backward_kernel(size, chips, grouping, head_size, block, pair_count, *refs):
-    pairs, refs = split_pairs(refs, pair_count)
+def attention_backward_kernel(size, grouping, head_size, block, first_columns, *refs):
+    operands, refs = split_operands(refs, size, first_columns)
     (
         state_ref, weight_ref, raw_ref, mixed_ref, total_ref, few_cosines_ref, few_sines_ref,
-        query_gain_ref, key_gain_ref, hidden_state_ref,
-    ) = refs[:10]
-    chain_refs, own_block_ref = refs[10:14], refs[14]
-    slope_ref, gain_ref, output_ref, chain_total_ref = refs[15:19]
-    (
+        query_gain_ref, key_gain_ref, hidden_state_ref, slope_ref, gain_ref, output_ref,
         query_ref, key_ref, value_ref, out_slope_ref, turned_ref, key_sum_ref, value_sum_ref, cosine_ref, sine_ref,
-    ) = refs[19:28]
-    buffers = 5 if size == 4 else 4
-    scatter = Scatter(size, *refs[28 : 28 + buffers])
-    own_block, own_sem = refs[28 + buffers : 30 + buffers]
-    chain = Chain(
-        chips, (chips - 1,), chain_refs[:1], chain_refs[1:2], *chain_refs[2:], *refs[30 + buffers :]
-    )
-    own_load = pltpu.make_async_copy(own_block_ref, own_block, own_sem.at[0])
+    ) = refs[:22]
+    scatter = Scatter(size, *refs[22:])
     step = pl.program_id(0) * pl.num_programs(1) + pl.program_id(1)
     steps = pl.num_programs(0) * pl.num_programs(1)
 
     @pl.when(step == 0)
     def _():
-        chain.load()
-        own_load.start()
-        greet(neighbours(size) + chain.neighbours)
-        chain.step(0)
-        scatter.fill(pairs)
+        scatter.load(operands)
+        greet(neighbours(size))
+        scatter.fill(operands)
 
     attend_backward_head(
         grouping, head_size, block, state_ref, weight_ref, raw_ref, mixed_ref, total_ref, few_cosines_ref,
@@ -829,27 +880,7 @@
             )
 
         over_pieces(output_ref.shape[0], finish)
-        own_load.wait()
-        chain.wait(0)
-        from_under, from_above = chain.arrives(0)
-
-        @pl.when(from_under)
-        def _():
-            def add(piece):
-                own_block[piece, :] = add_rounded(own_block[piece, :], chain.up[1, piece, :])
-
-            over_pieces(own_block.shape[0], add)
-
-        @pl.when(from_above)
-        def _():
-            def add(piece):
-                own_block[piece, :] = add_rounded(own_block[piece, :], chain.down[1, piece, :])
-
-            over_pieces(own_block.shape[0], add)
-
-        chain_total_ref[...] = own_block[...]
         scatter.drain()
-        chain.drain()
 
 
 def attend_backward_head(
@@ -916,7 +947,7 @@
 
 def attention_backward(
     state_rows, weight, weight_start, raw, mixed, totals, tables, query_gain, key_gain, heads, grouping,
-    triples, hidden_state, chain_arrays, own_block, sizes, collective_id,
+    triples, hidden_state, size, collective_id,
 ):
     total_rows, depth = state_rows.shape
     head_size = query_gain.shape[0]
@@ -925,26 +956,13 @@
     out_width = grouping * head_size
     block = min(256, SEQUENCE_LENGTH)
     first_block = weight_start // out_width
-    data_size, size = sizes
-    chips = data_size // 2
     single = pl.Buffered(1)
     table = pl.BlockSpec(tables[0].shape, lambda s, h: (0, 0))
     gain = pl.BlockSpec((1, head_size), lambda s, h: (0, 0))
     elements = heads * grouping * total_rows * SEQUENCE_LENGTH // 2
     whole_rows = pltpu.VMEM((SEQUENCE_LENGTH, head_size), jnp.float32)
-    in_specs = []
-    operands = []
-    for left, other_weight, first_column in triples:
-        part = left.shape[1]
-        in_specs += [
-            pl.BlockSpec(left.shape, lambda s, h: (0, 0), pipeline_mode=single),
-            pl.BlockSpec(
-                (other_weight.shape[0], part),
-                lambda s, h, at=first_column // part: (0, at),
-                pipeline_mode=single,
-            ),
-        ]
-        operands += [left, other_weight]
+    operands = [array for left, other_weight, _ in triples for array in (left, other_weight)]
+    in_specs = [pl.BlockSpec(memory_space=pl.ANY)] * len(operands)
     in_specs += [
         pl.BlockSpec((SEQUENCE_LENGTH, depth), lambda s, h: (s, 0), pipeline_mode=single),
         pl.BlockSpec((depth, out_width), lambda s, h: (0, first_block + h)),
@@ -956,28 +974,27 @@
         gain,
         gain,
         pl.BlockSpec(hidden_state.shape, lambda s, h: (0, 0), pipeline_mode=single),
-    ] + [pl.BlockSpec(memory_space=pl.ANY)] * 5
+    ]
     operands += [
         state_rows, weight, raw, mixed, totals, *tables, query_gain.reshape(1, -1), key_gain.reshape(1, -1),
-        hidden_state, *chain_arrays, own_block,
+        hidden_state,
     ]
     return pl.pallas_call(
         functools.partial(
-            attention_backward_kernel, size, chips, grouping, head_size, block, len(triples)
+            attention_backward_kernel, size, grouping, head_size, block,
+            tuple(first for _, _, first in triples),
         ),
         grid=(sequences, heads),
         out_shape=[
             jax.ShapeDtypeStruct((total_rows, heads * width), jnp.bfloat16),
             jax.ShapeDtypeStruct((8, head_size), jnp.float32),
             jax.ShapeDtypeStruct(hidden_state.shape, jnp.bfloat16),
-            jax.ShapeDtypeStruct(own_block.shape, jnp.bfloat16),
         ],
         in_specs=in_specs,
         out_specs=[
             pl.BlockSpec((SEQUENCE_LENGTH, width), lambda s, h: (s, h)),
             pl.BlockSpec((8, head_size), lambda s, h: (0, 0)),
             pl.BlockSpec(hidden_state.shape, lambda s, h: (0, 0)),
-            pl.BlockSpec(own_block.shape, lambda s, h: (0, 0)),
         ],
         scratch_shapes=[
             pltpu.VMEM((grouping, SEQUENCE_LENGTH, head_size), jnp.bfloat16),
@@ -990,9 +1007,7 @@
             whole_rows,
             whole_rows,
             *Scatter.scratch(size, *hidden_state.shape),
-            pltpu.VMEM(own_block.shape, jnp.bfloat16),
-            pltpu.SemaphoreType.DMA((1,)),
-            *Chain.scratch(1, *own_block.shape),
+            *[part for left, other, _ in triples for part in Operand.scratch(size, left, other)],
         ],
         compiler_params=pltpu.CompilerParams(
             collective_id=collective_id, has_side_effects=True, vmem_limit_bytes=VMEM_LIMIT
@@ -1199,14 +1214,19 @@
     output_ref[...] = output_total_ref[...].astype(jnp.float32).T
 
 
-def finish_feed_kernel(first_ref, second_ref, gate_ref, up_ref, down_ref):
+def finish_feed_kernel(own_ref, up_ref, down_ref, second_ref, gate_out_ref, up_out_ref, down_out_ref):
     start = 0
-    for total_ref in (first_ref, second_ref):
-        width = total_ref.shape[1] // 3
+    for total_refs in ((own_ref, up_ref, down_ref), (second_ref,)):
+        width = total_refs[0].shape[1] // 3
         part = slice(start, start + width)
-        gate_ref[:, part] = total_ref[:, :width].astype(jnp.float32)
-        up_ref[:, part] = total_ref[:, width : 2 * width].astype(jnp.float32)
-        down_ref[part, :] = total_ref[:, 2 * width :].astype(jnp.float32).T
+
+        def total(index):
+            columns = slice(index * width, (index + 1) * width)
+            return sum(ref[:, columns].astype(jnp.float32) for ref in total_refs)
+
+        gate_out_ref[:, part] = total(0)
+        up_out_ref[:, part] = total(1)
+        down_out_ref[part, :] = total(2).T
         start += width
 
 
@@ -1289,9 +1309,11 @@
     scatter_scratch = Scatter.scratch(size, *local_shape)
     gather_scratch = Gather.scratch(size, *local_shape)
     feed_rows, hidden_state = scatter_call(
-        functools.partial(between_forward_kernel, size, 1),
-        [[(mixed_rows, mixing_full, qkv_columns)]],
+        functools.partial(between_forward_kernel, size),
+        [(mixed_rows, mixing_full, qkv_columns)],
+        size,
         [block_input, feed_gain.reshape(1, -1)],
+        [],
         [gathered_shape, local_float],
         True,
         [own_rows, *scatter_scratch, *gather_scratch],
@@ -1313,10 +1335,14 @@
     chips = sizes[0] // 2
     middle_steps = tuple(range(2, chips - 1))
     chain_block = jax.ShapeDtypeStruct(blocks[0].shape, jnp.bfloat16)
-    state_rows, state_slope, feed_term, up, down = scatter_call(
-        functools.partial(between_backward_kernel, size, chips, middle_steps, 2),
-        [[(slope_first, feed_full[0], 0), (slope_second, later_full, 0)]],
+    state_rows, state_slope, feed_term, rising, falling = scatter_call(
+        functools.partial(between_backward_kernel, size, chips, middle_steps),
+        [(slope_first, feed_full[0], 0), (slope_second, later_full, 0)],
+        size,
         [hidden_state, out_cotangent, feed_gain.reshape(1, -1)],
+        [blocks[chips - step] for step in middle_steps]
+        + [blocks[step] for step in middle_steps]
+        + [up, down, blocks[1], blocks[chips - 1]],
         [
             gathered_shape,
             local_float,
@@ -1328,44 +1354,52 @@
         [
             own_rows,
             row_sum,
+            pltpu.SemaphoreType.DMA((2,)),
             *scatter_scratch,
             *gather_scratch,
             *Chain.scratch(len(middle_steps), *blocks[0].shape),
         ],
         2,
-        [blocks[chips - step] for step in middle_steps]
-        + [blocks[step] for step in middle_steps]
-        + [up, down],
+    )
+    up = lax.ppermute(
+        rising, "dp", [(device, device + 2) for device in range(sizes[0] - 2)]
+    )
+    down = lax.ppermute(
+        falling, "dp", [(device, device - 2) for device in range(2, sizes[0])]
     )
     output_grad = grad_blocks(plain_order, [(state_rows, mixed_rows)]).reshape(model_width, -1)
     output_grad, state_rows = lax.optimization_barrier((output_grad, state_rows))
     output_total = lax.psum_scatter(output_grad, "dp", scatter_dimension=0, tiled=True)
-    qkv_slope, head_terms, block_output, first_total = attention_backward(
+    qkv_slope, head_terms, block_output = attention_backward(
         state_rows, mixing_full, qkv_columns, raw, mixed_rows, totals, tables,
         query_gain, key_gain, heads, grouping,
         [
             (hidden_first, feed_full[0], 2 * first_columns),
             (hidden_second, later_full, 2 * second_columns),
         ],
-        hidden_state, [blocks[1], blocks[chips - 1], up, down], blocks[0], sizes, 4,
+        hidden_state, size, 4,
     )
     mixing_grad = grad_blocks(plain_order, [(mixer_rows, qkv_slope)]).reshape(model_width, -1)
     mixing_grad, qkv_slope = lax.optimization_barrier((mixing_grad, qkv_slope))
     mixing_total = lax.psum_scatter(mixing_grad, "dp", scatter_dimension=0, tiled=True)
     terms_shape = (2 * gain_rows + head_terms.shape[0], head_size)
     input_gradient, terms = scatter_call(
-        functools.partial(last_kernel, sizes, 1),
-        [[(qkv_slope, mixing_full, 0)]],
+        functools.partial(last_kernel, sizes),
+        [(qkv_slope, mixing_full, 0)],
+        size,
         [
             block_input,
             attention_gain.reshape(1, -1),
             state_slope,
             jnp.concatenate([feed_term, head_terms], axis=0),
-        ],
+            mixer_rows,
+        ],
+        [],
         [local_half, jax.ShapeDtypeStruct(terms_shape, jnp.float32)],
         False,
         [
             row_sum,
+            pltpu.VMEM(terms_shape, jnp.float32),
             pltpu.VMEM(terms_shape, jnp.float32),
             pltpu.VMEM((size, *terms_shape), jnp.float32),
             pltpu.VMEM((sizes[0], *terms_shape), jnp.float32),
@@ -1391,7 +1425,7 @@
             jax.ShapeDtypeStruct((block_width, hidden_columns), jnp.float32),
             jax.ShapeDtypeStruct((hidden_columns, block_width), jnp.float32),
         ],
-        first_total, second_total,
+        blocks[0], up, down, second_total,
     )
     return (
         block_output,
@@ -1442,6 +1476,4 @@
         P("tensor", "dp"),
     )
 
-    return jax.shard_map(
-        per_device, mesh=mesh, in_specs=in_specs, out_specs=out_specs, check_vma=False
-    )
+    return jax.shard_map(per_device, mesh=mesh, in_specs=in_specs, out_specs=out_specs, check_vma=False)

time: 605 us -> 621 us (1.026)
  starting transfers between devices: 3.83 us -> 10.3 us
    ppermute x0 -> x2, starting transfers between devices: none -> 6.49 us  [the longest x1 4.98 us: per_device(): lax.ppermute(rising, 'dp', [(device, device + 2) for device in range(size...]
  transfers between devices with their start and end apart: 9 -> 11, of which waited for: 5 -> 5; matrix products, arithmetic and copies ran while one was open for 1% -> 1% of each run, Pallas kernels for 63% -> 62%
where the time goes in v6:
time: 621 us; the launch traced here: 620 us
  Pallas kernels  495 us (80%)
  waiting for transfers between devices  89 us (14%)
  between operations  14.3 us (2%)
  starting transfers between devices  10.3 us (2%)
  local copies, waits for them, and re-layouts  8.67 us (1%)
    pallas_call x3, Pallas kernels, scatter_call(): pl.pallas_call(functools.partial(body, tuple((first for _, _, first in tr...  247 us
    pallas_call x1, Pallas kernels, gather_rows(): pl.pallas_call(functools.partial(gather_kernel, size, count), out_shape=[...  75.2 us
    reduce_scatter x1, waiting for transfers between devices, per_device(): lax.psum_scatter(second_grad, 'dp', scatter_dimension=0, tiled=True)  64 us
    pallas_call x5, Pallas kernels, grad_blocks(): pl.pallas_call(functools.partial(grad_kernel, len(pairs), other is not No...  59.5 us
    pallas_call x1, Pallas kernels, attention_backward(): pl.pallas_call(functools.partial(attention_backward_kernel, size, groupin...  44.7 us
    pallas_call x2, Pallas kernels, feed_half(): pl.pallas_call(functools.partial(feed_half_kernel, half, tile), grid=(tot...  36.9 us
    pallas_call x1, Pallas kernels, attention_forward(): pl.pallas_call(functools.partial(attention_forward_kernel, grouping, head...  18.5 us
    pallas_call x4, Pallas kernels, whole_call(): pl.pallas_call(body, out_shape=shapes, in_specs=[pl.BlockSpec(memory_spac...  13.3 us
  transfers between devices with their start and end apart: 11, of which 5 were waited for; matrix products, arithmetic and copies ran while one was open for 1% of the time, Pallas kernels for 62%

profile of v6, /device:TPU:0, one launch (start us, length us, event | category | flops | bytes accessed | tf_op | source)
XLA Modules:
  0.0 620.3 jit_solution(14431041100074869827)
XLA Ops:
  7.2 0.0 all-gather.4.cloned.1.call-start
  7.2 2.2 shard_map.246
  9.4 0.0 all-gather.6.cloned.1.call-start
  9.5 3.4 shard_map.248
  12.9 0.0 all-gather.8.cloned.1.call-start
  12.9 0.7 all-gather.8.cloned.1.call-update
  13.6 0.0 reduce-scatter.6.cloned.1.call-start
  13.7 0.3 fusion
  14.0 1.3 fusion.2.refs_0_
  15.3 75.2 %gather_rows.1 = (bf16[1024,2048]{1,0:T(8,128)(2,1)}, bf16[1024,2048]{1,0:T(8,128)(2,1)}) custom-call(bf16[256,2048]{1,0:T(8,128)(2,1)} %fusion.2.refs_0_, bf16[256,2048]{1,0:T(8,128)(2,1)} %refs_5_.1), custom_call_target="tpu_custom_call" | custom-call | bytes 125829120 | tf_op jit(solution)/shard_map/gather_rows/pallas_call | solution.py:169
  90.4 0.5 broadcast_add_fusion.order_ref
  91.0 18.5 %attention_forward.1 = (f32[1024,1024]{1,0:T(8,128)}, bf16[1024,512]{1,0:T(8,128)(2,1)}, f32[2,2,1024]{2,1,0:T(2,128)}) custom-call(bf16[1024,2048]{1,0:T(8,128)(2,1)} %get-tuple-element.58.rows_ref.refs_0_.refs_6_, bf16[2048,1536]{1,0:T(8,128)(2,1)} %all-gather.4.cloned.1.call-done.weight_ref.refs_1_.refs_5_, ...), custom_call_target="tpu_custom_call" | custom-call | flops 5368709120 | bytes 8388608 | tf_op jit(solution)/shard_map/attention_forward/pallas_call | solution.py:798
  109.5 77.6 %shard_map.247 = (bf16[1024,2048]{1,0:T(8,128)(2,1)}, f32[256,2048]{1,0:T(8,128)}) custom-call(bf16[1024,512]{1,0:T(8,128)(2,1)} %get-tuple-element.59.refs_0_.refs_1_.refs_7_, bf16[2048,1536]{1,0:T(8,128)(2,1)} %all-gather.4.cloned.1.call-done.weight_ref.refs_1_.refs_5_, bf16[256,2048]{1,0:T(8,128)(2,1)} %refs_2_.3, f32[1,2048]{1,0:T(1,128)} %bitcast.18), custom_call_target="tpu_custom_call" | custom-call | flops 2147483648 | bytes 150000000 | tf_op jit(solution)/shard_map/pallas_call | solution.py:663
  187.1 8.2 %all-gather.6.cloned.1.call-done.weight_ref.refs_1_ = bf16[2048,3072]{1,0:T(8,128)(2,1)} async-done(((bf16[256,3072]{1,0:T(8,128)(2,1)}), bf16[2048,3072]{1,0:T(8,128)(2,1)}) %all-gather.6.cloned.1.call-update) | async-done | bytes 12582928 | tf_op jit(solution)/shard_map/all_gather | solution.py:1290
  195.3 23.5 %feed_half.2 = (bf16[1024,1024]{1,0:T(8,128)(2,1)}, bf16[1024,2048]{1,0:T(8,128)(2,1)}) custom-call(bf16[1024,2048]{1,0:T(8,128)(2,1)} %get-tuple-element.60.rows_ref.refs_0_, bf16[1024,2048]{1,0:T(8,128)(2,1)} %get-tuple-element.61.cotangent_ref.refs_2_, bf16[2048,3072]{1,0:T(8,128)(2,1)} %all-gather.6.cloned.1.call-done.weight_ref.refs_1_), custom_call_target="tpu_custom_call" | custom-call | flops 12884901888 | bytes 20971520 | tf_op jit(solution)/shard_map/feed_half/pallas_call | solution.py:1050
  218.7 12.6 %grad_blocks.5 = bf16[4,256,3072]{2,1,0:T(8,128)(2,1)} custom-call(s32[4]{0:T(128)} %broadcast_add_fusion.order_ref, bf16[1024,2048]{1,0:T(8,128)(2,1)} %get-tuple-element.60.rows_ref.refs_0_, bf16[1024,2048]{1,0:T(8,128)(2,1)} %get-tuple-element.64.refs_1_.refs_0_, bf16[1024,2048]{1,0:T(8,128)(2,1)} %get-tuple-element.61.cotangent_ref.refs_2_, ...), custom_call_target="tpu_custom_call" | custom-call | flops 6442450944 | bytes 16777216 | tf_op jit(solution)/shard_map/grad_blocks/pallas_call | solution.py:1140
  231.3 0.3 collective-permute-start
  231.6 0.5 broadcast_add_fusion.1.order_ref
  232.2 10.5 %collective-permute-done.refs_4_ = bf16[4,256,3072]{2,1,0:T(8,128)(2,1)} collective-permute-done((bf16[4,256,3072]{2,1,0:T(8,128)(2,1)}, bf16[4,256,3072]{2,1,0:T(8,128)(2,1)}, u32[]{:S(2)}, u32[]{:S(2)}) %collective-permute-start) | collective-permute-done | bytes 6291488 | tf_op jit(solution)/shard_map/ppermute | solution.py:1167
  242.6 13.6 %grad_blocks.6 = (bf16[256,3072]{1,0:T(8,128)(2,1)}, bf16[256,3072]{1,0:T(8,128)(2,1)}, bf16[256,3072]{1,0:T(8,128)(2,1)}, bf16[256,3072]{1,0:T(8,128)(2,1)}) custom-call(s32[4]{0:T(128)} %broadcast_add_fusion.1.order_ref, bf16[1024,2048]{1,0:T(8,128)(2,1)} %get-tuple-element.60.rows_ref.refs_0_, bf16[1024,2048]{1,0:T(8,128)(2,1)} %get-tuple-element.64.refs_1_.refs_0_, ...), custom_call_target="tpu_custom_call" | custom-call | flops 6442450944 | bytes 16777216 | tf_op jit(solution)/shard_map/grad_blocks/pallas_call | solution.py:1140
  256.3 1.4 collective-permute-start.1
  257.7 1.8 collective-permute-start.2
  259.5 0.3 all-gather.8.cloned.1.call-done.weight_ref.refs_3_
  259.8 13.4 %feed_half.3 = (bf16[1024,512]{1,0:T(8,128)(2,1)}, bf16[1024,1024]{1,0:T(8,128)(2,1)}) custom-call(bf16[1024,2048]{1,0:T(8,128)(2,1)} %get-tuple-element.60.rows_ref.refs_0_, bf16[1024,2048]{1,0:T(8,128)(2,1)} %get-tuple-element.61.cotangent_ref.refs_2_, bf16[2048,1536]{1,0:T(8,128)(2,1)} %all-gather.8.cloned.1.call-done.weight_ref.refs_3_), custom_call_target="tpu_custom_call" | custom-call | flops 6442450944 | bytes 14680064 | tf_op jit(solution)/shard_map/feed_half/pallas_call | solution.py:1050
  273.3 0.5 iota.12.order_ref
  273.8 13.7 %grad_blocks.7 = bf16[8,256,1536]{2,1,0:T(8,128)(2,1)} custom-call(s32[8]{0:T(128)} %iota.12.order_ref, bf16[1024,2048]{1,0:T(8,128)(2,1)} %get-tuple-element.60.rows_ref.refs_0_, bf16[1024,1024]{1,0:T(8,128)(2,1)} %get-tuple-element.73.refs_1_.refs_2_, bf16[1024,2048]{1,0:T(8,128)(2,1)} %get-tuple-element.61.cotangent_ref.refs_2_, ...), custom_call_target="tpu_custom_call" | custom-call | flops 6442450944 | bytes 17825792 | tf_op jit(solution)/shard_map/grad_blocks/pallas_call | solution.py:1140
  287.4 4.7 collective-permute-done.1.refs_9_
  292.2 1.2 copy-done.6
  293.3 91.9 %shard_map.249 = (bf16[1024,2048]{1,0:T(8,128)(2,1)}, f32[256,2048]{1,0:T(8,128)}, f32[16,128]{1,0:T(8,128)}, bf16[256,3072]{1,0:T(8,128)(2,1)}, bf16[256,3072]{1,0:T(8,128)(2,1)}) custom-call(bf16[1024,2048]{1,0:T(8,128)(2,1)} %get-tuple-element.64.refs_1_.refs_0_, bf16[2048,3072]{1,0:T(8,128)(2,1)} %all-gather.6.cloned.1.call-done.weight_ref.refs_1_, ...), custom_call_target="tpu_custom_call" | custom-call | flops 12884901888 | bytes 150000000 | tf_op jit(solution)/shard_map/pallas_call | solution.py:663
  385.2 0.5 iota.11.order_ref
  385.8 8.8 %grad_blocks.8 = bf16[8,256,512]{2,1,0:T(8,128)(2,1)} custom-call(s32[8]{0:T(128)} %iota.11.order_ref, bf16[1024,2048]{1,0:T(8,128)(2,1)} %get-tuple-element.79.refs_0_.refs_4_, bf16[1024,512]{1,0:T(8,128)(2,1)} %get-tuple-element.59.refs_0_.refs_1_.refs_7_), custom_call_target="tpu_custom_call" | custom-call | flops 2147483648 | bytes 7340032 | tf_op jit(solution)/shard_map/grad_blocks/pallas_call | solution.py:1140
  394.6 0.0 reduce-scatter.4.cloned.1.call-start
  394.6 44.7 %attention_backward.1 = (bf16[1024,1024]{1,0:T(8,128)(2,1)}, f32[8,128]{1,0:T(8,128)}, bf16[256,2048]{1,0:T(8,128)(2,1)}) custom-call(bf16[1024,1024]{1,0:T(8,128)(2,1)} %get-tuple-element.63.refs_3_.refs_0_, bf16[2048,3072]{1,0:T(8,128)(2,1)} %all-gather.6.cloned.1.call-done.weight_ref.refs_1_, bf16[1024,512]{1,0:T(8,128)(2,1)} %get-tuple-element.71.refs_3_.refs_2_, ...), custom_call_target="tpu_custom_call" | custom-call | flops 4831838208 | bytes 100000000 | tf_op jit(solution)/shard_map/attention_backward/pallas_call | solution.py:982
  439.3 0.5 iota.13.order_ref
  439.8 10.8 %grad_blocks.9 = bf16[8,256,1024]{2,1,0:T(8,128)(2,1)} custom-call(s32[8]{0:T(128)} %iota.13.order_ref, bf16[1024,2048]{1,0:T(8,128)(2,1)} %get-tuple-element.58.rows_ref.refs_0_.refs_6_, bf16[1024,1024]{1,0:T(8,128)(2,1)} %get-tuple-element.84.refs_1_.refs_0_), custom_call_target="tpu_custom_call" | custom-call | flops 4294967296 | bytes 10485760 | tf_op jit(solution)/shard_map/grad_blocks/pallas_call | solution.py:1140
  450.7 0.0 reduce-scatter.8.cloned.1.call-start
  450.8 0.5 reduce-scatter.8.cloned.1.call-update
  451.3 5.0 collective-permute-start.3
  456.3 1.5 collective-permute-start.4
  457.8 0.6 pad_maximum_fusion.refs_5_
  458.4 77.3 %shard_map.250 = (bf16[256,2048]{1,0:T(8,128)(2,1)}, f32[40,128]{1,0:T(8,128)}) custom-call(bf16[1024,1024]{1,0:T(8,128)(2,1)} %get-tuple-element.84.refs_1_.refs_0_, bf16[2048,1536]{1,0:T(8,128)(2,1)} %all-gather.4.cloned.1.call-done.weight_ref.refs_1_.refs_5_, bf16[256,2048]{1,0:T(8,128)(2,1)} %refs_2_.3, f32[1,2048]{1,0:T(1,128)} %bitcast.20, ...), custom_call_target="tpu_custom_call" | custom-call | flops 4294967296 | bytes 150000000 | tf_op jit(solution)/shard_map/pallas_call | solution.py:663
  535.7 1.3 slice_bitcast_fusion.2
  537.0 1.3 slice_bitcast_fusion
  538.3 2.3 shard_map.251
  540.6 64.0 %reduce-scatter.8.cloned.1.call-done.second_ref = bf16[256,1536]{1,0:T(8,128)(2,1)} async-done(((bf16[2048,1536]{1,0:T(8,128)(2,1)}), bf16[256,1536]{1,0:T(8,128)(2,1)}) %reduce-scatter.8.cloned.1.call-update) | async-done | bytes 786448 | tf_op jit(solution)/shard_map/reduce_scatter | solution.py:1334
  604.6 5.4 shard_map.252
  610.1 2.4 copy.30
  612.5 1.0 copy.31
  (24 shorter events, 0.1 us)
Async XLA Ops:
  7.2 83.8 %all-gather.4.cloned.1.call-start = ((), (), s32[]{:S(2)}) async-start(), calls=%async_computation.3 | async-start | bytes 7077888 | tf_op jit(solution)/shard_map/all_gather | solution.py:1281
  9.4 4.3 copy-start
  9.4 185.8 %all-gather.6.cloned.1.call-start = ((), (), s32[]{:S(2)}) async-start(), calls=%async_computation.4 | async-start | bytes 14155776 | tf_op jit(solution)/shard_map/all_gather | solution.py:1290
  12.8 1.1 copy-start.3
  12.9 246.9 %all-gather.8.cloned.1.call-start = ((), (), s32[]{:S(2)}) async-start(), calls=%async_computation.5 | async-start | bytes 7077888 | tf_op jit(solution)/shard_map/all_gather | solution.py:1290
  13.6 524.7 %reduce-scatter.6.cloned.1.call-start = ((), (), s32[]{:S(2)}) async-start(), calls=%async_computation.7 | async-start | bytes 2359296 | tf_op jit(solution)/shard_map/reduce_scatter | solution.py:1372
  231.3 11.3 %collective-permute-start = (bf16[4,256,3072]{2,1,0:T(8,128)(2,1)}, bf16[4,256,3072]{2,1,0:T(8,128)(2,1)}, u32[]{:S(2)}, u32[]{:S(2)}) collective-permute-start(bf16[4,256,3072]{2,1,0:T(8,128)(2,1)} %grad_blocks.5), channel_id=1, source_target_pairs={{0,4},{4,0},{8,12},{12,8},{16,20},{20,16},{24,28},{28,24},{1,5},{5... | collective-permute-start | bytes 18874376 | tf_op jit(solution)/shard_map/ppermute | solution.py:1167
  256.3 35.9 %collective-permute-start.1 = (bf16[256,3072]{1,0:T(8,128)(2,1)}, bf16[256,3072]{1,0:T(8,128)(2,1)S(1)}, u32[]{:S(2)}, u32[]{:S(2)}) collective-permute-start(bf16[256,3072]{1,0:T(8,128)(2,1)} %get-tuple-element.77.refs_12_), channel_id=1, source_target_pairs={{0,8},{4,12},{1,9},{5,13},{2,10},{6,14},{3,11},{7,15}} | collective-permute-start | bytes 4718600 | tf_op jit(solution)/shard_map/ppermute | solution.py:1173
  257.7 34.5 %collective-permute-start.2 = (bf16[256,3072]{1,0:T(8,128)(2,1)}, bf16[256,3072]{1,0:T(8,128)(2,1)}, u32[]{:S(2)}, u32[]{:S(2)}) collective-permute-start(bf16[256,3072]{1,0:T(8,128)(2,1)} %get-tuple-element.76.refs_11_), channel_id=1, source_target_pairs={{24,16},{28,20},{25,17},{29,21},{26,18},{30,22},{27,19},{31,23}} | collective-permute-start | bytes 4718600 | tf_op jit(solution)/shard_map/ppermute | solution.py:1174
  292.2 1.2 copy-start.6
  394.6 143.7 %reduce-scatter.4.cloned.1.call-start = ((), (), s32[]{:S(2)}) async-start(), calls=%async_computation.6 | async-start | bytes 4718592 | tf_op jit(solution)/shard_map/reduce_scatter | solution.py:1384
  450.7 7.1 %copy-start.4 = (f32[16,128]{1,0:T(8,128)S(1)}, f32[16,128]{1,0:T(8,128)}, u32[]{:S(2)}) copy-start(f32[16,128]{1,0:T(8,128)} %get-tuple-element.86) | copy-start | bytes 24580
  450.7 7.1 %copy-start.5 = (f32[8,128]{1,0:T(8,128)S(1)}, f32[8,128]{1,0:T(8,128)}, u32[]{:S(2)}) copy-start(f32[8,128]{1,0:T(8,128)} %get-tuple-element.87) | copy-start | bytes 12292
  450.7 153.9 %reduce-scatter.8.cloned.1.call-start = ((), (), s32[]{:S(2)}) async-start(), calls=%async_computation.8 | async-start | bytes 7077888 | tf_op jit(solution)/shard_map/reduce_scatter | solution.py:1334
  451.3 89.3 %collective-permute-start.3 = (bf16[256,3072]{1,0:T(8,128)(2,1)}, bf16[256,3072]{1,0:T(8,128)(2,1)S(1)}, u32[]{:S(2)}, u32[]{:S(2)}) collective-permute-start(bf16[256,3072]{1,0:T(8,128)(2,1)} %get-tuple-element.97), channel_id=1, source_target_pairs={{0,8},{4,12},{8,16},{12,20},{16,24},{20,28},{1,9},{5,13},{9,17},{1... | collective-permute-start | bytes 4718600 | tf_op jit(solution)/shard_map/ppermute | solution.py:1364
  456.3 84.3 %collective-permute-start.4 = (bf16[256,3072]{1,0:T(8,128)(2,1)}, bf16[256,3072]{1,0:T(8,128)(2,1)}, u32[]{:S(2)}, u32[]{:S(2)}) collective-permute-start(bf16[256,3072]{1,0:T(8,128)(2,1)} %get-tuple-element.98), channel_id=1, source_target_pairs={{8,0},{12,4},{16,8},{20,12},{24,16},{28,20},{9,1},{13,5},{17,9},{2... | collective-permute-start | bytes 4718600 | tf_op jit(solution)/shard_map/ppermute | solution.py:1367
  540.6 64.0 %copy-start.1 = (bf16[256,3072]{1,0:T(8,128)(2,1)}, bf16[256,3072]{1,0:T(8,128)(2,1)S(1)}, u32[]{:S(2)}) copy-start(bf16[256,3072]{1,0:T(8,128)(2,1)S(1)} %collective-permute-done.3.up_ref) | copy-start | bytes 4718596
  610.1 2.4 copy-start.2
Sparse Core Ops, SparseCore 0:
  10.2 67.4 all-gather.3
  79.9 115.3 all-gather.5
  196.9 62.8 all-gather.7
  394.7 35.7 reduce-scatter.5
  450.8 83.5 reduce-scatter.3
  536.5 68.0 reduce-scatter.7

commit v7 on v6

--- a/solution.py
+++ b/solution.py
@@ -70,20 +70,26 @@
 
 
 class Gather:
-    def __init__(self, size, own_ref, out_ref, held_ref, send_sem, recv_sem, local_sem):
+    def __init__(
+        self, size, own_ref, out_ref, turned_out_ref, held_ref, turned_ref, send_sem, recv_sem, local_sem, turned_sem
+    ):
         self.size, self.own, self.out, self.held = size, own_ref, out_ref, held_ref
+        self.turned_out, self.turned = turned_out_ref, turned_ref
         self.send_sem, self.recv_sem, self.local_sem = send_sem, recv_sem, local_sem
+        self.turned_sem = turned_sem
         self.me = lax.axis_index("tensor")
         self.rows = own_ref.shape[0]
-        self.copies, self.stores = [], []
+        self.copies, self.stores, self.turns = [], [], []
 
     @staticmethod
     def scratch(size, rows, columns):
-        sends, local = (6, 7) if size == 4 else (size - 1, size)
+        sends, local = (6, 8) if size == 4 else (size - 1, size)
         return [
             pltpu.VMEM((size, rows, columns), jnp.bfloat16),
+            pltpu.VMEM((columns, size * rows), jnp.bfloat16),
             pltpu.SemaphoreType.DMA((sends,)),
             pltpu.SemaphoreType.DMA((sends,)),
+            pltpu.SemaphoreType.DMA((local,)),
             pltpu.SemaphoreType.DMA((local,)),
         ]
 
@@ -95,32 +101,53 @@
         return copy
 
     def store(self, source, start, count):
-        target = self.out.at[pl.ds(pl.multiple_of(start, count), count)]
-        copy = pltpu.make_async_copy(source, target, self.local_sem.at[len(self.stores)])
+        piece = pl.ds(pl.multiple_of(start, count), count)
+        copy = pltpu.make_async_copy(source, self.out.at[piece], self.local_sem.at[len(self.stores)])
         copy.start()
         self.stores.append(copy)
+        width = min(256, self.turned.shape[0])
+
+        def turn_part(index, carry):
+            columns = pl.ds(pl.multiple_of(index * width, width), width)
+            self.turned[columns, piece] = source[:, columns].T
+            return carry
+
+        lax.fori_loop(0, self.turned.shape[0] // width, turn_part, 0)
+        turn_copy = pltpu.make_async_copy(
+            self.turned.at[:, piece], self.turned_out.at[:, piece], self.turned_sem.at[len(self.turns)]
+        )
+        turn_copy.start()
+        self.turns.append(turn_copy)
 
     def start(self):
         own, held, rows = self.own, self.held, self.rows
         if self.size != 4:
             for peer in other_members("tensor", self.size):
                 self.send(own, held.at[self.me], peer)
+            return
+        beside, below, _ = square_peers(self.me)
+        half = rows // 2
+        first, second = pl.ds(0, half), pl.ds(half, half)
+        self.send(own.at[first], held.at[self.me, first], beside)
+        self.send(own.at[second], held.at[self.me, second], below)
+        self.send(own.at[second], held.at[self.me, second], beside)
+        self.send(own.at[first], held.at[self.me, first], below)
+
+    def forward(self):
+        own, held, rows = self.own, self.held, self.rows
+        if self.size != 4:
             self.store(own, self.me * rows, rows)
             return
         beside, below, _ = square_peers(self.me)
         half = rows // 2
         first, second = pl.ds(0, half), pl.ds(half, half)
-        x_first = self.send(own.at[first], held.at[self.me, first], beside)
-        y_second = self.send(own.at[second], held.at[self.me, second], below)
-        self.send(own.at[second], held.at[self.me, second], beside)
-        self.send(own.at[first], held.at[self.me, first], below)
-        self.store(own, self.me * rows, rows)
+        x_first, y_second = self.copies[:2]
+        self.store(own.at[first], self.me * rows, half)
+        self.store(own.at[second], self.me * rows + half, half)
         x_first.wait_recv()
         self.send(held.at[beside, first], held.at[beside, first], below)
         y_second.wait_recv()
         self.send(held.at[below, second], held.at[below, second], beside)
-        self.store(held.at[beside, first], beside * rows, half)
-        self.store(held.at[below, second], below * rows + half, half)
 
     def finish(self):
         held, rows = self.held, self.rows
@@ -134,6 +161,8 @@
             half = rows // 2
             first, second = pl.ds(0, half), pl.ds(half, half)
             x_second, y_first, y_pass, x_pass = self.copies[2:]
+            self.store(held.at[beside, first], beside * rows, half)
+            self.store(held.at[below, second], below * rows + half, half)
             x_second.wait_recv()
             self.store(held.at[beside, second], beside * rows + half, half)
             y_first.wait_recv()
@@ -144,18 +173,20 @@
             self.store(held.at[across, second], across * rows + half, half)
         for copy in self.copies:
             copy.wait_send()
-        for copy in self.stores:
+        for copy in self.stores + self.turns:
             copy.wait()
 
 
 def gather_kernel(size, count, *refs):
-    own_refs, out_refs, rest = refs[:count], refs[count : 2 * count], refs[2 * count :]
+    own_refs, out_refs, rest = refs[:count], refs[count : 3 * count], refs[3 * count :]
     greet(neighbours(size))
     gathers = [
-        Gather(size, own_refs[k], out_refs[k], *rest[4 * k : 4 * k + 4]) for k in range(count)
+        Gather(size, own_refs[k], *out_refs[2 * k : 2 * k + 2], *rest[6 * k : 6 * k + 6])
+        for k in range(count)
     ]
     for gather in gathers:
         gather.start()
+        gather.forward()
     for gather in gathers:
         gather.finish()
 
@@ -164,13 +195,18 @@
     count = len(arrays)
     rows, columns = arrays[0].shape
     scratch = []
+    out_shape = []
     for _ in arrays:
         scratch += Gather.scratch(size, rows, columns)
+        out_shape += [
+            jax.ShapeDtypeStruct((size * rows, columns), jnp.bfloat16),
+            jax.ShapeDtypeStruct((columns, size * rows), jnp.bfloat16),
+        ]
     return pl.pallas_call(
         functools.partial(gather_kernel, size, count),
-        out_shape=[jax.ShapeDtypeStruct((size * rows, columns), a.dtype) for a in arrays],
+        out_shape=out_shape,
         in_specs=[pl.BlockSpec(memory_space=pltpu.VMEM)] * count,
-        out_specs=[pl.BlockSpec(memory_space=pl.ANY)] * count,
+        out_specs=[pl.BlockSpec(memory_space=pl.ANY)] * len(out_shape),
         scratch_shapes=scratch,
         compiler_params=pltpu.CompilerParams(
             collective_id=collective_id, has_side_effects=True, vmem_limit_bytes=VMEM_LIMIT
@@ -307,7 +343,7 @@
             for operand in operands:
                 operand.left_copy(slot, self.owner(slot)).start()
 
-    def fill(self, operands, look=None):
+    def fill(self, operands, look=None, slots=None):
         rows = self.rows
 
         def step(slot, carry):
@@ -325,7 +361,7 @@
                 pl.when(slot == at)(self.copies[index].start)
             return carry
 
-        lax.fori_loop(0, self.size, step, 0)
+        lax.fori_loop(*(slots or (0, self.size)), step, 0)
 
     def relay(self):
         if self.size != 4:
@@ -507,10 +543,10 @@
 
 def between_forward_kernel(size, first_columns, *refs):
     operands, refs = split_operands(refs, size, first_columns)
-    input_ref, gain_ref, gathered_ref, state_ref, own_ref = refs[:5]
+    input_ref, gain_ref, gathered_ref, turned_ref, state_ref, own_ref = refs[:6]
     buffers = 5 if size == 4 else 4
-    scatter = Scatter(size, *refs[5 : 5 + buffers])
-    gather = Gather(size, own_ref, gathered_ref, *refs[5 + buffers :])
+    scatter = Scatter(size, *refs[6 : 6 + buffers])
+    gather = Gather(size, own_ref, gathered_ref, turned_ref, *refs[6 + buffers :])
     scatter.load(operands)
     greet(neighbours(size))
     scatter.fill(operands)
@@ -524,6 +560,7 @@
 
     over_pieces(own_ref.shape[0], norm)
     gather.start()
+    gather.forward()
     gather.finish()
     scatter.drain()
 
@@ -533,13 +570,14 @@
     state_ref, cotangent_ref, gain_ref = refs[:3]
     chain_count = 2 * len(steps) + 2
     chain_refs, last_refs, refs = refs[3 : 3 + chain_count], refs[3 + chain_count : 5 + chain_count], refs[5 + chain_count :]
-    gathered_ref, slope_ref, term_ref, rising_ref, falling_ref, own_ref, sum_ref, last_sem = refs[:8]
+    gathered_ref, gathered_turned_ref, slope_ref, term_ref, rising_ref, falling_ref = refs[:6]
+    own_ref, sum_ref, last_sem = refs[6:9]
     buffers = 5 if size == 4 else 4
-    scatter = Scatter(size, *refs[8 : 8 + buffers])
-    gather = Gather(size, own_ref, gathered_ref, *refs[8 + buffers : 12 + buffers])
+    scatter = Scatter(size, *refs[9 : 9 + buffers])
+    gather = Gather(size, own_ref, gathered_ref, gathered_turned_ref, *refs[9 + buffers : 15 + buffers])
     chain = Chain(
         chips, steps, chain_refs[: len(steps)], chain_refs[len(steps) : -2], *chain_refs[-2:],
-        *refs[12 + buffers :],
+        *refs[15 + buffers :],
     )
     last_loads = [
         pltpu.make_async_copy(source, target, last_sem.at[index])
@@ -550,8 +588,9 @@
     for load in last_loads:
         load.start()
     greet(neighbours(size) + chain.neighbours)
+    scatter.fill(operands, slots=(0, 1))
     chain.step(0)
-    scatter.fill(operands)
+    scatter.fill(operands, slots=(1, size))
     scatter.relay()
     sum_ref[...] = jnp.zeros_like(sum_ref)
     scatter.collect()
@@ -572,6 +611,7 @@
     over_pieces(own_ref.shape[0], norm)
     gather.start()
     store_row(term_ref, sum_ref)
+    gather.forward()
     chain.wait(0)
     for index in range(1, len(steps)):
         chain.step(index)
@@ -659,7 +699,7 @@
     in_specs += [far_spec] * len(far)
     out_specs = [pl.BlockSpec(out.shape, lambda i: (0, 0)) for out in outs]
     if gathered:
-        out_specs[0] = far_spec
+        out_specs[:2] = [far_spec] * 2
     return pl.pallas_call(
         functools.partial(body, tuple(first for _, _, first in triples)),
         grid=(1,),
@@ -1021,47 +1061,108 @@
     )(*operands)
 
 
-def feed_half_kernel(half, tile, rows_ref, cotangent_ref, weight_ref, hidden_ref, slope_ref):
-    rows, cotangent = rows_ref[...], cotangent_ref[...]
-
-    def step(index, carry):
-        start = pl.multiple_of(index * tile, tile)
-        gate = simple_product(rows, weight_ref[:, pl.ds(start, tile)])
-        up = simple_product(rows, weight_ref[:, pl.ds(half + start, tile)])
-        back = simple_product(cotangent, weight_ref[:, pl.ds(2 * half + start, tile)])
-        sigmoid = 1.0 / (1.0 + jnp.exp(-gate))
-        gated = gate * sigmoid
-        hidden_ref[:, pl.ds(start, tile)] = (gated * up).astype(jnp.bfloat16)
-        slope_ref[:, pl.ds(start, tile)] = (
-            back * up * sigmoid * (1.0 + gate * (1.0 - sigmoid))
-        ).astype(jnp.bfloat16)
-        slope_ref[:, pl.ds(half + start, tile)] = (back * gated).astype(jnp.bfloat16)
+def feed_half_kernel(
+    half, tile, block, rows_far, cotangent_far, weight_far, hidden_far, slope_far,
+    rows_ref, cotangent_ref, weight_ref, hidden_ref, slope_ref, row_sem, weight_sem, out_sem,
+):
+    total = rows_ref.shape[0]
+    blocks = total // block
+    tiles = half // tile
+
+    def row_copies(index):
+        piece = pl.ds(pl.multiple_of(index * block, block), block)
+        return [
+            pltpu.make_async_copy(far.at[piece], ref.at[piece], row_sem.at[at, index])
+            for at, (far, ref) in enumerate(((rows_far, rows_ref), (cotangent_far, cotangent_ref)))
+        ]
+
+    def weight_copies(index):
+        copies = []
+        for part in range(3):
+            columns = pl.ds(pl.multiple_of(part * half + index * tile, tile), tile)
+            copies.append(
+                pltpu.make_async_copy(
+                    weight_far.at[:, columns], weight_ref.at[part, index], weight_sem.at[part, index]
+                )
+            )
+        return copies
+
+    def out_copies(index):
+        piece = pl.ds(pl.multiple_of(index * block, block), block)
+        return [
+            pltpu.make_async_copy(ref.at[piece], far.at[piece], out_sem.at[at, index])
+            for at, (far, ref) in enumerate(((hidden_far, hidden_ref), (slope_far, slope_ref)))
+        ]
+
+    for copy in row_copies(0) + weight_copies(0):
+        copy.start()
+    for index in range(1, tiles):
+        for copy in weight_copies(index):
+            copy.start()
+    for index in range(1, blocks):
+        for copy in row_copies(index):
+            copy.start()
+
+    def row_step(row_index, carry):
+        piece = pl.ds(pl.multiple_of(row_index * block, block), block)
+        for copy in row_copies(row_index):
+            copy.wait()
+
+        def step(index, carry):
+            @pl.when(row_index == 0)
+            def _():
+                for copy in weight_copies(index):
+                    copy.wait()
+
+            start = pl.multiple_of(index * tile, tile)
+            rows = rows_ref[piece, :]
+            gate = simple_product(rows, weight_ref[0, index])
+            up = simple_product(rows, weight_ref[1, index])
+            back = simple_product(cotangent_ref[piece, :], weight_ref[2, index])
+            sigmoid = 1.0 / (1.0 + jnp.exp(-gate))
+            gated = gate * sigmoid
+            hidden_ref[piece, pl.ds(start, tile)] = (gated * up).astype(jnp.bfloat16)
+            slope_ref[piece, pl.ds(start, tile)] = (
+                back * up * sigmoid * (1.0 + gate * (1.0 - sigmoid))
+            ).astype(jnp.bfloat16)
+            slope_ref[piece, pl.ds(half + start, tile)] = (back * gated).astype(jnp.bfloat16)
+            return carry
+
+        lax.fori_loop(0, tiles, step, 0)
+        for copy in out_copies(row_index):
+            copy.start()
         return carry
 
-    lax.fori_loop(0, half // tile, step, 0)
+    lax.fori_loop(0, blocks, row_step, 0)
+    for index in range(blocks):
+        for copy in out_copies(index):
+            copy.wait()
 
 
 def feed_half(rows, cotangent, weight):
     total_rows, depth = rows.shape
+    block = min(512, total_rows)
     half = weight.shape[1] // 3
-    block = min(512, total_rows)
     tile = 256 if half % 256 == 0 else 128
-    row_block = pl.BlockSpec((block, depth), lambda i: (i, 0))
+    blocks, tiles = total_rows // block, half // tile
+    far = pl.BlockSpec(memory_space=pl.ANY)
     return pl.pallas_call(
-        functools.partial(feed_half_kernel, half, tile),
-        grid=(total_rows // block,),
+        functools.partial(feed_half_kernel, half, tile, block),
         out_shape=[
             jax.ShapeDtypeStruct((total_rows, half), jnp.bfloat16),
             jax.ShapeDtypeStruct((total_rows, 2 * half), jnp.bfloat16),
         ],
-        in_specs=[
-            row_block,
-            row_block,
-            pl.BlockSpec(weight.shape, lambda i: (0, 0), pipeline_mode=pl.Buffered(1)),
-        ],
-        out_specs=[
-            pl.BlockSpec((block, half), lambda i: (i, 0)),
-            pl.BlockSpec((block, 2 * half), lambda i: (i, 0)),
+        in_specs=[far] * 3,
+        out_specs=[far] * 2,
+        scratch_shapes=[
+            pltpu.VMEM(rows.shape, rows.dtype),
+            pltpu.VMEM(rows.shape, rows.dtype),
+            pltpu.VMEM((3, tiles, depth, tile), weight.dtype),
+            pltpu.VMEM((total_rows, half), jnp.bfloat16),
+            pltpu.VMEM((total_rows, 2 * half), jnp.bfloat16),
+            pltpu.SemaphoreType.DMA((2, blocks)),
+            pltpu.SemaphoreType.DMA((3, tiles)),
+            pltpu.SemaphoreType.DMA((2, blocks)),
         ],
         compiler_params=pltpu.CompilerParams(vmem_limit_bytes=VMEM_LIMIT),
         cost_estimate=pl.CostEstimate(
@@ -1079,17 +1180,15 @@
     step = pl.program_id(0)
     if with_other:
         other_ref, refs = refs[0], refs[1:]
-        out_refs, held_ref, copy_sem = refs[:-3], refs[-3], refs[-2]
+        out_refs, held_ref, copy_sem = refs[:-2], refs[-2], refs[-1]
     else:
         out_ref = refs[0]
-    turned_ref = refs[-1]
     start = 0
     for left_ref, right_ref in pairs:
-        turned_ref[...] = left_ref[...].T
         width = right_ref.shape[1]
         tile = next(t for t in (768, 512, 384, 256, 128) if width % t == 0)
         for column in range(0, width, tile):
-            values = simple_product(turned_ref[...], right_ref[:, column : column + tile])
+            values = simple_product(left_ref[...], right_ref[:, column : column + tile])
             columns = slice(start + column, start + column + tile)
             if with_other:
                 values = values + other_ref[0, :, columns].astype(jnp.float32)
@@ -1113,18 +1212,18 @@
 
 def grad_blocks(order, pairs, other=None):
     count = order.shape[0]
-    total_rows, depth = pairs[0][0].shape
+    depth, total_rows = pairs[0][0].shape
     block = depth // lax.axis_size("dp")
     width = sum(right.shape[1] for _, right in pairs)
     in_specs = []
     operands = []
     for left, right in pairs:
         in_specs += [
-            pl.BlockSpec((total_rows, block), lambda k, at: (0, at[k])),
+            pl.BlockSpec((block, total_rows), lambda k, at: (at[k], 0)),
             pl.BlockSpec(right.shape, lambda k, at: (0, 0), pipeline_mode=pl.Buffered(1)),
         ]
         operands += [left, right]
-    scratch = [pltpu.VMEM((block, total_rows), jnp.bfloat16)]
+    scratch = []
     if other is not None:
         in_specs.append(pl.BlockSpec((1, block, width), lambda k, at: (k, 0, 0)))
         operands.append(other)
@@ -1133,7 +1232,7 @@
         scratch = [
             pltpu.VMEM((count, block, width), jnp.bfloat16),
             pltpu.SemaphoreType.DMA((count,)),
-        ] + scratch
+        ]
     else:
         out_shape = [jax.ShapeDtypeStruct((count, block, width), jnp.bfloat16)]
         out_specs = [pl.BlockSpec((1, block, width), lambda k, at: (k, 0, 0))]
@@ -1201,20 +1300,18 @@
         start += width
 
 
-def finish_mixing_kernel(heads, total_ref, output_total_ref, query_ref, key_ref, value_ref, output_ref):
-    query_width = query_ref.shape[1] // heads
-    head_size = key_ref.shape[1] // heads
-    start = 0
-    for head in range(heads):
-        for ref, part in ((query_ref, query_width), (key_ref, head_size), (value_ref, head_size)):
-            ref[:, head * part : (head + 1) * part] = total_ref[:, start : start + part].astype(
-                jnp.float32
-            )
-            start += part
-    output_ref[...] = output_total_ref[...].astype(jnp.float32).T
-
-
-def finish_feed_kernel(own_ref, up_ref, down_ref, second_ref, gate_out_ref, up_out_ref, down_out_ref):
+def finish_kernel(
+    heads, own_ref, up_ref, down_ref, second_ref, mixing_ref, output_total_ref, terms_ref, output_rows_ref, input_rows_ref,
+    output_rows_out, input_rows_out, attention_term_out, query_out, key_out, value_out, query_gain_out, key_gain_out,
+    output_out, feed_term_out, gate_out, up_out, down_out,
+):
+    output_rows_out[...] = output_rows_ref[...]
+    input_rows_out[...] = input_rows_ref[...]
+    count = attention_term_out.shape[0]
+    attention_term_out[...] = terms_ref[:count, :]
+    feed_term_out[...] = terms_ref[count : 2 * count, :]
+    query_gain_out[...] = terms_ref[2 * count : 2 * count + 1, :]
+    key_gain_out[...] = terms_ref[2 * count + 1 : 2 * count + 2, :]
     start = 0
     for total_refs in ((own_ref, up_ref, down_ref), (second_ref,)):
         width = total_refs[0].shape[1] // 3
@@ -1224,10 +1321,20 @@
             columns = slice(index * width, (index + 1) * width)
             return sum(ref[:, columns].astype(jnp.float32) for ref in total_refs)
 
-        gate_out_ref[:, part] = total(0)
-        up_out_ref[:, part] = total(1)
-        down_out_ref[part, :] = total(2).T
+        gate_out[:, part] = total(0)
+        up_out[:, part] = total(1)
+        down_out[part, :] = total(2).T
         start += width
+    query_width = query_out.shape[1] // heads
+    head_size = key_out.shape[1] // heads
+    start = 0
+    for head in range(heads):
+        for out, part in ((query_out, query_width), (key_out, head_size), (value_out, head_size)):
+            out[:, head * part : (head + 1) * part] = mixing_ref[:, start : start + part].astype(
+                jnp.float32
+            )
+            start += part
+    output_out[...] = output_total_ref[...].astype(jnp.float32).T
 
 
 def whole_call(body, shapes, *operands):
@@ -1293,7 +1400,9 @@
     first_scale = row_scale(input_float)
     first_unit = input_float * first_scale
     mixer_local = (first_unit * attention_gain).astype(jnp.bfloat16)
-    mixer_rows, cotangent_rows = gather_rows((mixer_local, out_cotangent), size, 0)
+    mixer_rows, mixer_turned, cotangent_rows, cotangent_turned = gather_rows(
+        (mixer_local, out_cotangent), size, 0
+    )
 
     raw, mixed_rows, totals = attention_forward(
         mixer_rows, mixing_full, tables, query_gain, key_gain, heads, grouping
@@ -1301,20 +1410,23 @@
     local_shape = block_input.shape
     local_rows = local_shape[0]
     gain_rows = model_width // head_size
-    gathered_shape = jax.ShapeDtypeStruct((size * local_rows, model_width), jnp.bfloat16)
+    gathered_shapes = [
+        jax.ShapeDtypeStruct((size * local_rows, model_width), jnp.bfloat16),
+        jax.ShapeDtypeStruct((model_width, size * local_rows), jnp.bfloat16),
+    ]
     local_float = jax.ShapeDtypeStruct(local_shape, jnp.float32)
     local_half = jax.ShapeDtypeStruct(local_shape, jnp.bfloat16)
     row_sum = pltpu.VMEM((1, model_width), jnp.float32)
     own_rows = pltpu.VMEM(local_shape, jnp.bfloat16)
     scatter_scratch = Scatter.scratch(size, *local_shape)
     gather_scratch = Gather.scratch(size, *local_shape)
-    feed_rows, hidden_state = scatter_call(
+    feed_rows, feed_turned, hidden_state = scatter_call(
         functools.partial(between_forward_kernel, size),
         [(mixed_rows, mixing_full, qkv_columns)],
         size,
         [block_input, feed_gain.reshape(1, -1)],
         [],
-        [gathered_shape, local_float],
+        [*gathered_shapes, local_float],
         True,
         [own_rows, *scatter_scratch, *gather_scratch],
         1,
@@ -1322,20 +1434,20 @@
 
     hidden_first, slope_first = feed_half(feed_rows, cotangent_rows, feed_full[0])
     blocks, up, down = reduce_over_chips(
-        [(feed_rows, slope_first), (cotangent_rows, hidden_first)], sizes
+        [(feed_turned, slope_first), (cotangent_turned, hidden_first)], sizes
     )
     blocks, later_full = lax.optimization_barrier((blocks, feed_full[1]))
     hidden_second, slope_second = feed_half(feed_rows, cotangent_rows, later_full)
     plain_order = jnp.arange(sizes[0], dtype=jnp.int32)
     second_grad = grad_blocks(
-        plain_order, [(feed_rows, slope_second), (cotangent_rows, hidden_second)]
+        plain_order, [(feed_turned, slope_second), (cotangent_turned, hidden_second)]
     ).reshape(model_width, -1)
     second_grad, slope_second = lax.optimization_barrier((second_grad, slope_second))
     second_total = lax.psum_scatter(second_grad, "dp", scatter_dimension=0, tiled=True)
     chips = sizes[0] // 2
     middle_steps = tuple(range(2, chips - 1))
     chain_block = jax.ShapeDtypeStruct(blocks[0].shape, jnp.bfloat16)
-    state_rows, state_slope, feed_term, rising, falling = scatter_call(
+    state_rows, state_turned, state_slope, feed_term, rising, falling = scatter_call(
         functools.partial(between_backward_kernel, size, chips, middle_steps),
         [(slope_first, feed_full[0], 0), (slope_second, later_full, 0)],
         size,
@@ -1344,7 +1456,7 @@
         + [blocks[step] for step in middle_steps]
         + [up, down, blocks[1], blocks[chips - 1]],
         [
-            gathered_shape,
+            *gathered_shapes,
             local_float,
             jax.ShapeDtypeStruct((gain_rows, head_size), jnp.float32),
             chain_block,
@@ -1367,7 +1479,7 @@
     down = lax.ppermute(
         falling, "dp", [(device, device - 2) for device in range(2, sizes[0])]
     )
-    output_grad = grad_blocks(plain_order, [(state_rows, mixed_rows)]).reshape(model_width, -1)
+    output_grad = grad_blocks(plain_order, [(state_turned, mixed_rows)]).reshape(model_width, -1)
     output_grad, state_rows = lax.optimization_barrier((output_grad, state_rows))
     output_total = lax.psum_scatter(output_grad, "dp", scatter_dimension=0, tiled=True)
     qkv_slope, head_terms, block_output = attention_backward(
@@ -1379,7 +1491,7 @@
         ],
         hidden_state, size, 4,
     )
-    mixing_grad = grad_blocks(plain_order, [(mixer_rows, qkv_slope)]).reshape(model_width, -1)
+    mixing_grad = grad_blocks(plain_order, [(mixer_turned, qkv_slope)]).reshape(model_width, -1)
     mixing_grad, qkv_slope = lax.optimization_barrier((mixing_grad, qkv_slope))
     mixing_total = lax.psum_scatter(mixing_grad, "dp", scatter_dimension=0, tiled=True)
     terms_shape = (2 * gain_rows + head_terms.shape[0], head_size)
@@ -1408,39 +1520,31 @@
         ],
         3,
     )
-    query_gradient, key_gradient, value_gradient, output_gradient = whole_call(
-        functools.partial(finish_mixing_kernel, heads),
+
+    def whole_float(*shape):
+        return jax.ShapeDtypeStruct(shape, jnp.float32)
+
+    outs = whole_call(
+        functools.partial(finish_kernel, heads),
         [
-            jax.ShapeDtypeStruct((block_width, query_columns), jnp.float32),
-            jax.ShapeDtypeStruct((block_width, key_columns), jnp.float32),
-            jax.ShapeDtypeStruct((block_width, key_columns), jnp.float32),
-            jax.ShapeDtypeStruct((query_columns, block_width), jnp.float32),
+            local_half,
+            local_half,
+            whole_float(gain_rows, head_size),
+            whole_float(block_width, query_columns),
+            whole_float(block_width, key_columns),
+            whole_float(block_width, key_columns),
+            whole_float(1, head_size),
+            whole_float(1, head_size),
+            whole_float(query_columns, block_width),
+            whole_float(gain_rows, head_size),
+            whole_float(block_width, hidden_columns),
+            whole_float(block_width, hidden_columns),
+            whole_float(hidden_columns, block_width),
         ],
-        mixing_total, output_total,
-    )
-    gate_gradient, up_gradient, down_gradient = whole_call(
-        finish_feed_kernel,
-        [
-            jax.ShapeDtypeStruct((block_width, hidden_columns), jnp.float32),
-            jax.ShapeDtypeStruct((block_width, hidden_columns), jnp.float32),
-            jax.ShapeDtypeStruct((hidden_columns, block_width), jnp.float32),
-        ],
-        blocks[0], up, down, second_total,
-    )
-    return (
-        block_output,
-        input_gradient,
-        terms[:gain_rows].reshape(-1),
-        query_gradient,
-        key_gradient,
-        value_gradient,
-        terms[2 * gain_rows],
-        terms[2 * gain_rows + 1],
-        output_gradient,
-        terms[gain_rows : 2 * gain_rows].reshape(-1),
-        gate_gradient,
-        up_gradient,
-        down_gradient,
+        blocks[0], up, down, second_total, mixing_total, output_total, terms, block_output, input_gradient,
+    )
+    return tuple(
+        out.reshape(-1) if index in (2, 6, 7, 9) else out for index, out in enumerate(outs)
     )
 
 

time: 621 us -> 615 us (level)
  local copies, waits for them, and re-layouts: 8.67 us -> 1.57 us
  waiting for transfers between devices: 89 us -> 95.6 us
    pallas_call x4 -> x3, Pallas kernels: 13.3 us -> 12.9 us  [whole_call(): pl.pallas_call(body, out_shape=shapes, in_specs=[pl.BlockSpec(memory_spac...]
where the time goes in v7:
time: 615 us; the launch traced here: 614 us
  Pallas kernels  489 us (80%)
  waiting for transfers between devices  95.6 us (16%)
  between operations  14.3 us (2%)
  starting transfers between devices  9.89 us (2%)
    pallas_call x3, Pallas kernels, scatter_call(): pl.pallas_call(functools.partial(body, tuple((first for _, _, first in tr...  244 us
    pallas_call x1, Pallas kernels, gather_rows(): pl.pallas_call(functools.partial(gather_kernel, size, count), out_shape=o...  76.4 us
    reduce_scatter x1, waiting for transfers between devices, per_device(): lax.psum_scatter(second_grad, 'dp', scatter_dimension=0, tiled=True)  70 us
    pallas_call x5, Pallas kernels, grad_blocks(): pl.pallas_call(functools.partial(grad_kernel, len(pairs), other is not No...  58.9 us
    pallas_call x1, Pallas kernels, attention_backward(): pl.pallas_call(functools.partial(attention_backward_kernel, size, groupin...  45 us
    pallas_call x2, Pallas kernels, feed_half(): pl.pallas_call(functools.partial(feed_half_kernel, half, tile, block), ou...  33.9 us
    pallas_call x1, Pallas kernels, attention_forward(): pl.pallas_call(functools.partial(attention_forward_kernel, grouping, head...  18.4 us
    pallas_call x3, Pallas kernels, whole_call(): pl.pallas_call(body, out_shape=shapes, in_specs=[pl.BlockSpec(memory_spac...  12.9 us
  transfers between devices with their start and end apart: 11, of which 5 were waited for; matrix products, arithmetic and copies ran while one was open for 1% of the time, Pallas kernels for 62%

profile of v7, /device:TPU:0, one launch (start us, length us, event | category | flops | bytes accessed | tf_op | source)
XLA Modules:
  0.0 613.9 jit_solution(7471549780718511731)
XLA Ops:
  7.2 0.0 all-gather.4.cloned.1.call-start
  7.2 2.2 shard_map.246
  9.4 0.0 all-gather.4.cloned.1.call-update
  9.4 0.0 all-gather.6.cloned.1.call-start
  9.5 3.4 shard_map.248
  12.9 0.0 all-gather.6.cloned.1.call-update
  12.9 0.0 all-gather.8.cloned.1.call-start
  13.0 0.7 all-gather.8.cloned.1.call-update
  13.7 0.0 reduce-scatter.8.cloned.1.call-start
  13.8 0.3 fusion
  14.1 1.3 fusion.2.refs_0_
  15.3 76.4 %gather_rows.1 = (bf16[1024,2048]{1,0:T(8,128)(2,1)}, bf16[2048,1024]{1,0:T(8,128)(2,1)}, bf16[1024,2048]{1,0:T(8,128)(2,1)}, bf16[2048,1024]{1,0:T(8,128)(2,1)}) custom-call(bf16[256,2048]{1,0:T(8,128)(2,1)} %fusion.2.refs_0_, bf16[256,2048]{1,0:T(8,128)(2,1)} %refs_5_.1), custom_call_target="tpu_custom_call" | custom-call | bytes 125829120 | tf_op jit(solution)/shard_map/gather_rows/pallas_call | solution.py:205
  91.7 0.5 broadcast_add_fusion.order_ref
  92.2 18.4 %attention_forward.1 = (f32[1024,1024]{1,0:T(8,128)}, bf16[1024,512]{1,0:T(8,128)(2,1)}, f32[2,2,1024]{2,1,0:T(2,128)}) custom-call(bf16[1024,2048]{1,0:T(8,128)(2,1)} %get-tuple-element.68.rows_ref.refs_6_, bf16[2048,1536]{1,0:T(8,128)(2,1)} %all-gather.4.cloned.1.call-done.weight_ref.refs_1_.refs_5_, f32[136,128]{1,0:T(8,128)} %constant.38.clone.few_cosines_ref.refs_9_, ...), custom_call_target="tpu_custom_call" | custom-call | flops 5368709120 | bytes 8388608 | tf_op jit(solution)/shard_map/attention_forward/pallas_call | solution.py:838
  110.7 77.8 %shard_map.247 = (bf16[1024,2048]{1,0:T(8,128)(2,1)}, bf16[2048,1024]{1,0:T(8,128)(2,1)}, f32[256,2048]{1,0:T(8,128)}) custom-call(bf16[1024,512]{1,0:T(8,128)(2,1)} %get-tuple-element.69.refs_0_.refs_1_.refs_7_, bf16[2048,1536]{1,0:T(8,128)(2,1)} %all-gather.4.cloned.1.call-done.weight_ref.refs_1_.refs_5_, bf16[256,2048]{1,0:T(8,128)(2,1)} %refs_2_.3, ...), custom_call_target="tpu_custom_call" | custom-call | flops 2147483648 | bytes 150000000 | tf_op jit(solution)/shard_map/pallas_call | solution.py:703
  188.5 6.8 %all-gather.6.cloned.1.call-done.weight_far.refs_1_ = bf16[2048,3072]{1,0:T(8,128)(2,1)} async-done(((bf16[256,3072]{1,0:T(8,128)(2,1)}), bf16[2048,3072]{1,0:T(8,128)(2,1)}) %all-gather.6.cloned.1.call-update) | async-done | bytes 12582928 | tf_op jit(solution)/shard_map/all_gather | solution.py:1397
  195.3 22.0 %feed_half.2 = (bf16[1024,1024]{1,0:T(8,128)(2,1)}, bf16[1024,2048]{1,0:T(8,128)(2,1)}) custom-call(bf16[1024,2048]{1,0:T(8,128)(2,1)} %get-tuple-element.71.rows_far, bf16[1024,2048]{1,0:T(8,128)(2,1)} %get-tuple-element.72.cotangent_far, bf16[2048,3072]{1,0:T(8,128)(2,1)} %all-gather.6.cloned.1.call-done.weight_far.refs_1_), custom_call_target="tpu_custom_call" | custom-call | flops 12884901888 | bytes 20971520 | tf_op jit(solution)/shard_map/feed_half/pallas_call | solution.py:1149
  217.2 12.4 %grad_blocks.5 = bf16[4,256,3072]{2,1,0:T(8,128)(2,1)} custom-call(s32[4]{0:T(128)} %broadcast_add_fusion.order_ref, bf16[2048,1024]{1,0:T(8,128)(2,1)} %get-tuple-element.70.refs_0_, bf16[1024,2048]{1,0:T(8,128)(2,1)} %get-tuple-element.74.refs_1_.refs_0_, bf16[2048,1024]{1,0:T(8,128)(2,1)} %get-tuple-element.75.refs_2_, ...), custom_call_target="tpu_custom_call" | custom-call | flops 6442450944 | bytes 16777216 | tf_op jit(solution)/shard_map/grad_blocks/pallas_call | solution.py:1239
  229.6 0.3 collective-permute-start
  229.9 0.5 broadcast_add_fusion.1.order_ref
  230.5 10.3 %collective-permute-done.refs_4_ = bf16[4,256,3072]{2,1,0:T(8,128)(2,1)} collective-permute-done((bf16[4,256,3072]{2,1,0:T(8,128)(2,1)}, bf16[4,256,3072]{2,1,0:T(8,128)(2,1)}, u32[]{:S(2)}, u32[]{:S(2)}) %collective-permute-start) | collective-permute-done | bytes 6291488 | tf_op jit(solution)/shard_map/ppermute | solution.py:1266
  240.8 13.6 %grad_blocks.6 = (bf16[256,3072]{1,0:T(8,128)(2,1)}, bf16[256,3072]{1,0:T(8,128)(2,1)}, bf16[256,3072]{1,0:T(8,128)(2,1)}, bf16[256,3072]{1,0:T(8,128)(2,1)}) custom-call(s32[4]{0:T(128)} %broadcast_add_fusion.1.order_ref, bf16[2048,1024]{1,0:T(8,128)(2,1)} %get-tuple-element.70.refs_0_, bf16[1024,2048]{1,0:T(8,128)(2,1)} %get-tuple-element.74.refs_1_.refs_0_, ...), custom_call_target="tpu_custom_call" | custom-call | flops 6442450944 | bytes 16777216 | tf_op jit(solution)/shard_map/grad_blocks/pallas_call | solution.py:1239
  254.3 0.8 collective-permute-start.2
  255.1 2.5 collective-permute-start.1
  257.7 2.2 all-gather.8.cloned.1.call-done.weight_far.refs_3_
  259.8 11.9 %feed_half.3 = (bf16[1024,512]{1,0:T(8,128)(2,1)}, bf16[1024,1024]{1,0:T(8,128)(2,1)}) custom-call(bf16[1024,2048]{1,0:T(8,128)(2,1)} %get-tuple-element.71.rows_far, bf16[1024,2048]{1,0:T(8,128)(2,1)} %get-tuple-element.72.cotangent_far, bf16[2048,1536]{1,0:T(8,128)(2,1)} %all-gather.8.cloned.1.call-done.weight_far.refs_3_), custom_call_target="tpu_custom_call" | custom-call | flops 6442450944 | bytes 14680064 | tf_op jit(solution)/shard_map/feed_half/pallas_call | solution.py:1149
  271.8 0.5 iota.11.order_ref
  272.3 13.6 %grad_blocks.7 = bf16[8,256,1536]{2,1,0:T(8,128)(2,1)} custom-call(s32[8]{0:T(128)} %iota.11.order_ref, bf16[2048,1024]{1,0:T(8,128)(2,1)} %get-tuple-element.70.refs_0_, bf16[1024,1024]{1,0:T(8,128)(2,1)} %get-tuple-element.86.refs_1_.refs_2_, bf16[2048,1024]{1,0:T(8,128)(2,1)} %get-tuple-element.75.refs_2_, bf16[1024,512]{1,0:T(8,128)(2,1)} %get-tuple-element.85.refs_3_.refs_2_), custom_call_target="tpu_custom_call" | custom-call | flops 6442450944 | bytes 17825792 | tf_op jit(solution)/shard_map/grad_blocks/pallas_call | solution.py:1239
  285.9 5.2 collective-permute-done.1.refs_9_
  291.1 89.1 %shard_map.249 = (bf16[1024,2048]{1,0:T(8,128)(2,1)}, bf16[2048,1024]{1,0:T(8,128)(2,1)}, f32[256,2048]{1,0:T(8,128)}, f32[16,128]{1,0:T(8,128)}, bf16[256,3072]{1,0:T(8,128)(2,1)}, /*index=5*/bf16[256,3072]{1,0:T(8,128)(2,1)}) custom-call(bf16[1024,2048]{1,0:T(8,128)(2,1)} %get-tuple-element.74.refs_1_.refs_0_, ...), custom_call_target="tpu_custom_call" | custom-call | flops 12884901888 | bytes 150000000 | tf_op jit(solution)/shard_map/pallas_call | solution.py:703
  380.2 0.5 iota.13.order_ref
  380.7 8.7 %grad_blocks.8 = bf16[8,256,512]{2,1,0:T(8,128)(2,1)} custom-call(s32[8]{0:T(128)} %iota.13.order_ref, bf16[2048,1024]{1,0:T(8,128)(2,1)} %get-tuple-element.95.refs_0_, bf16[1024,512]{1,0:T(8,128)(2,1)} %get-tuple-element.69.refs_0_.refs_1_.refs_7_), custom_call_target="tpu_custom_call" | custom-call | flops 2147483648 | bytes 7340032 | tf_op jit(solution)/shard_map/grad_blocks/pallas_call | solution.py:1239
  389.4 0.0 reduce-scatter.8.cloned.1.call-update
  389.4 0.0 reduce-scatter.6.cloned.1.call-start
  389.5 45.0 %attention_backward.1 = (bf16[1024,1024]{1,0:T(8,128)(2,1)}, f32[8,128]{1,0:T(8,128)}, bf16[256,2048]{1,0:T(8,128)(2,1)}) custom-call(bf16[1024,1024]{1,0:T(8,128)(2,1)} %get-tuple-element.76.refs_3_.refs_0_, bf16[2048,3072]{1,0:T(8,128)(2,1)} %all-gather.6.cloned.1.call-done.weight_far.refs_1_, bf16[1024,512]{1,0:T(8,128)(2,1)} %get-tuple-element.85.refs_3_.refs_2_, ...), custom_call_target="tpu_custom_call" | custom-call | flops 4831838208 | bytes 100000000 | tf_op jit(solution)/shard_map/attention_backward/pallas_call | solution.py:1022
  434.5 0.5 iota.12.order_ref
  435.0 10.7 %grad_blocks.9 = bf16[8,256,1024]{2,1,0:T(8,128)(2,1)} custom-call(s32[8]{0:T(128)} %iota.12.order_ref, bf16[2048,1024]{1,0:T(8,128)(2,1)} %get-tuple-element.94.refs_0_, bf16[1024,1024]{1,0:T(8,128)(2,1)} %get-tuple-element.103.refs_1_.refs_0_), custom_call_target="tpu_custom_call" | custom-call | flops 4294967296 | bytes 10485760 | tf_op jit(solution)/shard_map/grad_blocks/pallas_call | solution.py:1239
  445.6 0.0 reduce-scatter.6.cloned.1.call-update
  445.7 0.3 reduce-scatter.4.cloned.1.call-start
  446.0 0.3 reduce-scatter.4.cloned.1.call-update
  446.3 4.5 collective-permute-start.3
  450.8 1.3 collective-permute-start.4
  452.1 0.6 pad_maximum_fusion.refs_5_
  452.7 77.0 %shard_map.250 = (bf16[256,2048]{1,0:T(8,128)(2,1)}, f32[40,128]{1,0:T(8,128)}) custom-call(bf16[1024,1024]{1,0:T(8,128)(2,1)} %get-tuple-element.103.refs_1_.refs_0_, bf16[2048,1536]{1,0:T(8,128)(2,1)} %all-gather.4.cloned.1.call-done.weight_ref.refs_1_.refs_5_, bf16[256,2048]{1,0:T(8,128)(2,1)} %refs_2_.3, f32[1,2048]{1,0:T(1,128)} %bitcast.16, ...), custom_call_target="tpu_custom_call" | custom-call | flops 4294967296 | bytes 150000000 | tf_op jit(solution)/shard_map/pallas_call | solution.py:703
  529.8 0.0 reduce-scatter.8.cloned.1.call-done.output_total_ref
  529.8 0.0 reduce-scatter.6.cloned.1.call-done.mixing_ref
  529.9 70.0 %reduce-scatter.4.cloned.1.call-done.second_ref = bf16[256,1536]{1,0:T(8,128)(2,1)} async-done(((bf16[2048,1536]{1,0:T(8,128)(2,1)}), bf16[256,1536]{1,0:T(8,128)(2,1)}) %reduce-scatter.4.cloned.1.call-update) | async-done | bytes 786448 | tf_op jit(solution)/shard_map/reduce_scatter | solution.py:1446
  599.8 7.3 %shard_map.251 = (bf16[256,2048]{1,0:T(8,128)(2,1)}, bf16[256,2048]{1,0:T(8,128)(2,1)}, f32[16,128]{1,0:T(8,128)}, f32[256,512]{1,0:T(8,128)}, f32[256,256]{1,0:...) custom-call(bf16[256,3072]{1,0:T(8,128)(2,1)} %get-tuple-element.82., ...), custom_call_target="tpu_custom_call" | custom-call | bytes 16797696 | tf_op jit(solution)/shard_map/pallas_call | solution.py:1341
  (17 shorter events, 0.0 us)
Async XLA Ops:
  7.2 85.1 %all-gather.4.cloned.1.call-start = ((), (), s32[]{:S(2)}) async-start(), calls=%async_computation.3 | async-start | bytes 7077888 | tf_op jit(solution)/shard_map/all_gather | solution.py:1388
  9.4 4.3 copy-start
  9.4 185.8 %all-gather.6.cloned.1.call-start = ((), (), s32[]{:S(2)}) async-start(), calls=%async_computation.4 | async-start | bytes 14155776 | tf_op jit(solution)/shard_map/all_gather | solution.py:1397
  12.9 1.1 copy-start.2
  12.9 246.9 %all-gather.8.cloned.1.call-start = ((), (), s32[]{:S(2)}) async-start(), calls=%async_computation.5 | async-start | bytes 7077888 | tf_op jit(solution)/shard_map/all_gather | solution.py:1397
  13.7 516.1 %reduce-scatter.8.cloned.1.call-start = ((), (), s32[]{:S(2)}) async-start(), calls=%async_computation.8 | async-start | bytes 2359296 | tf_op jit(solution)/shard_map/reduce_scatter | solution.py:1484
  229.6 11.1 %collective-permute-start = (bf16[4,256,3072]{2,1,0:T(8,128)(2,1)}, bf16[4,256,3072]{2,1,0:T(8,128)(2,1)}, u32[]{:S(2)}, u32[]{:S(2)}) collective-permute-start(bf16[4,256,3072]{2,1,0:T(8,128)(2,1)} %grad_blocks.5), channel_id=1, source_target_pairs={{0,4},{4,0},{8,12},{12,8},{16,20},{20,16},{24,28},{28,24},{1,5},{5... | collective-permute-start | bytes 18874376 | tf_op jit(solution)/shard_map/ppermute | solution.py:1266
  254.3 31.5 %collective-permute-start.2 = (bf16[256,3072]{1,0:T(8,128)(2,1)}, bf16[256,3072]{1,0:T(8,128)(2,1)S(1)}, u32[]{:S(2)}, u32[]{:S(2)}) collective-permute-start(bf16[256,3072]{1,0:T(8,128)(2,1)} %get-tuple-element.89.refs_11_), channel_id=1, source_target_pairs={{24,16},{28,20},{25,17},{29,21},{26,18},{30,22},{27,19},{31,23}} | collective-permute-start | bytes 4718600 | tf_op jit(solution)/shard_map/ppermute | solution.py:1273
  255.1 36.0 %collective-permute-start.1 = (bf16[256,3072]{1,0:T(8,128)(2,1)}, bf16[256,3072]{1,0:T(8,128)(2,1)}, u32[]{:S(2)}, u32[]{:S(2)}) collective-permute-start(bf16[256,3072]{1,0:T(8,128)(2,1)} %get-tuple-element.90.refs_12_), channel_id=1, source_target_pairs={{0,8},{4,12},{1,9},{5,13},{2,10},{6,14},{3,11},{7,15}} | collective-permute-start | bytes 4718600 | tf_op jit(solution)/shard_map/ppermute | solution.py:1272
  285.9 5.2 copy-start.5
  389.4 140.4 %reduce-scatter.6.cloned.1.call-start = ((), (), s32[]{:S(2)}) async-start(), calls=%async_computation.7 | async-start | bytes 4718592 | tf_op jit(solution)/shard_map/reduce_scatter | solution.py:1496
  445.7 6.4 %copy-start.3 = (f32[16,128]{1,0:T(8,128)S(1)}, f32[16,128]{1,0:T(8,128)}, u32[]{:S(2)}) copy-start(f32[16,128]{1,0:T(8,128)} %get-tuple-element.105) | copy-start | bytes 24580
  445.7 6.4 %copy-start.4 = (f32[8,128]{1,0:T(8,128)S(1)}, f32[8,128]{1,0:T(8,128)}, u32[]{:S(2)}) copy-start(f32[8,128]{1,0:T(8,128)} %get-tuple-element.106) | copy-start | bytes 12292
  445.7 154.1 %reduce-scatter.4.cloned.1.call-start = ((), (), s32[]{:S(2)}) async-start(), calls=%async_computation.6 | async-start | bytes 7077888 | tf_op jit(solution)/shard_map/reduce_scatter | solution.py:1446
  446.3 83.5 %collective-permute-start.3 = (bf16[256,3072]{1,0:T(8,128)(2,1)}, bf16[256,3072]{1,0:T(8,128)(2,1)S(1)}, u32[]{:S(2)}, u32[]{:S(2)}) collective-permute-start(bf16[256,3072]{1,0:T(8,128)(2,1)} %get-tuple-element.91), channel_id=1, source_target_pairs={{0,8},{4,12},{8,16},{12,20},{16,24},{20,28},{1,9},{5,13},{9,17},{1... | collective-permute-start | bytes 4718600 | tf_op jit(solution)/shard_map/ppermute | solution.py:1476
  450.8 79.0 %collective-permute-start.4 = (bf16[256,3072]{1,0:T(8,128)(2,1)}, bf16[256,3072]{1,0:T(8,128)(2,1)}, u32[]{:S(2)}, u32[]{:S(2)}) collective-permute-start(bf16[256,3072]{1,0:T(8,128)(2,1)} %get-tuple-element.92), channel_id=1, source_target_pairs={{8,0},{12,4},{16,8},{20,12},{24,16},{28,20},{9,1},{13,5},{17,9},{2... | collective-permute-start | bytes 4718600 | tf_op jit(solution)/shard_map/ppermute | solution.py:1479
  529.8 70.1 %copy-start.1 = (bf16[256,3072]{1,0:T(8,128)(2,1)}, bf16[256,3072]{1,0:T(8,128)(2,1)S(1)}, u32[]{:S(2)}) copy-start(bf16[256,3072]{1,0:T(8,128)(2,1)S(1)} %collective-permute-done.3.up_ref) | copy-start | bytes 4718596
Sparse Core Ops, SparseCore 0:
  10.2 67.4 all-gather.3
  79.9 115.3 all-gather.5
  196.9 62.8 all-gather.7
  389.5 36.2 reduce-scatter.7
  445.8 84.0 reduce-scatter.5
  532.0 67.7 reduce-scatter.3

commit v8 on v7

--- a/solution.py
+++ b/solution.py
@@ -569,24 +569,18 @@
     operands, refs = split_operands(refs, size, first_columns)
     state_ref, cotangent_ref, gain_ref = refs[:3]
     chain_count = 2 * len(steps) + 2
-    chain_refs, last_refs, refs = refs[3 : 3 + chain_count], refs[3 + chain_count : 5 + chain_count], refs[5 + chain_count :]
-    gathered_ref, gathered_turned_ref, slope_ref, term_ref, rising_ref, falling_ref = refs[:6]
-    own_ref, sum_ref, last_sem = refs[6:9]
+    chain_refs, refs = refs[3 : 3 + chain_count], refs[3 + chain_count :]
+    gathered_ref, gathered_turned_ref, slope_ref, term_ref, up_out_ref, down_out_ref = refs[:6]
+    own_ref, sum_ref = refs[6:8]
     buffers = 5 if size == 4 else 4
-    scatter = Scatter(size, *refs[9 : 9 + buffers])
-    gather = Gather(size, own_ref, gathered_ref, gathered_turned_ref, *refs[9 + buffers : 15 + buffers])
+    scatter = Scatter(size, *refs[8 : 8 + buffers])
+    gather = Gather(size, own_ref, gathered_ref, gathered_turned_ref, *refs[8 + buffers : 14 + buffers])
     chain = Chain(
         chips, steps, chain_refs[: len(steps)], chain_refs[len(steps) : -2], *chain_refs[-2:],
-        *refs[15 + buffers :],
-    )
-    last_loads = [
-        pltpu.make_async_copy(source, target, last_sem.at[index])
-        for index, (source, target) in enumerate(zip(last_refs, (rising_ref, falling_ref)))
-    ]
+        *refs[14 + buffers :],
+    )
     chain.load()
     scatter.load(operands)
-    for load in last_loads:
-        load.start()
     greet(neighbours(size) + chain.neighbours)
     scatter.fill(operands, slots=(0, 1))
     chain.step(0)
@@ -616,20 +610,20 @@
     for index in range(1, len(steps)):
         chain.step(index)
         chain.wait(index)
-    for load in last_loads:
-        load.wait()
     last = len(steps)
-    for needed, landing, out_ref in (
-        ((chain.chip > 0) & (chain.chip < chips - 1), chain.up, rising_ref),
-        ((chain.chip > 0) & (chain.chip < chips - 1), chain.down, falling_ref),
+    from_under, from_above = chain.arrives(last - 1)
+    for arrived, landing, out_ref in (
+        (from_under, chain.up, up_out_ref),
+        (from_above, chain.down, down_out_ref),
     ):
 
-        @pl.when(needed)
+        @pl.when(arrived)
         def _(landing=landing, out_ref=out_ref):
-            def add(piece):
-                out_ref[piece, :] = add_rounded(out_ref[piece, :], landing[last, piece, :])
-
-            over_pieces(out_ref.shape[0], add)
+            out_ref[...] = landing[last]
+
+        @pl.when(jnp.logical_not(arrived))
+        def _(out_ref=out_ref):
+            out_ref[...] = jnp.zeros_like(out_ref)
 
     gather.finish()
     scatter.drain()
@@ -883,22 +877,36 @@
     return slope.astype(jnp.bfloat16), jnp.sum(term, axis=0, keepdims=True)
 
 
-def attention_backward_kernel(size, grouping, head_size, block, first_columns, *refs):
+def attention_backward_kernel(size, chips, grouping, head_size, block, first_columns, *refs):
     operands, refs = split_operands(refs, size, first_columns)
     (
         state_ref, weight_ref, raw_ref, mixed_ref, total_ref, few_cosines_ref, few_sines_ref,
-        query_gain_ref, key_gain_ref, hidden_state_ref, slope_ref, gain_ref, output_ref,
+        query_gain_ref, key_gain_ref, hidden_state_ref,
+    ) = refs[:10]
+    chain_refs, own_block_ref = refs[10:14], refs[14]
+    slope_ref, gain_ref, output_ref, chain_total_ref = refs[15:19]
+    (
         query_ref, key_ref, value_ref, out_slope_ref, turned_ref, key_sum_ref, value_sum_ref, cosine_ref, sine_ref,
-    ) = refs[:22]
-    scatter = Scatter(size, *refs[22:])
+    ) = refs[19:28]
+    buffers = 5 if size == 4 else 4
+    scatter = Scatter(size, *refs[28 : 28 + buffers])
+    own_sem = refs[28 + buffers]
+    chain = Chain(
+        chips, (chips - 1,), chain_refs[:1], chain_refs[1:2], *chain_refs[2:], *refs[29 + buffers :]
+    )
+    own_load = pltpu.make_async_copy(own_block_ref, chain_total_ref, own_sem.at[0])
     step = pl.program_id(0) * pl.num_programs(1) + pl.program_id(1)
     steps = pl.num_programs(0) * pl.num_programs(1)
 
     @pl.when(step == 0)
     def _():
+        chain.load()
         scatter.load(operands)
-        greet(neighbours(size))
-        scatter.fill(operands)
+        own_load.start()
+        greet(neighbours(size) + chain.neighbours)
+        scatter.fill(operands, slots=(0, 1))
+        chain.step(0)
+        scatter.fill(operands, slots=(1, size))
 
     attend_backward_head(
         grouping, head_size, block, state_ref, weight_ref, raw_ref, mixed_ref, total_ref, few_cosines_ref,
@@ -920,7 +928,21 @@
             )
 
         over_pieces(output_ref.shape[0], finish)
+        own_load.wait()
+        chain.wait(0)
+        for arrived, landing in zip(chain.arrives(0), (chain.up, chain.down)):
+
+            @pl.when(arrived)
+            def _(landing=landing):
+                def add(piece):
+                    chain_total_ref[piece, :] = add_rounded(
+                        chain_total_ref[piece, :], landing[1, piece, :]
+                    )
+
+                over_pieces(chain_total_ref.shape[0], add)
+
         scatter.drain()
+        chain.drain()
 
 
 def attend_backward_head(
@@ -987,7 +1009,7 @@
 
 def attention_backward(
     state_rows, weight, weight_start, raw, mixed, totals, tables, query_gain, key_gain, heads, grouping,
-    triples, hidden_state, size, collective_id,
+    triples, hidden_state, chain_arrays, own_block, sizes, collective_id,
 ):
     total_rows, depth = state_rows.shape
     head_size = query_gain.shape[0]
@@ -995,6 +1017,8 @@
     width = (grouping + 2) * head_size
     out_width = grouping * head_size
     block = min(256, SEQUENCE_LENGTH)
+    data_size, size = sizes
+    chips = data_size // 2
     first_block = weight_start // out_width
     single = pl.Buffered(1)
     table = pl.BlockSpec(tables[0].shape, lambda s, h: (0, 0))
@@ -1014,14 +1038,14 @@
         gain,
         gain,
         pl.BlockSpec(hidden_state.shape, lambda s, h: (0, 0), pipeline_mode=single),
-    ]
+    ] + [pl.BlockSpec(memory_space=pl.ANY)] * 5
     operands += [
         state_rows, weight, raw, mixed, totals, *tables, query_gain.reshape(1, -1), key_gain.reshape(1, -1),
-        hidden_state,
+        hidden_state, *chain_arrays, own_block,
     ]
     return pl.pallas_call(
         functools.partial(
-            attention_backward_kernel, size, grouping, head_size, block,
+            attention_backward_kernel, size, chips, grouping, head_size, block,
             tuple(first for _, _, first in triples),
         ),
         grid=(sequences, heads),
@@ -1029,12 +1053,14 @@
             jax.ShapeDtypeStruct((total_rows, heads * width), jnp.bfloat16),
             jax.ShapeDtypeStruct((8, head_size), jnp.float32),
             jax.ShapeDtypeStruct(hidden_state.shape, jnp.bfloat16),
+            jax.ShapeDtypeStruct(own_block.shape, jnp.bfloat16),
         ],
         in_specs=in_specs,
         out_specs=[
             pl.BlockSpec((SEQUENCE_LENGTH, width), lambda s, h: (s, h)),
             pl.BlockSpec((8, head_size), lambda s, h: (0, 0)),
             pl.BlockSpec(hidden_state.shape, lambda s, h: (0, 0)),
+            pl.BlockSpec(own_block.shape, lambda s, h: (0, 0)),
         ],
         scratch_shapes=[
             pltpu.VMEM((grouping, SEQUENCE_LENGTH, head_size), jnp.bfloat16),
@@ -1047,6 +1073,8 @@
             whole_rows,
             whole_rows,
             *Scatter.scratch(size, *hidden_state.shape),
+            pltpu.SemaphoreType.DMA((1,)),
+            *Chain.scratch(1, *own_block.shape),
             *[part for left, other, _ in triples for part in Operand.scratch(size, left, other)],
         ],
         compiler_params=pltpu.CompilerParams(
@@ -1194,7 +1222,7 @@
                 values = values + other_ref[0, :, columns].astype(jnp.float32)
                 held_ref[step, :, columns] = values.astype(jnp.bfloat16)
             else:
-                out_ref[0, :, columns] = values.astype(jnp.bfloat16)
+                out_ref[:, :, columns] = values.reshape(*out_ref.shape[:2], tile).astype(jnp.bfloat16)
         start += width
     if with_other:
         copies = [
@@ -1210,7 +1238,7 @@
                 copy.wait()
 
 
-def grad_blocks(order, pairs, other=None):
+def grad_blocks(order, pairs, other=None, group=1):
     count = order.shape[0]
     depth, total_rows = pairs[0][0].shape
     block = depth // lax.axis_size("dp")
@@ -1219,7 +1247,10 @@
     operands = []
     for left, right in pairs:
         in_specs += [
-            pl.BlockSpec((block, total_rows), lambda k, at: (at[k], 0)),
+            pl.BlockSpec(
+                (group * block, total_rows),
+                (lambda k, at: (at[k], 0)) if group == 1 else (lambda k, at: (k, 0)),
+            ),
             pl.BlockSpec(right.shape, lambda k, at: (0, 0), pipeline_mode=pl.Buffered(1)),
         ]
         operands += [left, right]
@@ -1235,12 +1266,12 @@
         ]
     else:
         out_shape = [jax.ShapeDtypeStruct((count, block, width), jnp.bfloat16)]
-        out_specs = [pl.BlockSpec((1, block, width), lambda k, at: (k, 0, 0))]
+        out_specs = [pl.BlockSpec((group, block, width), lambda k, at: (k, 0, 0))]
     out = pl.pallas_call(
         functools.partial(grad_kernel, len(pairs), other is not None),
         grid_spec=pltpu.PrefetchScalarGridSpec(
             num_scalar_prefetch=1,
-            grid=(count,),
+            grid=(count // group,),
             in_specs=in_specs,
             out_specs=out_specs,
             scratch_shapes=scratch,
@@ -1301,7 +1332,7 @@
 
 
 def finish_kernel(
-    heads, own_ref, up_ref, down_ref, second_ref, mixing_ref, output_total_ref, terms_ref, output_rows_ref, input_rows_ref,
+    heads, first_ref, second_ref, mixing_ref, output_total_ref, terms_ref, output_rows_ref, input_rows_ref,
     output_rows_out, input_rows_out, attention_term_out, query_out, key_out, value_out, query_gain_out, key_gain_out,
     output_out, feed_term_out, gate_out, up_out, down_out,
 ):
@@ -1313,17 +1344,12 @@
     query_gain_out[...] = terms_ref[2 * count : 2 * count + 1, :]
     key_gain_out[...] = terms_ref[2 * count + 1 : 2 * count + 2, :]
     start = 0
-    for total_refs in ((own_ref, up_ref, down_ref), (second_ref,)):
-        width = total_refs[0].shape[1] // 3
+    for total_ref in (first_ref, second_ref):
+        width = total_ref.shape[1] // 3
         part = slice(start, start + width)
-
-        def total(index):
-            columns = slice(index * width, (index + 1) * width)
-            return sum(ref[:, columns].astype(jnp.float32) for ref in total_refs)
-
-        gate_out[:, part] = total(0)
-        up_out[:, part] = total(1)
-        down_out[part, :] = total(2).T
+        gate_out[:, part] = total_ref[:, :width].astype(jnp.float32)
+        up_out[:, part] = total_ref[:, width : 2 * width].astype(jnp.float32)
+        down_out[part, :] = total_ref[:, 2 * width :].astype(jnp.float32).T
         start += width
     query_width = query_out.shape[1] // heads
     head_size = key_out.shape[1] // heads
@@ -1375,7 +1401,7 @@
     grouping = query_columns // key_columns
     hidden_columns = gate_weight.shape[1]
     qkv_columns = query_columns + 2 * key_columns
-    first_columns = hidden_columns * 2 // 3 // 256 * 256 or hidden_columns // 2
+    first_columns = hidden_columns // 2
     second_columns = hidden_columns - first_columns
     tables = turn_tables(head_size)
 
@@ -1440,21 +1466,21 @@
     hidden_second, slope_second = feed_half(feed_rows, cotangent_rows, later_full)
     plain_order = jnp.arange(sizes[0], dtype=jnp.int32)
     second_grad = grad_blocks(
-        plain_order, [(feed_turned, slope_second), (cotangent_turned, hidden_second)]
+        plain_order, [(feed_turned, slope_second), (cotangent_turned, hidden_second)], group=2
     ).reshape(model_width, -1)
     second_grad, slope_second = lax.optimization_barrier((second_grad, slope_second))
     second_total = lax.psum_scatter(second_grad, "dp", scatter_dimension=0, tiled=True)
     chips = sizes[0] // 2
     middle_steps = tuple(range(2, chips - 1))
     chain_block = jax.ShapeDtypeStruct(blocks[0].shape, jnp.bfloat16)
-    state_rows, state_turned, state_slope, feed_term, rising, falling = scatter_call(
+    state_rows, state_turned, state_slope, feed_term, up, down = scatter_call(
         functools.partial(between_backward_kernel, size, chips, middle_steps),
         [(slope_first, feed_full[0], 0), (slope_second, later_full, 0)],
         size,
         [hidden_state, out_cotangent, feed_gain.reshape(1, -1)],
         [blocks[chips - step] for step in middle_steps]
         + [blocks[step] for step in middle_steps]
-        + [up, down, blocks[1], blocks[chips - 1]],
+        + [up, down],
         [
             *gathered_shapes,
             local_float,
@@ -1466,32 +1492,25 @@
         [
             own_rows,
             row_sum,
-            pltpu.SemaphoreType.DMA((2,)),
             *scatter_scratch,
             *gather_scratch,
             *Chain.scratch(len(middle_steps), *blocks[0].shape),
         ],
         2,
     )
-    up = lax.ppermute(
-        rising, "dp", [(device, device + 2) for device in range(sizes[0] - 2)]
-    )
-    down = lax.ppermute(
-        falling, "dp", [(device, device - 2) for device in range(2, sizes[0])]
-    )
-    output_grad = grad_blocks(plain_order, [(state_turned, mixed_rows)]).reshape(model_width, -1)
+    output_grad = grad_blocks(plain_order, [(state_turned, mixed_rows)], group=4).reshape(model_width, -1)
     output_grad, state_rows = lax.optimization_barrier((output_grad, state_rows))
     output_total = lax.psum_scatter(output_grad, "dp", scatter_dimension=0, tiled=True)
-    qkv_slope, head_terms, block_output = attention_backward(
+    qkv_slope, head_terms, block_output, first_total = attention_backward(
         state_rows, mixing_full, qkv_columns, raw, mixed_rows, totals, tables,
         query_gain, key_gain, heads, grouping,
         [
             (hidden_first, feed_full[0], 2 * first_columns),
             (hidden_second, later_full, 2 * second_columns),
         ],
-        hidden_state, size, 4,
-    )
-    mixing_grad = grad_blocks(plain_order, [(mixer_turned, qkv_slope)]).reshape(model_width, -1)
+        hidden_state, [blocks[1], blocks[chips - 1], up, down], blocks[0], sizes, 4,
+    )
+    mixing_grad = grad_blocks(plain_order, [(mixer_turned, qkv_slope)], group=2).reshape(model_width, -1)
     mixing_grad, qkv_slope = lax.optimization_barrier((mixing_grad, qkv_slope))
     mixing_total = lax.psum_scatter(mixing_grad, "dp", scatter_dimension=0, tiled=True)
     terms_shape = (2 * gain_rows + head_terms.shape[0], head_size)
@@ -1541,7 +1560,7 @@
             whole_float(block_width, hidden_columns),
             whole_float(hidden_columns, block_width),
         ],
-        blocks[0], up, down, second_total, mixing_total, output_total, terms, block_output, input_gradient,
+        first_total, second_total, mixing_total, output_total, terms, block_output, input_gradient,
     )
     return tuple(
         out.reshape(-1) if index in (2, 6, 7, 9) else out for index, out in enumerate(outs)

time: 615 us -> 638 us (1.037)
  waiting for transfers between devices: 95.6 us -> 142 us
  Pallas kernels: 489 us -> 469 us
    reduce_scatter x1, waiting for transfers between devices: 70 us -> 100 us  [per_device(): lax.psum_scatter(second_grad, 'dp', scatter_dimension=0, tiled=True)]
    pallas_call x3, Pallas kernels: 244 us -> 215 us  [scatter_call(): pl.pallas_call(functools.partial(body, tuple((first for _, _, first in tr...]
    all_gather x2, waiting for transfers between devices: 8.96 us -> 28.8 us  [per_device(): lax.all_gather(part, 'dp', axis=0, tiled=True)]
    pallas_call x1, Pallas kernels: 45 us -> 61.4 us  [attention_backward(): pl.pallas_call(functools.partial(attention_backward_kernel, size, chips,...]
  transfers between devices with their start and end apart: 11 -> 9, of which waited for: 5 -> 4; matrix products, arithmetic and copies ran while one was open for 1% -> 1% of each run, Pallas kernels for 62% -> 57%
where the time goes in v8:
time: 638 us; the launch traced here: 637 us
  Pallas kernels  469 us (74%)
  waiting for transfers between devices  142 us (22%)
  between operations  14.3 us (2%)
    pallas_call x3, Pallas kernels, scatter_call(): pl.pallas_call(functools.partial(body, tuple((first for _, _, first in tr...  215 us
    reduce_scatter x1, waiting for transfers between devices, per_device(): lax.psum_scatter(second_grad, 'dp', scatter_dimension=0, tiled=True)  100 us
    pallas_call x1, Pallas kernels, gather_rows(): pl.pallas_call(functools.partial(gather_kernel, size, count), out_shape=o...  76.4 us
    pallas_call x1, Pallas kernels, attention_backward(): pl.pallas_call(functools.partial(attention_backward_kernel, size, chips,...  61.4 us
    pallas_call x5, Pallas kernels, grad_blocks(): pl.pallas_call(functools.partial(grad_kernel, len(pairs), other is not No...  52.6 us
    pallas_call x2, Pallas kernels, feed_half(): pl.pallas_call(functools.partial(feed_half_kernel, half, tile, block), ou...  33.8 us
    all_gather x2, waiting for transfers between devices, per_device(): lax.all_gather(part, 'dp', axis=0, tiled=True)  28.8 us
    pallas_call x1, Pallas kernels, attention_forward(): pl.pallas_call(functools.partial(attention_forward_kernel, grouping, head...  18.5 us
  transfers between devices with their start and end apart: 9, of which 4 were waited for; matrix products, arithmetic and copies ran while one was open for 1% of the time, Pallas kernels for 57%

profile of v8, /device:TPU:0, one launch (start us, length us, event | category | flops | bytes accessed | tf_op | source)
XLA Modules:
  0.0 637.1 jit_solution(9388501933669592487)
XLA Ops:
  7.2 0.0 all-gather.4.cloned.1.call-start
  7.2 2.2 shard_map.246
  9.4 0.0 all-gather.4.cloned.1.call-update
  9.4 0.0 copy-start
  9.4 0.0 all-gather.6.cloned.1.call-start
  9.5 3.3 shard_map.248
  12.8 0.0 all-gather.6.cloned.1.call-update
  12.8 0.0 all-gather.8.cloned.1.call-start
  12.9 0.7 all-gather.8.cloned.1.call-update
  13.6 0.0 reduce-scatter.8.cloned.1.call-start
  13.6 0.3 fusion
  13.9 1.3 fusion.2.refs_0_
  15.2 76.4 %gather_rows.1 = (bf16[1024,2048]{1,0:T(8,128)(2,1)}, bf16[2048,1024]{1,0:T(8,128)(2,1)}, bf16[1024,2048]{1,0:T(8,128)(2,1)}, bf16[2048,1024]{1,0:T(8,128)(2,1)}) custom-call(bf16[256,2048]{1,0:T(8,128)(2,1)} %fusion.2.refs_0_, bf16[256,2048]{1,0:T(8,128)(2,1)} %refs_5_.1), custom_call_target="tpu_custom_call" | custom-call | bytes 125829120 | tf_op jit(solution)/shard_map/gather_rows/pallas_call | solution.py:205
  91.6 0.5 broadcast_add_fusion.order_ref
  92.1 18.5 %attention_forward.1 = (f32[1024,1024]{1,0:T(8,128)}, bf16[1024,512]{1,0:T(8,128)(2,1)}, f32[2,2,1024]{2,1,0:T(2,128)}) custom-call(bf16[1024,2048]{1,0:T(8,128)(2,1)} %get-tuple-element.69.rows_ref.refs_6_, bf16[2048,1536]{1,0:T(8,128)(2,1)} %all-gather.4.cloned.1.call-done.weight_ref.refs_1_.refs_5_, f32[136,128]{1,0:T(8,128)} %constant.38.clone.few_cosines_ref.refs_9_, ...), custom_call_target="tpu_custom_call" | custom-call | flops 5368709120 | bytes 8388608 | tf_op jit(solution)/shard_map/attention_forward/pallas_call | solution.py:832
  110.6 77.5 %shard_map.247 = (bf16[1024,2048]{1,0:T(8,128)(2,1)}, bf16[2048,1024]{1,0:T(8,128)(2,1)}, f32[256,2048]{1,0:T(8,128)}) custom-call(bf16[1024,512]{1,0:T(8,128)(2,1)} %get-tuple-element.70.refs_0_.refs_1_.refs_7_, bf16[2048,1536]{1,0:T(8,128)(2,1)} %all-gather.4.cloned.1.call-done.weight_ref.refs_1_.refs_5_, bf16[256,2048]{1,0:T(8,128)(2,1)} %refs_2_.3, ...), custom_call_target="tpu_custom_call" | custom-call | flops 2147483648 | bytes 150000000 | tf_op jit(solution)/shard_map/pallas_call | solution.py:697
  188.2 0.0 all-gather.6.cloned.1.call-done.weight_far.refs_1_
  188.2 17.0 %feed_half.2 = (bf16[1024,768]{1,0:T(8,128)(2,1)}, bf16[1024,1536]{1,0:T(8,128)(2,1)}) custom-call(bf16[1024,2048]{1,0:T(8,128)(2,1)} %get-tuple-element.71.rows_far, bf16[1024,2048]{1,0:T(8,128)(2,1)} %get-tuple-element.72.cotangent_far, bf16[2048,2304]{1,0:T(8,128)(2,1)} %all-gather.6.cloned.1.call-done.weight_far.refs_1_), custom_call_target="tpu_custom_call" | custom-call | flops 9663676416 | bytes 17825792 | tf_op jit(solution)/shard_map/feed_half/pallas_call | solution.py:1177
  205.2 10.4 %grad_blocks.5 = bf16[4,256,2304]{2,1,0:T(8,128)(2,1)} custom-call(s32[4]{0:T(128)} %broadcast_add_fusion.order_ref, bf16[2048,1024]{1,0:T(8,128)(2,1)} %get-tuple-element.75.refs_0_, bf16[1024,1536]{1,0:T(8,128)(2,1)} %get-tuple-element.76.refs_1_.refs_0_, bf16[2048,1024]{1,0:T(8,128)(2,1)} %get-tuple-element.77.refs_2_, ...), custom_call_target="tpu_custom_call" | custom-call | flops 4831838208 | bytes 13631488 | tf_op jit(solution)/shard_map/grad_blocks/pallas_call | solution.py:1270
  215.6 0.5 broadcast_add_fusion.1.order_ref
  216.1 8.2 %collective-permute-done.refs_4_ = bf16[4,256,2304]{2,1,0:T(8,128)(2,1)} collective-permute-done((bf16[4,256,2304]{2,1,0:T(8,128)(2,1)}, bf16[4,256,2304]{2,1,0:T(8,128)(2,1)}, u32[]{:S(2)}, u32[]{:S(2)}) %collective-permute-start) | collective-permute-done | bytes 4718624 | tf_op jit(solution)/shard_map/ppermute | solution.py:1297
  224.4 11.4 %grad_blocks.6 = (bf16[256,2304]{1,0:T(8,128)(2,1)}, bf16[256,2304]{1,0:T(8,128)(2,1)}, bf16[256,2304]{1,0:T(8,128)(2,1)}, bf16[256,2304]{1,0:T(8,128)(2,1)}) custom-call(s32[4]{0:T(128)} %broadcast_add_fusion.1.order_ref, bf16[2048,1024]{1,0:T(8,128)(2,1)} %get-tuple-element.75.refs_0_, bf16[1024,1536]{1,0:T(8,128)(2,1)} %get-tuple-element.76.refs_1_.refs_0_, ...), custom_call_target="tpu_custom_call" | custom-call | flops 4831838208 | bytes 13631488 | tf_op jit(solution)/shard_map/grad_blocks/pallas_call | solution.py:1270
  235.7 0.7 collective-permute-start.2
  236.5 4.6 collective-permute-start.1
  241.1 28.8 %all-gather.8.cloned.1.call-done.weight_far.refs_3_ = bf16[2048,2304]{1,0:T(8,128)(2,1)} async-done(((bf16[256,2304]{1,0:T(8,128)(2,1)}), bf16[2048,2304]{1,0:T(8,128)(2,1)}) %all-gather.8.cloned.1.call-update) | async-done | bytes 9437200 | tf_op jit(solution)/shard_map/all_gather | solution.py:1423
  269.9 16.9 %feed_half.3 = (bf16[1024,768]{1,0:T(8,128)(2,1)}, bf16[1024,1536]{1,0:T(8,128)(2,1)}) custom-call(bf16[1024,2048]{1,0:T(8,128)(2,1)} %get-tuple-element.71.rows_far, bf16[1024,2048]{1,0:T(8,128)(2,1)} %get-tuple-element.72.cotangent_far, bf16[2048,2304]{1,0:T(8,128)(2,1)} %all-gather.8.cloned.1.call-done.weight_far.refs_3_), custom_call_target="tpu_custom_call" | custom-call | flops 9663676416 | bytes 17825792 | tf_op jit(solution)/shard_map/feed_half/pallas_call | solution.py:1177
  286.7 0.5 iota.12.order_ref
  287.2 15.7 %grad_blocks.7 = bf16[8,256,2304]{2,1,0:T(8,128)(2,1)} custom-call(s32[8]{0:T(128)} %iota.12.order_ref, bf16[2048,1024]{1,0:T(8,128)(2,1)} %get-tuple-element.75.refs_0_, bf16[1024,1536]{1,0:T(8,128)(2,1)} %get-tuple-element.86.refs_1_.refs_2_, bf16[2048,1024]{1,0:T(8,128)(2,1)} %get-tuple-element.77.refs_2_, bf16[1024,768]{1,0:T(8,128)(2,1)} %get-tuple-element.84.refs_3_.refs_2_), custom_call_target="tpu_custom_call" | custom-call | flops 9663676416 | bytes 22544384 | tf_op jit(solution)/shard_map/grad_blocks/pallas_call | solution.py:1270
  303.0 0.0 collective-permute-done.2.refs_10_
  303.0 1.0 copy-done.4
  304.0 88.9 %shard_map.249 = (bf16[1024,2048]{1,0:T(8,128)(2,1)}, bf16[2048,1024]{1,0:T(8,128)(2,1)}, f32[256,2048]{1,0:T(8,128)}, f32[16,128]{1,0:T(8,128)}, bf16[256,2304]{1,0:T(8,128)(2,1)}, /*index=5*/bf16[256,2304]{1,0:T(8,128)(2,1)}) custom-call(bf16[1024,1536]{1,0:T(8,128)(2,1)} %get-tuple-element.76.refs_1_.refs_0_, ...), custom_call_target="tpu_custom_call" | custom-call | flops 12884901888 | bytes 150000000 | tf_op jit(solution)/shard_map/pallas_call | solution.py:697
  392.9 0.5 iota.11.order_ref
  393.4 6.0 grad_blocks.8
  399.4 0.0 reduce-scatter.8.cloned.1.call-update
  399.4 0.3 reduce-scatter.6.cloned.1.call-start
  399.7 61.4 %attention_backward.1 = (bf16[1024,1024]{1,0:T(8,128)(2,1)}, f32[8,128]{1,0:T(8,128)}, bf16[256,2048]{1,0:T(8,128)(2,1)}, bf16[256,2304]{1,0:T(8,128)(2,1)}) custom-call(bf16[1024,768]{1,0:T(8,128)(2,1)} %get-tuple-element.74.refs_3_.refs_0_, bf16[2048,2304]{1,0:T(8,128)(2,1)} %all-gather.6.cloned.1.call-done.weight_far.refs_1_, ...), custom_call_target="tpu_custom_call" | custom-call | flops 4831838208 | bytes 100000000 | tf_op jit(solution)/shard_map/attention_backward/pallas_call | solution.py:1046
  461.1 0.5 iota.13.order_ref
  461.6 9.1 %grad_blocks.9 = bf16[8,256,1024]{2,1,0:T(8,128)(2,1)} custom-call(s32[8]{0:T(128)} %iota.13.order_ref, bf16[2048,1024]{1,0:T(8,128)(2,1)} %get-tuple-element.101.refs_0_, bf16[1024,1024]{1,0:T(8,128)(2,1)} %get-tuple-element.105.refs_1_.refs_0_), custom_call_target="tpu_custom_call" | custom-call | flops 4294967296 | bytes 10485760 | tf_op jit(solution)/shard_map/grad_blocks/pallas_call | solution.py:1270
  470.7 0.0 reduce-scatter.6.cloned.1.call-update
  470.8 0.0 reduce-scatter.4.cloned.1.call-start
  470.8 0.5 reduce-scatter.4.cloned.1.call-update
  471.3 0.1 copy-done.2
  471.4 0.6 pad_maximum_fusion.refs_5_
  472.0 48.6 %shard_map.250 = (bf16[256,2048]{1,0:T(8,128)(2,1)}, f32[40,128]{1,0:T(8,128)}) custom-call(bf16[1024,1024]{1,0:T(8,128)(2,1)} %get-tuple-element.105.refs_1_.refs_0_, bf16[2048,1536]{1,0:T(8,128)(2,1)} %all-gather.4.cloned.1.call-done.weight_ref.refs_1_.refs_5_, bf16[256,2048]{1,0:T(8,128)(2,1)} %refs_2_.3, f32[1,2048]{1,0:T(1,128)} %bitcast.16, ...), custom_call_target="tpu_custom_call" | custom-call | flops 4294967296 | bytes 150000000 | tf_op jit(solution)/shard_map/pallas_call | solution.py:697
  520.6 0.0 reduce-scatter.8.cloned.1.call-done.output_total_ref
  520.7 3.2 reduce-scatter.6.cloned.1.call-done.mixing_ref
  523.9 100.1 %reduce-scatter.4.cloned.1.call-done.second_ref = bf16[256,2304]{1,0:T(8,128)(2,1)} async-done(((bf16[2048,2304]{1,0:T(8,128)(2,1)}), bf16[256,2304]{1,0:T(8,128)(2,1)}) %reduce-scatter.4.cloned.1.call-update) | async-done | bytes 1179664 | tf_op jit(solution)/shard_map/reduce_scatter | solution.py:1472
  624.0 6.2 shard_map.251
  (11 shorter events, 0.0 us)
Async XLA Ops:
  7.2 84.9 %all-gather.4.cloned.1.call-start = ((), (), s32[]{:S(2)}) async-start(), calls=%async_computation.3 | async-start | bytes 7077888 | tf_op jit(solution)/shard_map/all_gather | solution.py:1414
  9.4 4.2 copy-start
  9.4 178.8 %all-gather.6.cloned.1.call-start = ((), (), s32[]{:S(2)}) async-start(), calls=%async_computation.4 | async-start | bytes 10616832 | tf_op jit(solution)/shard_map/all_gather | solution.py:1423
  12.8 1.1 copy-start.1
  12.8 257.0 %all-gather.8.cloned.1.call-start = ((), (), s32[]{:S(2)}) async-start(), calls=%async_computation.5 | async-start | bytes 10616832 | tf_op jit(solution)/shard_map/all_gather | solution.py:1423
  13.6 507.1 %reduce-scatter.8.cloned.1.call-start = ((), (), s32[]{:S(2)}) async-start(), calls=%async_computation.8 | async-start | bytes 2359296 | tf_op jit(solution)/shard_map/reduce_scatter | solution.py:1503
  215.6 8.7 %collective-permute-start = (bf16[4,256,2304]{2,1,0:T(8,128)(2,1)}, bf16[4,256,2304]{2,1,0:T(8,128)(2,1)}, u32[]{:S(2)}, u32[]{:S(2)}) collective-permute-start(bf16[4,256,2304]{2,1,0:T(8,128)(2,1)} %grad_blocks.5), channel_id=1, source_target_pairs={{0,4},{4,0},{8,12},{12,8},{16,20},{20,16},{24,28},{28,24},{1,5},{5... | collective-permute-start | bytes 14155784 | tf_op jit(solution)/shard_map/ppermute | solution.py:1297
  235.7 67.2 %collective-permute-start.2 = (bf16[256,2304]{1,0:T(8,128)(2,1)}, bf16[256,2304]{1,0:T(8,128)(2,1)S(1)}, u32[]{:S(2)}, u32[]{:S(2)}) collective-permute-start(bf16[256,2304]{1,0:T(8,128)(2,1)} %get-tuple-element.94.refs_14_), channel_id=1, source_target_pairs={{24,16},{28,20},{25,17},{29,21},{26,18},{30,22},{27,19},{31,23}} | collective-permute-start | bytes 3538952 | tf_op jit(solution)/shard_map/ppermute | solution.py:1304
  236.5 66.5 %collective-permute-start.1 = (bf16[256,2304]{1,0:T(8,128)(2,1)}, bf16[256,2304]{1,0:T(8,128)(2,1)}, u32[]{:S(2)}, u32[]{:S(2)}) collective-permute-start(bf16[256,2304]{1,0:T(8,128)(2,1)} %get-tuple-element.95.refs_15_), channel_id=1, source_target_pairs={{0,8},{4,12},{1,9},{5,13},{2,10},{6,14},{3,11},{7,15}} | collective-permute-start | bytes 3538952 | tf_op jit(solution)/shard_map/ppermute | solution.py:1303
  303.0 1.0 copy-start.4
  399.4 124.5 %reduce-scatter.6.cloned.1.call-start = ((), (), s32[]{:S(2)}) async-start(), calls=%async_computation.7 | async-start | bytes 4718592 | tf_op jit(solution)/shard_map/reduce_scatter | solution.py:1515
  470.7 0.7 copy-start.2
  470.8 0.7 copy-start.3
  470.8 153.2 %reduce-scatter.4.cloned.1.call-start = ((), (), s32[]{:S(2)}) async-start(), calls=%async_computation.6 | async-start | bytes 10616832 | tf_op jit(solution)/shard_map/reduce_scatter | solution.py:1472
Sparse Core Ops, SparseCore 0:
  10.2 67.4 all-gather.3
  79.9 89.3 all-gather.5
  171.5 98.2 all-gather.7
  399.5 52.7 reduce-scatter.7
  470.9 53.0 reduce-scatter.5
  526.1 97.8 reduce-scatter.3

commit v9 on v7

--- a/solution.py
+++ b/solution.py
@@ -83,7 +83,7 @@
 
     @staticmethod
     def scratch(size, rows, columns):
-        sends, local = (6, 8) if size == 4 else (size - 1, size)
+        sends, local = (12, 8) if size == 4 else (size - 1, size)
         return [
             pltpu.VMEM((size, rows, columns), jnp.bfloat16),
             pltpu.VMEM((columns, size * rows), jnp.bfloat16),
@@ -119,19 +119,22 @@
         turn_copy.start()
         self.turns.append(turn_copy)
 
-    def start(self):
-        own, held, rows = self.own, self.held, self.rows
+    def quarters(self):
+        quarter = self.rows // 4
+        return [pl.ds(index * quarter, quarter) for index in range(4)]
+
+    def start(self, stage):
+        own, held = self.own, self.held
         if self.size != 4:
-            for peer in other_members("tensor", self.size):
-                self.send(own, held.at[self.me], peer)
+            if stage == 0:
+                for peer in other_members("tensor", self.size):
+                    self.send(own, held.at[self.me], peer)
             return
         beside, below, _ = square_peers(self.me)
-        half = rows // 2
-        first, second = pl.ds(0, half), pl.ds(half, half)
-        self.send(own.at[first], held.at[self.me, first], beside)
-        self.send(own.at[second], held.at[self.me, second], below)
-        self.send(own.at[second], held.at[self.me, second], beside)
-        self.send(own.at[first], held.at[self.me, first], below)
+        parts = self.quarters()
+        upper, lower = parts[stage], parts[2 + stage]
+        for part, peer in ((upper, beside), (lower, below), (lower, beside), (upper, below)):
+            self.send(own.at[part], held.at[self.me, part], peer)
 
     def forward(self):
         own, held, rows = self.own, self.held, self.rows
@@ -140,14 +143,14 @@
             return
         beside, below, _ = square_peers(self.me)
         half = rows // 2
-        first, second = pl.ds(0, half), pl.ds(half, half)
-        x_first, y_second = self.copies[:2]
-        self.store(own.at[first], self.me * rows, half)
-        self.store(own.at[second], self.me * rows + half, half)
-        x_first.wait_recv()
-        self.send(held.at[beside, first], held.at[beside, first], below)
-        y_second.wait_recv()
-        self.send(held.at[below, second], held.at[below, second], beside)
+        self.store(own.at[pl.ds(0, half)], self.me * rows, half)
+        self.store(own.at[pl.ds(half, half)], self.me * rows + half, half)
+        parts = self.quarters()
+        for stage in range(2):
+            self.copies[4 * stage].wait_recv()
+            self.send(held.at[beside, parts[stage]], held.at[beside, parts[stage]], below)
+            self.copies[4 * stage + 1].wait_recv()
+            self.send(held.at[below, parts[2 + stage]], held.at[below, parts[2 + stage]], beside)
 
     def finish(self):
         held, rows = self.held, self.rows
@@ -160,17 +163,17 @@
             beside, below, across = square_peers(self.me)
             half = rows // 2
             first, second = pl.ds(0, half), pl.ds(half, half)
-            x_second, y_first, y_pass, x_pass = self.copies[2:]
             self.store(held.at[beside, first], beside * rows, half)
             self.store(held.at[below, second], below * rows + half, half)
-            x_second.wait_recv()
-            self.store(held.at[beside, second], beside * rows + half, half)
-            y_first.wait_recv()
-            self.store(held.at[below, first], below * rows, half)
-            y_pass.wait_recv()
-            self.store(held.at[across, first], across * rows, half)
-            x_pass.wait_recv()
-            self.store(held.at[across, second], across * rows + half, half)
+            for indices, slot, start in (
+                ((2, 6), beside, half),
+                ((3, 7), below, 0),
+                ((8, 10), across, 0),
+                ((9, 11), across, half),
+            ):
+                for index in indices:
+                    self.copies[index].wait_recv()
+                self.store(held.at[slot, pl.ds(start, half)], slot * rows + start, half)
         for copy in self.copies:
             copy.wait_send()
         for copy in self.stores + self.turns:
@@ -185,7 +188,8 @@
         for k in range(count)
     ]
     for gather in gathers:
-        gather.start()
+        gather.start(0)
+        gather.start(1)
         gather.forward()
     for gather in gathers:
         gather.finish()
@@ -249,7 +253,7 @@
         )
 
 
-def block_product(operands, start, rows, fresh, write):
+def block_product(operands, start, rows, fresh, write, after):
     total = operands[0].weight.shape[0]
     tile = operands[0].tile
     start = pl.multiple_of(start, rows)
@@ -268,6 +272,7 @@
             )
             values = part if values is None else values + part
         write(columns, values)
+        after(index)
         return carry
 
     lax.fori_loop(0, total // tile, step, 0)
@@ -281,12 +286,13 @@
         self.arriving, self.send_sem, self.recv_sem = rest
         self.rows = outgoing.shape[1]
         self.me = lax.axis_index("tensor")
-        self.copies, self.starts = self.plan()
+        self.stages = 2 if size == 4 else 1
+        self.plan()
 
     @staticmethod
     def scratch(size, rows, columns):
         if size == 4:
-            sends = 6
+            sends = 10
             buffers = [
                 pltpu.VMEM((4, rows, columns), jnp.bfloat16),
                 pltpu.VMEM((2, rows // 2, columns), jnp.bfloat16),
@@ -306,23 +312,33 @@
     def plan(self):
         outgoing, arriving = self.outgoing, self.arriving
         if self.size != 4:
-            copies = [
+            self.copies = [
                 self.prepare(step, outgoing.at[step], arriving.at[step], peer)
                 for step, peer in enumerate(other_members("tensor", self.size))
             ]
-            return copies, tuple((step, step) for step in range(self.size - 1))
+            self.early, self.starts = (), tuple((step, step) for step in range(self.size - 1))
+            return
         beside, below, _ = square_peers(self.me)
-        half = self.rows // 2
+        half, quarter = self.rows // 2, self.rows // 4
         first, second = pl.ds(0, half), pl.ds(half, half)
-        copies = [
-            self.prepare(0, outgoing.at[0, first], self.passing.at[0], beside),
-            self.prepare(1, outgoing.at[0, second], self.passing.at[1], below),
-            self.prepare(2, outgoing.at[1, first], arriving.at[0, first], beside),
-            self.prepare(3, outgoing.at[2, second], arriving.at[1, second], below),
-            self.prepare(4, outgoing.at[1, second], arriving.at[0, second], beside),
-            self.prepare(5, outgoing.at[2, first], arriving.at[1, first], below),
+        middle = outgoing.shape[2] // 2
+        left, right = pl.ds(0, middle), pl.ds(middle, middle)
+        upper = [pl.ds(stage * quarter, quarter) for stage in range(2)]
+        lower = [pl.ds(half + stage * quarter, quarter) for stage in range(2)]
+        everything = pl.ds(0, half)
+        self.copies = [
+            self.prepare(0, outgoing.at[0, first, left], self.passing.at[0, everything, left], beside),
+            self.prepare(1, outgoing.at[0, second, left], self.passing.at[1, everything, left], below),
+            self.prepare(2, outgoing.at[0, first, right], self.passing.at[0, everything, right], beside),
+            self.prepare(3, outgoing.at[0, second, right], self.passing.at[1, everything, right], below),
+            self.prepare(4, outgoing.at[1, first], arriving.at[0, first], beside),
+            self.prepare(5, outgoing.at[2, second], arriving.at[1, second], below),
+            self.prepare(6, outgoing.at[1, lower[0]], arriving.at[0, lower[0]], beside),
+            self.prepare(7, outgoing.at[2, upper[0]], arriving.at[1, upper[0]], below),
+            self.prepare(8, outgoing.at[1, lower[1]], arriving.at[0, lower[1]], beside),
+            self.prepare(9, outgoing.at[2, upper[1]], arriving.at[1, upper[1]], below),
         ]
-        return copies, ((0, 0), (0, 1), (1, 2), (2, 3))
+        self.early, self.starts = (0, 1), ((0, 2), (0, 3), (1, 4), (2, 5))
 
     def owner(self, slot):
         if self.size != 4:
@@ -343,7 +359,7 @@
             for operand in operands:
                 operand.left_copy(slot, self.owner(slot)).start()
 
-    def fill(self, operands, look=None, slots=None):
+    def fill(self, operands, look=None, between=None):
         rows = self.rows
 
         def step(slot, carry):
@@ -356,33 +372,65 @@
                 if look is not None:
                     look(owner, columns, values)
 
-            block_product(operands, owner * rows, rows, slot == 0, write)
+            tiles = operands[0].weight.shape[0] // operands[0].tile
+
+            def after(index):
+                for early in self.early:
+                    pl.when((slot == 0) & (index == max(tiles // 2, 1) - 1))(self.copies[early].start)
+
+            block_product(operands, owner * rows, rows, slot == 0, write, after)
             for at, index in self.starts:
                 pl.when(slot == at)(self.copies[index].start)
+            if between is not None:
+                pl.when(slot == 0)(between)
             return carry
 
-        lax.fori_loop(*(slots or (0, self.size)), step, 0)
+        lax.fori_loop(0, self.size, step, 0)
 
     def relay(self):
         if self.size != 4:
             return
-        half = self.rows // 2
-        x_pass, y_pass, _, _, x_second, y_first = self.copies
-        for arrival, source, slot, start, onward in (
-            (y_pass, 1, 1, half, x_second),
-            (x_pass, 0, 2, 0, y_first),
-        ):
-            arrival.wait_recv()
-            piece = pl.ds(start, half)
-            self.outgoing[slot, piece, :] = (
-                self.outgoing[slot, piece, :].astype(jnp.float32)
-                + self.passing[source].astype(jnp.float32)
-            ).astype(self.outgoing.dtype)
-            onward.start()
-
-    def collect(self):
-        for copy in self.copies[2:] if self.size == 4 else self.copies:
-            copy.wait_recv()
+        half, quarter = self.rows // 2, self.rows // 4
+        for stage in range(2):
+            for arrivals, source, slot, start, onward in (
+                ((1, 3), 1, 1, half, 6 + 2 * stage),
+                ((0, 2), 0, 2, 0, 7 + 2 * stage),
+            ):
+                if stage == 0:
+                    for index in arrivals:
+                        self.copies[index].wait_recv()
+                piece = pl.ds(start + stage * quarter, quarter)
+                self.outgoing[slot, piece, :] = add_rounded(
+                    self.outgoing[slot, piece, :],
+                    self.passing[source, stage * quarter : (stage + 1) * quarter, :],
+                )
+                self.copies[onward].start()
+
+    def collect(self, stage):
+        if self.size != 4:
+            for copy in self.copies:
+                copy.wait_recv()
+            return
+        if stage == 0:
+            self.copies[4].wait_recv()
+            self.copies[5].wait_recv()
+        self.copies[6 + 2 * stage].wait_recv()
+        self.copies[7 + 2 * stage].wait_recv()
+
+    def over_rows(self, stage, body):
+        if self.size != 4:
+            over_pieces(self.rows, body)
+            return
+        half, quarter = self.rows // 2, self.rows // 4
+        over_pieces(quarter, body, stage * quarter)
+        over_pieces(quarter, body, half + stage * quarter)
+
+    def over_stages(self, body, done=None):
+        for stage in range(self.stages):
+            self.collect(stage)
+            self.over_rows(stage, body)
+            if done is not None:
+                done(stage)
 
     def total(self, piece):
         total = self.outgoing[self.size - 1, piece, :].astype(jnp.float32)
@@ -495,11 +543,11 @@
     return (first.astype(jnp.float32) + second.astype(jnp.float32)).astype(jnp.bfloat16)
 
 
-def over_pieces(rows, body):
+def over_pieces(rows, body, start=0):
     count = min(32, rows)
 
     def step(index, carry):
-        body(pl.ds(pl.multiple_of(index * count, count), count))
+        body(pl.ds(pl.multiple_of(start + index * count, count), count))
         return carry
 
     lax.fori_loop(0, rows // count, step, 0)
@@ -551,15 +599,13 @@
     greet(neighbours(size))
     scatter.fill(operands)
     scatter.relay()
-    scatter.collect()
 
     def norm(piece):
         state = input_ref[piece, :].astype(jnp.float32) + scatter.total(piece)
         state_ref[piece, :] = state
         own_ref[piece, :] = (state * row_scale(state) * gain_ref[...]).astype(own_ref.dtype)
 
-    over_pieces(own_ref.shape[0], norm)
-    gather.start()
+    scatter.over_stages(norm, gather.start)
     gather.forward()
     gather.finish()
     scatter.drain()
@@ -588,12 +634,9 @@
     for load in last_loads:
         load.start()
     greet(neighbours(size) + chain.neighbours)
-    scatter.fill(operands, slots=(0, 1))
-    chain.step(0)
-    scatter.fill(operands, slots=(1, size))
+    scatter.fill(operands, between=lambda: chain.step(0))
     scatter.relay()
     sum_ref[...] = jnp.zeros_like(sum_ref)
-    scatter.collect()
 
     def norm(piece):
         back = scatter.total(piece)
@@ -608,8 +651,7 @@
         slope_ref[piece, :] = slope
         own_ref[piece, :] = slope.astype(own_ref.dtype)
 
-    over_pieces(own_ref.shape[0], norm)
-    gather.start()
+    scatter.over_stages(norm, gather.start)
     store_row(term_ref, sum_ref)
     gather.forward()
     chain.wait(0)
@@ -671,7 +713,6 @@
         "dp", other_members("dp", data_size), group_ref, outer, outer_send, outer_recv
     )
     terms_out_ref[...] = add_terms(outer, outer_copies)
-    mixing.collect()
 
     def norm(piece):
         back = mixing.total(piece)
@@ -684,7 +725,7 @@
             + scale * (unit_slope - unit * jnp.mean(unit_slope * unit, axis=-1, keepdims=True))
         ).astype(gradient_ref.dtype)
 
-    over_pieces(rows, norm)
+    mixing.over_stages(norm)
     for copy in inner_copies + outer_copies:
         copy.wait_send()
     mixing.drain()
@@ -912,14 +953,12 @@
 
     @pl.when(step == steps - 1)
     def _():
-        scatter.collect()
-
         def finish(piece):
             output_ref[piece, :] = (hidden_state_ref[piece, :] + scatter.total(piece)).astype(
                 output_ref.dtype
             )
 
-        over_pieces(output_ref.shape[0], finish)
+        scatter.over_stages(finish)
         scatter.drain()
 
 
@@ -1194,7 +1233,7 @@
                 values = values + other_ref[0, :, columns].astype(jnp.float32)
                 held_ref[step, :, columns] = values.astype(jnp.bfloat16)
             else:
-                out_ref[0, :, columns] = values.astype(jnp.bfloat16)
+                out_ref[:, :, columns] = values.reshape(*out_ref.shape[:2], tile).astype(jnp.bfloat16)
         start += width
     if with_other:
         copies = [
@@ -1210,7 +1249,7 @@
                 copy.wait()
 
 
-def grad_blocks(order, pairs, other=None):
+def grad_blocks(order, pairs, other=None, group=1):
     count = order.shape[0]
     depth, total_rows = pairs[0][0].shape
     block = depth // lax.axis_size("dp")
@@ -1219,7 +1258,10 @@
     operands = []
     for left, right in pairs:
         in_specs += [
-            pl.BlockSpec((block, total_rows), lambda k, at: (at[k], 0)),
+            pl.BlockSpec(
+                (group * block, total_rows),
+                (lambda k, at: (at[k], 0)) if group == 1 else (lambda k, at: (k, 0)),
+            ),
             pl.BlockSpec(right.shape, lambda k, at: (0, 0), pipeline_mode=pl.Buffered(1)),
         ]
         operands += [left, right]
@@ -1235,12 +1277,12 @@
         ]
     else:
         out_shape = [jax.ShapeDtypeStruct((count, block, width), jnp.bfloat16)]
-        out_specs = [pl.BlockSpec((1, block, width), lambda k, at: (k, 0, 0))]
+        out_specs = [pl.BlockSpec((group, block, width), lambda k, at: (k, 0, 0))]
     out = pl.pallas_call(
         functools.partial(grad_kernel, len(pairs), other is not None),
         grid_spec=pltpu.PrefetchScalarGridSpec(
             num_scalar_prefetch=1,
-            grid=(count,),
+            grid=(count // group,),
             in_specs=in_specs,
             out_specs=out_specs,
             scratch_shapes=scratch,
@@ -1440,7 +1482,7 @@
     hidden_second, slope_second = feed_half(feed_rows, cotangent_rows, later_full)
     plain_order = jnp.arange(sizes[0], dtype=jnp.int32)
     second_grad = grad_blocks(
-        plain_order, [(feed_turned, slope_second), (cotangent_turned, hidden_second)]
+        plain_order, [(feed_turned, slope_second), (cotangent_turned, hidden_second)], group=2
     ).reshape(model_width, -1)
     second_grad, slope_second = lax.optimization_barrier((second_grad, slope_second))
     second_total = lax.psum_scatter(second_grad, "dp", scatter_dimension=0, tiled=True)
@@ -1479,7 +1521,7 @@
     down = lax.ppermute(
         falling, "dp", [(device, device - 2) for device in range(2, sizes[0])]
     )
-    output_grad = grad_blocks(plain_order, [(state_turned, mixed_rows)]).reshape(model_width, -1)
+    output_grad = grad_blocks(plain_order, [(state_turned, mixed_rows)], group=4).reshape(model_width, -1)
     output_grad, state_rows = lax.optimization_barrier((output_grad, state_rows))
     output_total = lax.psum_scatter(output_grad, "dp", scatter_dimension=0, tiled=True)
     qkv_slope, head_terms, block_output = attention_backward(
@@ -1491,7 +1533,7 @@
         ],
         hidden_state, size, 4,
     )
-    mixing_grad = grad_blocks(plain_order, [(mixer_turned, qkv_slope)]).reshape(model_width, -1)
+    mixing_grad = grad_blocks(plain_order, [(mixer_turned, qkv_slope)], group=2).reshape(model_width, -1)
     mixing_grad, qkv_slope = lax.optimization_barrier((mixing_grad, qkv_slope))
     mixing_total = lax.psum_scatter(mixing_grad, "dp", scatter_dimension=0, tiled=True)
     terms_shape = (2 * gain_rows + head_terms.shape[0], head_size)

time: 615 us -> 605 us (0.984)
  Pallas kernels: 489 us -> 475 us
    pallas_call x3, Pallas kernels: 244 us -> 236 us  [scatter_call(): pl.pallas_call(functools.partial(body, tuple((first for _, _, first in tr...]
where the time goes in v9:
time: 605 us; the launch traced here: 604 us
  Pallas kernels  475 us (79%)
  waiting for transfers between devices  99.7 us (16%)
  between operations  14.3 us (2%)
  starting transfers between devices  10.2 us (2%)
    pallas_call x3, Pallas kernels, scatter_call(): pl.pallas_call(functools.partial(body, tuple((first for _, _, first in tr...  236 us
    pallas_call x1, Pallas kernels, gather_rows(): pl.pallas_call(functools.partial(gather_kernel, size, count), out_shape=o...  76.6 us
    reduce_scatter x1, waiting for transfers between devices, per_device(): lax.psum_scatter(second_grad, 'dp', scatter_dimension=0, tiled=True)  69.9 us
    pallas_call x5, Pallas kernels, grad_blocks(): pl.pallas_call(functools.partial(grad_kernel, len(pairs), other is not No...  53.1 us
    pallas_call x1, Pallas kernels, attention_backward(): pl.pallas_call(functools.partial(attention_backward_kernel, size, groupin...  44.8 us
    pallas_call x2, Pallas kernels, feed_half(): pl.pallas_call(functools.partial(feed_half_kernel, half, tile, block), ou...  33.9 us
    pallas_call x1, Pallas kernels, attention_forward(): pl.pallas_call(functools.partial(attention_forward_kernel, grouping, head...  18.4 us
    pallas_call x3, Pallas kernels, whole_call(): pl.pallas_call(body, out_shape=shapes, in_specs=[pl.BlockSpec(memory_spac...  12.9 us
  transfers between devices with their start and end apart: 11, of which 5 were waited for; matrix products, arithmetic and copies ran while one was open for 1% of the time, Pallas kernels for 62%

profile of v9, /device:TPU:0, one launch (start us, length us, event | category | flops | bytes accessed | tf_op | source)
XLA Modules:
  0.0 604.3 jit_solution(195278793685206456)
XLA Ops:
  7.2 0.0 all-gather.4.cloned.1.call-start
  7.2 2.2 shard_map.246
  9.4 0.0 all-gather.4.cloned.1.call-update
  9.4 0.0 all-gather.6.cloned.1.call-start
  9.5 3.4 shard_map.248
  12.9 0.0 all-gather.6.cloned.1.call-update
  12.9 0.0 all-gather.8.cloned.1.call-start
  13.0 0.7 all-gather.8.cloned.1.call-update
  13.7 0.0 reduce-scatter.8.cloned.1.call-start
  13.8 0.3 fusion
  14.1 1.3 fusion.2.refs_0_
  15.3 76.6 %gather_rows.1 = (bf16[1024,2048]{1,0:T(8,128)(2,1)}, bf16[2048,1024]{1,0:T(8,128)(2,1)}, bf16[1024,2048]{1,0:T(8,128)(2,1)}, bf16[2048,1024]{1,0:T(8,128)(2,1)}) custom-call(bf16[256,2048]{1,0:T(8,128)(2,1)} %fusion.2.refs_0_, bf16[256,2048]{1,0:T(8,128)(2,1)} %refs_5_.1), custom_call_target="tpu_custom_call" | custom-call | bytes 125829120 | tf_op jit(solution)/shard_map/gather_rows/pallas_call | solution.py:209
  91.9 0.5 broadcast_add_fusion.order_ref
  92.5 18.4 %attention_forward.1 = (f32[1024,1024]{1,0:T(8,128)}, bf16[1024,512]{1,0:T(8,128)(2,1)}, f32[2,2,1024]{2,1,0:T(2,128)}) custom-call(bf16[1024,2048]{1,0:T(8,128)(2,1)} %get-tuple-element.68.rows_ref.refs_6_, bf16[2048,1536]{1,0:T(8,128)(2,1)} %all-gather.4.cloned.1.call-done.weight_ref.refs_1_.refs_5_, f32[136,128]{1,0:T(8,128)} %constant.38.clone.few_cosines_ref.refs_9_, ...), custom_call_target="tpu_custom_call" | custom-call | flops 5368709120 | bytes 8388608 | tf_op jit(solution)/shard_map/attention_forward/pallas_call | solution.py:879
  110.9 75.0 %shard_map.247 = (bf16[1024,2048]{1,0:T(8,128)(2,1)}, bf16[2048,1024]{1,0:T(8,128)(2,1)}, f32[256,2048]{1,0:T(8,128)}) custom-call(bf16[1024,512]{1,0:T(8,128)(2,1)} %get-tuple-element.69.refs_0_.refs_1_.refs_7_, bf16[2048,1536]{1,0:T(8,128)(2,1)} %all-gather.4.cloned.1.call-done.weight_ref.refs_1_.refs_5_, bf16[256,2048]{1,0:T(8,128)(2,1)} %refs_2_.3, ...), custom_call_target="tpu_custom_call" | custom-call | flops 2147483648 | bytes 150000000 | tf_op jit(solution)/shard_map/pallas_call | solution.py:744
  185.9 9.3 %all-gather.6.cloned.1.call-done.weight_far.refs_1_ = bf16[2048,3072]{1,0:T(8,128)(2,1)} async-done(((bf16[256,3072]{1,0:T(8,128)(2,1)}), bf16[2048,3072]{1,0:T(8,128)(2,1)}) %all-gather.6.cloned.1.call-update) | async-done | bytes 12582928 | tf_op jit(solution)/shard_map/all_gather | solution.py:1439
  195.3 22.0 %feed_half.2 = (bf16[1024,1024]{1,0:T(8,128)(2,1)}, bf16[1024,2048]{1,0:T(8,128)(2,1)}) custom-call(bf16[1024,2048]{1,0:T(8,128)(2,1)} %get-tuple-element.71.rows_far, bf16[1024,2048]{1,0:T(8,128)(2,1)} %get-tuple-element.72.cotangent_far, bf16[2048,3072]{1,0:T(8,128)(2,1)} %all-gather.6.cloned.1.call-done.weight_far.refs_1_), custom_call_target="tpu_custom_call" | custom-call | flops 12884901888 | bytes 20971520 | tf_op jit(solution)/shard_map/feed_half/pallas_call | solution.py:1188
  217.2 12.4 %grad_blocks.5 = bf16[4,256,3072]{2,1,0:T(8,128)(2,1)} custom-call(s32[4]{0:T(128)} %broadcast_add_fusion.order_ref, bf16[2048,1024]{1,0:T(8,128)(2,1)} %get-tuple-element.70.refs_0_, bf16[1024,2048]{1,0:T(8,128)(2,1)} %get-tuple-element.74.refs_1_.refs_0_, bf16[2048,1024]{1,0:T(8,128)(2,1)} %get-tuple-element.75.refs_2_, ...), custom_call_target="tpu_custom_call" | custom-call | flops 6442450944 | bytes 16777216 | tf_op jit(solution)/shard_map/grad_blocks/pallas_call | solution.py:1281
  229.6 0.3 collective-permute-start
  229.9 0.5 broadcast_add_fusion.1.order_ref
  230.5 10.3 %collective-permute-done.refs_4_ = bf16[4,256,3072]{2,1,0:T(8,128)(2,1)} collective-permute-done((bf16[4,256,3072]{2,1,0:T(8,128)(2,1)}, bf16[4,256,3072]{2,1,0:T(8,128)(2,1)}, u32[]{:S(2)}, u32[]{:S(2)}) %collective-permute-start) | collective-permute-done | bytes 6291488 | tf_op jit(solution)/shard_map/ppermute | solution.py:1308
  240.8 13.6 %grad_blocks.6 = (bf16[256,3072]{1,0:T(8,128)(2,1)}, bf16[256,3072]{1,0:T(8,128)(2,1)}, bf16[256,3072]{1,0:T(8,128)(2,1)}, bf16[256,3072]{1,0:T(8,128)(2,1)}) custom-call(s32[4]{0:T(128)} %broadcast_add_fusion.1.order_ref, bf16[2048,1024]{1,0:T(8,128)(2,1)} %get-tuple-element.70.refs_0_, bf16[1024,2048]{1,0:T(8,128)(2,1)} %get-tuple-element.74.refs_1_.refs_0_, ...), custom_call_target="tpu_custom_call" | custom-call | flops 6442450944 | bytes 16777216 | tf_op jit(solution)/shard_map/grad_blocks/pallas_call | solution.py:1281
  254.3 0.9 collective-permute-start.2
  255.3 2.5 collective-permute-start.1
  257.8 2.0 all-gather.8.cloned.1.call-done.weight_far.refs_3_
  259.8 12.0 %feed_half.3 = (bf16[1024,512]{1,0:T(8,128)(2,1)}, bf16[1024,1024]{1,0:T(8,128)(2,1)}) custom-call(bf16[1024,2048]{1,0:T(8,128)(2,1)} %get-tuple-element.71.rows_far, bf16[1024,2048]{1,0:T(8,128)(2,1)} %get-tuple-element.72.cotangent_far, bf16[2048,1536]{1,0:T(8,128)(2,1)} %all-gather.8.cloned.1.call-done.weight_far.refs_3_), custom_call_target="tpu_custom_call" | custom-call | flops 6442450944 | bytes 14680064 | tf_op jit(solution)/shard_map/feed_half/pallas_call | solution.py:1188
  271.8 0.5 iota.11.order_ref
  272.3 12.1 %grad_blocks.7 = bf16[8,256,1536]{2,1,0:T(8,128)(2,1)} custom-call(s32[8]{0:T(128)} %iota.11.order_ref, bf16[2048,1024]{1,0:T(8,128)(2,1)} %get-tuple-element.70.refs_0_, bf16[1024,1024]{1,0:T(8,128)(2,1)} %get-tuple-element.86.refs_1_.refs_2_, bf16[2048,1024]{1,0:T(8,128)(2,1)} %get-tuple-element.75.refs_2_, bf16[1024,512]{1,0:T(8,128)(2,1)} %get-tuple-element.85.refs_3_.refs_2_), custom_call_target="tpu_custom_call" | custom-call | flops 6442450944 | bytes 17825792 | tf_op jit(solution)/shard_map/grad_blocks/pallas_call | solution.py:1281
  284.4 6.9 %collective-permute-done.1.refs_9_ = bf16[256,3072]{1,0:T(8,128)(2,1)} collective-permute-done((bf16[256,3072]{1,0:T(8,128)(2,1)}, bf16[256,3072]{1,0:T(8,128)(2,1)}, u32[]{:S(2)}, u32[]{:S(2)}) %collective-permute-start.1) | collective-permute-done | bytes 1572896 | tf_op jit(solution)/shard_map/ppermute | solution.py:1314
  291.3 82.8 %shard_map.249 = (bf16[1024,2048]{1,0:T(8,128)(2,1)}, bf16[2048,1024]{1,0:T(8,128)(2,1)}, f32[256,2048]{1,0:T(8,128)}, f32[16,128]{1,0:T(8,128)}, bf16[256,3072]{1,0:T(8,128)(2,1)}, /*index=5*/bf16[256,3072]{1,0:T(8,128)(2,1)}) custom-call(bf16[1024,2048]{1,0:T(8,128)(2,1)} %get-tuple-element.74.refs_1_.refs_0_, ...), custom_call_target="tpu_custom_call" | custom-call | flops 12884901888 | bytes 150000000 | tf_op jit(solution)/shard_map/pallas_call | solution.py:744
  374.1 0.5 iota.13.order_ref
  374.7 6.0 grad_blocks.8
  380.7 0.0 reduce-scatter.8.cloned.1.call-update
  380.7 0.0 reduce-scatter.6.cloned.1.call-start
  380.8 44.8 %attention_backward.1 = (bf16[1024,1024]{1,0:T(8,128)(2,1)}, f32[8,128]{1,0:T(8,128)}, bf16[256,2048]{1,0:T(8,128)(2,1)}) custom-call(bf16[1024,1024]{1,0:T(8,128)(2,1)} %get-tuple-element.76.refs_3_.refs_0_, bf16[2048,3072]{1,0:T(8,128)(2,1)} %all-gather.6.cloned.1.call-done.weight_far.refs_1_, bf16[1024,512]{1,0:T(8,128)(2,1)} %get-tuple-element.85.refs_3_.refs_2_, ...), custom_call_target="tpu_custom_call" | custom-call | flops 4831838208 | bytes 100000000 | tf_op jit(solution)/shard_map/attention_backward/pallas_call | solution.py:1061
  425.6 0.5 iota.12.order_ref
  426.1 9.0 %grad_blocks.9 = bf16[8,256,1024]{2,1,0:T(8,128)(2,1)} custom-call(s32[8]{0:T(128)} %iota.12.order_ref, bf16[2048,1024]{1,0:T(8,128)(2,1)} %get-tuple-element.94.refs_0_, bf16[1024,1024]{1,0:T(8,128)(2,1)} %get-tuple-element.103.refs_1_.refs_0_), custom_call_target="tpu_custom_call" | custom-call | flops 4294967296 | bytes 10485760 | tf_op jit(solution)/shard_map/grad_blocks/pallas_call | solution.py:1281
  435.1 0.0 reduce-scatter.6.cloned.1.call-update
  435.2 0.0 reduce-scatter.4.cloned.1.call-start
  435.2 0.5 reduce-scatter.4.cloned.1.call-update
  435.7 4.9 collective-permute-start.3
  440.6 1.3 collective-permute-start.4
  441.9 0.6 pad_maximum_fusion.refs_5_
  442.5 77.7 %shard_map.250 = (bf16[256,2048]{1,0:T(8,128)(2,1)}, f32[40,128]{1,0:T(8,128)}) custom-call(bf16[1024,1024]{1,0:T(8,128)(2,1)} %get-tuple-element.103.refs_1_.refs_0_, bf16[2048,1536]{1,0:T(8,128)(2,1)} %all-gather.4.cloned.1.call-done.weight_ref.refs_1_.refs_5_, bf16[256,2048]{1,0:T(8,128)(2,1)} %refs_2_.3, f32[1,2048]{1,0:T(1,128)} %bitcast.16, ...), custom_call_target="tpu_custom_call" | custom-call | flops 4294967296 | bytes 150000000 | tf_op jit(solution)/shard_map/pallas_call | solution.py:744
  520.2 0.0 reduce-scatter.8.cloned.1.call-done.output_total_ref
  520.3 0.0 reduce-scatter.6.cloned.1.call-done.mixing_ref
  520.3 69.9 %reduce-scatter.4.cloned.1.call-done.second_ref = bf16[256,1536]{1,0:T(8,128)(2,1)} async-done(((bf16[2048,1536]{1,0:T(8,128)(2,1)}), bf16[256,1536]{1,0:T(8,128)(2,1)}) %reduce-scatter.4.cloned.1.call-update) | async-done | bytes 786448 | tf_op jit(solution)/shard_map/reduce_scatter | solution.py:1488
  590.2 7.3 %shard_map.251 = (bf16[256,2048]{1,0:T(8,128)(2,1)}, bf16[256,2048]{1,0:T(8,128)(2,1)}, f32[16,128]{1,0:T(8,128)}, f32[256,512]{1,0:T(8,128)}, f32[256,256]{1,0:...) custom-call(bf16[256,3072]{1,0:T(8,128)(2,1)} %get-tuple-element.82., ...), custom_call_target="tpu_custom_call" | custom-call | bytes 16797696 | tf_op jit(solution)/shard_map/pallas_call | solution.py:1383
  (17 shorter events, 0.0 us)
Async XLA Ops:
  7.2 85.3 %all-gather.4.cloned.1.call-start = ((), (), s32[]{:S(2)}) async-start(), calls=%async_computation.3 | async-start | bytes 7077888 | tf_op jit(solution)/shard_map/all_gather | solution.py:1430
  9.4 4.3 copy-start
  9.4 185.8 %all-gather.6.cloned.1.call-start = ((), (), s32[]{:S(2)}) async-start(), calls=%async_computation.4 | async-start | bytes 14155776 | tf_op jit(solution)/shard_map/all_gather | solution.py:1439
  12.9 1.1 copy-start.2
  12.9 246.9 %all-gather.8.cloned.1.call-start = ((), (), s32[]{:S(2)}) async-start(), calls=%async_computation.5 | async-start | bytes 7077888 | tf_op jit(solution)/shard_map/all_gather | solution.py:1439
  13.7 506.6 %reduce-scatter.8.cloned.1.call-start = ((), (), s32[]{:S(2)}) async-start(), calls=%async_computation.8 | async-start | bytes 2359296 | tf_op jit(solution)/shard_map/reduce_scatter | solution.py:1526
  229.6 11.1 %collective-permute-start = (bf16[4,256,3072]{2,1,0:T(8,128)(2,1)}, bf16[4,256,3072]{2,1,0:T(8,128)(2,1)}, u32[]{:S(2)}, u32[]{:S(2)}) collective-permute-start(bf16[4,256,3072]{2,1,0:T(8,128)(2,1)} %grad_blocks.5), channel_id=1, source_target_pairs={{0,4},{4,0},{8,12},{12,8},{16,20},{20,16},{24,28},{28,24},{1,5},{5... | collective-permute-start | bytes 18874376 | tf_op jit(solution)/shard_map/ppermute | solution.py:1308
  254.3 30.1 %collective-permute-start.2 = (bf16[256,3072]{1,0:T(8,128)(2,1)}, bf16[256,3072]{1,0:T(8,128)(2,1)S(1)}, u32[]{:S(2)}, u32[]{:S(2)}) collective-permute-start(bf16[256,3072]{1,0:T(8,128)(2,1)} %get-tuple-element.89.refs_11_), channel_id=1, source_target_pairs={{24,16},{28,20},{25,17},{29,21},{26,18},{30,22},{27,19},{31,23}} | collective-permute-start | bytes 4718600 | tf_op jit(solution)/shard_map/ppermute | solution.py:1315
  255.3 36.0 %collective-permute-start.1 = (bf16[256,3072]{1,0:T(8,128)(2,1)}, bf16[256,3072]{1,0:T(8,128)(2,1)}, u32[]{:S(2)}, u32[]{:S(2)}) collective-permute-start(bf16[256,3072]{1,0:T(8,128)(2,1)} %get-tuple-element.90.refs_12_), channel_id=1, source_target_pairs={{0,8},{4,12},{1,9},{5,13},{2,10},{6,14},{3,11},{7,15}} | collective-permute-start | bytes 4718600 | tf_op jit(solution)/shard_map/ppermute | solution.py:1314
  284.4 6.9 %copy-start.5 = (bf16[256,3072]{1,0:T(8,128)(2,1)}, bf16[256,3072]{1,0:T(8,128)(2,1)S(1)}, u32[]{:S(2)}) copy-start(bf16[256,3072]{1,0:T(8,128)(2,1)S(1)} %collective-permute-done.2.refs_10_) | copy-start | bytes 4718596
  380.7 139.6 %reduce-scatter.6.cloned.1.call-start = ((), (), s32[]{:S(2)}) async-start(), calls=%async_computation.7 | async-start | bytes 4718592 | tf_op jit(solution)/shard_map/reduce_scatter | solution.py:1538
  435.1 6.8 %copy-start.3 = (f32[16,128]{1,0:T(8,128)S(1)}, f32[16,128]{1,0:T(8,128)}, u32[]{:S(2)}) copy-start(f32[16,128]{1,0:T(8,128)} %get-tuple-element.105) | copy-start | bytes 24580
  435.1 6.8 %copy-start.4 = (f32[8,128]{1,0:T(8,128)S(1)}, f32[8,128]{1,0:T(8,128)}, u32[]{:S(2)}) copy-start(f32[8,128]{1,0:T(8,128)} %get-tuple-element.106) | copy-start | bytes 12292
  435.2 155.0 %reduce-scatter.4.cloned.1.call-start = ((), (), s32[]{:S(2)}) async-start(), calls=%async_computation.6 | async-start | bytes 7077888 | tf_op jit(solution)/shard_map/reduce_scatter | solution.py:1488
  435.7 84.5 %collective-permute-start.3 = (bf16[256,3072]{1,0:T(8,128)(2,1)}, bf16[256,3072]{1,0:T(8,128)(2,1)S(1)}, u32[]{:S(2)}, u32[]{:S(2)}) collective-permute-start(bf16[256,3072]{1,0:T(8,128)(2,1)} %get-tuple-element.91), channel_id=1, source_target_pairs={{0,8},{4,12},{8,16},{12,20},{16,24},{20,28},{1,9},{5,13},{9,17},{1... | collective-permute-start | bytes 4718600 | tf_op jit(solution)/shard_map/ppermute | solution.py:1518
  440.6 79.6 %collective-permute-start.4 = (bf16[256,3072]{1,0:T(8,128)(2,1)}, bf16[256,3072]{1,0:T(8,128)(2,1)}, u32[]{:S(2)}, u32[]{:S(2)}) collective-permute-start(bf16[256,3072]{1,0:T(8,128)(2,1)} %get-tuple-element.92), channel_id=1, source_target_pairs={{8,0},{12,4},{16,8},{20,12},{24,16},{28,20},{9,1},{13,5},{17,9},{2... | collective-permute-start | bytes 4718600 | tf_op jit(solution)/shard_map/ppermute | solution.py:1521
  520.2 70.0 %copy-start.1 = (bf16[256,3072]{1,0:T(8,128)(2,1)}, bf16[256,3072]{1,0:T(8,128)(2,1)S(1)}, u32[]{:S(2)}) copy-start(bf16[256,3072]{1,0:T(8,128)(2,1)S(1)} %collective-permute-done.3.up_ref) | copy-start | bytes 4718596
Sparse Core Ops, SparseCore 0:
  10.2 67.4 all-gather.3
  79.9 115.3 all-gather.5
  196.9 62.8 all-gather.7
  380.8 36.7 reduce-scatter.7
  435.3 84.9 reduce-scatter.5
  522.4 67.7 reduce-scatter.3

commit v10 on v9

--- a/solution.py
+++ b/solution.py
@@ -1213,104 +1213,179 @@
     )(rows, cotangent, weight)
 
 
-def grad_kernel(pair_count, with_other, order_ref, *refs):
+def grad_kernel(pair_count, *refs):
     pairs = [refs[2 * p : 2 * p + 2] for p in range(pair_count)]
-    refs = refs[2 * pair_count :]
-    step = pl.program_id(0)
-    if with_other:
-        other_ref, refs = refs[0], refs[1:]
-        out_refs, held_ref, copy_sem = refs[:-2], refs[-2], refs[-1]
-    else:
-        out_ref = refs[0]
+    out_ref = refs[-1]
     start = 0
     for left_ref, right_ref in pairs:
         width = right_ref.shape[1]
         tile = next(t for t in (768, 512, 384, 256, 128) if width % t == 0)
         for column in range(0, width, tile):
             values = simple_product(left_ref[...], right_ref[:, column : column + tile])
-            columns = slice(start + column, start + column + tile)
-            if with_other:
-                values = values + other_ref[0, :, columns].astype(jnp.float32)
-                held_ref[step, :, columns] = values.astype(jnp.bfloat16)
-            else:
-                out_ref[:, :, columns] = values.reshape(*out_ref.shape[:2], tile).astype(jnp.bfloat16)
+            out_ref[:, start + column : start + column + tile] = values.astype(jnp.bfloat16)
         start += width
-    if with_other:
-        copies = [
-            pltpu.make_async_copy(held_ref.at[index], out_ref, copy_sem.at[index])
-            for index, out_ref in enumerate(out_refs)
-        ]
-        for index, copy in enumerate(copies):
-            pl.when(step == index)(copy.start)
-
-        @pl.when(step == len(copies) - 1)
-        def _():
-            for copy in copies:
-                copy.wait()
-
-
-def grad_blocks(order, pairs, other=None, group=1):
-    count = order.shape[0]
+
+
+def grad_blocks(pairs, rows):
     depth, total_rows = pairs[0][0].shape
-    block = depth // lax.axis_size("dp")
     width = sum(right.shape[1] for _, right in pairs)
     in_specs = []
     operands = []
     for left, right in pairs:
         in_specs += [
-            pl.BlockSpec(
-                (group * block, total_rows),
-                (lambda k, at: (at[k], 0)) if group == 1 else (lambda k, at: (k, 0)),
-            ),
-            pl.BlockSpec(right.shape, lambda k, at: (0, 0), pipeline_mode=pl.Buffered(1)),
+            pl.BlockSpec((rows, total_rows), lambda k: (k, 0)),
+            pl.BlockSpec(right.shape, lambda k: (0, 0), pipeline_mode=pl.Buffered(1)),
         ]
         operands += [left, right]
-    scratch = []
-    if other is not None:
-        in_specs.append(pl.BlockSpec((1, block, width), lambda k, at: (k, 0, 0)))
-        operands.append(other)
-        out_shape = [jax.ShapeDtypeStruct((block, width), jnp.bfloat16)] * count
-        out_specs = [pl.BlockSpec(memory_space=pl.ANY)] * count
-        scratch = [
-            pltpu.VMEM((count, block, width), jnp.bfloat16),
-            pltpu.SemaphoreType.DMA((count,)),
-        ]
-    else:
-        out_shape = [jax.ShapeDtypeStruct((count, block, width), jnp.bfloat16)]
-        out_specs = [pl.BlockSpec((group, block, width), lambda k, at: (k, 0, 0))]
-    out = pl.pallas_call(
-        functools.partial(grad_kernel, len(pairs), other is not None),
-        grid_spec=pltpu.PrefetchScalarGridSpec(
-            num_scalar_prefetch=1,
-            grid=(count // group,),
-            in_specs=in_specs,
-            out_specs=out_specs,
-            scratch_shapes=scratch,
-        ),
-        out_shape=out_shape,
+    return pl.pallas_call(
+        functools.partial(grad_kernel, len(pairs)),
+        grid=(depth // rows,),
+        in_specs=in_specs,
+        out_specs=pl.BlockSpec((rows, width), lambda k: (k, 0)),
+        out_shape=jax.ShapeDtypeStruct((depth, width), jnp.bfloat16),
         compiler_params=pltpu.CompilerParams(vmem_limit_bytes=VMEM_LIMIT),
         cost_estimate=pl.CostEstimate(
-            flops=2 * total_rows * count * block * width,
-            bytes_accessed=2 * (total_rows * count * block * len(pairs) + width * (total_rows + count * block)),
+            flops=2 * total_rows * depth * width,
+            bytes_accessed=2 * (total_rows * depth * len(pairs) + width * (total_rows + depth)),
             transcendentals=0,
         ),
         name="grad_blocks",
-    )(order, *operands)
-    return out if other is not None else out[0]
-
-
-def reduce_over_chips(pairs, sizes):
+    )(*operands)
+
+
+def pair_grad_kernel(chips, pair_count, *refs):
+    lefts, rights = refs[:pair_count], refs[pair_count : 2 * pair_count]
+    out_refs = refs[2 * pair_count : 2 * pair_count + chips]
+    held = refs[2 * pair_count + chips : -6]
+    sent, landed, left_sem, send_sem, recv_sem, out_sem = refs[-6:]
+    block = sent.shape[1]
+    device = lax.axis_index("dp")
+    chip, core = device // 2, lax.rem(device, 2)
+    other = chip * 2 + 1 - core
+
+    def loads(index):
+        owner = lax.rem(chip + lax.rem(index, chips), chips) * 2
+        owner = owner + jnp.where(index < chips, 1 - core, core)
+        piece = pl.ds(pl.multiple_of(owner * block, block), block)
+        slot = lax.rem(index, 2)
+        return [
+            pltpu.make_async_copy(left.at[piece], hold.at[slot], left_sem.at[at, slot])
+            for at, (left, hold) in enumerate(zip(lefts, held))
+        ]
+
+    for load in loads(0):
+        load.start()
+    greet([("dp", other)])
+    copies = [
+        pltpu.make_async_remote_copy(
+            src_ref=sent.at[place],
+            dst_ref=landed.at[place],
+            send_sem=send_sem.at[place],
+            recv_sem=recv_sem.at[place],
+            device_id={"dp": other},
+            device_id_type=MESH,
+        )
+        for place in range(chips)
+    ]
+
+    def products(index, write):
+        slot = lax.rem(index, 2)
+        for load in loads(index):
+            load.wait()
+
+        @pl.when(index + 1 < 2 * chips)
+        def _():
+            for load in loads(index + 1):
+                load.start()
+
+        start = 0
+        for hold, right in zip(held, rights):
+            width = right.shape[1]
+            tile = next(t for t in (512, 384, 256, 128) if width % t == 0)
+
+            def step(at, carry, hold=hold, right=right, start=start, tile=tile):
+                column = pl.multiple_of(at * tile, tile)
+                write(
+                    pl.ds(start + column, tile),
+                    simple_product(hold[slot], right[:, pl.ds(column, tile)]),
+                )
+                return carry
+
+            lax.fori_loop(0, width // tile, step, 0)
+            start += width
+
+    def send_step(place, carry):
+        def write(columns, values):
+            sent[place, :, columns] = values.astype(jnp.bfloat16)
+
+        products(place, write)
+        for at in range(chips):
+            pl.when(place == at)(copies[at].start)
+        return carry
+
+    lax.fori_loop(0, chips, send_step, 0)
+    outs = [
+        pltpu.make_async_copy(landed.at[place], out_ref, out_sem.at[place])
+        for place, out_ref in enumerate(out_refs)
+    ]
+
+    def own_step(place, carry):
+        for at in range(chips):
+            pl.when(place == at)(copies[at].wait_recv)
+
+        def write(columns, values):
+            landed[place, :, columns] = (
+                values + landed[place, :, columns].astype(jnp.float32)
+            ).astype(jnp.bfloat16)
+
+        products(place + chips, write)
+        for at in range(chips):
+            pl.when(place == at)(outs[at].start)
+        return carry
+
+    lax.fori_loop(0, chips, own_step, 0)
+    for copy in copies:
+        copy.wait_send()
+    for copy in outs:
+        copy.wait()
+
+
+def pair_grads(pairs, sizes, collective_id):
+    chips = sizes[0] // 2
+    depth, total_rows = pairs[0][0].shape
+    block = depth // sizes[0]
+    width = sum(right.shape[1] for _, right in pairs)
+    far = pl.BlockSpec(memory_space=pl.ANY)
+    return pl.pallas_call(
+        functools.partial(pair_grad_kernel, chips, len(pairs)),
+        out_shape=[jax.ShapeDtypeStruct((block, width), jnp.bfloat16)] * chips,
+        in_specs=[far] * len(pairs) + [pl.BlockSpec(memory_space=pltpu.VMEM)] * len(pairs),
+        out_specs=[far] * chips,
+        scratch_shapes=[pltpu.VMEM((2, block, total_rows), jnp.bfloat16) for _ in pairs]
+        + [
+            pltpu.VMEM((chips, block, width), jnp.bfloat16),
+            pltpu.VMEM((chips, block, width), jnp.bfloat16),
+            pltpu.SemaphoreType.DMA((len(pairs), 2)),
+            pltpu.SemaphoreType.DMA((chips,)),
+            pltpu.SemaphoreType.DMA((chips,)),
+            pltpu.SemaphoreType.DMA((chips,)),
+        ],
+        compiler_params=pltpu.CompilerParams(
+            collective_id=collective_id, has_side_effects=True, vmem_limit_bytes=VMEM_LIMIT
+        ),
+        cost_estimate=pl.CostEstimate(
+            flops=2 * total_rows * depth * width,
+            bytes_accessed=2 * (total_rows * depth * len(pairs) + width * (total_rows + depth)),
+            transcendentals=0,
+        ),
+        name="pair_grads",
+    )(*[left for left, _ in pairs], *[right for _, right in pairs])
+
+
+def reduce_over_chips(pairs, sizes, collective_id):
     data_size = sizes[0]
     chips = data_size // 2
-    me = lax.axis_index("dp")
-    chip, core = me // 2, lax.rem(me, 2)
-    ahead = lax.rem(chip + jnp.arange(chips, dtype=jnp.int32), chips) * 2
-    other = lax.ppermute(
-        grad_blocks(ahead + (1 - core), pairs),
-        "dp",
-        [(device, device ^ 1) for device in range(data_size)],
-    )
-    blocks = grad_blocks(ahead + core, pairs, other)
+    blocks = pair_grads(pairs, sizes, collective_id)
     up = lax.ppermute(blocks[chips - 1], "dp", [(device, device + 2) for device in range(2)])
     down = lax.ppermute(
         blocks[1],
@@ -1476,14 +1551,13 @@
 
     hidden_first, slope_first = feed_half(feed_rows, cotangent_rows, feed_full[0])
     blocks, up, down = reduce_over_chips(
-        [(feed_turned, slope_first), (cotangent_turned, hidden_first)], sizes
+        [(feed_turned, slope_first), (cotangent_turned, hidden_first)], sizes, 5
     )
     blocks, later_full = lax.optimization_barrier((blocks, feed_full[1]))
     hidden_second, slope_second = feed_half(feed_rows, cotangent_rows, later_full)
-    plain_order = jnp.arange(sizes[0], dtype=jnp.int32)
     second_grad = grad_blocks(
-        plain_order, [(feed_turned, slope_second), (cotangent_turned, hidden_second)], group=2
-    ).reshape(model_width, -1)
+        [(feed_turned, slope_second), (cotangent_turned, hidden_second)], 2 * block_width
+    )
     second_grad, slope_second = lax.optimization_barrier((second_grad, slope_second))
     second_total = lax.psum_scatter(second_grad, "dp", scatter_dimension=0, tiled=True)
     chips = sizes[0] // 2
@@ -1521,7 +1595,7 @@
     down = lax.ppermute(
         falling, "dp", [(device, device - 2) for device in range(2, sizes[0])]
     )
-    output_grad = grad_blocks(plain_order, [(state_turned, mixed_rows)], group=4).reshape(model_width, -1)
+    output_grad = grad_blocks([(state_turned, mixed_rows)], 4 * block_width)
     output_grad, state_rows = lax.optimization_barrier((output_grad, state_rows))
     output_total = lax.psum_scatter(output_grad, "dp", scatter_dimension=0, tiled=True)
     qkv_slope, head_terms, block_output = attention_backward(
@@ -1533,7 +1607,7 @@
         ],
         hidden_state, size, 4,
     )
-    mixing_grad = grad_blocks(plain_order, [(mixer_turned, qkv_slope)], group=2).reshape(model_width, -1)
+    mixing_grad = grad_blocks([(mixer_turned, qkv_slope)], 2 * block_width)
     mixing_grad, qkv_slope = lax.optimization_barrier((mixing_grad, qkv_slope))
     mixing_total = lax.psum_scatter(mixing_grad, "dp", scatter_dimension=0, tiled=True)
     terms_shape = (2 * gain_rows + head_terms.shape[0], head_size)

time: 605 us -> 607 us (level)
    all_gather x2, waiting for transfers between devices: 11.3 us -> 25.7 us  [per_device(): lax.all_gather(part, 'dp', axis=0, tiled=True)]
    ppermute x1 -> x0, waiting for transfers between devices: 10.3 us -> none  [reduce_over_chips(): lax.ppermute(grad_blocks(ahead + (1 - core), pairs), 'dp', [(device, devi...]
    pallas_call x5 -> x4, Pallas kernels: 53.1 us -> 52.2 us  [the longest x1 27.1 us: pair_grads(): pl.pallas_call(functools.partial(pair_grad_kernel, chips, len(pairs)), ou...]
  transfers between devices with their start and end apart: 11 -> 10, of which waited for: 5 -> 4; matrix products, arithmetic and copies ran while one was open for 1% -> 0% of each run, Pallas kernels for 62% -> 63%
where the time goes in v10:
time: 607 us; the launch traced here: 606 us
  Pallas kernels  479 us (79%)
  waiting for transfers between devices  99.2 us (16%)
  between operations  14.3 us (2%)
  starting transfers between devices  11 us (2%)
    pallas_call x3, Pallas kernels, scatter_call(): pl.pallas_call(functools.partial(body, tuple((first for _, _, first in tr...  240 us
    pallas_call x1, Pallas kernels, gather_rows(): pl.pallas_call(functools.partial(gather_kernel, size, count), out_shape=o...  76.6 us
    reduce_scatter x1, waiting for transfers between devices, per_device(): lax.psum_scatter(second_grad, 'dp', scatter_dimension=0, tiled=True)  69.9 us
    pallas_call x1, Pallas kernels, attention_backward(): pl.pallas_call(functools.partial(attention_backward_kernel, size, groupin...  45.1 us
    pallas_call x2, Pallas kernels, feed_half(): pl.pallas_call(functools.partial(feed_half_kernel, half, tile, block), ou...  33.9 us
    pallas_call x1, Pallas kernels, pair_grads(): pl.pallas_call(functools.partial(pair_grad_kernel, chips, len(pairs)), ou...  27.1 us
    all_gather x2, waiting for transfers between devices, per_device(): lax.all_gather(part, 'dp', axis=0, tiled=True)  25.7 us
    pallas_call x3, Pallas kernels, grad_blocks(): pl.pallas_call(functools.partial(grad_kernel, len(pairs)), grid=(depth //...  25.1 us
  transfers between devices with their start and end apart: 10, of which 4 were waited for; matrix products, arithmetic and copies ran while one was open for 0% of the time, Pallas kernels for 63%

profile of v10, /device:TPU:0, one launch (start us, length us, event | category | flops | bytes accessed | tf_op | source)
XLA Modules:
  0.0 606.1 jit_solution(3218601405588658969)
XLA Ops:
  7.2 0.0 all-gather.4.cloned.1.call-start
  7.2 2.2 shard_map.246
  9.4 0.0 all-gather.4.cloned.1.call-update
  9.4 0.0 copy-start
  9.4 0.0 all-gather.6.cloned.1.call-start
  9.5 3.4 shard_map.248
  12.8 0.0 all-gather.6.cloned.1.call-update
  12.9 0.0 all-gather.8.cloned.1.call-start
  12.9 0.7 all-gather.8.cloned.1.call-update
  13.6 0.0 reduce-scatter.8.cloned.1.call-start
  13.6 0.0 copy-done
  13.7 0.3 fusion
  14.0 1.3 fusion.2.refs_0_
  15.2 76.6 %gather_rows.1 = (bf16[1024,2048]{1,0:T(8,128)(2,1)}, bf16[2048,1024]{1,0:T(8,128)(2,1)}, bf16[1024,2048]{1,0:T(8,128)(2,1)}, bf16[2048,1024]{1,0:T(8,128)(2,1)}) custom-call(bf16[256,2048]{1,0:T(8,128)(2,1)} %fusion.2.refs_0_, bf16[256,2048]{1,0:T(8,128)(2,1)} %refs_5_.1), custom_call_target="tpu_custom_call" | custom-call | bytes 125829120 | tf_op jit(solution)/shard_map/gather_rows/pallas_call | solution.py:209
  91.8 0.0 all-gather.4.cloned.1.call-done.weight_ref.refs_1_.refs_5_
  91.9 18.5 %attention_forward.1 = (f32[1024,1024]{1,0:T(8,128)}, bf16[1024,512]{1,0:T(8,128)(2,1)}, f32[2,2,1024]{2,1,0:T(2,128)}) custom-call(bf16[1024,2048]{1,0:T(8,128)(2,1)} %get-tuple-element.68.rows_ref.refs_6_, bf16[2048,1536]{1,0:T(8,128)(2,1)} %all-gather.4.cloned.1.call-done.weight_ref.refs_1_.refs_5_, f32[136,128]{1,0:T(8,128)} %constant.11.clone.few_cosines_ref.refs_9_, ...), custom_call_target="tpu_custom_call" | custom-call | flops 5368709120 | bytes 8388608 | tf_op jit(solution)/shard_map/attention_forward/pallas_call | solution.py:879
  110.3 75.1 %shard_map.247 = (bf16[1024,2048]{1,0:T(8,128)(2,1)}, bf16[2048,1024]{1,0:T(8,128)(2,1)}, f32[256,2048]{1,0:T(8,128)}) custom-call(bf16[1024,512]{1,0:T(8,128)(2,1)} %get-tuple-element.69.refs_0_.refs_1_.refs_7_, bf16[2048,1536]{1,0:T(8,128)(2,1)} %all-gather.4.cloned.1.call-done.weight_ref.refs_1_.refs_5_, bf16[256,2048]{1,0:T(8,128)(2,1)} %refs_2_.3, ...), custom_call_target="tpu_custom_call" | custom-call | flops 2147483648 | bytes 150000000 | tf_op jit(solution)/shard_map/pallas_call | solution.py:744
  185.5 9.8 %all-gather.6.cloned.1.call-done.weight_far.refs_1_ = bf16[2048,3072]{1,0:T(8,128)(2,1)} async-done(((bf16[256,3072]{1,0:T(8,128)(2,1)}), bf16[2048,3072]{1,0:T(8,128)(2,1)}) %all-gather.6.cloned.1.call-update) | async-done | bytes 12582928 | tf_op jit(solution)/shard_map/all_gather | solution.py:1514
  195.3 21.9 %feed_half.2 = (bf16[1024,1024]{1,0:T(8,128)(2,1)}, bf16[1024,2048]{1,0:T(8,128)(2,1)}) custom-call(bf16[1024,2048]{1,0:T(8,128)(2,1)} %get-tuple-element.72.rows_far, bf16[1024,2048]{1,0:T(8,128)(2,1)} %get-tuple-element.73.cotangent_far, bf16[2048,3072]{1,0:T(8,128)(2,1)} %all-gather.6.cloned.1.call-done.weight_far.refs_1_), custom_call_target="tpu_custom_call" | custom-call | flops 12884901888 | bytes 20971520 | tf_op jit(solution)/shard_map/feed_half/pallas_call | solution.py:1188
  217.2 27.1 %pair_grads.1 = (bf16[256,3072]{1,0:T(8,128)(2,1)}, bf16[256,3072]{1,0:T(8,128)(2,1)}, bf16[256,3072]{1,0:T(8,128)(2,1)}, bf16[256,3072]{1,0:T(8,128)(2,1)}) custom-call(bf16[2048,1024]{1,0:T(8,128)(2,1)} %get-tuple-element.70.refs_0_, bf16[2048,1024]{1,0:T(8,128)(2,1)} %get-tuple-element.71.refs_1_.refs_2_, ...), custom_call_target="tpu_custom_call" | custom-call | flops 12884901888 | bytes 27262976 | tf_op jit(solution)/shard_map/pair_grads/pallas_call | solution.py:1359
  244.3 0.8 collective-permute-start.1
  245.1 2.5 collective-permute-start
  247.5 15.9 %all-gather.8.cloned.1.call-done.weight_far.refs_3_ = bf16[2048,1536]{1,0:T(8,128)(2,1)} async-done(((bf16[256,1536]{1,0:T(8,128)(2,1)}), bf16[2048,1536]{1,0:T(8,128)(2,1)}) %all-gather.8.cloned.1.call-update) | async-done | bytes 6291472 | tf_op jit(solution)/shard_map/all_gather | solution.py:1514
  263.4 12.0 %feed_half.3 = (bf16[1024,512]{1,0:T(8,128)(2,1)}, bf16[1024,1024]{1,0:T(8,128)(2,1)}) custom-call(bf16[1024,2048]{1,0:T(8,128)(2,1)} %get-tuple-element.72.rows_far, bf16[1024,2048]{1,0:T(8,128)(2,1)} %get-tuple-element.73.cotangent_far, bf16[2048,1536]{1,0:T(8,128)(2,1)} %all-gather.8.cloned.1.call-done.weight_far.refs_3_), custom_call_target="tpu_custom_call" | custom-call | flops 6442450944 | bytes 14680064 | tf_op jit(solution)/shard_map/feed_half/pallas_call | solution.py:1188
  275.3 11.4 %grad_blocks.3 = bf16[2048,1536]{1,0:T(8,128)(2,1)} custom-call(bf16[2048,1024]{1,0:T(8,128)(2,1)} %get-tuple-element.70.refs_0_, bf16[1024,1024]{1,0:T(8,128)(2,1)} %get-tuple-element.86.refs_1_.refs_2_, bf16[2048,1024]{1,0:T(8,128)(2,1)} %get-tuple-element.71.refs_1_.refs_2_, bf16[1024,512]{1,0:T(8,128)(2,1)} %get-tuple-element.85.refs_3_.refs_2_), custom_call_target="tpu_custom_call" | custom-call | flops 6442450944 | bytes 17825792 | tf_op jit(solution)/shard_map/grad_blocks/pallas_call | solution.py:1240
  286.7 0.0 collective-permute-done.1.refs_10_
  286.7 2.3 collective-permute-done.refs_9_
  289.1 83.4 %shard_map.249 = (bf16[1024,2048]{1,0:T(8,128)(2,1)}, bf16[2048,1024]{1,0:T(8,128)(2,1)}, f32[256,2048]{1,0:T(8,128)}, f32[16,128]{1,0:T(8,128)}, bf16[256,3072]{1,0:T(8,128)(2,1)}, /*index=5*/bf16[256,3072]{1,0:T(8,128)(2,1)}) custom-call(bf16[1024,2048]{1,0:T(8,128)(2,1)} %get-tuple-element.75.refs_2_.refs_0_, ...), custom_call_target="tpu_custom_call" | custom-call | flops 12884901888 | bytes 150000000 | tf_op jit(solution)/shard_map/pallas_call | solution.py:744
  372.5 5.4 grad_blocks.4
  377.9 0.0 reduce-scatter.8.cloned.1.call-update
  377.9 0.3 reduce-scatter.6.cloned.1.call-start
  378.2 45.1 %attention_backward.1 = (bf16[1024,1024]{1,0:T(8,128)(2,1)}, f32[8,128]{1,0:T(8,128)}, bf16[256,2048]{1,0:T(8,128)(2,1)}) custom-call(bf16[1024,1024]{1,0:T(8,128)(2,1)} %get-tuple-element.76.refs_3_.refs_0_, bf16[2048,3072]{1,0:T(8,128)(2,1)} %all-gather.6.cloned.1.call-done.weight_far.refs_1_, bf16[1024,512]{1,0:T(8,128)(2,1)} %get-tuple-element.85.refs_3_.refs_2_, ...), custom_call_target="tpu_custom_call" | custom-call | flops 4831838208 | bytes 100000000 | tf_op jit(solution)/shard_map/attention_backward/pallas_call | solution.py:1061
  423.3 8.4 %grad_blocks.5 = bf16[2048,1024]{1,0:T(8,128)(2,1)} custom-call(bf16[2048,1024]{1,0:T(8,128)(2,1)} %get-tuple-element.94.refs_0_, bf16[1024,1024]{1,0:T(8,128)(2,1)} %get-tuple-element.103.refs_1_.refs_0_), custom_call_target="tpu_custom_call" | custom-call | flops 4294967296 | bytes 10485760 | tf_op jit(solution)/shard_map/grad_blocks/pallas_call | solution.py:1240
  431.7 0.0 reduce-scatter.6.cloned.1.call-update
  431.7 0.0 copy-start.3
  431.7 0.0 copy-start.4
  431.8 0.0 reduce-scatter.4.cloned.1.call-start
  431.8 0.5 reduce-scatter.4.cloned.1.call-update
  432.3 6.0 collective-permute-start.2
  438.4 1.3 collective-permute-start.3
  439.7 0.6 pad_maximum_fusion.refs_5_
  440.3 81.7 %shard_map.250 = (bf16[256,2048]{1,0:T(8,128)(2,1)}, f32[40,128]{1,0:T(8,128)}) custom-call(bf16[1024,1024]{1,0:T(8,128)(2,1)} %get-tuple-element.103.refs_1_.refs_0_, bf16[2048,1536]{1,0:T(8,128)(2,1)} %all-gather.4.cloned.1.call-done.weight_ref.refs_1_.refs_5_, bf16[256,2048]{1,0:T(8,128)(2,1)} %refs_2_.3, f32[1,2048]{1,0:T(1,128)} %bitcast.10, ...), custom_call_target="tpu_custom_call" | custom-call | flops 4294967296 | bytes 150000000 | tf_op jit(solution)/shard_map/pallas_call | solution.py:744
  522.0 0.0 collective-permute-done.2.up_ref
  522.0 0.0 collective-permute-done.3.down_ref
  522.0 0.0 reduce-scatter.8.cloned.1.call-done.output_total_ref
  522.0 0.0 reduce-scatter.6.cloned.1.call-done.mixing_ref
  522.1 69.9 %reduce-scatter.4.cloned.1.call-done.second_ref = bf16[256,1536]{1,0:T(8,128)(2,1)} async-done(((bf16[2048,1536]{1,0:T(8,128)(2,1)}), bf16[256,1536]{1,0:T(8,128)(2,1)}) %reduce-scatter.4.cloned.1.call-update) | async-done | bytes 786448 | tf_op jit(solution)/shard_map/reduce_scatter | solution.py:1562
  592.0 7.3 %shard_map.251 = (bf16[256,2048]{1,0:T(8,128)(2,1)}, bf16[256,2048]{1,0:T(8,128)(2,1)}, f32[16,128]{1,0:T(8,128)}, f32[256,512]{1,0:T(8,128)}, f32[256,256]{1,0:...) custom-call(bf16[256,3072]{1,0:T(8,128)(2,1)} %get-tuple-element.82., ...), custom_call_target="tpu_custom_call" | custom-call | bytes 16797696 | tf_op jit(solution)/shard_map/pallas_call | solution.py:1458
  (9 shorter events, 0.0 us)
Async XLA Ops:
  7.2 84.7 %all-gather.4.cloned.1.call-start = ((), (), s32[]{:S(2)}) async-start(), calls=%async_computation.3 | async-start | bytes 7077888 | tf_op jit(solution)/shard_map/all_gather | solution.py:1505
  9.4 4.2 copy-start
  9.4 185.9 %all-gather.6.cloned.1.call-start = ((), (), s32[]{:S(2)}) async-start(), calls=%async_computation.4 | async-start | bytes 14155776 | tf_op jit(solution)/shard_map/all_gather | solution.py:1514
  12.8 1.1 copy-start.2
  12.9 250.5 %all-gather.8.cloned.1.call-start = ((), (), s32[]{:S(2)}) async-start(), calls=%async_computation.5 | async-start | bytes 7077888 | tf_op jit(solution)/shard_map/all_gather | solution.py:1514
  13.6 508.4 %reduce-scatter.8.cloned.1.call-start = ((), (), s32[]{:S(2)}) async-start(), calls=%async_computation.8 | async-start | bytes 2359296 | tf_op jit(solution)/shard_map/reduce_scatter | solution.py:1600
  244.3 42.4 %collective-permute-start.1 = (bf16[256,3072]{1,0:T(8,128)(2,1)}, bf16[256,3072]{1,0:T(8,128)(2,1)S(1)}, u32[]{:S(2)}, u32[]{:S(2)}) collective-permute-start(bf16[256,3072]{1,0:T(8,128)(2,1)} %get-tuple-element.89.refs_11_), channel_id=1, source_target_pairs={{24,16},{28,20},{25,17},{29,21},{26,18},{30,22},{27,19},{31,23}} | collective-permute-start | bytes 4718600 | tf_op jit(solution)/shard_map/ppermute | solution.py:1390
  245.1 44.0 %collective-permute-start = (bf16[256,3072]{1,0:T(8,128)(2,1)}, bf16[256,3072]{1,0:T(8,128)(2,1)}, u32[]{:S(2)}, u32[]{:S(2)}) collective-permute-start(bf16[256,3072]{1,0:T(8,128)(2,1)} %get-tuple-element.90.refs_12_), channel_id=1, source_target_pairs={{0,8},{4,12},{1,9},{5,13},{2,10},{6,14},{3,11},{7,15}} | collective-permute-start | bytes 4718600 | tf_op jit(solution)/shard_map/ppermute | solution.py:1389
  286.7 2.4 copy-start.5
  377.9 144.1 %reduce-scatter.6.cloned.1.call-start = ((), (), s32[]{:S(2)}) async-start(), calls=%async_computation.7 | async-start | bytes 4718592 | tf_op jit(solution)/shard_map/reduce_scatter | solution.py:1612
  431.7 7.9 %copy-start.3 = (f32[16,128]{1,0:T(8,128)S(1)}, f32[16,128]{1,0:T(8,128)}, u32[]{:S(2)}) copy-start(f32[16,128]{1,0:T(8,128)} %get-tuple-element.105) | copy-start | bytes 24580
  431.7 7.9 %copy-start.4 = (f32[8,128]{1,0:T(8,128)S(1)}, f32[8,128]{1,0:T(8,128)}, u32[]{:S(2)}) copy-start(f32[8,128]{1,0:T(8,128)} %get-tuple-element.106) | copy-start | bytes 12292
  431.8 160.2 %reduce-scatter.4.cloned.1.call-start = ((), (), s32[]{:S(2)}) async-start(), calls=%async_computation.6 | async-start | bytes 7077888 | tf_op jit(solution)/shard_map/reduce_scatter | solution.py:1562
  432.3 89.7 %collective-permute-start.2 = (bf16[256,3072]{1,0:T(8,128)(2,1)}, bf16[256,3072]{1,0:T(8,128)(2,1)S(1)}, u32[]{:S(2)}, u32[]{:S(2)}) collective-permute-start(bf16[256,3072]{1,0:T(8,128)(2,1)} %get-tuple-element.91), channel_id=1, source_target_pairs={{0,8},{4,12},{8,16},{12,20},{16,24},{20,28},{1,9},{5,13},{9,17},{1... | collective-permute-start | bytes 4718600 | tf_op jit(solution)/shard_map/ppermute | solution.py:1592
  438.4 83.7 %collective-permute-start.3 = (bf16[256,3072]{1,0:T(8,128)(2,1)}, bf16[256,3072]{1,0:T(8,128)(2,1)}, u32[]{:S(2)}, u32[]{:S(2)}) collective-permute-start(bf16[256,3072]{1,0:T(8,128)(2,1)} %get-tuple-element.92), channel_id=1, source_target_pairs={{8,0},{12,4},{16,8},{20,12},{24,16},{28,20},{9,1},{13,5},{17,9},{2... | collective-permute-start | bytes 4718600 | tf_op jit(solution)/shard_map/ppermute | solution.py:1595
  522.0 70.0 %copy-start.1 = (bf16[256,3072]{1,0:T(8,128)(2,1)}, bf16[256,3072]{1,0:T(8,128)(2,1)S(1)}, u32[]{:S(2)}) copy-start(bf16[256,3072]{1,0:T(8,128)(2,1)S(1)} %collective-permute-done.2.up_ref) | copy-start | bytes 4718596
Sparse Core Ops, SparseCore 0:
  10.2 67.4 all-gather.3
  79.9 115.3 all-gather.5
  197.5 65.8 all-gather.7
  378.0 40.1 reduce-scatter.7
  431.9 90.1 reduce-scatter.5
  524.2 67.7 reduce-scatter.3

commit v11 on v10

--- a/solution.py
+++ b/solution.py
@@ -611,28 +611,22 @@
     scatter.drain()
 
 
-def between_backward_kernel(size, chips, steps, first_columns, *refs):
+def between_backward_kernel(size, chips, first_columns, *refs):
     operands, refs = split_operands(refs, size, first_columns)
     state_ref, cotangent_ref, gain_ref = refs[:3]
-    chain_count = 2 * len(steps) + 2
-    chain_refs, last_refs, refs = refs[3 : 3 + chain_count], refs[3 + chain_count : 5 + chain_count], refs[5 + chain_count :]
-    gathered_ref, gathered_turned_ref, slope_ref, term_ref, rising_ref, falling_ref = refs[:6]
-    own_ref, sum_ref, last_sem = refs[6:9]
+    chain_refs, own_block_ref, refs = refs[3:7], refs[7], refs[8:]
+    gathered_ref, gathered_turned_ref, slope_ref, term_ref, chain_total_ref = refs[:5]
+    own_ref, sum_ref, own_sem = refs[5:8]
     buffers = 5 if size == 4 else 4
-    scatter = Scatter(size, *refs[9 : 9 + buffers])
-    gather = Gather(size, own_ref, gathered_ref, gathered_turned_ref, *refs[9 + buffers : 15 + buffers])
+    scatter = Scatter(size, *refs[8 : 8 + buffers])
+    gather = Gather(size, own_ref, gathered_ref, gathered_turned_ref, *refs[8 + buffers : 14 + buffers])
     chain = Chain(
-        chips, steps, chain_refs[: len(steps)], chain_refs[len(steps) : -2], *chain_refs[-2:],
-        *refs[15 + buffers :],
-    )
-    last_loads = [
-        pltpu.make_async_copy(source, target, last_sem.at[index])
-        for index, (source, target) in enumerate(zip(last_refs, (rising_ref, falling_ref)))
-    ]
+        chips, (chips - 1,), chain_refs[:1], chain_refs[1:2], *chain_refs[2:], *refs[14 + buffers :]
+    )
+    own_load = pltpu.make_async_copy(own_block_ref, chain_total_ref, own_sem.at[0])
     chain.load()
     scatter.load(operands)
-    for load in last_loads:
-        load.start()
+    own_load.start()
     greet(neighbours(size) + chain.neighbours)
     scatter.fill(operands, between=lambda: chain.step(0))
     scatter.relay()
@@ -654,26 +648,20 @@
     scatter.over_stages(norm, gather.start)
     store_row(term_ref, sum_ref)
     gather.forward()
+    gather.finish()
+    own_load.wait()
     chain.wait(0)
-    for index in range(1, len(steps)):
-        chain.step(index)
-        chain.wait(index)
-    for load in last_loads:
-        load.wait()
-    last = len(steps)
-    for needed, landing, out_ref in (
-        ((chain.chip > 0) & (chain.chip < chips - 1), chain.up, rising_ref),
-        ((chain.chip > 0) & (chain.chip < chips - 1), chain.down, falling_ref),
-    ):
-
-        @pl.when(needed)
-        def _(landing=landing, out_ref=out_ref):
+    for arrived, landing in zip(chain.arrives(0), (chain.up, chain.down)):
+
+        @pl.when(arrived)
+        def _(landing=landing):
             def add(piece):
-                out_ref[piece, :] = add_rounded(out_ref[piece, :], landing[last, piece, :])
-
-            over_pieces(out_ref.shape[0], add)
-
-    gather.finish()
+                chain_total_ref[piece, :] = add_rounded(
+                    chain_total_ref[piece, :], landing[1, piece, :]
+                )
+
+            over_pieces(chain_total_ref.shape[0], add)
+
     scatter.drain()
     chain.drain()
 
@@ -1386,12 +1374,15 @@
     data_size = sizes[0]
     chips = data_size // 2
     blocks = pair_grads(pairs, sizes, collective_id)
-    up = lax.ppermute(blocks[chips - 1], "dp", [(device, device + 2) for device in range(2)])
-    down = lax.ppermute(
-        blocks[1],
-        "dp",
-        [(device, device - 2) for device in range(data_size - 2, data_size)],
-    )
+    up = down = None
+    for step in range(1, chips - 1):
+        rising, falling = blocks[chips - step], blocks[step]
+        if up is not None:
+            rising, falling = add_rounded(rising, up), add_rounded(falling, down)
+        up = lax.ppermute(
+            rising, "dp", [(device, device + 2) for device in range(2 * step)]
+        )
+        down = lax.ppermute(falling, "dp", [(device, device - 2) for device in range(data_size - 2 * step, data_size)])
     return blocks, up, down
 
 
@@ -1417,31 +1408,29 @@
         start += width
 
 
-def finish_kernel(
-    heads, own_ref, up_ref, down_ref, second_ref, mixing_ref, output_total_ref, terms_ref, output_rows_ref, input_rows_ref,
-    output_rows_out, input_rows_out, attention_term_out, query_out, key_out, value_out, query_gain_out, key_gain_out,
-    output_out, feed_term_out, gate_out, up_out, down_out,
-):
-    output_rows_out[...] = output_rows_ref[...]
-    input_rows_out[...] = input_rows_ref[...]
-    count = attention_term_out.shape[0]
-    attention_term_out[...] = terms_ref[:count, :]
-    feed_term_out[...] = terms_ref[count : 2 * count, :]
-    query_gain_out[...] = terms_ref[2 * count : 2 * count + 1, :]
-    key_gain_out[...] = terms_ref[2 * count + 1 : 2 * count + 2, :]
+def finish_kernel(heads, *refs):
+    first_ref, second_ref, mixing_ref, output_total_ref, terms_ref, output_rows_ref, input_rows_ref = refs[:7]
+    far, held, sem = refs[7:20], refs[20:31], refs[31]
+    (
+        attention_term_out, query_out, key_out, value_out, query_gain_out, key_gain_out,
+        output_out, feed_term_out, gate_out, up_out, down_out,
+    ) = held
+    copies = [
+        pltpu.make_async_copy(source, target, sem.at[index])
+        for index, (source, target) in enumerate(zip((output_rows_ref, input_rows_ref, *held), far))
+    ]
+    copies[0].start()
+    copies[1].start()
     start = 0
-    for total_refs in ((own_ref, up_ref, down_ref), (second_ref,)):
-        width = total_refs[0].shape[1] // 3
+    for total_ref in (first_ref, second_ref):
+        width = total_ref.shape[1] // 3
         part = slice(start, start + width)
-
-        def total(index):
-            columns = slice(index * width, (index + 1) * width)
-            return sum(ref[:, columns].astype(jnp.float32) for ref in total_refs)
-
-        gate_out[:, part] = total(0)
-        up_out[:, part] = total(1)
-        down_out[part, :] = total(2).T
+        gate_out[:, part] = total_ref[:, :width].astype(jnp.float32)
+        up_out[:, part] = total_ref[:, width : 2 * width].astype(jnp.float32)
+        down_out[part, :] = total_ref[:, 2 * width :].astype(jnp.float32).T
         start += width
+    for copy in copies[10:13]:
+        copy.start()
     query_width = query_out.shape[1] // heads
     head_size = key_out.shape[1] // heads
     start = 0
@@ -1452,6 +1441,15 @@
             )
             start += part
     output_out[...] = output_total_ref[...].astype(jnp.float32).T
+    count = attention_term_out.shape[0]
+    attention_term_out[...] = terms_ref[:count, :]
+    feed_term_out[...] = terms_ref[count : 2 * count, :]
+    query_gain_out[...] = terms_ref[2 * count : 2 * count + 1, :]
+    key_gain_out[...] = terms_ref[2 * count + 1 : 2 * count + 2, :]
+    for copy in copies[2:10]:
+        copy.start()
+    for copy in copies:
+        copy.wait()
 
 
 def whole_call(body, shapes, *operands):
@@ -1492,7 +1490,7 @@
     grouping = query_columns // key_columns
     hidden_columns = gate_weight.shape[1]
     qkv_columns = query_columns + 2 * key_columns
-    first_columns = hidden_columns * 2 // 3 // 256 * 256 or hidden_columns // 2
+    first_columns = hidden_columns // 2
     second_columns = hidden_columns - first_columns
     tables = turn_tables(head_size)
 
@@ -1511,7 +1509,9 @@
         ],
         gate_weight, up_weight, down_weight,
     )
-    feed_full = [lax.all_gather(part, "dp", axis=0, tiled=True) for part in feed_locals]
+    first_full = lax.all_gather(feed_locals[0], "dp", axis=0, tiled=True)
+    second_full = lax.all_gather(feed_locals[1], "dp", axis=0, tiled=True)
+    feed_full = [first_full, second_full]
 
     input_float = block_input.astype(jnp.float32)
     first_scale = row_scale(input_float)
@@ -1561,39 +1561,28 @@
     second_grad, slope_second = lax.optimization_barrier((second_grad, slope_second))
     second_total = lax.psum_scatter(second_grad, "dp", scatter_dimension=0, tiled=True)
     chips = sizes[0] // 2
-    middle_steps = tuple(range(2, chips - 1))
-    chain_block = jax.ShapeDtypeStruct(blocks[0].shape, jnp.bfloat16)
-    state_rows, state_turned, state_slope, feed_term, rising, falling = scatter_call(
-        functools.partial(between_backward_kernel, size, chips, middle_steps),
+    state_rows, state_turned, state_slope, feed_term, first_total = scatter_call(
+        functools.partial(between_backward_kernel, size, chips),
         [(slope_first, feed_full[0], 0), (slope_second, later_full, 0)],
         size,
         [hidden_state, out_cotangent, feed_gain.reshape(1, -1)],
-        [blocks[chips - step] for step in middle_steps]
-        + [blocks[step] for step in middle_steps]
-        + [up, down, blocks[1], blocks[chips - 1]],
+        [blocks[1], blocks[chips - 1], up, down, blocks[0]],
         [
             *gathered_shapes,
             local_float,
             jax.ShapeDtypeStruct((gain_rows, head_size), jnp.float32),
-            chain_block,
-            chain_block,
+            jax.ShapeDtypeStruct(blocks[0].shape, jnp.bfloat16),
         ],
         True,
         [
             own_rows,
             row_sum,
-            pltpu.SemaphoreType.DMA((2,)),
+            pltpu.SemaphoreType.DMA((1,)),
             *scatter_scratch,
             *gather_scratch,
-            *Chain.scratch(len(middle_steps), *blocks[0].shape),
+            *Chain.scratch(1, *blocks[0].shape),
         ],
         2,
-    )
-    up = lax.ppermute(
-        rising, "dp", [(device, device + 2) for device in range(sizes[0] - 2)]
-    )
-    down = lax.ppermute(
-        falling, "dp", [(device, device - 2) for device in range(2, sizes[0])]
     )
     output_grad = grad_blocks([(state_turned, mixed_rows)], 4 * block_width)
     output_grad, state_rows = lax.optimization_barrier((output_grad, state_rows))
@@ -1640,25 +1629,30 @@
     def whole_float(*shape):
         return jax.ShapeDtypeStruct(shape, jnp.float32)
 
-    outs = whole_call(
+    float_shapes = [
+        whole_float(gain_rows, head_size),
+        whole_float(block_width, query_columns),
+        whole_float(block_width, key_columns),
+        whole_float(block_width, key_columns),
+        whole_float(1, head_size),
+        whole_float(1, head_size),
+        whole_float(query_columns, block_width),
+        whole_float(gain_rows, head_size),
+        whole_float(block_width, hidden_columns),
+        whole_float(block_width, hidden_columns),
+        whole_float(hidden_columns, block_width),
+    ]
+    outs = pl.pallas_call(
         functools.partial(finish_kernel, heads),
-        [
-            local_half,
-            local_half,
-            whole_float(gain_rows, head_size),
-            whole_float(block_width, query_columns),
-            whole_float(block_width, key_columns),
-            whole_float(block_width, key_columns),
-            whole_float(1, head_size),
-            whole_float(1, head_size),
-            whole_float(query_columns, block_width),
-            whole_float(gain_rows, head_size),
-            whole_float(block_width, hidden_columns),
-            whole_float(block_width, hidden_columns),
-            whole_float(hidden_columns, block_width),
-        ],
-        blocks[0], up, down, second_total, mixing_total, output_total, terms, block_output, input_gradient,
-    )
+        out_shape=[local_half, local_half, *float_shapes],
+        in_specs=[pl.BlockSpec(memory_space=pltpu.VMEM)] * 7,
+        out_specs=[pl.BlockSpec(memory_space=pl.ANY)] * 13,
+        scratch_shapes=[pltpu.VMEM(shape.shape, shape.dtype) for shape in float_shapes]
+        + [pltpu.SemaphoreType.DMA((13,))],
+        compiler_params=pltpu.CompilerParams(vmem_limit_bytes=VMEM_LIMIT),
+        cost_estimate=pl.CostEstimate(flops=0, bytes_accessed=20_000_000, transcendentals=0),
+        name="finish",
+    )(first_total, second_total, mixing_total, output_total, terms, block_output, input_gradient)
     return tuple(
         out.reshape(-1) if index in (2, 6, 7, 9) else out for index, out in enumerate(outs)
     )

time: 607 us -> 632 us (1.041)
  waiting for transfers between devices: 99.2 us -> 157 us
  Pallas kernels: 479 us -> 441 us
    pallas_call x3, Pallas kernels: 240 us -> 204 us  [scatter_call(): pl.pallas_call(functools.partial(body, tuple((first for _, _, first in tr...]
    reduce_scatter x1, waiting for transfers between devices: 69.9 us -> 100 us  [per_device(): lax.psum_scatter(second_grad, 'dp', scatter_dimension=0, tiled=True)]
    all_gather x2, waiting for transfers between devices: 25.7 us -> 50 us  [the longest x1 50 us: per_device(): second_full = lax.all_gather(feed_locals[1], 'dp', axis=0, tiled=True)]
    pallas_call x3 -> x2, Pallas kernels: 12.8 us -> 5.5 us  [whole_call(): pl.pallas_call(body, out_shape=shapes, in_specs=[pl.BlockSpec(memory_spac...]
  transfers between devices with their start and end apart: 10 -> 10, of which waited for: 4 -> 4; matrix products, arithmetic and copies ran while one was open for 0% -> 0% of each run, Pallas kernels for 63% -> 55%
where the time goes in v11:
time: 632 us; the launch traced here: 631 us
  Pallas kernels  441 us (70%)
  waiting for transfers between devices  157 us (25%)
  between operations  14.3 us (2%)
  starting transfers between devices  14 us (2%)
    pallas_call x3, Pallas kernels, scatter_call(): pl.pallas_call(functools.partial(body, tuple((first for _, _, first in tr...  204 us
    reduce_scatter x1, waiting for transfers between devices, per_device(): lax.psum_scatter(second_grad, 'dp', scatter_dimension=0, tiled=True)  100 us
    pallas_call x1, Pallas kernels, gather_rows(): pl.pallas_call(functools.partial(gather_kernel, size, count), out_shape=o...  76.6 us
    all_gather x1, waiting for transfers between devices, per_device(): second_full = lax.all_gather(feed_locals[1], 'dp', axis=0, tiled=True)  50 us
    pallas_call x1, Pallas kernels, attention_backward(): pl.pallas_call(functools.partial(attention_backward_kernel, size, groupin...  45.2 us
    pallas_call x2, Pallas kernels, feed_half(): pl.pallas_call(functools.partial(feed_half_kernel, half, tile, block), ou...  33.8 us
    pallas_call x3, Pallas kernels, grad_blocks(): pl.pallas_call(functools.partial(grad_kernel, len(pairs)), grid=(depth //...  28.7 us
    pallas_call x1, Pallas kernels, pair_grads(): pl.pallas_call(functools.partial(pair_grad_kernel, chips, len(pairs)), ou...  22.7 us
  transfers between devices with their start and end apart: 10, of which 4 were waited for; matrix products, arithmetic and copies ran while one was open for 0% of the time, Pallas kernels for 55%

profile of v11, /device:TPU:0, one launch (start us, length us, event | category | flops | bytes accessed | tf_op | source)
XLA Modules:
  0.0 631.3 jit_solution(10449535810627987300)
XLA Ops:
  7.2 0.0 all-gather.4.cloned.1.call-start
  7.2 2.2 shard_map.246
  9.4 0.0 all-gather.4.cloned.1.call-update
  9.4 0.0 copy-start
  9.4 0.0 all-gather.6.cloned.1.call-start
  9.5 3.3 shard_map.248
  12.8 0.0 all-gather.6.cloned.1.call-update
  12.8 0.0 all-gather.8.cloned.1.call-start
  12.9 0.7 all-gather.8.cloned.1.call-update
  13.6 0.0 reduce-scatter.8.cloned.1.call-start
  13.6 0.3 fusion.2
  13.9 1.3 fusion.4.refs_0_
  15.2 76.6 %gather_rows.1 = (bf16[1024,2048]{1,0:T(8,128)(2,1)}, bf16[2048,1024]{1,0:T(8,128)(2,1)}, bf16[1024,2048]{1,0:T(8,128)(2,1)}, bf16[2048,1024]{1,0:T(8,128)(2,1)}) custom-call(bf16[256,2048]{1,0:T(8,128)(2,1)} %fusion.4.refs_0_, bf16[256,2048]{1,0:T(8,128)(2,1)} %refs_5_.1), custom_call_target="tpu_custom_call" | custom-call | bytes 125829120 | tf_op jit(solution)/shard_map/gather_rows/pallas_call | solution.py:209
  91.8 0.0 all-gather.4.cloned.1.call-done.weight_ref.refs_1_.refs_5_
  91.8 18.6 %attention_forward.1 = (f32[1024,1024]{1,0:T(8,128)}, bf16[1024,512]{1,0:T(8,128)(2,1)}, f32[2,2,1024]{2,1,0:T(2,128)}) custom-call(bf16[1024,2048]{1,0:T(8,128)(2,1)} %get-tuple-element.66.rows_ref.refs_6_, bf16[2048,1536]{1,0:T(8,128)(2,1)} %all-gather.4.cloned.1.call-done.weight_ref.refs_1_.refs_5_, f32[136,128]{1,0:T(8,128)} %constant.11.clone.few_cosines_ref.refs_9_, ...), custom_call_target="tpu_custom_call" | custom-call | flops 5368709120 | bytes 8388608 | tf_op jit(solution)/shard_map/attention_forward/pallas_call | solution.py:867
  110.4 75.0 %shard_map.247 = (bf16[1024,2048]{1,0:T(8,128)(2,1)}, bf16[2048,1024]{1,0:T(8,128)(2,1)}, f32[256,2048]{1,0:T(8,128)}) custom-call(bf16[1024,512]{1,0:T(8,128)(2,1)} %get-tuple-element.67.refs_0_.refs_1_.refs_7_, bf16[2048,1536]{1,0:T(8,128)(2,1)} %all-gather.4.cloned.1.call-done.weight_ref.refs_1_.refs_5_, bf16[256,2048]{1,0:T(8,128)(2,1)} %refs_2_.3, ...), custom_call_target="tpu_custom_call" | custom-call | flops 2147483648 | bytes 150000000 | tf_op jit(solution)/shard_map/pallas_call | solution.py:732
  185.4 0.0 all-gather.6.cloned.1.call-done.weight_far.refs_1_
  185.4 17.0 %feed_half.2 = (bf16[1024,768]{1,0:T(8,128)(2,1)}, bf16[1024,1536]{1,0:T(8,128)(2,1)}) custom-call(bf16[1024,2048]{1,0:T(8,128)(2,1)} %get-tuple-element.68.rows_far, bf16[1024,2048]{1,0:T(8,128)(2,1)} %get-tuple-element.69.cotangent_far, bf16[2048,2304]{1,0:T(8,128)(2,1)} %all-gather.6.cloned.1.call-done.weight_far.refs_1_), custom_call_target="tpu_custom_call" | custom-call | flops 9663676416 | bytes 17825792 | tf_op jit(solution)/shard_map/feed_half/pallas_call | solution.py:1176
  202.4 22.7 %pair_grads.1 = (bf16[256,2304]{1,0:T(8,128)(2,1)}, bf16[256,2304]{1,0:T(8,128)(2,1)}, bf16[256,2304]{1,0:T(8,128)(2,1)}, bf16[256,2304]{1,0:T(8,128)(2,1)}) custom-call(bf16[2048,1024]{1,0:T(8,128)(2,1)} %get-tuple-element.72.refs_0_, bf16[2048,1024]{1,0:T(8,128)(2,1)} %get-tuple-element.73.refs_1_.refs_2_, ...), custom_call_target="tpu_custom_call" | custom-call | flops 9663676416 | bytes 22544384 | tf_op jit(solution)/shard_map/pair_grads/pallas_call | solution.py:1347
  225.1 0.7 collective-permute-start.2
  225.8 4.6 collective-permute-start
  230.5 50.0 %all-gather.8.cloned.1.call-done.weight_far.refs_3_ = bf16[2048,2304]{1,0:T(8,128)(2,1)} async-done(((bf16[256,2304]{1,0:T(8,128)(2,1)}), bf16[2048,2304]{1,0:T(8,128)(2,1)}) %all-gather.8.cloned.1.call-update) | async-done | bytes 9437200 | tf_op jit(solution)/shard_map/all_gather | solution.py:1513
  280.4 0.0 collective-permute-done.2
  280.4 0.1 collective-permute-done
  280.5 3.1 fusion.1
  283.6 1.7 collective-permute-start.3
  285.3 6.5 %collective-permute-start.1 = (bf16[256,2304]{1,0:T(8,128)(2,1)S(1)}, bf16[256,2304]{1,0:T(8,128)(2,1)}, u32[]{:S(2)}, u32[]{:S(2)}) collective-permute-start(bf16[256,2304]{1,0:T(8,128)(2,1)S(1)} %get-tuple-element.120), channel_id=1, source_target_pairs={{0,8},{4,12},{8,16},{12,20},{1,9},{5,13},{9,17},{13,21},{2,10},{6,... | collective-permute-start | bytes 3538952 | tf_op jit(solution)/shard_map/ppermute | solution.py:1382
  291.8 16.8 %feed_half.3 = (bf16[1024,768]{1,0:T(8,128)(2,1)}, bf16[1024,1536]{1,0:T(8,128)(2,1)}) custom-call(bf16[1024,2048]{1,0:T(8,128)(2,1)} %get-tuple-element.68.rows_far, bf16[1024,2048]{1,0:T(8,128)(2,1)} %get-tuple-element.69.cotangent_far, bf16[2048,2304]{1,0:T(8,128)(2,1)} %all-gather.8.cloned.1.call-done.weight_far.refs_3_), custom_call_target="tpu_custom_call" | custom-call | flops 9663676416 | bytes 17825792 | tf_op jit(solution)/shard_map/feed_half/pallas_call | solution.py:1176
  308.6 14.9 %grad_blocks.3 = bf16[2048,2304]{1,0:T(8,128)(2,1)} custom-call(bf16[2048,1024]{1,0:T(8,128)(2,1)} %get-tuple-element.72.refs_0_, bf16[1024,1536]{1,0:T(8,128)(2,1)} %get-tuple-element.83.refs_1_.refs_2_, bf16[2048,1024]{1,0:T(8,128)(2,1)} %get-tuple-element.73.refs_1_.refs_2_, bf16[1024,768]{1,0:T(8,128)(2,1)} %get-tuple-element.82.refs_3_.refs_2_), custom_call_target="tpu_custom_call" | custom-call | flops 9663676416 | bytes 22544384 | tf_op jit(solution)/shard_map/grad_blocks/pallas_call | solution.py:1228
  323.6 0.0 collective-permute-done.3.refs_10_
  323.6 0.0 collective-permute-done.1.refs_9_
  323.6 82.5 %shard_map.249 = (bf16[1024,2048]{1,0:T(8,128)(2,1)}, bf16[2048,1024]{1,0:T(8,128)(2,1)}, f32[256,2048]{1,0:T(8,128)}, f32[16,128]{1,0:T(8,128)}, bf16[256,2304]{1,0:T(8,128)(2,1)}) custom-call(bf16[1024,1536]{1,0:T(8,128)(2,1)} %get-tuple-element.71.refs_2_.refs_0_, bf16[2048,2304]{1,0:T(8,128)(2,1)} %all-gather.6.cloned.1.call-done.weight_far.refs_1_, ...), custom_call_target="tpu_custom_call" | custom-call | flops 12884901888 | bytes 150000000 | tf_op jit(solution)/shard_map/pallas_call | solution.py:732
  406.1 5.4 grad_blocks.4
  411.4 0.0 reduce-scatter.8.cloned.1.call-update
  411.4 0.3 reduce-scatter.6.cloned.1.call-start
  411.7 45.2 %attention_backward.1 = (bf16[1024,1024]{1,0:T(8,128)(2,1)}, f32[8,128]{1,0:T(8,128)}, bf16[256,2048]{1,0:T(8,128)(2,1)}) custom-call(bf16[1024,768]{1,0:T(8,128)(2,1)} %get-tuple-element.74.refs_3_.refs_0_, bf16[2048,2304]{1,0:T(8,128)(2,1)} %all-gather.6.cloned.1.call-done.weight_far.refs_1_, bf16[1024,768]{1,0:T(8,128)(2,1)} %get-tuple-element.82.refs_3_.refs_2_, ...), custom_call_target="tpu_custom_call" | custom-call | flops 4831838208 | bytes 100000000 | tf_op jit(solution)/shard_map/attention_backward/pallas_call | solution.py:1049
  456.9 8.4 %grad_blocks.5 = bf16[2048,1024]{1,0:T(8,128)(2,1)} custom-call(bf16[2048,1024]{1,0:T(8,128)(2,1)} %get-tuple-element.90.refs_0_, bf16[1024,1024]{1,0:T(8,128)(2,1)} %get-tuple-element.99.refs_1_.refs_0_), custom_call_target="tpu_custom_call" | custom-call | flops 4294967296 | bytes 10485760 | tf_op jit(solution)/shard_map/grad_blocks/pallas_call | solution.py:1228
  465.3 0.0 reduce-scatter.6.cloned.1.call-update
  465.3 0.0 copy-start.2
  465.3 0.0 reduce-scatter.4.cloned.1.call-start
  465.4 0.5 reduce-scatter.4.cloned.1.call-update
  465.9 0.1 copy-done.2
  466.0 0.6 pad_maximum_fusion.refs_5_
  466.6 46.6 %shard_map.250 = (bf16[256,2048]{1,0:T(8,128)(2,1)}, f32[40,128]{1,0:T(8,128)}) custom-call(bf16[1024,1024]{1,0:T(8,128)(2,1)} %get-tuple-element.99.refs_1_.refs_0_, bf16[2048,1536]{1,0:T(8,128)(2,1)} %all-gather.4.cloned.1.call-done.weight_ref.refs_1_.refs_5_, bf16[256,2048]{1,0:T(8,128)(2,1)} %refs_2_.3, f32[1,2048]{1,0:T(1,128)} %bitcast.10, ...), custom_call_target="tpu_custom_call" | custom-call | flops 4294967296 | bytes 150000000 | tf_op jit(solution)/shard_map/pallas_call | solution.py:732
  513.2 0.0 reduce-scatter.8.cloned.1.call-done.refs_3_
  513.2 5.2 reduce-scatter.6.cloned.1.call-done.refs_2_
  518.4 100.1 %reduce-scatter.4.cloned.1.call-done.refs_1_ = bf16[256,2304]{1,0:T(8,128)(2,1)} async-done(((bf16[2048,2304]{1,0:T(8,128)(2,1)}), bf16[256,2304]{1,0:T(8,128)(2,1)}) %reduce-scatter.4.cloned.1.call-update) | async-done | bytes 1179664 | tf_op jit(solution)/shard_map/reduce_scatter | solution.py:1562
  618.5 5.9 finish.1
  (6 shorter events, 0.0 us)
Async XLA Ops:
  7.2 84.7 %all-gather.4.cloned.1.call-start = ((), (), s32[]{:S(2)}) async-start(), calls=%async_computation.3 | async-start | bytes 7077888 | tf_op jit(solution)/shard_map/all_gather | solution.py:1503
  9.4 4.2 copy-start
  9.4 176.0 %all-gather.6.cloned.1.call-start = ((), (), s32[]{:S(2)}) async-start(), calls=%async_computation.4 | async-start | bytes 10616832 | tf_op jit(solution)/shard_map/all_gather | solution.py:1512
  12.8 1.1 copy-start.1
  12.8 267.6 %all-gather.8.cloned.1.call-start = ((), (), s32[]{:S(2)}) async-start(), calls=%async_computation.5 | async-start | bytes 10616832 | tf_op jit(solution)/shard_map/all_gather | solution.py:1513
  13.6 499.6 %reduce-scatter.8.cloned.1.call-start = ((), (), s32[]{:S(2)}) async-start(), calls=%async_computation.8 | async-start | bytes 2359296 | tf_op jit(solution)/shard_map/reduce_scatter | solution.py:1589
  225.1 55.4 %collective-permute-start.2 = (bf16[256,2304]{1,0:T(8,128)(2,1)}, bf16[256,2304]{1,0:T(8,128)(2,1)S(1)}, u32[]{:S(2)}, u32[]{:S(2)}) collective-permute-start(bf16[256,2304]{1,0:T(8,128)(2,1)} %get-tuple-element.85.refs_7_), channel_id=1, source_target_pairs={{24,16},{28,20},{25,17},{29,21},{26,18},{30,22},{27,19},{31,23}} | collective-permute-start | bytes 3538952 | tf_op jit(solution)/shard_map/ppermute | solution.py:1385
  225.8 54.7 %collective-permute-start = (bf16[256,2304]{1,0:T(8,128)(2,1)}, bf16[256,2304]{1,0:T(8,128)(2,1)}, u32[]{:S(2)}, u32[]{:S(2)}) collective-permute-start(bf16[256,2304]{1,0:T(8,128)(2,1)} %get-tuple-element.86.refs_8_), channel_id=1, source_target_pairs={{0,8},{4,12},{1,9},{5,13},{2,10},{6,14},{3,11},{7,15}} | collective-permute-start | bytes 3538952 | tf_op jit(solution)/shard_map/ppermute | solution.py:1382
  283.6 39.9 %collective-permute-start.3 = (bf16[256,2304]{1,0:T(8,128)(2,1)}, bf16[256,2304]{1,0:T(8,128)(2,1)}, u32[]{:S(2)}, u32[]{:S(2)}) collective-permute-start(bf16[256,2304]{1,0:T(8,128)(2,1)} %get-tuple-element.119), channel_id=1, source_target_pairs={{16,8},{20,12},{24,16},{28,20},{17,9},{21,13},{25,17},{29,21},{18,... | collective-permute-start | bytes 3538952 | tf_op jit(solution)/shard_map/ppermute | solution.py:1385
  285.3 38.2 %collective-permute-start.1 = (bf16[256,2304]{1,0:T(8,128)(2,1)S(1)}, bf16[256,2304]{1,0:T(8,128)(2,1)}, u32[]{:S(2)}, u32[]{:S(2)}) collective-permute-start(bf16[256,2304]{1,0:T(8,128)(2,1)S(1)} %get-tuple-element.120), channel_id=1, source_target_pairs={{0,8},{4,12},{8,16},{12,20},{1,9},{5,13},{9,17},{13,21},{2,10},{6,... | collective-permute-start | bytes 3538952 | tf_op jit(solution)/shard_map/ppermute | solution.py:1382
  411.4 107.0 %reduce-scatter.6.cloned.1.call-start = ((), (), s32[]{:S(2)}) async-start(), calls=%async_computation.7 | async-start | bytes 4718592 | tf_op jit(solution)/shard_map/reduce_scatter | solution.py:1601
  465.3 0.7 copy-start.2
  465.3 0.7 copy-start.3
  465.3 153.2 %reduce-scatter.4.cloned.1.call-start = ((), (), s32[]{:S(2)}) async-start(), calls=%async_computation.6 | async-start | bytes 10616832 | tf_op jit(solution)/shard_map/reduce_scatter | solution.py:1562
Sparse Core Ops, SparseCore 0:
  10.2 67.4 all-gather.3
  79.9 89.3 all-gather.5
  171.5 108.8 all-gather.7
  411.6 36.4 reduce-scatter.7
  465.4 52.9 reduce-scatter.5
  520.6 97.8 reduce-scatter.3

commit v12 on v11

--- a/solution.py
+++ b/solution.py
@@ -533,6 +533,22 @@
         pl.when(from_under)(self.rises[index].wait_recv)
         pl.when(from_above)(self.falls[index].wait_recv)
 
+    def advance(self, index):
+        self.wait(index - 1)
+        self.step(index)
+
+    def add_last(self, total_ref):
+        last = len(self.steps)
+        self.wait(last - 1)
+        for arrived, landing in zip(self.arrives(last - 1), (self.up, self.down)):
+
+            @pl.when(arrived)
+            def _(landing=landing):
+                def add(piece):
+                    total_ref[piece, :] = add_rounded(total_ref[piece, :], landing[last, piece, :])
+
+                over_pieces(total_ref.shape[0], add)
+
     def drain(self):
         for index, step in enumerate(self.steps):
             pl.when(self.chip < step)(self.rises[index].wait_send)
@@ -614,14 +630,17 @@
 def between_backward_kernel(size, chips, first_columns, *refs):
     operands, refs = split_operands(refs, size, first_columns)
     state_ref, cotangent_ref, gain_ref = refs[:3]
-    chain_refs, own_block_ref, refs = refs[3:7], refs[7], refs[8:]
+    steps = tuple(range(2, chips))
+    chain_count = 2 * len(steps) + 2
+    chain_refs, own_block_ref, refs = refs[3 : 3 + chain_count], refs[3 + chain_count], refs[4 + chain_count :]
     gathered_ref, gathered_turned_ref, slope_ref, term_ref, chain_total_ref = refs[:5]
     own_ref, sum_ref, own_sem = refs[5:8]
     buffers = 5 if size == 4 else 4
     scatter = Scatter(size, *refs[8 : 8 + buffers])
     gather = Gather(size, own_ref, gathered_ref, gathered_turned_ref, *refs[8 + buffers : 14 + buffers])
     chain = Chain(
-        chips, (chips - 1,), chain_refs[:1], chain_refs[1:2], *chain_refs[2:], *refs[14 + buffers :]
+        chips, steps, chain_refs[: len(steps)], chain_refs[len(steps) : -2], *chain_refs[-2:],
+        *refs[14 + buffers :],
     )
     own_load = pltpu.make_async_copy(own_block_ref, chain_total_ref, own_sem.at[0])
     chain.load()
@@ -645,23 +664,19 @@
         slope_ref[piece, :] = slope
         own_ref[piece, :] = slope.astype(own_ref.dtype)
 
-    scatter.over_stages(norm, gather.start)
+    def done(stage):
+        gather.start(stage)
+        if stage == 0 and len(steps) > 1:
+            chain.advance(1)
+
+    scatter.over_stages(norm, done)
     store_row(term_ref, sum_ref)
     gather.forward()
+    for index in range(2, len(steps)):
+        chain.advance(index)
     gather.finish()
     own_load.wait()
-    chain.wait(0)
-    for arrived, landing in zip(chain.arrives(0), (chain.up, chain.down)):
-
-        @pl.when(arrived)
-        def _(landing=landing):
-            def add(piece):
-                chain_total_ref[piece, :] = add_rounded(
-                    chain_total_ref[piece, :], landing[1, piece, :]
-                )
-
-            over_pieces(chain_total_ref.shape[0], add)
-
+    chain.add_last(chain_total_ref)
     scatter.drain()
     chain.drain()
 
@@ -670,11 +685,23 @@
     data_size, size = sizes
     operands, refs = split_operands(refs, size, first_columns)
     input_ref, gain_ref, slope_ref, terms_ref, rows_ref = refs[:5]
-    gradient_ref, terms_out_ref, sum_ref, partial_ref, group_ref, inner, outer = refs[5:12]
-    inner_send, inner_recv, outer_send, outer_recv = refs[12:16]
-    mixing = Scatter(size, *refs[16:])
+    chips = data_size // 2
+    steps = tuple(range(1, chips))
+    chain_count = 2 * len(steps) + 2
+    chain_refs, own_block_ref, refs = refs[5 : 5 + chain_count], refs[5 + chain_count], refs[6 + chain_count :]
+    gradient_ref, terms_out_ref, chain_total_ref, sum_ref, partial_ref, group_ref, inner, outer = refs[:8]
+    inner_send, inner_recv, outer_send, outer_recv, own_sem = refs[8:13]
+    buffers = 5 if size == 4 else 4
+    mixing = Scatter(size, *refs[13 : 13 + buffers])
+    chain = Chain(
+        chips, steps, chain_refs[: len(steps)], chain_refs[len(steps) : -2], *chain_refs[-2:],
+        *refs[13 + buffers :],
+    )
+    own_load = pltpu.make_async_copy(own_block_ref, chain_total_ref, own_sem.at[0])
     rows = gradient_ref.shape[0]
+    chain.load()
     mixing.load(operands)
+    own_load.start()
     greet(
         [("tensor", peer) for peer in other_members("tensor", size)]
         + [("dp", peer) for peer in other_members("dp", data_size)]
@@ -687,7 +714,7 @@
             values * rows_ref[piece, columns].astype(jnp.float32), axis=0, keepdims=True
         )
 
-    mixing.fill(operands, look)
+    mixing.fill(operands, look, lambda: chain.step(0))
     sum_ref[...] = sum_ref[...] / gain_ref[...]
     kept = partial_ref.shape[0] - terms_ref.shape[0]
     partial_ref[kept:, :] = terms_ref[...]
@@ -696,6 +723,7 @@
         "tensor", other_members("tensor", size), partial_ref, inner, inner_send, inner_recv
     )
     mixing.relay()
+    chain.advance(1)
     group_ref[...] = add_terms(inner, inner_copies)
     outer_copies = send_terms(
         "dp", other_members("dp", data_size), group_ref, outer, outer_send, outer_recv
@@ -713,7 +741,12 @@
             + scale * (unit_slope - unit * jnp.mean(unit_slope * unit, axis=-1, keepdims=True))
         ).astype(gradient_ref.dtype)
 
+    for index in range(2, len(steps)):
+        chain.advance(index)
     mixing.over_stages(norm)
+    own_load.wait()
+    chain.add_last(chain_total_ref)
+    chain.drain()
     for copy in inner_copies + outer_copies:
         copy.wait_send()
     mixing.drain()
@@ -1374,15 +1407,12 @@
     data_size = sizes[0]
     chips = data_size // 2
     blocks = pair_grads(pairs, sizes, collective_id)
-    up = down = None
-    for step in range(1, chips - 1):
-        rising, falling = blocks[chips - step], blocks[step]
-        if up is not None:
-            rising, falling = add_rounded(rising, up), add_rounded(falling, down)
-        up = lax.ppermute(
-            rising, "dp", [(device, device + 2) for device in range(2 * step)]
-        )
-        down = lax.ppermute(falling, "dp", [(device, device - 2) for device in range(data_size - 2 * step, data_size)])
+    up = lax.ppermute(blocks[chips - 1], "dp", [(device, device + 2) for device in range(2)])
+    down = lax.ppermute(
+        blocks[1],
+        "dp",
+        [(device, device - 2) for device in range(data_size - 2, data_size)],
+    )
     return blocks, up, down
 
 
@@ -1490,7 +1520,7 @@
     grouping = query_columns // key_columns
     hidden_columns = gate_weight.shape[1]
     qkv_columns = query_columns + 2 * key_columns
-    first_columns = hidden_columns // 2
+    first_columns = hidden_columns * 2 // 3 // 256 * 256 or hidden_columns // 2
     second_columns = hidden_columns - first_columns
     tables = turn_tables(head_size)
 
@@ -1509,9 +1539,7 @@
         ],
         gate_weight, up_weight, down_weight,
     )
-    first_full = lax.all_gather(feed_locals[0], "dp", axis=0, tiled=True)
-    second_full = lax.all_gather(feed_locals[1], "dp", axis=0, tiled=True)
-    feed_full = [first_full, second_full]
+    feed_full = [lax.all_gather(part, "dp", axis=0, tiled=True) for part in feed_locals]
 
     input_float = block_input.astype(jnp.float32)
     first_scale = row_scale(input_float)
@@ -1559,14 +1587,16 @@
         [(feed_turned, slope_second), (cotangent_turned, hidden_second)], 2 * block_width
     )
     second_grad, slope_second = lax.optimization_barrier((second_grad, slope_second))
-    second_total = lax.psum_scatter(second_grad, "dp", scatter_dimension=0, tiled=True)
     chips = sizes[0] // 2
+    later_steps = range(2, chips)
     state_rows, state_turned, state_slope, feed_term, first_total = scatter_call(
         functools.partial(between_backward_kernel, size, chips),
         [(slope_first, feed_full[0], 0), (slope_second, later_full, 0)],
         size,
         [hidden_state, out_cotangent, feed_gain.reshape(1, -1)],
-        [blocks[1], blocks[chips - 1], up, down, blocks[0]],
+        [blocks[chips - step] for step in later_steps]
+        + [blocks[step] for step in later_steps]
+        + [up, down, blocks[0]],
         [
             *gathered_shapes,
             local_float,
@@ -1580,10 +1610,12 @@
             pltpu.SemaphoreType.DMA((1,)),
             *scatter_scratch,
             *gather_scratch,
-            *Chain.scratch(1, *blocks[0].shape),
+            *Chain.scratch(len(later_steps), *blocks[0].shape),
         ],
         2,
     )
+    second_grad, state_turned = lax.optimization_barrier((second_grad, state_turned))
+    second_total = lax.psum_scatter(second_grad, "dp", scatter_dimension=0, tiled=True)
     output_grad = grad_blocks([(state_turned, mixed_rows)], 4 * block_width)
     output_grad, state_rows = lax.optimization_barrier((output_grad, state_rows))
     output_total = lax.psum_scatter(output_grad, "dp", scatter_dimension=0, tiled=True)
@@ -1596,11 +1628,9 @@
         ],
         hidden_state, size, 4,
     )
-    mixing_grad = grad_blocks([(mixer_turned, qkv_slope)], 2 * block_width)
-    mixing_grad, qkv_slope = lax.optimization_barrier((mixing_grad, qkv_slope))
-    mixing_total = lax.psum_scatter(mixing_grad, "dp", scatter_dimension=0, tiled=True)
+    mixing_blocks = pair_grads([(mixer_turned, qkv_slope)], sizes, 6)
     terms_shape = (2 * gain_rows + head_terms.shape[0], head_size)
-    input_gradient, terms = scatter_call(
+    input_gradient, terms, mixing_total = scatter_call(
         functools.partial(last_kernel, sizes),
         [(qkv_slope, mixing_full, 0)],
         size,
@@ -1611,8 +1641,14 @@
             jnp.concatenate([feed_term, head_terms], axis=0),
             mixer_rows,
         ],
-        [],
-        [local_half, jax.ShapeDtypeStruct(terms_shape, jnp.float32)],
+        [mixing_blocks[chips - step] for step in range(1, chips)]
+        + [mixing_blocks[step] for step in range(1, chips)]
+        + [mixing_blocks[0]] * 3,
+        [
+            local_half,
+            jax.ShapeDtypeStruct(terms_shape, jnp.float32),
+            jax.ShapeDtypeStruct(mixing_blocks[0].shape, jnp.bfloat16),
+        ],
         False,
         [
             row_sum,
@@ -1621,7 +1657,9 @@
             pltpu.VMEM((size, *terms_shape), jnp.float32),
             pltpu.VMEM((sizes[0], *terms_shape), jnp.float32),
             *[pltpu.SemaphoreType.DMA((count - 1,)) for count in (size, size, *sizes[:1] * 2)],
+            pltpu.SemaphoreType.DMA((1,)),
             *scatter_scratch,
+            *Chain.scratch(chips - 1, *mixing_blocks[0].shape),
         ],
         3,
     )

time: 632 us -> 540 us (0.85)
  waiting for transfers between devices: 157 us -> 29.1 us
  Pallas kernels: 441 us -> 489 us
  starting transfers between devices: 14 us -> 3.73 us
    reduce_scatter x1, waiting for transfers between devices: 100 us -> 0.02 us  [per_device(): lax.psum_scatter(second_grad, 'dp', scatter_dimension=0, tiled=True)]
    pallas_call x3, Pallas kernels: 204 us -> 249 us  [scatter_call(): pl.pallas_call(functools.partial(body, tuple((first for _, _, first in tr...]
    all_gather x2, waiting for transfers between devices: 50 us -> 25.8 us  [per_device(): lax.all_gather(part, 'dp', axis=0, tiled=True)]
    pallas_call x1 -> x2, Pallas kernels: 22.7 us -> 38.8 us  [pair_grads(): pl.pallas_call(functools.partial(pair_grad_kernel, chips, len(pairs)), ou...]
    pallas_call x3 -> x2, Pallas kernels: 28.7 us -> 16.8 us  [grad_blocks(): pl.pallas_call(functools.partial(grad_kernel, len(pairs)), grid=(depth //...]
    ppermute x4 -> x2, starting transfers between devices: 13.5 us -> 3.31 us  [the longest x1 2.54 us: reduce_over_chips(): lax.ppermute(blocks[chips - 1], 'dp', [(device, device + 2) for device in...]
  transfers between devices with their start and end apart: 10 -> 7, of which waited for: 4 -> 3; matrix products, arithmetic and copies ran while one was open for 0% -> 1% of each run, Pallas kernels for 55% -> 71%
where the time goes in v12:
time: 540 us; the launch traced here: 539 us
  Pallas kernels  489 us (91%)
  waiting for transfers between devices  29.1 us (5%)
  between operations  14 us (3%)
    pallas_call x3, Pallas kernels, scatter_call(): pl.pallas_call(functools.partial(body, tuple((first for _, _, first in tr...  249 us
    pallas_call x1, Pallas kernels, gather_rows(): pl.pallas_call(functools.partial(gather_kernel, size, count), out_shape=o...  76.6 us
    pallas_call x1, Pallas kernels, attention_backward(): pl.pallas_call(functools.partial(attention_backward_kernel, size, groupin...  44.2 us
    pallas_call x2, Pallas kernels, pair_grads(): pl.pallas_call(functools.partial(pair_grad_kernel, chips, len(pairs)), ou...  38.8 us
    pallas_call x2, Pallas kernels, feed_half(): pl.pallas_call(functools.partial(feed_half_kernel, half, tile, block), ou...  33.9 us
    all_gather x2, waiting for transfers between devices, per_device(): lax.all_gather(part, 'dp', axis=0, tiled=True)  25.8 us
    pallas_call x1, Pallas kernels, attention_forward(): pl.pallas_call(functools.partial(attention_forward_kernel, grouping, head...  18.5 us
    pallas_call x2, Pallas kernels, grad_blocks(): pl.pallas_call(functools.partial(grad_kernel, len(pairs)), grid=(depth //...  16.8 us
  transfers between devices with their start and end apart: 7, of which 3 were waited for; matrix products, arithmetic and copies ran while one was open for 1% of the time, Pallas kernels for 71%

profile of v12, /device:TPU:0, one launch (start us, length us, event | category | flops | bytes accessed | tf_op | source)
XLA Modules:
  0.0 538.9 jit_solution(13087085996993541664)
XLA Ops:
  7.2 0.0 all-gather.4.cloned.1.call-start
  7.2 2.2 shard_map.246
  9.4 0.0 all-gather.4.cloned.1.call-update
  9.4 0.0 copy-start
  9.4 0.0 all-gather.6.cloned.1.call-start
  9.5 3.4 shard_map.248
  12.8 0.0 copy-start.1
  12.8 0.0 all-gather.6.cloned.1.call-update
  12.9 0.0 all-gather.8.cloned.1.call-start
  12.9 0.7 all-gather.8.cloned.1.call-update
  13.6 0.0 reduce-scatter.5.cloned.1.call-start
  13.6 0.0 copy-done
  13.7 0.3 fusion
  14.0 0.0 copy-done.1
  14.0 1.3 fusion.2.refs_0_
  15.2 76.6 %gather_rows.1 = (bf16[1024,2048]{1,0:T(8,128)(2,1)}, bf16[2048,1024]{1,0:T(8,128)(2,1)}, bf16[1024,2048]{1,0:T(8,128)(2,1)}, bf16[2048,1024]{1,0:T(8,128)(2,1)}) custom-call(bf16[256,2048]{1,0:T(8,128)(2,1)} %fusion.2.refs_0_, bf16[256,2048]{1,0:T(8,128)(2,1)} %refs_5_.1), custom_call_target="tpu_custom_call" | custom-call | bytes 125829120 | tf_op jit(solution)/shard_map/gather_rows/pallas_call | solution.py:209
  91.9 0.0 all-gather.4.cloned.1.call-done.weight_ref.refs_1_.refs_5_
  91.9 18.5 %attention_forward.1 = (f32[1024,1024]{1,0:T(8,128)}, bf16[1024,512]{1,0:T(8,128)(2,1)}, f32[2,2,1024]{2,1,0:T(2,128)}) custom-call(bf16[1024,2048]{1,0:T(8,128)(2,1)} %get-tuple-element.72.rows_ref.refs_6_, bf16[2048,1536]{1,0:T(8,128)(2,1)} %all-gather.4.cloned.1.call-done.weight_ref.refs_1_.refs_5_, f32[136,128]{1,0:T(8,128)} %constant.11.clone.few_cosines_ref.refs_9_, ...), custom_call_target="tpu_custom_call" | custom-call | flops 5368709120 | bytes 8388608 | tf_op jit(solution)/shard_map/attention_forward/pallas_call | solution.py:900
  110.4 75.0 %shard_map.247 = (bf16[1024,2048]{1,0:T(8,128)(2,1)}, bf16[2048,1024]{1,0:T(8,128)(2,1)}, f32[256,2048]{1,0:T(8,128)}) custom-call(bf16[1024,512]{1,0:T(8,128)(2,1)} %get-tuple-element.73.refs_0_.refs_1_.refs_7_, bf16[2048,1536]{1,0:T(8,128)(2,1)} %all-gather.4.cloned.1.call-done.weight_ref.refs_1_.refs_5_, bf16[256,2048]{1,0:T(8,128)(2,1)} %refs_2_.3, ...), custom_call_target="tpu_custom_call" | custom-call | flops 2147483648 | bytes 150000000 | tf_op jit(solution)/shard_map/pallas_call | solution.py:765
  185.4 9.9 %all-gather.6.cloned.1.call-done.weight_far.refs_1_ = bf16[2048,3072]{1,0:T(8,128)(2,1)} async-done(((bf16[256,3072]{1,0:T(8,128)(2,1)}), bf16[2048,3072]{1,0:T(8,128)(2,1)}) %all-gather.6.cloned.1.call-update) | async-done | bytes 12582928 | tf_op jit(solution)/shard_map/all_gather | solution.py:1542
  195.3 21.9 %feed_half.2 = (bf16[1024,1024]{1,0:T(8,128)(2,1)}, bf16[1024,2048]{1,0:T(8,128)(2,1)}) custom-call(bf16[1024,2048]{1,0:T(8,128)(2,1)} %get-tuple-element.74.rows_far, bf16[1024,2048]{1,0:T(8,128)(2,1)} %get-tuple-element.75.cotangent_far, bf16[2048,3072]{1,0:T(8,128)(2,1)} %all-gather.6.cloned.1.call-done.weight_far.refs_1_), custom_call_target="tpu_custom_call" | custom-call | flops 12884901888 | bytes 20971520 | tf_op jit(solution)/shard_map/feed_half/pallas_call | solution.py:1209
  217.2 27.0 %pair_grads.2 = (bf16[256,3072]{1,0:T(8,128)(2,1)}, bf16[256,3072]{1,0:T(8,128)(2,1)}, bf16[256,3072]{1,0:T(8,128)(2,1)}, bf16[256,3072]{1,0:T(8,128)(2,1)}) custom-call(bf16[2048,1024]{1,0:T(8,128)(2,1)} %get-tuple-element.78.refs_0_, bf16[2048,1024]{1,0:T(8,128)(2,1)} %get-tuple-element.79.refs_1_.refs_2_, ...), custom_call_target="tpu_custom_call" | custom-call | flops 12884901888 | bytes 27262976 | tf_op jit(solution)/shard_map/pair_grads/pallas_call | solution.py:1380
  244.2 0.8 collective-permute-start.1
  245.0 2.5 collective-permute-start
  247.6 15.9 %all-gather.8.cloned.1.call-done.weight_far.refs_3_ = bf16[2048,1536]{1,0:T(8,128)(2,1)} async-done(((bf16[256,1536]{1,0:T(8,128)(2,1)}), bf16[2048,1536]{1,0:T(8,128)(2,1)}) %all-gather.8.cloned.1.call-update) | async-done | bytes 6291472 | tf_op jit(solution)/shard_map/all_gather | solution.py:1542
  263.4 12.0 %feed_half.3 = (bf16[1024,512]{1,0:T(8,128)(2,1)}, bf16[1024,1024]{1,0:T(8,128)(2,1)}) custom-call(bf16[1024,2048]{1,0:T(8,128)(2,1)} %get-tuple-element.74.rows_far, bf16[1024,2048]{1,0:T(8,128)(2,1)} %get-tuple-element.75.cotangent_far, bf16[2048,1536]{1,0:T(8,128)(2,1)} %all-gather.8.cloned.1.call-done.weight_far.refs_3_), custom_call_target="tpu_custom_call" | custom-call | flops 6442450944 | bytes 14680064 | tf_op jit(solution)/shard_map/feed_half/pallas_call | solution.py:1209
  275.4 11.4 %grad_blocks.2 = bf16[2048,1536]{1,0:T(8,128)(2,1)} custom-call(bf16[2048,1024]{1,0:T(8,128)(2,1)} %get-tuple-element.78.refs_0_, bf16[1024,1024]{1,0:T(8,128)(2,1)} %get-tuple-element.89.refs_1_.refs_2_, bf16[2048,1024]{1,0:T(8,128)(2,1)} %get-tuple-element.79.refs_1_.refs_2_, bf16[1024,512]{1,0:T(8,128)(2,1)} %get-tuple-element.88.refs_3_.refs_2_), custom_call_target="tpu_custom_call" | custom-call | flops 6442450944 | bytes 17825792 | tf_op jit(solution)/shard_map/grad_blocks/pallas_call | solution.py:1261
  286.8 0.0 collective-permute-done.1.refs_12_
  286.8 0.0 copy-start.3
  286.8 2.3 collective-permute-done.refs_11_
  289.1 0.0 copy-done.3
  289.1 92.3 %shard_map.249 = (bf16[1024,2048]{1,0:T(8,128)(2,1)}, bf16[2048,1024]{1,0:T(8,128)(2,1)}, f32[256,2048]{1,0:T(8,128)}, f32[16,128]{1,0:T(8,128)}, bf16[256,3072]{1,0:T(8,128)(2,1)}) custom-call(bf16[1024,2048]{1,0:T(8,128)(2,1)} %get-tuple-element.77.refs_2_.refs_0_, bf16[2048,3072]{1,0:T(8,128)(2,1)} %all-gather.6.cloned.1.call-done.weight_far.refs_1_, ...), custom_call_target="tpu_custom_call" | custom-call | flops 12884901888 | bytes 150000000 | tf_op jit(solution)/shard_map/pallas_call | solution.py:765
  381.4 5.4 %grad_blocks.3 = bf16[2048,512]{1,0:T(8,128)(2,1)} custom-call(bf16[2048,1024]{1,0:T(8,128)(2,1)} %get-tuple-element.99.refs_0_, bf16[1024,512]{1,0:T(8,128)(2,1)} %get-tuple-element.73.refs_0_.refs_1_.refs_7_), custom_call_target="tpu_custom_call" | custom-call | flops 2147483648 | bytes 7340032 | tf_op jit(solution)/shard_map/grad_blocks/pallas_call | solution.py:1261
  386.8 0.0 reduce-scatter.5.cloned.1.call-update
  386.8 0.3 reduce-scatter.3.cloned.1.call-start
  387.1 0.3 reduce-scatter.3.cloned.1.call-update
  387.4 0.0 copy-start.2
  387.4 44.2 %attention_backward.1 = (bf16[1024,1024]{1,0:T(8,128)(2,1)}, f32[8,128]{1,0:T(8,128)}, bf16[256,2048]{1,0:T(8,128)(2,1)}) custom-call(bf16[1024,1024]{1,0:T(8,128)(2,1)} %get-tuple-element.80.refs_3_.refs_0_, bf16[2048,3072]{1,0:T(8,128)(2,1)} %all-gather.6.cloned.1.call-done.weight_far.refs_1_, bf16[1024,512]{1,0:T(8,128)(2,1)} %get-tuple-element.88.refs_3_.refs_2_, ...), custom_call_target="tpu_custom_call" | custom-call | flops 4831838208 | bytes 100000000 | tf_op jit(solution)/shard_map/attention_backward/pallas_call | solution.py:1082
  431.6 0.0 copy-done.2
  431.6 1.3 pad_maximum_fusion.refs_5_
  432.9 11.8 %pair_grads.3 = (bf16[256,1024]{1,0:T(8,128)(2,1)}, bf16[256,1024]{1,0:T(8,128)(2,1)}, bf16[256,1024]{1,0:T(8,128)(2,1)}, bf16[256,1024]{1,0:T(8,128)(2,1)}) custom-call(bf16[2048,1024]{1,0:T(8,128)(2,1)} %get-tuple-element.108.refs_0_, bf16[1024,1024]{1,0:T(8,128)(2,1)} %get-tuple-element.104.refs_1_.refs_0_), custom_call_target="tpu_custom_call" | custom-call | flops 4294967296 | bytes 10485760 | tf_op jit(solution)/shard_map/pair_grads/pallas_call | solution.py:1380
  444.7 81.6 %shard_map.250 = (bf16[256,2048]{1,0:T(8,128)(2,1)}, f32[40,128]{1,0:T(8,128)}, bf16[256,1024]{1,0:T(8,128)(2,1)}) custom-call(bf16[1024,1024]{1,0:T(8,128)(2,1)} %get-tuple-element.104.refs_1_.refs_0_, bf16[2048,1536]{1,0:T(8,128)(2,1)} %all-gather.4.cloned.1.call-done.weight_ref.refs_1_.refs_5_, bf16[256,2048]{1,0:T(8,128)(2,1)} %refs_2_.3, ...), custom_call_target="tpu_custom_call" | custom-call | flops 4294967296 | bytes 150000000 | tf_op jit(solution)/shard_map/pallas_call | solution.py:765
  526.3 0.0 reduce-scatter.5.cloned.1.call-done.refs_3_
  526.3 0.0 reduce-scatter.3.cloned.1.call-done.refs_1_
  526.4 6.0 %finish.1 = (bf16[256,2048]{1,0:T(8,128)(2,1)}, bf16[256,2048]{1,0:T(8,128)(2,1)}, f32[16,128]{1,0:T(8,128)}, f32[256,512]{1,0:T(8,128)}, f32[256,256]{1,0:T(8,1...) custom-call(bf16[256,3072]{1,0:T(8,128)(2,1)} %get-tuple-element.95., ...), custom_call_target="tpu_custom_call" | custom-call | bytes 20000000 | tf_op jit(solution)/shard_map/finish/pallas_call | solution.py:1683
  (1 shorter events, 0.0 us)
Async XLA Ops:
  7.2 84.7 %all-gather.4.cloned.1.call-start = ((), (), s32[]{:S(2)}) async-start(), calls=%async_computation.2 | async-start | bytes 7077888 | tf_op jit(solution)/shard_map/all_gather | solution.py:1533
  9.4 4.2 copy-start
  9.4 185.9 %all-gather.6.cloned.1.call-start = ((), (), s32[]{:S(2)}) async-start(), calls=%async_computation.3 | async-start | bytes 14155776 | tf_op jit(solution)/shard_map/all_gather | solution.py:1542
  12.8 1.1 copy-start.1
  12.9 250.6 %all-gather.8.cloned.1.call-start = ((), (), s32[]{:S(2)}) async-start(), calls=%async_computation.4 | async-start | bytes 7077888 | tf_op jit(solution)/shard_map/all_gather | solution.py:1542
  13.6 512.7 %reduce-scatter.5.cloned.1.call-start = ((), (), s32[]{:S(2)}) async-start(), calls=%async_computation.6 | async-start | bytes 2359296 | tf_op jit(solution)/shard_map/reduce_scatter | solution.py:1621
  244.2 42.6 %collective-permute-start.1 = (bf16[256,3072]{1,0:T(8,128)(2,1)}, bf16[256,3072]{1,0:T(8,128)(2,1)S(1)}, u32[]{:S(2)}, u32[]{:S(2)}) collective-permute-start(bf16[256,3072]{1,0:T(8,128)(2,1)} %get-tuple-element.92.refs_8_), channel_id=1, source_target_pairs={{24,16},{28,20},{25,17},{29,21},{26,18},{30,22},{27,19},{31,23}} | collective-permute-start | bytes 4718600 | tf_op jit(solution)/shard_map/ppermute | solution.py:1411
  245.0 44.1 %collective-permute-start = (bf16[256,3072]{1,0:T(8,128)(2,1)}, bf16[256,3072]{1,0:T(8,128)(2,1)}, u32[]{:S(2)}, u32[]{:S(2)}) collective-permute-start(bf16[256,3072]{1,0:T(8,128)(2,1)} %get-tuple-element.93.refs_10_), channel_id=1, source_target_pairs={{0,8},{4,12},{1,9},{5,13},{2,10},{6,14},{3,11},{7,15}} | collective-permute-start | bytes 4718600 | tf_op jit(solution)/shard_map/ppermute | solution.py:1410
  286.8 2.3 copy-start.3
  386.8 139.5 %reduce-scatter.3.cloned.1.call-start = ((), (), s32[]{:S(2)}) async-start(), calls=%async_computation.5 | async-start | bytes 7077888 | tf_op jit(solution)/shard_map/reduce_scatter | solution.py:1618
  387.4 44.2 %copy-start.2 = (f32[16,128]{1,0:T(8,128)S(1)}, f32[16,128]{1,0:T(8,128)}, u32[]{:S(2)}) copy-start(f32[16,128]{1,0:T(8,128)} %get-tuple-element.106) | copy-start | bytes 24580
Sparse Core Ops, SparseCore 0:
  10.2 67.4 all-gather.3
  79.9 115.3 all-gather.5
  197.5 65.8 all-gather.7
  386.9 35.1 reduce-scatter.4
  424.2 100.9 reduce-scatter.2

commit v13 on v9

--- a/solution.py
+++ b/solution.py
@@ -1033,7 +1033,7 @@
     sequences = total_rows // SEQUENCE_LENGTH
     width = (grouping + 2) * head_size
     out_width = grouping * head_size
-    block = min(256, SEQUENCE_LENGTH)
+    block = min(512, SEQUENCE_LENGTH)
     first_block = weight_start // out_width
     single = pl.Buffered(1)
     table = pl.BlockSpec(tables[0].shape, lambda s, h: (0, 0))
@@ -1342,31 +1342,53 @@
         start += width
 
 
-def finish_kernel(
-    heads, own_ref, up_ref, down_ref, second_ref, mixing_ref, output_total_ref, terms_ref, output_rows_ref, input_rows_ref,
-    output_rows_out, input_rows_out, attention_term_out, query_out, key_out, value_out, query_gain_out, key_gain_out,
-    output_out, feed_term_out, gate_out, up_out, down_out,
+def finish_feed_kernel(
+    own_ref, up_ref, down_ref, second_ref, output_rows_ref,
+    output_rows_far, gate_far, up_far, down_far, gate_out, up_out, down_out, sem,
 ):
-    output_rows_out[...] = output_rows_ref[...]
-    input_rows_out[...] = input_rows_ref[...]
-    count = attention_term_out.shape[0]
-    attention_term_out[...] = terms_ref[:count, :]
-    feed_term_out[...] = terms_ref[count : 2 * count, :]
-    query_gain_out[...] = terms_ref[2 * count : 2 * count + 1, :]
-    key_gain_out[...] = terms_ref[2 * count + 1 : 2 * count + 2, :]
-    start = 0
-    for total_refs in ((own_ref, up_ref, down_ref), (second_ref,)):
-        width = total_refs[0].shape[1] // 3
-        part = slice(start, start + width)
-
-        def total(index):
+    copies = [
+        pltpu.make_async_copy(source, target, sem.at[index])
+        for index, (source, target) in enumerate(
+            (
+                (output_rows_ref, output_rows_far),
+                (gate_out, gate_far),
+                (up_out, up_far),
+                (down_out, down_far),
+            )
+        )
+    ]
+    copies[0].start()
+    for index, out in enumerate((gate_out, up_out, down_out)):
+        start = 0
+        for total_refs in ((own_ref, up_ref, down_ref), (second_ref,)):
+            width = total_refs[0].shape[1] // 3
+            part = slice(start, start + width)
             columns = slice(index * width, (index + 1) * width)
-            return sum(ref[:, columns].astype(jnp.float32) for ref in total_refs)
-
-        gate_out[:, part] = total(0)
-        up_out[:, part] = total(1)
-        down_out[part, :] = total(2).T
-        start += width
+            total = sum(ref[:, columns].astype(jnp.float32) for ref in total_refs)
+            if index == 2:
+                out[part, :] = total.T
+            else:
+                out[:, part] = total
+            start += width
+        copies[1 + index].start()
+    for copy in copies:
+        copy.wait()
+
+
+def finish_kernel(heads, *refs):
+    mixing_ref, output_total_ref, terms_ref, input_rows_ref = refs[:4]
+    far, held, sem = refs[4:13], refs[13:21], refs[21]
+    (
+        attention_term_out, query_out, key_out, value_out, query_gain_out, key_gain_out,
+        output_out, feed_term_out,
+    ) = held
+    copies = [
+        pltpu.make_async_copy(source, target, sem.at[index])
+        for index, (source, target) in enumerate(zip((input_rows_ref, *held), far))
+    ]
+    copies[0].start()
+    output_out[...] = output_total_ref[...].astype(jnp.float32).T
+    copies[7].start()
     query_width = query_out.shape[1] // heads
     head_size = key_out.shape[1] // heads
     start = 0
@@ -1376,7 +1398,28 @@
                 jnp.float32
             )
             start += part
-    output_out[...] = output_total_ref[...].astype(jnp.float32).T
+    count = attention_term_out.shape[0]
+    attention_term_out[...] = terms_ref[:count, :]
+    feed_term_out[...] = terms_ref[count : 2 * count, :]
+    query_gain_out[...] = terms_ref[2 * count : 2 * count + 1, :]
+    key_gain_out[...] = terms_ref[2 * count + 1 : 2 * count + 2, :]
+    for index in (1, 2, 3, 4, 5, 6, 8):
+        copies[index].start()
+    for copy in copies:
+        copy.wait()
+
+
+def finish_call(body, rows_shape, float_shapes, *operands):
+    return pl.pallas_call(
+        body,
+        out_shape=[rows_shape, *float_shapes],
+        in_specs=[pl.BlockSpec(memory_space=pltpu.VMEM)] * len(operands),
+        out_specs=[pl.BlockSpec(memory_space=pl.ANY)] * (1 + len(float_shapes)),
+        scratch_shapes=[pltpu.VMEM(shape.shape, shape.dtype) for shape in float_shapes]
+        + [pltpu.SemaphoreType.DMA((1 + len(float_shapes),))],
+        compiler_params=pltpu.CompilerParams(vmem_limit_bytes=VMEM_LIMIT),
+        cost_estimate=pl.CostEstimate(flops=0, bytes_accessed=10_000_000, transcendentals=0),
+    )(*operands)
 
 
 def whole_call(body, shapes, *operands):
@@ -1533,7 +1576,7 @@
         ],
         hidden_state, size, 4,
     )
-    mixing_grad = grad_blocks(plain_order, [(mixer_turned, qkv_slope)], group=2).reshape(model_width, -1)
+    mixing_grad = grad_blocks(plain_order, [(mixer_turned, qkv_slope)], group=4).reshape(model_width, -1)
     mixing_grad, qkv_slope = lax.optimization_barrier((mixing_grad, qkv_slope))
     mixing_total = lax.psum_scatter(mixing_grad, "dp", scatter_dimension=0, tiled=True)
     terms_shape = (2 * gain_rows + head_terms.shape[0], head_size)
@@ -1566,11 +1609,23 @@
     def whole_float(*shape):
         return jax.ShapeDtypeStruct(shape, jnp.float32)
 
-    outs = whole_call(
+    block_output, gate_gradient, up_gradient, down_gradient = finish_call(
+        finish_feed_kernel,
+        local_half,
+        [
+            whole_float(block_width, hidden_columns),
+            whole_float(block_width, hidden_columns),
+            whole_float(hidden_columns, block_width),
+        ],
+        blocks[0], up, down, second_total, block_output,
+    )
+    (
+        input_gradient, attention_term, query_gradient, key_gradient, value_gradient,
+        query_term, key_term, output_gradient, feed_term,
+    ) = finish_call(
         functools.partial(finish_kernel, heads),
+        local_half,
         [
-            local_half,
-            local_half,
             whole_float(gain_rows, head_size),
             whole_float(block_width, query_columns),
             whole_float(block_width, key_columns),
@@ -1579,14 +1634,23 @@
             whole_float(1, head_size),
             whole_float(query_columns, block_width),
             whole_float(gain_rows, head_size),
-            whole_float(block_width, hidden_columns),
-            whole_float(block_width, hidden_columns),
-            whole_float(hidden_columns, block_width),
         ],
-        blocks[0], up, down, second_total, mixing_total, output_total, terms, block_output, input_gradient,
-    )
-    return tuple(
-        out.reshape(-1) if index in (2, 6, 7, 9) else out for index, out in enumerate(outs)
+        mixing_total, output_total, terms, input_gradient,
+    )
+    return (
+        block_output,
+        input_gradient,
+        attention_term.reshape(-1),
+        query_gradient,
+        key_gradient,
+        value_gradient,
+        query_term.reshape(-1),
+        key_term.reshape(-1),
+        output_gradient,
+        feed_term.reshape(-1),
+        gate_gradient,
+        up_gradient,
+        down_gradient,
     )
 
 

time: 605 us -> 603 us (level)
    pallas_call x0 -> x2, Pallas kernels: none -> 8.84 us  [finish_call(): pl.pallas_call(body, out_shape=[rows_shape, *float_shapes], in_specs=[pl....]
    pallas_call x3 -> x2, Pallas kernels: 12.9 us -> 5.6 us  [whole_call(): pl.pallas_call(body, out_shape=shapes, in_specs=[pl.BlockSpec(memory_spac...]
  transfers between devices with their start and end apart: 11 -> 11, of which waited for: 5 -> 5; matrix products, arithmetic and copies ran while one was open for 1% -> 1% of each run, Pallas kernels for 62% -> 63%
where the time goes in v13:
time: 603 us
  Pallas kernels  477 us (79%)
  waiting for transfers between devices  96.6 us (16%)
  between operations  14.4 us (2%)
  starting transfers between devices  10.2 us (2%)
    pallas_call x3, Pallas kernels, scatter_call(): pl.pallas_call(functools.partial(body, tuple((first for _, _, first in tr...  236 us
    pallas_call x1, Pallas kernels, gather_rows(): pl.pallas_call(functools.partial(gather_kernel, size, count), out_shape=o...  76.6 us
    reduce_scatter x1, waiting for transfers between devices, per_device(): lax.psum_scatter(second_grad, 'dp', scatter_dimension=0, tiled=True)  66.8 us
    pallas_call x5, Pallas kernels, grad_blocks(): pl.pallas_call(functools.partial(grad_kernel, len(pairs), other is not No...  53 us
    pallas_call x1, Pallas kernels, attention_backward(): pl.pallas_call(functools.partial(attention_backward_kernel, size, groupin...  44.8 us
    pallas_call x2, Pallas kernels, feed_half(): pl.pallas_call(functools.partial(feed_half_kernel, half, tile, block), ou...  33.9 us
    pallas_call x1, Pallas kernels, attention_forward(): pl.pallas_call(functools.partial(attention_forward_kernel, grouping, head...  18.5 us
  transfers between devices with their start and end apart: 11, of which 5 were waited for; matrix products, arithmetic and copies ran while one was open for 1% of the time, Pallas kernels for 63%

profile of v13, /device:TPU:0, one launch (start us, length us, event | category | flops | bytes accessed | tf_op | source)
XLA Modules:
  0.0 602.8 jit_solution(729449908769903104)
XLA Ops:
  7.2 0.0 all-gather.4.cloned.1.call-start
  7.2 2.2 shard_map.246
  9.4 0.0 all-gather.4.cloned.1.call-update
  9.4 0.0 all-gather.6.cloned.1.call-start
  9.5 3.4 shard_map.248
  12.9 0.0 all-gather.6.cloned.1.call-update
  12.9 0.0 all-gather.8.cloned.1.call-start
  13.0 0.7 all-gather.8.cloned.1.call-update
  13.7 0.0 reduce-scatter.8.cloned.1.call-start
  13.7 0.3 fusion
  14.1 1.3 fusion.2.refs_0_
  15.3 76.6 %gather_rows.1 = (bf16[1024,2048]{1,0:T(8,128)(2,1)}, bf16[2048,1024]{1,0:T(8,128)(2,1)}, bf16[1024,2048]{1,0:T(8,128)(2,1)}, bf16[2048,1024]{1,0:T(8,128)(2,1)}) custom-call(bf16[256,2048]{1,0:T(8,128)(2,1)} %fusion.2.refs_0_, bf16[256,2048]{1,0:T(8,128)(2,1)} %refs_5_.1), custom_call_target="tpu_custom_call" | custom-call | bytes 125829120 | tf_op jit(solution)/shard_map/gather_rows/pallas_call | solution.py:209
  91.9 0.5 broadcast_add_fusion.order_ref
  92.4 18.5 %attention_forward.1 = (f32[1024,1024]{1,0:T(8,128)}, bf16[1024,512]{1,0:T(8,128)(2,1)}, f32[2,2,1024]{2,1,0:T(2,128)}) custom-call(bf16[1024,2048]{1,0:T(8,128)(2,1)} %get-tuple-element.68.rows_ref.refs_6_, bf16[2048,1536]{1,0:T(8,128)(2,1)} %all-gather.4.cloned.1.call-done.weight_ref.refs_1_.refs_5_, f32[136,128]{1,0:T(8,128)} %constant.38.clone.few_cosines_ref.refs_9_, ...), custom_call_target="tpu_custom_call" | custom-call | flops 5368709120 | bytes 8388608 | tf_op jit(solution)/shard_map/attention_forward/pallas_call | solution.py:879
  110.9 75.0 %shard_map.247 = (bf16[1024,2048]{1,0:T(8,128)(2,1)}, bf16[2048,1024]{1,0:T(8,128)(2,1)}, f32[256,2048]{1,0:T(8,128)}) custom-call(bf16[1024,512]{1,0:T(8,128)(2,1)} %get-tuple-element.69.refs_0_.refs_1_.refs_7_, bf16[2048,1536]{1,0:T(8,128)(2,1)} %all-gather.4.cloned.1.call-done.weight_ref.refs_1_.refs_5_, bf16[256,2048]{1,0:T(8,128)(2,1)} %refs_2_.3, ...), custom_call_target="tpu_custom_call" | custom-call | flops 2147483648 | bytes 150000000 | tf_op jit(solution)/shard_map/pallas_call | solution.py:744
  185.9 9.3 %all-gather.6.cloned.1.call-done.weight_far.refs_1_ = bf16[2048,3072]{1,0:T(8,128)(2,1)} async-done(((bf16[256,3072]{1,0:T(8,128)(2,1)}), bf16[2048,3072]{1,0:T(8,128)(2,1)}) %all-gather.6.cloned.1.call-update) | async-done | bytes 12582928 | tf_op jit(solution)/shard_map/all_gather | solution.py:1482
  195.3 22.0 %feed_half.2 = (bf16[1024,1024]{1,0:T(8,128)(2,1)}, bf16[1024,2048]{1,0:T(8,128)(2,1)}) custom-call(bf16[1024,2048]{1,0:T(8,128)(2,1)} %get-tuple-element.71.rows_far, bf16[1024,2048]{1,0:T(8,128)(2,1)} %get-tuple-element.72.cotangent_far, bf16[2048,3072]{1,0:T(8,128)(2,1)} %all-gather.6.cloned.1.call-done.weight_far.refs_1_), custom_call_target="tpu_custom_call" | custom-call | flops 12884901888 | bytes 20971520 | tf_op jit(solution)/shard_map/feed_half/pallas_call | solution.py:1188
  217.2 12.4 %grad_blocks.5 = bf16[4,256,3072]{2,1,0:T(8,128)(2,1)} custom-call(s32[4]{0:T(128)} %broadcast_add_fusion.order_ref, bf16[2048,1024]{1,0:T(8,128)(2,1)} %get-tuple-element.70.refs_0_, bf16[1024,2048]{1,0:T(8,128)(2,1)} %get-tuple-element.74.refs_1_.refs_0_, bf16[2048,1024]{1,0:T(8,128)(2,1)} %get-tuple-element.75.refs_2_, ...), custom_call_target="tpu_custom_call" | custom-call | flops 6442450944 | bytes 16777216 | tf_op jit(solution)/shard_map/grad_blocks/pallas_call | solution.py:1281
  229.6 0.3 collective-permute-start
  229.9 0.5 broadcast_add_fusion.1.order_ref
  230.4 10.3 %collective-permute-done.refs_4_ = bf16[4,256,3072]{2,1,0:T(8,128)(2,1)} collective-permute-done((bf16[4,256,3072]{2,1,0:T(8,128)(2,1)}, bf16[4,256,3072]{2,1,0:T(8,128)(2,1)}, u32[]{:S(2)}, u32[]{:S(2)}) %collective-permute-start) | collective-permute-done | bytes 6291488 | tf_op jit(solution)/shard_map/ppermute | solution.py:1308
  240.8 13.6 %grad_blocks.6 = (bf16[256,3072]{1,0:T(8,128)(2,1)}, bf16[256,3072]{1,0:T(8,128)(2,1)}, bf16[256,3072]{1,0:T(8,128)(2,1)}, bf16[256,3072]{1,0:T(8,128)(2,1)}) custom-call(s32[4]{0:T(128)} %broadcast_add_fusion.1.order_ref, bf16[2048,1024]{1,0:T(8,128)(2,1)} %get-tuple-element.70.refs_0_, bf16[1024,2048]{1,0:T(8,128)(2,1)} %get-tuple-element.74.refs_1_.refs_0_, ...), custom_call_target="tpu_custom_call" | custom-call | flops 6442450944 | bytes 16777216 | tf_op jit(solution)/shard_map/grad_blocks/pallas_call | solution.py:1281
  254.3 0.9 collective-permute-start.2
  255.3 2.5 collective-permute-start.1
  257.8 2.0 all-gather.8.cloned.1.call-done.weight_far.refs_3_
  259.8 11.9 %feed_half.3 = (bf16[1024,512]{1,0:T(8,128)(2,1)}, bf16[1024,1024]{1,0:T(8,128)(2,1)}) custom-call(bf16[1024,2048]{1,0:T(8,128)(2,1)} %get-tuple-element.71.rows_far, bf16[1024,2048]{1,0:T(8,128)(2,1)} %get-tuple-element.72.cotangent_far, bf16[2048,1536]{1,0:T(8,128)(2,1)} %all-gather.8.cloned.1.call-done.weight_far.refs_3_), custom_call_target="tpu_custom_call" | custom-call | flops 6442450944 | bytes 14680064 | tf_op jit(solution)/shard_map/feed_half/pallas_call | solution.py:1188
  271.8 0.5 iota.11.order_ref
  272.3 12.1 %grad_blocks.7 = bf16[8,256,1536]{2,1,0:T(8,128)(2,1)} custom-call(s32[8]{0:T(128)} %iota.11.order_ref, bf16[2048,1024]{1,0:T(8,128)(2,1)} %get-tuple-element.70.refs_0_, bf16[1024,1024]{1,0:T(8,128)(2,1)} %get-tuple-element.86.refs_1_.refs_2_, bf16[2048,1024]{1,0:T(8,128)(2,1)} %get-tuple-element.75.refs_2_, bf16[1024,512]{1,0:T(8,128)(2,1)} %get-tuple-element.85.refs_3_.refs_2_), custom_call_target="tpu_custom_call" | custom-call | flops 6442450944 | bytes 17825792 | tf_op jit(solution)/shard_map/grad_blocks/pallas_call | solution.py:1281
  284.4 6.9 %collective-permute-done.1.refs_9_ = bf16[256,3072]{1,0:T(8,128)(2,1)} collective-permute-done((bf16[256,3072]{1,0:T(8,128)(2,1)}, bf16[256,3072]{1,0:T(8,128)(2,1)}, u32[]{:S(2)}, u32[]{:S(2)}) %collective-permute-start.1) | collective-permute-done | bytes 1572896 | tf_op jit(solution)/shard_map/ppermute | solution.py:1314
  291.3 83.0 %shard_map.249 = (bf16[1024,2048]{1,0:T(8,128)(2,1)}, bf16[2048,1024]{1,0:T(8,128)(2,1)}, f32[256,2048]{1,0:T(8,128)}, f32[16,128]{1,0:T(8,128)}, bf16[256,3072]{1,0:T(8,128)(2,1)}, /*index=5*/bf16[256,3072]{1,0:T(8,128)(2,1)}) custom-call(bf16[1024,2048]{1,0:T(8,128)(2,1)} %get-tuple-element.74.refs_1_.refs_0_, ...), custom_call_target="tpu_custom_call" | custom-call | flops 12884901888 | bytes 150000000 | tf_op jit(solution)/shard_map/pallas_call | solution.py:744
  374.2 0.5 iota.12.order_ref
  374.8 6.0 grad_blocks.8
  380.8 0.0 reduce-scatter.8.cloned.1.call-update
  380.8 0.0 reduce-scatter.6.cloned.1.call-start
  380.9 44.8 %attention_backward.1 = (bf16[1024,1024]{1,0:T(8,128)(2,1)}, f32[8,128]{1,0:T(8,128)}, bf16[256,2048]{1,0:T(8,128)(2,1)}) custom-call(bf16[1024,1024]{1,0:T(8,128)(2,1)} %get-tuple-element.76.refs_3_.refs_0_, bf16[2048,3072]{1,0:T(8,128)(2,1)} %all-gather.6.cloned.1.call-done.weight_far.refs_1_, bf16[1024,512]{1,0:T(8,128)(2,1)} %get-tuple-element.85.refs_3_.refs_2_, ...), custom_call_target="tpu_custom_call" | custom-call | flops 4831838208 | bytes 100000000 | tf_op jit(solution)/shard_map/attention_backward/pallas_call | solution.py:1061
  425.6 0.5 iota.13.order_ref
  426.1 8.9 %grad_blocks.9 = bf16[8,256,1024]{2,1,0:T(8,128)(2,1)} custom-call(s32[8]{0:T(128)} %iota.13.order_ref, bf16[2048,1024]{1,0:T(8,128)(2,1)} %get-tuple-element.101.refs_0_, bf16[1024,1024]{1,0:T(8,128)(2,1)} %get-tuple-element.105.refs_1_.refs_0_), custom_call_target="tpu_custom_call" | custom-call | flops 4294967296 | bytes 10485760 | tf_op jit(solution)/shard_map/grad_blocks/pallas_call | solution.py:1281
  435.1 0.0 reduce-scatter.4.cloned.1.call-start
  435.1 0.5 reduce-scatter.4.cloned.1.call-update
  435.6 4.9 collective-permute-start.3
  440.5 1.3 collective-permute-start.4
  441.9 0.6 pad_maximum_fusion.refs_5_
  442.5 77.7 %shard_map.251 = (bf16[256,2048]{1,0:T(8,128)(2,1)}, f32[40,128]{1,0:T(8,128)}) custom-call(bf16[1024,1024]{1,0:T(8,128)(2,1)} %get-tuple-element.105.refs_1_.refs_0_, bf16[2048,1536]{1,0:T(8,128)(2,1)} %all-gather.4.cloned.1.call-done.weight_ref.refs_1_.refs_5_, bf16[256,2048]{1,0:T(8,128)(2,1)} %refs_2_.3, f32[1,2048]{1,0:T(1,128)} %bitcast.16, ...), custom_call_target="tpu_custom_call" | custom-call | flops 4294967296 | bytes 150000000 | tf_op jit(solution)/shard_map/pallas_call | solution.py:744
  520.2 0.0 reduce-scatter.8.cloned.1.call-done.refs_1_
  520.2 0.0 reduce-scatter.6.cloned.1.call-done.refs_0_
  520.3 3.1 shard_map.252
  523.4 66.8 %reduce-scatter.4.cloned.1.call-done.second_ref = bf16[256,1536]{1,0:T(8,128)(2,1)} async-done(((bf16[2048,1536]{1,0:T(8,128)(2,1)}), bf16[256,1536]{1,0:T(8,128)(2,1)}) %reduce-scatter.4.cloned.1.call-update) | async-done | bytes 786448 | tf_op jit(solution)/shard_map/reduce_scatter | solution.py:1531
  590.1 5.8 shard_map.250
  (18 shorter events, 0.1 us)
Async XLA Ops:
  7.2 85.3 %all-gather.4.cloned.1.call-start = ((), (), s32[]{:S(2)}) async-start(), calls=%async_computation.3 | async-start | bytes 7077888 | tf_op jit(solution)/shard_map/all_gather | solution.py:1473
  9.4 4.3 copy-start
  9.4 185.8 %all-gather.6.cloned.1.call-start = ((), (), s32[]{:S(2)}) async-start(), calls=%async_computation.4 | async-start | bytes 14155776 | tf_op jit(solution)/shard_map/all_gather | solution.py:1482
  12.9 1.1 copy-start.2
  12.9 246.9 %all-gather.8.cloned.1.call-start = ((), (), s32[]{:S(2)}) async-start(), calls=%async_computation.5 | async-start | bytes 7077888 | tf_op jit(solution)/shard_map/all_gather | solution.py:1482
  13.7 506.6 %reduce-scatter.8.cloned.1.call-start = ((), (), s32[]{:S(2)}) async-start(), calls=%async_computation.8 | async-start | bytes 2359296 | tf_op jit(solution)/shard_map/reduce_scatter | solution.py:1569
  229.6 11.1 %collective-permute-start = (bf16[4,256,3072]{2,1,0:T(8,128)(2,1)}, bf16[4,256,3072]{2,1,0:T(8,128)(2,1)}, u32[]{:S(2)}, u32[]{:S(2)}) collective-permute-start(bf16[4,256,3072]{2,1,0:T(8,128)(2,1)} %grad_blocks.5), channel_id=1, source_target_pairs={{0,4},{4,0},{8,12},{12,8},{16,20},{20,16},{24,28},{28,24},{1,5},{5... | collective-permute-start | bytes 18874376 | tf_op jit(solution)/shard_map/ppermute | solution.py:1308
  254.3 30.1 %collective-permute-start.2 = (bf16[256,3072]{1,0:T(8,128)(2,1)}, bf16[256,3072]{1,0:T(8,128)(2,1)S(1)}, u32[]{:S(2)}, u32[]{:S(2)}) collective-permute-start(bf16[256,3072]{1,0:T(8,128)(2,1)} %get-tuple-element.89.refs_11_), channel_id=1, source_target_pairs={{24,16},{28,20},{25,17},{29,21},{26,18},{30,22},{27,19},{31,23}} | collective-permute-start | bytes 4718600 | tf_op jit(solution)/shard_map/ppermute | solution.py:1315
  255.3 36.0 %collective-permute-start.1 = (bf16[256,3072]{1,0:T(8,128)(2,1)}, bf16[256,3072]{1,0:T(8,128)(2,1)}, u32[]{:S(2)}, u32[]{:S(2)}) collective-permute-start(bf16[256,3072]{1,0:T(8,128)(2,1)} %get-tuple-element.90.refs_12_), channel_id=1, source_target_pairs={{0,8},{4,12},{1,9},{5,13},{2,10},{6,14},{3,11},{7,15}} | collective-permute-start | bytes 4718600 | tf_op jit(solution)/shard_map/ppermute | solution.py:1314
  284.4 6.9 %copy-start.5 = (bf16[256,3072]{1,0:T(8,128)(2,1)}, bf16[256,3072]{1,0:T(8,128)(2,1)S(1)}, u32[]{:S(2)}) copy-start(bf16[256,3072]{1,0:T(8,128)(2,1)S(1)} %collective-permute-done.2.refs_10_) | copy-start | bytes 4718596
  380.8 139.5 %reduce-scatter.6.cloned.1.call-start = ((), (), s32[]{:S(2)}) async-start(), calls=%async_computation.7 | async-start | bytes 4718592 | tf_op jit(solution)/shard_map/reduce_scatter | solution.py:1581
  435.0 6.8 %copy-start.3 = (f32[16,128]{1,0:T(8,128)S(1)}, f32[16,128]{1,0:T(8,128)}, u32[]{:S(2)}) copy-start(f32[16,128]{1,0:T(8,128)} %get-tuple-element.107) | copy-start | bytes 24580
  435.1 6.8 %copy-start.4 = (f32[8,128]{1,0:T(8,128)S(1)}, f32[8,128]{1,0:T(8,128)}, u32[]{:S(2)}) copy-start(f32[8,128]{1,0:T(8,128)} %get-tuple-element.108) | copy-start | bytes 12292
  435.1 155.1 %reduce-scatter.4.cloned.1.call-start = ((), (), s32[]{:S(2)}) async-start(), calls=%async_computation.6 | async-start | bytes 7077888 | tf_op jit(solution)/shard_map/reduce_scatter | solution.py:1531
  435.6 87.7 %collective-permute-start.3 = (bf16[256,3072]{1,0:T(8,128)(2,1)}, bf16[256,3072]{1,0:T(8,128)(2,1)S(1)}, u32[]{:S(2)}, u32[]{:S(2)}) collective-permute-start(bf16[256,3072]{1,0:T(8,128)(2,1)} %get-tuple-element.91), channel_id=1, source_target_pairs={{0,8},{4,12},{8,16},{12,20},{16,24},{20,28},{1,9},{5,13},{9,17},{1... | collective-permute-start | bytes 4718600 | tf_op jit(solution)/shard_map/ppermute | solution.py:1561
  440.5 82.8 %collective-permute-start.4 = (bf16[256,3072]{1,0:T(8,128)(2,1)}, bf16[256,3072]{1,0:T(8,128)(2,1)}, u32[]{:S(2)}, u32[]{:S(2)}) collective-permute-start(bf16[256,3072]{1,0:T(8,128)(2,1)} %get-tuple-element.92), channel_id=1, source_target_pairs={{8,0},{12,4},{16,8},{20,12},{24,16},{28,20},{9,1},{13,5},{17,9},{2... | collective-permute-start | bytes 4718600 | tf_op jit(solution)/shard_map/ppermute | solution.py:1564
  523.4 66.8 %copy-start.1 = (bf16[256,3072]{1,0:T(8,128)(2,1)}, bf16[256,3072]{1,0:T(8,128)(2,1)S(1)}, u32[]{:S(2)}) copy-start(bf16[256,3072]{1,0:T(8,128)(2,1)S(1)} %collective-permute-done.3.up_ref) | copy-start | bytes 4718596
Sparse Core Ops, SparseCore 0:
  10.2 67.4 all-gather.3
  79.9 115.3 all-gather.5
  196.9 62.8 all-gather.7
  380.9 36.7 reduce-scatter.7
  435.2 85.0 reduce-scatter.5
  522.4 67.7 reduce-scatter.3

commit v14 on v13

--- a/solution.py
+++ b/solution.py
@@ -359,7 +359,7 @@
             for operand in operands:
                 operand.left_copy(slot, self.owner(slot)).start()
 
-    def fill(self, operands, look=None, between=None):
+    def fill(self, operands, look=None):
         rows = self.rows
 
         def step(slot, carry):
@@ -381,8 +381,6 @@
             block_product(operands, owner * rows, rows, slot == 0, write, after)
             for at, index in self.starts:
                 pl.when(slot == at)(self.copies[index].start)
-            if between is not None:
-                pl.when(slot == 0)(between)
             return carry
 
         lax.fori_loop(0, self.size, step, 0)
@@ -634,7 +632,8 @@
     for load in last_loads:
         load.start()
     greet(neighbours(size) + chain.neighbours)
-    scatter.fill(operands, between=lambda: chain.step(0))
+    chain.step(0)
+    scatter.fill(operands)
     scatter.relay()
     sum_ref[...] = jnp.zeros_like(sum_ref)
 
@@ -1558,14 +1557,16 @@
         ],
         2,
     )
+    output_grad = grad_blocks(plain_order, [(state_turned, mixed_rows)], group=4).reshape(model_width, -1)
+    output_grad, state_rows, rising, falling = lax.optimization_barrier(
+        (output_grad, state_rows, rising, falling)
+    )
     up = lax.ppermute(
         rising, "dp", [(device, device + 2) for device in range(sizes[0] - 2)]
     )
     down = lax.ppermute(
         falling, "dp", [(device, device - 2) for device in range(2, sizes[0])]
     )
-    output_grad = grad_blocks(plain_order, [(state_turned, mixed_rows)], group=4).reshape(model_width, -1)
-    output_grad, state_rows = lax.optimization_barrier((output_grad, state_rows))
     output_total = lax.psum_scatter(output_grad, "dp", scatter_dimension=0, tiled=True)
     qkv_slope, head_terms, block_output = attention_backward(
         state_rows, mixing_full, qkv_columns, raw, mixed_rows, totals, tables,

time: 603 us -> 609 us (level)
  no operation moved by 1% of the time
where the time goes in v14:
time: 609 us; the launch traced here: 608 us
  Pallas kernels  482 us (79%)
  waiting for transfers between devices  96.6 us (16%)
  between operations  14.4 us (2%)
  starting transfers between devices  10.2 us (2%)
    pallas_call x3, Pallas kernels, scatter_call(): pl.pallas_call(functools.partial(body, tuple((first for _, _, first in tr...  241 us
    pallas_call x1, Pallas kernels, gather_rows(): pl.pallas_call(functools.partial(gather_kernel, size, count), out_shape=o...  76.6 us
    reduce_scatter x1, waiting for transfers between devices, per_device(): lax.psum_scatter(second_grad, 'dp', scatter_dimension=0, tiled=True)  66.8 us
    pallas_call x5, Pallas kernels, grad_blocks(): pl.pallas_call(functools.partial(grad_kernel, len(pairs), other is not No...  53 us
    pallas_call x1, Pallas kernels, attention_backward(): pl.pallas_call(functools.partial(attention_backward_kernel, size, groupin...  44.9 us
    pallas_call x2, Pallas kernels, feed_half(): pl.pallas_call(functools.partial(feed_half_kernel, half, tile, block), ou...  33.9 us
    pallas_call x1, Pallas kernels, attention_forward(): pl.pallas_call(functools.partial(attention_forward_kernel, grouping, head...  18.5 us
  transfers between devices with their start and end apart: 11, of which 5 were waited for; matrix products, arithmetic and copies ran while one was open for 1% of the time, Pallas kernels for 63%

profile of v14, /device:TPU:0, one launch (start us, length us, event | category | flops | bytes accessed | tf_op | source)
XLA Modules:
  0.0 608.2 jit_solution(7709303678645874573)
XLA Ops:
  7.2 0.0 all-gather.4.cloned.1.call-start
  7.2 2.2 shard_map.246
  9.4 0.0 all-gather.4.cloned.1.call-update
  9.4 0.0 all-gather.6.cloned.1.call-start
  9.5 3.4 shard_map.248
  12.9 0.0 all-gather.6.cloned.1.call-update
  12.9 0.0 all-gather.8.cloned.1.call-start
  13.0 0.7 all-gather.8.cloned.1.call-update
  13.7 0.0 reduce-scatter.8.cloned.1.call-start
  13.7 0.3 fusion
  14.1 1.3 fusion.2.refs_0_
  15.3 76.6 %gather_rows.1 = (bf16[1024,2048]{1,0:T(8,128)(2,1)}, bf16[2048,1024]{1,0:T(8,128)(2,1)}, bf16[1024,2048]{1,0:T(8,128)(2,1)}, bf16[2048,1024]{1,0:T(8,128)(2,1)}) custom-call(bf16[256,2048]{1,0:T(8,128)(2,1)} %fusion.2.refs_0_, bf16[256,2048]{1,0:T(8,128)(2,1)} %refs_5_.1), custom_call_target="tpu_custom_call" | custom-call | bytes 125829120 | tf_op jit(solution)/shard_map/gather_rows/pallas_call | solution.py:209
  91.9 0.5 broadcast_add_fusion.order_ref
  92.4 18.5 %attention_forward.1 = (f32[1024,1024]{1,0:T(8,128)}, bf16[1024,512]{1,0:T(8,128)(2,1)}, f32[2,2,1024]{2,1,0:T(2,128)}) custom-call(bf16[1024,2048]{1,0:T(8,128)(2,1)} %get-tuple-element.70.rows_ref.refs_6_, bf16[2048,1536]{1,0:T(8,128)(2,1)} %all-gather.4.cloned.1.call-done.weight_ref.refs_1_.refs_5_, f32[136,128]{1,0:T(8,128)} %constant.38.clone.few_cosines_ref.refs_9_, ...), custom_call_target="tpu_custom_call" | custom-call | flops 5368709120 | bytes 8388608 | tf_op jit(solution)/shard_map/attention_forward/pallas_call | solution.py:878
  110.9 75.0 %shard_map.247 = (bf16[1024,2048]{1,0:T(8,128)(2,1)}, bf16[2048,1024]{1,0:T(8,128)(2,1)}, f32[256,2048]{1,0:T(8,128)}) custom-call(bf16[1024,512]{1,0:T(8,128)(2,1)} %get-tuple-element.71.refs_0_.refs_1_.refs_7_, bf16[2048,1536]{1,0:T(8,128)(2,1)} %all-gather.4.cloned.1.call-done.weight_ref.refs_1_.refs_5_, bf16[256,2048]{1,0:T(8,128)(2,1)} %refs_2_.3, ...), custom_call_target="tpu_custom_call" | custom-call | flops 2147483648 | bytes 150000000 | tf_op jit(solution)/shard_map/pallas_call | solution.py:743
  185.9 9.3 %all-gather.6.cloned.1.call-done.weight_far.refs_1_ = bf16[2048,3072]{1,0:T(8,128)(2,1)} async-done(((bf16[256,3072]{1,0:T(8,128)(2,1)}), bf16[2048,3072]{1,0:T(8,128)(2,1)}) %all-gather.6.cloned.1.call-update) | async-done | bytes 12582928 | tf_op jit(solution)/shard_map/all_gather | solution.py:1481
  195.3 22.0 %feed_half.2 = (bf16[1024,1024]{1,0:T(8,128)(2,1)}, bf16[1024,2048]{1,0:T(8,128)(2,1)}) custom-call(bf16[1024,2048]{1,0:T(8,128)(2,1)} %get-tuple-element.73.rows_far, bf16[1024,2048]{1,0:T(8,128)(2,1)} %get-tuple-element.74.cotangent_far, bf16[2048,3072]{1,0:T(8,128)(2,1)} %all-gather.6.cloned.1.call-done.weight_far.refs_1_), custom_call_target="tpu_custom_call" | custom-call | flops 12884901888 | bytes 20971520 | tf_op jit(solution)/shard_map/feed_half/pallas_call | solution.py:1187
  217.2 12.4 %grad_blocks.5 = bf16[4,256,3072]{2,1,0:T(8,128)(2,1)} custom-call(s32[4]{0:T(128)} %broadcast_add_fusion.order_ref, bf16[2048,1024]{1,0:T(8,128)(2,1)} %get-tuple-element.72.refs_0_, bf16[1024,2048]{1,0:T(8,128)(2,1)} %get-tuple-element.76.refs_1_.refs_0_, bf16[2048,1024]{1,0:T(8,128)(2,1)} %get-tuple-element.77.refs_2_, ...), custom_call_target="tpu_custom_call" | custom-call | flops 6442450944 | bytes 16777216 | tf_op jit(solution)/shard_map/grad_blocks/pallas_call | solution.py:1280
  229.6 0.3 collective-permute-start
  229.9 0.5 broadcast_add_fusion.1.order_ref
  230.4 10.3 %collective-permute-done.refs_4_ = bf16[4,256,3072]{2,1,0:T(8,128)(2,1)} collective-permute-done((bf16[4,256,3072]{2,1,0:T(8,128)(2,1)}, bf16[4,256,3072]{2,1,0:T(8,128)(2,1)}, u32[]{:S(2)}, u32[]{:S(2)}) %collective-permute-start) | collective-permute-done | bytes 6291488 | tf_op jit(solution)/shard_map/ppermute | solution.py:1307
  240.8 13.6 %grad_blocks.6 = (bf16[256,3072]{1,0:T(8,128)(2,1)}, bf16[256,3072]{1,0:T(8,128)(2,1)}, bf16[256,3072]{1,0:T(8,128)(2,1)}, bf16[256,3072]{1,0:T(8,128)(2,1)}) custom-call(s32[4]{0:T(128)} %broadcast_add_fusion.1.order_ref, bf16[2048,1024]{1,0:T(8,128)(2,1)} %get-tuple-element.72.refs_0_, bf16[1024,2048]{1,0:T(8,128)(2,1)} %get-tuple-element.76.refs_1_.refs_0_, ...), custom_call_target="tpu_custom_call" | custom-call | flops 6442450944 | bytes 16777216 | tf_op jit(solution)/shard_map/grad_blocks/pallas_call | solution.py:1280
  254.3 0.9 collective-permute-start.2
  255.3 2.5 collective-permute-start.1
  257.8 2.0 all-gather.8.cloned.1.call-done.weight_far.refs_3_
  259.8 11.9 %feed_half.3 = (bf16[1024,512]{1,0:T(8,128)(2,1)}, bf16[1024,1024]{1,0:T(8,128)(2,1)}) custom-call(bf16[1024,2048]{1,0:T(8,128)(2,1)} %get-tuple-element.73.rows_far, bf16[1024,2048]{1,0:T(8,128)(2,1)} %get-tuple-element.74.cotangent_far, bf16[2048,1536]{1,0:T(8,128)(2,1)} %all-gather.8.cloned.1.call-done.weight_far.refs_3_), custom_call_target="tpu_custom_call" | custom-call | flops 6442450944 | bytes 14680064 | tf_op jit(solution)/shard_map/feed_half/pallas_call | solution.py:1187
  271.8 0.5 iota.12.order_ref
  272.3 12.1 %grad_blocks.7 = bf16[8,256,1536]{2,1,0:T(8,128)(2,1)} custom-call(s32[8]{0:T(128)} %iota.12.order_ref, bf16[2048,1024]{1,0:T(8,128)(2,1)} %get-tuple-element.72.refs_0_, bf16[1024,1024]{1,0:T(8,128)(2,1)} %get-tuple-element.88.refs_1_.refs_2_, bf16[2048,1024]{1,0:T(8,128)(2,1)} %get-tuple-element.77.refs_2_, bf16[1024,512]{1,0:T(8,128)(2,1)} %get-tuple-element.87.refs_3_.refs_2_), custom_call_target="tpu_custom_call" | custom-call | flops 6442450944 | bytes 17825792 | tf_op jit(solution)/shard_map/grad_blocks/pallas_call | solution.py:1280
  284.4 6.9 %collective-permute-done.1.refs_9_ = bf16[256,3072]{1,0:T(8,128)(2,1)} collective-permute-done((bf16[256,3072]{1,0:T(8,128)(2,1)}, bf16[256,3072]{1,0:T(8,128)(2,1)}, u32[]{:S(2)}, u32[]{:S(2)}) %collective-permute-start.1) | collective-permute-done | bytes 1572896 | tf_op jit(solution)/shard_map/ppermute | solution.py:1313
  291.3 87.7 %shard_map.249 = (bf16[1024,2048]{1,0:T(8,128)(2,1)}, bf16[2048,1024]{1,0:T(8,128)(2,1)}, f32[256,2048]{1,0:T(8,128)}, f32[16,128]{1,0:T(8,128)}, bf16[256,3072]{1,0:T(8,128)(2,1)}, /*index=5*/bf16[256,3072]{1,0:T(8,128)(2,1)}) custom-call(bf16[1024,2048]{1,0:T(8,128)(2,1)} %get-tuple-element.76.refs_1_.refs_0_, ...), custom_call_target="tpu_custom_call" | custom-call | flops 12884901888 | bytes 150000000 | tf_op jit(solution)/shard_map/pallas_call | solution.py:743
  379.0 0.5 iota.11.order_ref
  379.5 6.0 grad_blocks.8
  385.5 0.0 reduce-scatter.8.cloned.1.call-update
  385.5 0.0 reduce-scatter.6.cloned.1.call-start
  385.6 44.9 %attention_backward.1 = (bf16[1024,1024]{1,0:T(8,128)(2,1)}, f32[8,128]{1,0:T(8,128)}, bf16[256,2048]{1,0:T(8,128)(2,1)}) custom-call(bf16[1024,1024]{1,0:T(8,128)(2,1)} %get-tuple-element.78.refs_3_.refs_0_, bf16[2048,3072]{1,0:T(8,128)(2,1)} %all-gather.6.cloned.1.call-done.weight_far.refs_1_, bf16[1024,512]{1,0:T(8,128)(2,1)} %get-tuple-element.87.refs_3_.refs_2_, ...), custom_call_target="tpu_custom_call" | custom-call | flops 4831838208 | bytes 100000000 | tf_op jit(solution)/shard_map/attention_backward/pallas_call | solution.py:1060
  430.5 0.5 iota.13.order_ref
  431.0 8.9 %grad_blocks.9 = bf16[8,256,1024]{2,1,0:T(8,128)(2,1)} custom-call(s32[8]{0:T(128)} %iota.13.order_ref, bf16[2048,1024]{1,0:T(8,128)(2,1)} %get-tuple-element.105.refs_0_, bf16[1024,1024]{1,0:T(8,128)(2,1)} %get-tuple-element.109.refs_1_.refs_0_), custom_call_target="tpu_custom_call" | custom-call | flops 4294967296 | bytes 10485760 | tf_op jit(solution)/shard_map/grad_blocks/pallas_call | solution.py:1280
  439.9 0.0 reduce-scatter.4.cloned.1.call-start
  440.0 0.5 reduce-scatter.4.cloned.1.call-update
  440.5 4.9 collective-permute-start.3
  445.4 1.3 collective-permute-start.4
  446.7 0.6 pad_maximum_fusion.refs_5_
  447.3 78.3 %shard_map.251 = (bf16[256,2048]{1,0:T(8,128)(2,1)}, f32[40,128]{1,0:T(8,128)}) custom-call(bf16[1024,1024]{1,0:T(8,128)(2,1)} %get-tuple-element.109.refs_1_.refs_0_, bf16[2048,1536]{1,0:T(8,128)(2,1)} %all-gather.4.cloned.1.call-done.weight_ref.refs_1_.refs_5_, bf16[256,2048]{1,0:T(8,128)(2,1)} %refs_2_.3, f32[1,2048]{1,0:T(1,128)} %bitcast.16, ...), custom_call_target="tpu_custom_call" | custom-call | flops 4294967296 | bytes 150000000 | tf_op jit(solution)/shard_map/pallas_call | solution.py:743
  525.6 0.0 reduce-scatter.8.cloned.1.call-done.refs_1_
  525.6 0.0 reduce-scatter.6.cloned.1.call-done.refs_0_
  525.7 3.1 shard_map.252
  528.8 66.8 %reduce-scatter.4.cloned.1.call-done.second_ref = bf16[256,1536]{1,0:T(8,128)(2,1)} async-done(((bf16[2048,1536]{1,0:T(8,128)(2,1)}), bf16[256,1536]{1,0:T(8,128)(2,1)}) %reduce-scatter.4.cloned.1.call-update) | async-done | bytes 786448 | tf_op jit(solution)/shard_map/reduce_scatter | solution.py:1530
  595.5 5.8 shard_map.250
  (18 shorter events, 0.1 us)
Async XLA Ops:
  7.2 85.3 %all-gather.4.cloned.1.call-start = ((), (), s32[]{:S(2)}) async-start(), calls=%async_computation.3 | async-start | bytes 7077888 | tf_op jit(solution)/shard_map/all_gather | solution.py:1472
  9.4 4.3 copy-start
  9.4 185.8 %all-gather.6.cloned.1.call-start = ((), (), s32[]{:S(2)}) async-start(), calls=%async_computation.4 | async-start | bytes 14155776 | tf_op jit(solution)/shard_map/all_gather | solution.py:1481
  12.9 1.1 copy-start.2
  12.9 246.9 %all-gather.8.cloned.1.call-start = ((), (), s32[]{:S(2)}) async-start(), calls=%async_computation.5 | async-start | bytes 7077888 | tf_op jit(solution)/shard_map/all_gather | solution.py:1481
  13.7 512.0 %reduce-scatter.8.cloned.1.call-start = ((), (), s32[]{:S(2)}) async-start(), calls=%async_computation.8 | async-start | bytes 2359296 | tf_op jit(solution)/shard_map/reduce_scatter | solution.py:1570
  229.6 11.1 %collective-permute-start = (bf16[4,256,3072]{2,1,0:T(8,128)(2,1)}, bf16[4,256,3072]{2,1,0:T(8,128)(2,1)}, u32[]{:S(2)}, u32[]{:S(2)}) collective-permute-start(bf16[4,256,3072]{2,1,0:T(8,128)(2,1)} %grad_blocks.5), channel_id=1, source_target_pairs={{0,4},{4,0},{8,12},{12,8},{16,20},{20,16},{24,28},{28,24},{1,5},{5... | collective-permute-start | bytes 18874376 | tf_op jit(solution)/shard_map/ppermute | solution.py:1307
  254.3 30.1 %collective-permute-start.2 = (bf16[256,3072]{1,0:T(8,128)(2,1)}, bf16[256,3072]{1,0:T(8,128)(2,1)S(1)}, u32[]{:S(2)}, u32[]{:S(2)}) collective-permute-start(bf16[256,3072]{1,0:T(8,128)(2,1)} %get-tuple-element.91.refs_11_), channel_id=1, source_target_pairs={{24,16},{28,20},{25,17},{29,21},{26,18},{30,22},{27,19},{31,23}} | collective-permute-start | bytes 4718600 | tf_op jit(solution)/shard_map/ppermute | solution.py:1314
  255.3 36.0 %collective-permute-start.1 = (bf16[256,3072]{1,0:T(8,128)(2,1)}, bf16[256,3072]{1,0:T(8,128)(2,1)}, u32[]{:S(2)}, u32[]{:S(2)}) collective-permute-start(bf16[256,3072]{1,0:T(8,128)(2,1)} %get-tuple-element.92.refs_12_), channel_id=1, source_target_pairs={{0,8},{4,12},{1,9},{5,13},{2,10},{6,14},{3,11},{7,15}} | collective-permute-start | bytes 4718600 | tf_op jit(solution)/shard_map/ppermute | solution.py:1313
  284.4 6.9 %copy-start.5 = (bf16[256,3072]{1,0:T(8,128)(2,1)}, bf16[256,3072]{1,0:T(8,128)(2,1)S(1)}, u32[]{:S(2)}) copy-start(bf16[256,3072]{1,0:T(8,128)(2,1)S(1)} %collective-permute-done.2.refs_10_) | copy-start | bytes 4718596
  385.5 140.2 %reduce-scatter.6.cloned.1.call-start = ((), (), s32[]{:S(2)}) async-start(), calls=%async_computation.7 | async-start | bytes 4718592 | tf_op jit(solution)/shard_map/reduce_scatter | solution.py:1582
  439.9 6.8 %copy-start.3 = (f32[16,128]{1,0:T(8,128)S(1)}, f32[16,128]{1,0:T(8,128)}, u32[]{:S(2)}) copy-start(f32[16,128]{1,0:T(8,128)} %get-tuple-element.111) | copy-start | bytes 24580
  439.9 6.8 %copy-start.4 = (f32[8,128]{1,0:T(8,128)S(1)}, f32[8,128]{1,0:T(8,128)}, u32[]{:S(2)}) copy-start(f32[8,128]{1,0:T(8,128)} %get-tuple-element.112) | copy-start | bytes 12292
  439.9 155.6 %reduce-scatter.4.cloned.1.call-start = ((), (), s32[]{:S(2)}) async-start(), calls=%async_computation.6 | async-start | bytes 7077888 | tf_op jit(solution)/shard_map/reduce_scatter | solution.py:1530
  440.5 88.2 %collective-permute-start.3 = (bf16[256,3072]{1,0:T(8,128)(2,1)}, bf16[256,3072]{1,0:T(8,128)(2,1)S(1)}, u32[]{:S(2)}, u32[]{:S(2)}) collective-permute-start(bf16[256,3072]{1,0:T(8,128)(2,1)} %get-tuple-element.97), channel_id=1, source_target_pairs={{0,8},{4,12},{8,16},{12,20},{16,24},{20,28},{1,9},{5,13},{9,17},{1... | collective-permute-start | bytes 4718600 | tf_op jit(solution)/shard_map/ppermute | solution.py:1564
  445.4 83.3 %collective-permute-start.4 = (bf16[256,3072]{1,0:T(8,128)(2,1)}, bf16[256,3072]{1,0:T(8,128)(2,1)}, u32[]{:S(2)}, u32[]{:S(2)}) collective-permute-start(bf16[256,3072]{1,0:T(8,128)(2,1)} %get-tuple-element.98), channel_id=1, source_target_pairs={{8,0},{12,4},{16,8},{20,12},{24,16},{28,20},{9,1},{13,5},{17,9},{2... | collective-permute-start | bytes 4718600 | tf_op jit(solution)/shard_map/ppermute | solution.py:1567
  528.7 66.8 %copy-start.1 = (bf16[256,3072]{1,0:T(8,128)(2,1)}, bf16[256,3072]{1,0:T(8,128)(2,1)S(1)}, u32[]{:S(2)}) copy-start(bf16[256,3072]{1,0:T(8,128)(2,1)S(1)} %collective-permute-done.3.up_ref) | copy-start | bytes 4718596
Sparse Core Ops, SparseCore 0:
  10.2 67.4 all-gather.3
  79.9 115.3 all-gather.5
  196.9 62.8 all-gather.7
  385.6 36.7 reduce-scatter.7
  440.0 85.5 reduce-scatter.5
  527.8 67.7 reduce-scatter.3

commit v15 on v14

--- a/solution.py
+++ b/solution.py
@@ -1557,16 +1557,14 @@
         ],
         2,
     )
-    output_grad = grad_blocks(plain_order, [(state_turned, mixed_rows)], group=4).reshape(model_width, -1)
-    output_grad, state_rows, rising, falling = lax.optimization_barrier(
-        (output_grad, state_rows, rising, falling)
-    )
     up = lax.ppermute(
         rising, "dp", [(device, device + 2) for device in range(sizes[0] - 2)]
     )
     down = lax.ppermute(
         falling, "dp", [(device, device - 2) for device in range(2, sizes[0])]
     )
+    output_grad = grad_blocks(plain_order, [(state_turned, mixed_rows)], group=4).reshape(model_width, -1)
+    output_grad, state_rows = lax.optimization_barrier((output_grad, state_rows))
     output_total = lax.psum_scatter(output_grad, "dp", scatter_dimension=0, tiled=True)
     qkv_slope, head_terms, block_output = attention_backward(
         state_rows, mixing_full, qkv_columns, raw, mixed_rows, totals, tables,
@@ -1580,6 +1578,21 @@
     mixing_grad = grad_blocks(plain_order, [(mixer_turned, qkv_slope)], group=4).reshape(model_width, -1)
     mixing_grad, qkv_slope = lax.optimization_barrier((mixing_grad, qkv_slope))
     mixing_total = lax.psum_scatter(mixing_grad, "dp", scatter_dimension=0, tiled=True)
+
+    def whole_float(*shape):
+        return jax.ShapeDtypeStruct(shape, jnp.float32)
+
+    block_output, gate_gradient, up_gradient, down_gradient = finish_call(
+        finish_feed_kernel,
+        local_half,
+        [
+            whole_float(block_width, hidden_columns),
+            whole_float(block_width, hidden_columns),
+            whole_float(hidden_columns, block_width),
+        ],
+        blocks[0], up, down, second_total, block_output,
+    )
+    qkv_slope, gate_gradient = lax.optimization_barrier((qkv_slope, gate_gradient))
     terms_shape = (2 * gain_rows + head_terms.shape[0], head_size)
     input_gradient, terms = scatter_call(
         functools.partial(last_kernel, sizes),
@@ -1606,20 +1619,6 @@
         ],
         3,
     )
-
-    def whole_float(*shape):
-        return jax.ShapeDtypeStruct(shape, jnp.float32)
-
-    block_output, gate_gradient, up_gradient, down_gradient = finish_call(
-        finish_feed_kernel,
-        local_half,
-        [
-            whole_float(block_width, hidden_columns),
-            whole_float(block_width, hidden_columns),
-            whole_float(hidden_columns, block_width),
-        ],
-        blocks[0], up, down, second_total, block_output,
-    )
     (
         input_gradient, attention_term, query_gradient, key_gradient, value_gradient,
         query_term, key_term, output_gradient, feed_term,

time: 609 us -> 643 us (1.056)
  waiting for transfers between devices: 96.6 us -> 166 us
  Pallas kernels: 482 us -> 445 us
    reduce_scatter x1, waiting for transfers between devices: 66.8 us -> 0.01 us  [per_device(): lax.psum_scatter(second_grad, 'dp', scatter_dimension=0, tiled=True)]
    ppermute x1, waiting for transfers between devices: 0.01 us -> 64.5 us  [per_device(): lax.ppermute(rising, 'dp', [(device, device + 2) for device in range(size...]
    ppermute x1, waiting for transfers between devices: 6.87 us -> 67.8 us  [reduce_over_chips(): lax.ppermute(blocks[chips - 1], 'dp', [(device, device + 2) for device in...]
    pallas_call x3, Pallas kernels: 241 us -> 204 us  [scatter_call(): pl.pallas_call(functools.partial(body, tuple((first for _, _, first in tr...]
    ppermute x1, waiting for transfers between devices: 0.01 us -> 7.96 us  [per_device(): lax.ppermute(falling, 'dp', [(device, device - 2) for device in range(2,...]
  transfers between devices with their start and end apart: 11 -> 11, of which waited for: 5 -> 6; matrix products, arithmetic and copies ran while one was open for 1% -> 1% of each run, Pallas kernels for 63% -> 65%
where the time goes in v15:
time: 643 us; the launch traced here: 642 us
  Pallas kernels  445 us (69%)
  waiting for transfers between devices  166 us (26%)
  between operations  14.4 us (2%)
  starting transfers between devices  9.23 us (1%)
    pallas_call x3, Pallas kernels, scatter_call(): pl.pallas_call(functools.partial(body, tuple((first for _, _, first in tr...  204 us
    pallas_call x1, Pallas kernels, gather_rows(): pl.pallas_call(functools.partial(gather_kernel, size, count), out_shape=o...  76.6 us
    ppermute x1, waiting for transfers between devices, reduce_over_chips(): lax.ppermute(blocks[chips - 1], 'dp', [(device, device + 2) for device in...  67.8 us
    ppermute x1, waiting for transfers between devices, per_device(): lax.ppermute(rising, 'dp', [(device, device + 2) for device in range(size...  64.5 us
    pallas_call x5, Pallas kernels, grad_blocks(): pl.pallas_call(functools.partial(grad_kernel, len(pairs), other is not No...  53.1 us
    pallas_call x1, Pallas kernels, attention_backward(): pl.pallas_call(functools.partial(attention_backward_kernel, size, groupin...  44.5 us
    pallas_call x2, Pallas kernels, feed_half(): pl.pallas_call(functools.partial(feed_half_kernel, half, tile, block), ou...  33.9 us
    pallas_call x1, Pallas kernels, attention_forward(): pl.pallas_call(functools.partial(attention_forward_kernel, grouping, head...  18.5 us
  transfers between devices with their start and end apart: 11, of which 6 were waited for; matrix products, arithmetic and copies ran while one was open for 1% of the time, Pallas kernels for 65%

profile of v15, /device:TPU:0, one launch (start us, length us, event | category | flops | bytes accessed | tf_op | source)
XLA Modules:
  0.0 642.3 jit_solution(15447515333795186275)
XLA Ops:
  7.2 0.0 all-gather.4.cloned.1.call-start
  7.2 2.2 shard_map.246
  9.4 0.0 all-gather.4.cloned.1.call-update
  9.4 0.0 all-gather.6.cloned.1.call-start
  9.5 3.4 shard_map.248
  12.9 0.0 all-gather.8.cloned.1.call-start
  13.0 0.7 all-gather.8.cloned.1.call-update
  13.6 0.0 reduce-scatter.4.cloned.1.call-start
  13.7 0.3 fusion
  14.0 1.3 fusion.2.refs_0_
  15.3 76.6 %gather_rows.1 = (bf16[1024,2048]{1,0:T(8,128)(2,1)}, bf16[2048,1024]{1,0:T(8,128)(2,1)}, bf16[1024,2048]{1,0:T(8,128)(2,1)}, bf16[2048,1024]{1,0:T(8,128)(2,1)}) custom-call(bf16[256,2048]{1,0:T(8,128)(2,1)} %fusion.2.refs_0_, bf16[256,2048]{1,0:T(8,128)(2,1)} %refs_5_.1), custom_call_target="tpu_custom_call" | custom-call | bytes 125829120 | tf_op jit(solution)/shard_map/gather_rows/pallas_call | solution.py:209
  91.9 0.5 broadcast_add_fusion.order_ref
  92.4 18.5 %attention_forward.1 = (f32[1024,1024]{1,0:T(8,128)}, bf16[1024,512]{1,0:T(8,128)(2,1)}, f32[2,2,1024]{2,1,0:T(2,128)}) custom-call(bf16[1024,2048]{1,0:T(8,128)(2,1)} %get-tuple-element.70.rows_ref.refs_6_, bf16[2048,1536]{1,0:T(8,128)(2,1)} %all-gather.4.cloned.1.call-done.weight_ref.refs_1_.refs_5_, f32[136,128]{1,0:T(8,128)} %constant.38.clone.few_cosines_ref.refs_9_, ...), custom_call_target="tpu_custom_call" | custom-call | flops 5368709120 | bytes 8388608 | tf_op jit(solution)/shard_map/attention_forward/pallas_call | solution.py:878
  110.9 75.1 %shard_map.247 = (bf16[1024,2048]{1,0:T(8,128)(2,1)}, bf16[2048,1024]{1,0:T(8,128)(2,1)}, f32[256,2048]{1,0:T(8,128)}) custom-call(bf16[1024,512]{1,0:T(8,128)(2,1)} %get-tuple-element.71.refs_0_.refs_1_.refs_7_, bf16[2048,1536]{1,0:T(8,128)(2,1)} %all-gather.4.cloned.1.call-done.weight_ref.refs_1_.refs_5_, bf16[256,2048]{1,0:T(8,128)(2,1)} %refs_2_.3, ...), custom_call_target="tpu_custom_call" | custom-call | flops 2147483648 | bytes 150000000 | tf_op jit(solution)/shard_map/pallas_call | solution.py:743
  185.9 9.3 %all-gather.6.cloned.1.call-done.weight_far.refs_1_ = bf16[2048,3072]{1,0:T(8,128)(2,1)} async-done(((bf16[256,3072]{1,0:T(8,128)(2,1)}), bf16[2048,3072]{1,0:T(8,128)(2,1)}) %all-gather.6.cloned.1.call-update) | async-done | bytes 12582928 | tf_op jit(solution)/shard_map/all_gather | solution.py:1481
  195.3 22.0 %feed_half.2 = (bf16[1024,1024]{1,0:T(8,128)(2,1)}, bf16[1024,2048]{1,0:T(8,128)(2,1)}) custom-call(bf16[1024,2048]{1,0:T(8,128)(2,1)} %get-tuple-element.73.rows_far, bf16[1024,2048]{1,0:T(8,128)(2,1)} %get-tuple-element.74.cotangent_far, bf16[2048,3072]{1,0:T(8,128)(2,1)} %all-gather.6.cloned.1.call-done.weight_far.refs_1_), custom_call_target="tpu_custom_call" | custom-call | flops 12884901888 | bytes 20971520 | tf_op jit(solution)/shard_map/feed_half/pallas_call | solution.py:1187
  217.3 12.4 %grad_blocks.5 = bf16[4,256,3072]{2,1,0:T(8,128)(2,1)} custom-call(s32[4]{0:T(128)} %broadcast_add_fusion.order_ref, bf16[2048,1024]{1,0:T(8,128)(2,1)} %get-tuple-element.72.refs_0_, bf16[1024,2048]{1,0:T(8,128)(2,1)} %get-tuple-element.76.refs_1_.refs_0_, bf16[2048,1024]{1,0:T(8,128)(2,1)} %get-tuple-element.77.refs_2_, ...), custom_call_target="tpu_custom_call" | custom-call | flops 6442450944 | bytes 16777216 | tf_op jit(solution)/shard_map/grad_blocks/pallas_call | solution.py:1280
  229.7 0.3 collective-permute-start
  229.9 0.5 broadcast_add_fusion.1.order_ref
  230.5 10.3 %collective-permute-done.refs_4_ = bf16[4,256,3072]{2,1,0:T(8,128)(2,1)} collective-permute-done((bf16[4,256,3072]{2,1,0:T(8,128)(2,1)}, bf16[4,256,3072]{2,1,0:T(8,128)(2,1)}, u32[]{:S(2)}, u32[]{:S(2)}) %collective-permute-start) | collective-permute-done | bytes 6291488 | tf_op jit(solution)/shard_map/ppermute | solution.py:1307
  240.8 13.6 %grad_blocks.6 = (bf16[256,3072]{1,0:T(8,128)(2,1)}, bf16[256,3072]{1,0:T(8,128)(2,1)}, bf16[256,3072]{1,0:T(8,128)(2,1)}, bf16[256,3072]{1,0:T(8,128)(2,1)}) custom-call(s32[4]{0:T(128)} %broadcast_add_fusion.1.order_ref, bf16[2048,1024]{1,0:T(8,128)(2,1)} %get-tuple-element.72.refs_0_, bf16[1024,2048]{1,0:T(8,128)(2,1)} %get-tuple-element.76.refs_1_.refs_0_, ...), custom_call_target="tpu_custom_call" | custom-call | flops 6442450944 | bytes 16777216 | tf_op jit(solution)/shard_map/grad_blocks/pallas_call | solution.py:1280
  254.4 5.5 all-gather.8.cloned.1.call-done.weight_far.refs_3_
  259.9 12.0 %feed_half.3 = (bf16[1024,512]{1,0:T(8,128)(2,1)}, bf16[1024,1024]{1,0:T(8,128)(2,1)}) custom-call(bf16[1024,2048]{1,0:T(8,128)(2,1)} %get-tuple-element.73.rows_far, bf16[1024,2048]{1,0:T(8,128)(2,1)} %get-tuple-element.74.cotangent_far, bf16[2048,1536]{1,0:T(8,128)(2,1)} %all-gather.8.cloned.1.call-done.weight_far.refs_3_), custom_call_target="tpu_custom_call" | custom-call | flops 6442450944 | bytes 14680064 | tf_op jit(solution)/shard_map/feed_half/pallas_call | solution.py:1187
  271.9 0.5 iota.11.order_ref
  272.4 12.2 %grad_blocks.7 = bf16[8,256,1536]{2,1,0:T(8,128)(2,1)} custom-call(s32[8]{0:T(128)} %iota.11.order_ref, bf16[2048,1024]{1,0:T(8,128)(2,1)} %get-tuple-element.72.refs_0_, bf16[1024,1024]{1,0:T(8,128)(2,1)} %get-tuple-element.88.refs_1_.refs_2_, bf16[2048,1024]{1,0:T(8,128)(2,1)} %get-tuple-element.77.refs_2_, bf16[1024,512]{1,0:T(8,128)(2,1)} %get-tuple-element.87.refs_3_.refs_2_), custom_call_target="tpu_custom_call" | custom-call | flops 6442450944 | bytes 17825792 | tf_op jit(solution)/shard_map/grad_blocks/pallas_call | solution.py:1280
  284.6 0.0 reduce-scatter.8.cloned.1.call-start
  284.6 1.3 copy-done.5
  286.0 0.7 collective-permute-start.2
  286.7 1.4 collective-permute-start.1
  288.2 67.8 %collective-permute-done.1.refs_9_ = bf16[256,3072]{1,0:T(8,128)(2,1)S(1)} collective-permute-done((bf16[256,3072]{1,0:T(8,128)(2,1)S(1)}, bf16[256,3072]{1,0:T(8,128)(2,1)S(1)}, u32[]{:S(2)}, u32[]{:S(2)}) %collective-permute-start.1) | collective-permute-done | bytes 1572896 | tf_op jit(solution)/shard_map/ppermute | solution.py:1313
  356.0 1.2 copy-done.8
  357.2 86.3 %shard_map.249 = (bf16[1024,2048]{1,0:T(8,128)(2,1)}, bf16[2048,1024]{1,0:T(8,128)(2,1)}, f32[256,2048]{1,0:T(8,128)}, f32[16,128]{1,0:T(8,128)}, bf16[256,3072]{1,0:T(8,128)(2,1)}, /*index=5*/bf16[256,3072]{1,0:T(8,128)(2,1)}) custom-call(bf16[1024,2048]{1,0:T(8,128)(2,1)} %get-tuple-element.76.refs_1_.refs_0_, ...), custom_call_target="tpu_custom_call" | custom-call | flops 12884901888 | bytes 150000000 | tf_op jit(solution)/shard_map/pallas_call | solution.py:743
  443.4 0.5 iota.12.order_ref
  443.9 6.0 grad_blocks.8
  450.0 0.0 reduce-scatter.6.cloned.1.call-start
  450.0 44.5 %attention_backward.1 = (bf16[1024,1024]{1,0:T(8,128)(2,1)}, f32[8,128]{1,0:T(8,128)}, bf16[256,2048]{1,0:T(8,128)(2,1)}) custom-call(bf16[1024,1024]{1,0:T(8,128)(2,1)} %get-tuple-element.78.refs_3_.refs_0_, bf16[2048,3072]{1,0:T(8,128)(2,1)} %all-gather.6.cloned.1.call-done.weight_far.refs_1_, bf16[1024,512]{1,0:T(8,128)(2,1)} %get-tuple-element.87.refs_3_.refs_2_, ...), custom_call_target="tpu_custom_call" | custom-call | flops 4831838208 | bytes 100000000 | tf_op jit(solution)/shard_map/attention_backward/pallas_call | solution.py:1060
  494.6 0.5 iota.13.order_ref
  495.1 8.9 %grad_blocks.9 = bf16[8,256,1024]{2,1,0:T(8,128)(2,1)} custom-call(s32[8]{0:T(128)} %iota.13.order_ref, bf16[2048,1024]{1,0:T(8,128)(2,1)} %get-tuple-element.103.refs_0_, bf16[1024,1024]{1,0:T(8,128)(2,1)} %get-tuple-element.109.refs_1_.refs_0_), custom_call_target="tpu_custom_call" | custom-call | flops 4294967296 | bytes 10485760 | tf_op jit(solution)/shard_map/grad_blocks/pallas_call | solution.py:1280
  504.1 5.2 collective-permute-start.3
  509.3 1.3 collective-permute-start.4
  510.6 0.6 pad_maximum_fusion.refs_5_
  511.2 64.5 %collective-permute-done.3.up_ref = bf16[256,3072]{1,0:T(8,128)(2,1)S(1)} collective-permute-done((bf16[256,3072]{1,0:T(8,128)(2,1)}, bf16[256,3072]{1,0:T(8,128)(2,1)S(1)}, u32[]{:S(2)}, u32[]{:S(2)}) %collective-permute-start.3) | collective-permute-done | bytes 1572896 | tf_op jit(solution)/shard_map/ppermute | solution.py:1560
  575.7 8.0 %collective-permute-done.4.down_ref = bf16[256,3072]{1,0:T(8,128)(2,1)} collective-permute-done((bf16[256,3072]{1,0:T(8,128)(2,1)}, bf16[256,3072]{1,0:T(8,128)(2,1)}, u32[]{:S(2)}, u32[]{:S(2)}) %collective-permute-start.4) | collective-permute-done | bytes 1572896 | tf_op jit(solution)/shard_map/ppermute | solution.py:1563
  583.7 5.8 shard_map.250
  589.5 42.8 %shard_map.251 = (bf16[256,2048]{1,0:T(8,128)(2,1)}, f32[40,128]{1,0:T(8,128)}) custom-call(bf16[1024,1024]{1,0:T(8,128)(2,1)} %get-tuple-element.109.refs_1_.refs_0_, bf16[2048,1536]{1,0:T(8,128)(2,1)} %all-gather.4.cloned.1.call-done.weight_ref.refs_1_.refs_5_, bf16[256,2048]{1,0:T(8,128)(2,1)} %refs_2_.3, f32[1,2048]{1,0:T(1,128)} %bitcast.16, ...), custom_call_target="tpu_custom_call" | custom-call | flops 4294967296 | bytes 150000000 | tf_op jit(solution)/shard_map/pallas_call | solution.py:743
  632.3 0.0 reduce-scatter.8.cloned.1.call-done.refs_1_
  632.3 0.0 reduce-scatter.6.cloned.1.call-done.refs_0_
  632.4 3.1 shard_map.252
  (24 shorter events, 0.1 us)
Async XLA Ops:
  7.2 85.2 %all-gather.4.cloned.1.call-start = ((), (), s32[]{:S(2)}) async-start(), calls=%async_computation.3 | async-start | bytes 7077888 | tf_op jit(solution)/shard_map/all_gather | solution.py:1472
  9.4 4.3 copy-start
  9.4 185.9 %all-gather.6.cloned.1.call-start = ((), (), s32[]{:S(2)}) async-start(), calls=%async_computation.4 | async-start | bytes 14155776 | tf_op jit(solution)/shard_map/all_gather | solution.py:1481
  12.9 1.1 copy-start.2
  12.9 247.0 %all-gather.8.cloned.1.call-start = ((), (), s32[]{:S(2)}) async-start(), calls=%async_computation.5 | async-start | bytes 7077888 | tf_op jit(solution)/shard_map/all_gather | solution.py:1481
  13.6 570.0 %reduce-scatter.4.cloned.1.call-start = ((), (), s32[]{:S(2)}) async-start(), calls=%async_computation.6 | async-start | bytes 7077888 | tf_op jit(solution)/shard_map/reduce_scatter | solution.py:1530
  229.7 11.1 %collective-permute-start = (bf16[4,256,3072]{2,1,0:T(8,128)(2,1)}, bf16[4,256,3072]{2,1,0:T(8,128)(2,1)}, u32[]{:S(2)}, u32[]{:S(2)}) collective-permute-start(bf16[4,256,3072]{2,1,0:T(8,128)(2,1)} %grad_blocks.5), channel_id=1, source_target_pairs={{0,4},{4,0},{8,12},{12,8},{16,20},{20,16},{24,28},{28,24},{1,5},{5... | collective-permute-start | bytes 18874376 | tf_op jit(solution)/shard_map/ppermute | solution.py:1307
  284.6 1.4 copy-start.5
  284.6 2.2 copy-start.6
  284.6 347.8 %reduce-scatter.8.cloned.1.call-start = ((), (), s32[]{:S(2)}) async-start(), calls=%async_computation.8 | async-start | bytes 2359296 | tf_op jit(solution)/shard_map/reduce_scatter | solution.py:1568
  286.0 2.2 collective-permute-start.2
  286.7 69.2 %collective-permute-start.1 = (bf16[256,3072]{1,0:T(8,128)(2,1)S(1)}, bf16[256,3072]{1,0:T(8,128)(2,1)S(1)}, u32[]{:S(2)}, u32[]{:S(2)}) collective-permute-start(bf16[256,3072]{1,0:T(8,128)(2,1)S(1)} %copy-done.6), channel_id=1, source_target_pairs={{0,8},{4,12},{1,9},{5,13},{2,10},{6,14},{3,11},{7,15}} | collective-permute-start | bytes 4718600 | tf_op jit(solution)/shard_map/ppermute | solution.py:1313
  288.2 67.8 %copy-start.7 = (bf16[256,3072]{1,0:T(8,128)(2,1)}, bf16[256,3072]{1,0:T(8,128)(2,1)S(1)}, u32[]{:S(2)}) copy-start(bf16[256,3072]{1,0:T(8,128)(2,1)S(1)} %collective-permute-done.2.refs_10_) | copy-start | bytes 4718596
  356.0 1.2 copy-start.8
  450.0 182.4 %reduce-scatter.6.cloned.1.call-start = ((), (), s32[]{:S(2)}) async-start(), calls=%async_computation.7 | async-start | bytes 4718592 | tf_op jit(solution)/shard_map/reduce_scatter | solution.py:1580
  504.0 6.6 %copy-start.3 = (f32[16,128]{1,0:T(8,128)S(1)}, f32[16,128]{1,0:T(8,128)}, u32[]{:S(2)}) copy-start(f32[16,128]{1,0:T(8,128)} %get-tuple-element.111) | copy-start | bytes 24580
  504.0 6.6 %copy-start.4 = (f32[8,128]{1,0:T(8,128)S(1)}, f32[8,128]{1,0:T(8,128)}, u32[]{:S(2)}) copy-start(f32[8,128]{1,0:T(8,128)} %get-tuple-element.112) | copy-start | bytes 12292
  504.1 71.6 %collective-permute-start.3 = (bf16[256,3072]{1,0:T(8,128)(2,1)}, bf16[256,3072]{1,0:T(8,128)(2,1)S(1)}, u32[]{:S(2)}, u32[]{:S(2)}) collective-permute-start(bf16[256,3072]{1,0:T(8,128)(2,1)} %get-tuple-element.93), channel_id=1, source_target_pairs={{0,8},{4,12},{8,16},{12,20},{16,24},{20,28},{1,9},{5,13},{9,17},{1... | collective-permute-start | bytes 4718600 | tf_op jit(solution)/shard_map/ppermute | solution.py:1560
  509.3 74.4 %collective-permute-start.4 = (bf16[256,3072]{1,0:T(8,128)(2,1)}, bf16[256,3072]{1,0:T(8,128)(2,1)}, u32[]{:S(2)}, u32[]{:S(2)}) collective-permute-start(bf16[256,3072]{1,0:T(8,128)(2,1)} %get-tuple-element.94), channel_id=1, source_target_pairs={{8,0},{12,4},{16,8},{20,12},{24,16},{28,20},{9,1},{13,5},{17,9},{2... | collective-permute-start | bytes 4718600 | tf_op jit(solution)/shard_map/ppermute | solution.py:1563
  575.7 8.0 %copy-start.1 = (bf16[256,3072]{1,0:T(8,128)(2,1)}, bf16[256,3072]{1,0:T(8,128)(2,1)S(1)}, u32[]{:S(2)}) copy-start(bf16[256,3072]{1,0:T(8,128)(2,1)S(1)} %collective-permute-done.3.up_ref) | copy-start | bytes 4718596
Sparse Core Ops, SparseCore 0:
  10.2 67.4 all-gather.3
  79.9 115.3 all-gather.5
  196.9 62.8 all-gather.7
  284.7 114.2 reduce-scatter.3
  450.1 35.8 reduce-scatter.7
  504.2 79.8 reduce-scatter.5
